TPU v7x, 32 devices: a whole 2x2x4 slice. The times are simulated.
32 devices in a mesh: seq: 8 (over y, x, core), fsdp: 4 (over z).
Axes of the slice: x: 2, y: 2, z: 4, core: 2. Of those that a mesh axis runs over, the one named last changes fastest.
Arguments:
- inputs: bfloat16 [4, 1024, 2048], P('fsdp', 'seq'), may hold values from -6 to 6
- cotangent: bfloat16 [4, 1024, 2048], P('fsdp', 'seq'), may hold values from -6 to 6
- attention_gain: float32 [2048], replicated, may hold values from 0.5 to 1.5
- query_weight: bfloat16 [2048, 2048], P('fsdp'), may hold values from -0.125 to 0.125
- key_weight: bfloat16 [2048, 512], P('fsdp'), may hold values from -0.125 to 0.125
- value_weight: bfloat16 [2048, 512], P('fsdp'), may hold values from -0.125 to 0.125
- output_weight: bfloat16 [2048, 2048], P('fsdp'), may hold values from -1 to 1
- query_gain: float32 [64], replicated, may hold values from 0.5 to 1.5
- key_gain: float32 [64], replicated, may hold values from 0.5 to 1.5
- feedforward_gain: float32 [2048], replicated, may hold values from 0.5 to 1.5
- gate_weight: bfloat16 [2048, 8192], P(None, 'fsdp'), may hold values from -0.125 to 0.125
- up_weight: bfloat16 [2048, 8192], P(None, 'fsdp'), may hold values from -0.125 to 0.125
- down_weight: bfloat16 [2048, 8192], P(None, 'fsdp'), may hold values from -0.0625 to 0.0625
Outputs:
- block_out: bfloat16 [4, 1024, 2048], P('fsdp', 'seq')
- input_grad: bfloat16 [4, 1024, 2048], P('fsdp', 'seq')
- attention_slope: float32 [2048], replicated
- grad_query: float32 [2048, 2048], P('fsdp')
- grad_key: float32 [2048, 512], P('fsdp')
- grad_value: float32 [2048, 512], P('fsdp')
- grad_output: float32 [2048, 2048], P('fsdp')
- query_slope: float32 [64], replicated
- key_slope: float32 [64], replicated
- feedforward_slope: float32 [2048], replicated
- grad_gate: float32 [2048, 8192], P(None, 'fsdp')
- grad_up: float32 [2048, 8192], P(None, 'fsdp')
- grad_down: float32 [2048, 8192], P(None, 'fsdp')
All inputs are finite; a program needn't handle non-finite values.
Results may differ from a plain program's by a relative error of at most 0.022.
Values may be sent and summed in bfloat16 or wider, within the bound.
A program may use at most 320 MiB of HBM per device.

v0:
```python
import jax
import jax.numpy as jnp
from jax import lax
from jax.sharding import PartitionSpec as P

EPS = 1e-05
THETA = 1000000.0


def rotate_half(values):
    half = values.shape[-1] // 2
    return jnp.concatenate([-values[..., half:], values[..., :half]], axis=-1)


def rope_tables(positions, width):
    exponents = jnp.arange(width // 2).astype(jnp.float32) * 2.0 / width
    rates = jnp.power(jnp.float32(THETA), -exponents)
    angle = positions.astype(jnp.float32)[:, None] * rates[None, :]
    angle = jnp.concatenate([angle, angle], axis=-1)
    return (jnp.cos(angle), jnp.sin(angle))


def prepare(proj, gain, cosine, sine):
    rows = proj.shape[0]
    width = gain.shape[0]
    split = proj.reshape(rows, -1, width)
    factor = lax.rsqrt(jnp.mean(split * split, axis=-1, keepdims=True) + EPS)
    normed = split * factor * gain
    turned = normed * cosine[:, None, :] + rotate_half(normed) * sine[:, None, :]
    return turned.reshape(rows, -1)


def matmul(left, right):
    return jnp.dot(left, right, preferred_element_type=jnp.float32)


def inner_rows(left, right):
    return lax.dot_general(
        left, right, (((0,), (0,)), ((), ())), preferred_element_type=jnp.float32
    )


def inner_cols(left, right):
    return lax.dot_general(
        left, right, (((1,), (1,)), ((), ())), preferred_element_type=jnp.float32
    )


def rms_factor(values):
    return lax.rsqrt(jnp.mean(values * values, axis=-1, keepdims=True) + EPS)


def norm_back(grad, values, factor, gain):
    scaled = grad * gain
    return factor * (
        scaled - values * factor * factor * jnp.mean(scaled * values, axis=-1, keepdims=True)
    )


def gate_back(hidden_grad, gate, lifted):
    sigma = jax.nn.sigmoid(gate)
    gate_grad = (hidden_grad * lifted * sigma * (1.0 + gate * (1.0 - sigma))).astype(jnp.bfloat16)
    lifted_grad = (hidden_grad * gate * sigma).astype(jnp.bfloat16)
    return (gate_grad, lifted_grad)


def activate(gate, lifted):
    return (gate * jax.nn.sigmoid(gate) * lifted).astype(jnp.bfloat16)


def split_heads(query_rows, pair_rows, groups, width):
    length = query_rows.shape[0]
    key_heads = pair_rows.shape[1] // (2 * width)
    queries = query_rows.reshape(length, key_heads, groups, width)
    keys = pair_rows[:, : key_heads * width].reshape(length, key_heads, width)
    values = pair_rows[:, key_heads * width :].reshape(length, key_heads, width)
    return (queries, keys, values, key_heads)


def attend_heads(query_rows, pair_rows, groups, width):
    length = query_rows.shape[0]
    queries, keys, values, key_heads = split_heads(query_rows, pair_rows, groups, width)
    block = min(512, length)
    scale = width ** (-0.5)
    offsets = jnp.arange(block)

    def query_step(index, state):
        out_rows, log_rows = state
        query_block = lax.dynamic_slice_in_dim(queries, index * block, block, 0)

        def key_step(inner, carry):
            summed, total = carry
            key_block = lax.dynamic_slice_in_dim(keys, inner * block, block, 0)
            value_block = lax.dynamic_slice_in_dim(values, inner * block, block, 0)
            scores = (
                jnp.einsum(
                    "qhgd,shd->hgqs", query_block, key_block, preferred_element_type=jnp.float32
                )
                * scale
            )
            allowed = (index * block + offsets)[:, None] >= (inner * block + offsets)[None, :]
            weights = jnp.where(allowed, jnp.exp(scores), 0.0)
            summed = summed + jnp.einsum(
                "hgqs,shd->hgqd",
                weights.astype(jnp.bfloat16),
                value_block,
                preferred_element_type=jnp.float32,
            )
            return (summed, total + jnp.sum(weights, axis=-1))

        initial = (
            jnp.zeros((key_heads, groups, block, width), jnp.float32),
            jnp.zeros((key_heads, groups, block), jnp.float32),
        )
        summed, total = lax.fori_loop(0, index + 1, key_step, initial)
        result = (summed / total[..., None]).astype(jnp.bfloat16)
        result = result.transpose(2, 0, 1, 3).reshape(block, key_heads * groups * width)
        out_rows = lax.dynamic_update_slice_in_dim(out_rows, result, index * block, 0)
        log_rows = lax.dynamic_update_slice_in_dim(log_rows, jnp.log(total), index * block, 2)
        return (out_rows, log_rows)

    start = (
        jnp.zeros((length, key_heads * groups * width), jnp.bfloat16),
        jnp.zeros((key_heads, groups, length), jnp.float32),
    )
    return lax.fori_loop(0, length // block, query_step, start)


def attend_back(query_rows, pair_rows, out_rows, log_rows, grad_rows, groups, width):
    length = query_rows.shape[0]
    queries, keys, values, key_heads = split_heads(query_rows, pair_rows, groups, width)
    outs = out_rows.reshape(length, key_heads, groups, width)
    grads = grad_rows.reshape(length, key_heads, groups, width)
    correction = jnp.sum(grads.astype(jnp.float32) * outs.astype(jnp.float32), axis=-1)
    block = min(512, length)
    scale = width ** (-0.5)
    offsets = jnp.arange(block)

    def query_step(index, state):
        query_grad, key_grad, value_grad = state
        query_block = lax.dynamic_slice_in_dim(queries, index * block, block, 0)
        grad_block = lax.dynamic_slice_in_dim(grads, index * block, block, 0)
        shift_block = lax.dynamic_slice_in_dim(correction, index * block, block, 0).transpose(
            1, 2, 0
        )
        log_block = lax.dynamic_slice_in_dim(log_rows, index * block, block, 2)

        def key_step(inner, carry):
            block_grad, key_sum, value_sum = carry
            key_block = lax.dynamic_slice_in_dim(keys, inner * block, block, 0)
            value_block = lax.dynamic_slice_in_dim(values, inner * block, block, 0)
            scores = (
                jnp.einsum(
                    "qhgd,shd->hgqs", query_block, key_block, preferred_element_type=jnp.float32
                )
                * scale
            )
            allowed = (index * block + offsets)[:, None] >= (inner * block + offsets)[None, :]
            weights = jnp.where(allowed, jnp.exp(scores - log_block[..., None]), 0.0)
            value_part = jnp.einsum(
                "hgqs,qhgd->shd",
                weights.astype(jnp.bfloat16),
                grad_block,
                preferred_element_type=jnp.float32,
            )
            prob_grad = jnp.einsum(
                "qhgd,shd->hgqs", grad_block, value_block, preferred_element_type=jnp.float32
            )
            score_grad = (weights * (prob_grad - shift_block[..., None]) * scale).astype(
                jnp.bfloat16
            )
            block_grad = block_grad + jnp.einsum(
                "hgqs,shd->qhgd", score_grad, key_block, preferred_element_type=jnp.float32
            )
            key_part = jnp.einsum(
                "hgqs,qhgd->shd", score_grad, query_block, preferred_element_type=jnp.float32
            )
            key_sum = lax.dynamic_update_slice_in_dim(
                key_sum,
                lax.dynamic_slice_in_dim(key_sum, inner * block, block, 0) + key_part,
                inner * block,
                0,
            )
            value_sum = lax.dynamic_update_slice_in_dim(
                value_sum,
                lax.dynamic_slice_in_dim(value_sum, inner * block, block, 0) + value_part,
                inner * block,
                0,
            )
            return (block_grad, key_sum, value_sum)

        initial = (jnp.zeros((block, key_heads, groups, width), jnp.float32), key_grad, value_grad)
        block_grad, key_grad, value_grad = lax.fori_loop(0, index + 1, key_step, initial)
        query_grad = lax.dynamic_update_slice_in_dim(query_grad, block_grad, index * block, 0)
        return (query_grad, key_grad, value_grad)

    state = (
        jnp.zeros((length, key_heads, groups, width), jnp.float32),
        jnp.zeros((length, key_heads, width), jnp.float32),
        jnp.zeros((length, key_heads, width), jnp.float32),
    )
    query_grad, key_grad, value_grad = lax.fori_loop(0, length // block, query_step, state)
    pair_grad = jnp.concatenate(
        [
            key_grad.reshape(length, key_heads * width),
            value_grad.reshape(length, key_heads * width),
        ],
        axis=1,
    )
    return (query_grad.reshape(length, key_heads * groups * width), pair_grad)


def per_device(
    inputs,
    cotangent,
    attention_gain,
    query_weight,
    key_weight,
    value_weight,
    output_weight,
    query_gain,
    key_gain,
    feedforward_gain,
    gate_weight,
    up_weight,
    down_weight,
):
    tokens = inputs.shape[1]
    model = inputs.shape[2]
    width = query_gain.shape[0]
    heads = query_weight.shape[1] // width
    pair_heads = key_weight.shape[1] // width
    parts = lax.axis_size("seq")
    copies = max(1, parts // pair_heads)
    local_pairs = pair_heads * copies // parts
    local_heads = heads // parts
    local_groups = local_heads // local_pairs
    rows_in = inputs.reshape(tokens, model)
    cot_rows = cotangent.reshape(tokens, model)
    full_query, full_key, full_value, full_output = (
        lax.all_gather(query_weight, "fsdp", axis=0, tiled=True),
        lax.all_gather(key_weight, "fsdp", axis=0, tiled=True),
        lax.all_gather(value_weight, "fsdp", axis=0, tiled=True),
        lax.all_gather(output_weight, "fsdp", axis=0, tiled=True),
    )
    source = rows_in.astype(jnp.float32)
    first = rms_factor(source)
    normed_in = (source * first * attention_gain).astype(jnp.bfloat16)
    query_proj = matmul(normed_in, full_query)
    key_proj = matmul(normed_in, full_key)
    values = matmul(normed_in, full_value).astype(jnp.bfloat16)
    positions = lax.axis_index("seq") * tokens + jnp.arange(tokens, dtype=jnp.int32)
    cosine, sine = rope_tables(positions, width)
    queries = prepare(query_proj, query_gain, cosine, sine).astype(jnp.bfloat16)
    keys = prepare(key_proj, key_gain, cosine, sine).astype(jnp.bfloat16)
    key_copies = jnp.repeat(keys.reshape(tokens, pair_heads, width), copies, axis=1)
    value_copies = jnp.repeat(values.reshape(tokens, pair_heads, width), copies, axis=1)
    pair_send = jnp.concatenate([key_copies, value_copies], axis=2)
    pair_send = pair_send.reshape(tokens, parts * 2 * local_pairs * width)
    query_rows, pair_rows = (
        lax.all_to_all(queries, "seq", split_axis=1, concat_axis=0, tiled=True),
        lax.all_to_all(pair_send, "seq", split_axis=1, concat_axis=0, tiled=True),
    )
    out_rows, log_rows = attend_heads(query_rows, pair_rows, local_groups, width)
    attended = lax.all_to_all(out_rows, "seq", split_axis=0, concat_axis=1, tiled=True)
    middle = source + matmul(attended, full_output)
    second = rms_factor(middle)
    normed_mid = (middle * second * feedforward_gain).astype(jnp.bfloat16)
    mid_all, cot_all = (
        lax.all_gather(normed_mid, "fsdp", axis=0, tiled=True),
        lax.all_gather(cot_rows, "fsdp", axis=0, tiled=True),
    )
    gate = matmul(mid_all, gate_weight)
    lifted = matmul(mid_all, up_weight)
    hidden = activate(gate, lifted)
    block_rows = middle + lax.psum_scatter(
        inner_cols(hidden, down_weight).astype(jnp.bfloat16),
        "fsdp",
        scatter_dimension=0,
        tiled=True,
    ).astype(jnp.float32)
    hidden_grad = matmul(cot_all, down_weight)
    gate_grad, lifted_grad = gate_back(hidden_grad, gate, lifted)
    grad_gate = inner_rows(mid_all, gate_grad)
    grad_up = inner_rows(mid_all, lifted_grad)
    grad_down = inner_rows(cot_all, hidden)
    mid_grad = lax.psum_scatter(
        (inner_cols(gate_grad, gate_weight) + inner_cols(lifted_grad, up_weight)).astype(
            jnp.bfloat16
        ),
        "fsdp",
        scatter_dimension=0,
        tiled=True,
    ).astype(jnp.float32)
    feedforward_slope = jnp.sum(mid_grad * middle * second, axis=0)
    middle_grad = cot_rows.astype(jnp.float32) + norm_back(
        mid_grad, middle, second, feedforward_gain
    )
    middle_half = middle_grad.astype(jnp.bfloat16)
    attended_grad = inner_cols(middle_half, full_output).astype(jnp.bfloat16)
    grad_rows = lax.all_to_all(attended_grad, "seq", split_axis=1, concat_axis=0, tiled=True)
    query_grad_rows, pair_grad_rows = attend_back(
        query_rows, pair_rows, out_rows, log_rows, grad_rows, local_groups, width
    )
    query_back, pair_back = (
        lax.all_to_all(
            query_grad_rows.astype(jnp.bfloat16), "seq", split_axis=0, concat_axis=1, tiled=True
        ).astype(query_grad_rows.dtype),
        lax.all_to_all(
            pair_grad_rows.astype(jnp.bfloat16), "seq", split_axis=0, concat_axis=1, tiled=True
        ).astype(pair_grad_rows.dtype),
    )
    pair_back = pair_back.reshape(tokens, parts, 2, local_pairs, width)
    key_back = pair_back[:, :, 0].reshape(tokens, pair_heads, copies, width).sum(axis=2)
    value_back = pair_back[:, :, 1].reshape(tokens, pair_heads, copies, width).sum(axis=2)
    key_back = key_back.reshape(tokens, pair_heads * width)
    value_back = value_back.reshape(tokens, pair_heads * width)
    _, query_pull = jax.vjp(
        lambda proj_in, gain_in: prepare(proj_in, gain_in, cosine, sine), query_proj, query_gain
    )
    query_proj_grad, query_slope = query_pull(query_back)
    _, key_pull = jax.vjp(
        lambda proj_in, gain_in: prepare(proj_in, gain_in, cosine, sine), key_proj, key_gain
    )
    key_proj_grad, key_slope = key_pull(key_back)
    query_half = query_proj_grad.astype(jnp.bfloat16)
    key_half = key_proj_grad.astype(jnp.bfloat16)
    value_half = value_back.astype(jnp.bfloat16)
    proj_grads = jnp.concatenate([query_half, key_half, value_half], axis=1)
    attn_rows_sum = lax.psum_scatter(
        jnp.concatenate(
            [inner_rows(normed_in, proj_grads), inner_rows(attended, middle_half)], axis=1
        ).astype(jnp.bfloat16),
        "fsdp",
        scatter_dimension=0,
        tiled=True,
    ).astype(jnp.float32)
    pair_width = pair_heads * width
    grad_query = attn_rows_sum[:, :model]
    grad_key = attn_rows_sum[:, model : model + pair_width]
    grad_value = attn_rows_sum[:, model + pair_width : model + 2 * pair_width]
    grad_output = attn_rows_sum[:, model + 2 * pair_width :]
    in_grad = (
        inner_cols(query_half, full_query)
        + inner_cols(key_half, full_key)
        + inner_cols(value_half, full_value)
    )
    attention_slope = jnp.sum(in_grad * source * first, axis=0)
    input_rows = (middle_grad + norm_back(in_grad, source, first, attention_gain)).astype(
        jnp.bfloat16
    )
    grad_query, grad_key, grad_value, grad_output, grad_gate, grad_up, grad_down = (
        lax.psum(grad_query.astype(jnp.bfloat16), "seq").astype(jnp.float32),
        lax.psum(grad_key.astype(jnp.bfloat16), "seq").astype(jnp.float32),
        lax.psum(grad_value.astype(jnp.bfloat16), "seq").astype(jnp.float32),
        lax.psum(grad_output.astype(jnp.bfloat16), "seq").astype(jnp.float32),
        lax.psum(grad_gate.astype(jnp.bfloat16), "seq").astype(jnp.float32),
        lax.psum(grad_up.astype(jnp.bfloat16), "seq").astype(jnp.float32),
        lax.psum(grad_down.astype(jnp.bfloat16), "seq").astype(jnp.float32),
    )
    attention_slope, query_slope, key_slope, feedforward_slope = lax.psum(
        (attention_slope, query_slope, key_slope, feedforward_slope), ("seq", "fsdp")
    )
    block_out = block_rows.astype(jnp.bfloat16).reshape(1, tokens, model)
    input_grad = input_rows.reshape(1, tokens, model)
    return (
        block_out,
        input_grad,
        attention_slope,
        grad_query,
        grad_key,
        grad_value,
        grad_output,
        query_slope,
        key_slope,
        feedforward_slope,
        grad_gate,
        grad_up,
        grad_down,
    )


def solution(mesh):
    in_specs = (
        P("fsdp", "seq", None),
        P("fsdp", "seq", None),
        P(),
        P("fsdp", None),
        P("fsdp", None),
        P("fsdp", None),
        P("fsdp", None),
        P(),
        P(),
        P(),
        P(None, "fsdp"),
        P(None, "fsdp"),
        P(None, "fsdp"),
    )
    out_specs = (
        P("fsdp", "seq", None),
        P("fsdp", "seq", None),
        P(),
        P("fsdp", None),
        P("fsdp", None),
        P("fsdp", None),
        P("fsdp", None),
        P(),
        P(),
        P(),
        P(None, "fsdp"),
        P(None, "fsdp"),
        P(None, "fsdp"),
    )
    return jax.shard_map(
        per_device, mesh=mesh, in_specs=in_specs, out_specs=out_specs, check_vma=False
    )
```

profile of v0, /device:TPU:0, one launch (start us, length us, event | category | flops | bytes accessed | tf_op | source)
XLA Modules:
  0.0 1514.5 jit_solution(14504645511702948431)
XLA Ops:
  10.9 47.1 %all-gather.12.cloned.1.call-done = bf16[2048,512]{1,0:T(8,128)(2,1)} async-done(((bf16[512,512]{1,0:T(8,128)(2,1)}), bf16[2048,512]{1,0:T(8,128)(2,1)}) %all-gather.12.cloned.1.call-update) | async-done | bytes 2097168 | tf_op jit(solution)/shard_map/all_gather | solution.py:243
  58.0 2.3 convolution_convert_fusion.6
  60.4 43.7 %all-gather.10.cloned.1.call-done = bf16[2048,512]{1,0:T(8,128)(2,1)} async-done(((bf16[512,512]{1,0:T(8,128)(2,1)}), bf16[2048,512]{1,0:T(8,128)(2,1)}) %all-gather.10.cloned.1.call-update) | async-done | bytes 2097168 | tf_op jit(solution)/shard_map/all_gather | solution.py:242
  104.0 2.9 copy.106
  109.3 3.7 all-to-all-start.1
  113.0 141.1 %all-gather.8.cloned.1.call-done = bf16[2048,2048]{1,0:T(8,128)(2,1)} async-done(((bf16[512,2048]{1,0:T(8,128)(2,1)}), bf16[2048,2048]{1,0:T(8,128)(2,1)}) %all-gather.8.cloned.1.call-update) | async-done | bytes 8388624 | tf_op jit(solution)/shard_map/all_gather | solution.py:241
  254.1 12.2 copy.104
  266.3 5.9 multiply_reduce_fusion.3
  274.3 3.7 all-to-all-start
  279.8 7.8 all-to-all-done
  288.3 10.7 while.105
  288.4 3.4 while.108
  290.0 1.8 fusion.213
  292.1 6.8 while.108
  292.3 1.3 fusion.212
  293.6 1.8 fusion.213
  295.7 1.3 fusion.212
  297.0 1.8 fusion.213
  299.2 12.1 all_to_all.84
  311.6 116.8 %all-gather.14.cloned.1.call-done = bf16[2048,2048]{1,0:T(8,128)(2,1)} async-done(((bf16[512,2048]{1,0:T(8,128)(2,1)}), bf16[2048,2048]{1,0:T(8,128)(2,1)}) %all-gather.14.cloned.1.call-update) | async-done | bytes 8388624 | tf_op jit(solution)/shard_map/all_gather | solution.py:244
  428.4 4.8 multiply_reduce_fusion.2
  435.2 42.9 %all-gather.16.cloned.1.call-done = bf16[512,2048]{1,0:T(8,128)(2,1)} async-done(((bf16[128,2048]{1,0:T(8,128)(2,1)}), bf16[512,2048]{1,0:T(8,128)(2,1)}) %all-gather.16.cloned.1.call-update) | async-done | bytes 2097168 | tf_op jit(solution)/shard_map/all_gather | solution.py:270
  478.1 10.7 fusion.144
  488.8 9.4 fusion.143
  498.2 25.9 %all-gather.18.cloned.1.call-done = bf16[1,512,2048]{2,1,0:T(8,128)(2,1)} async-done(((bf16[1,128,2048]{2,1,0:T(8,128)(2,1)}), bf16[1,512,2048]{2,1,0:T(8,128)(2,1)}) %all-gather.18.cloned.1.call-update) | async-done | bytes 2097168 | tf_op jit(solution)/shard_map/all_gather | solution.py:271
  524.0 13.6 multiply_convert_fusion
  537.6 8.5 fusion.145
  546.1 9.4 add_convert_fusion
  555.8 9.9 convolution_convert_fusion.4
  565.7 32.4 %reduce-scatter.6.cloned.1.call-done = bf16[128,2048]{1,0:T(8,128)(2,1)} async-done(((bf16[512,2048]{1,0:T(8,128)(2,1)}), bf16[128,2048]{1,0:T(8,128)(2,1)}) %reduce-scatter.6.cloned.1.call-update) | async-done | bytes 524304 | tf_op jit(solution)/shard_map/reduce_scatter | solution.py:287
  598.1 2.0 fusion.103
  600.1 43.8 %reduce-scatter.4.cloned.1.call-done = bf16[128,2048]{1,0:T(8,128)(2,1)} async-done(((bf16[512,2048]{1,0:T(8,128)(2,1)}), bf16[128,2048]{1,0:T(8,128)(2,1)}) %reduce-scatter.4.cloned.1.call-update) | async-done | bytes 524304 | tf_op jit(solution)/shard_map/reduce_scatter | solution.py:276
  643.8 2.4 fusion.101
  646.3 6.6 convolution_convert_fusion.5
  653.8 3.7 all-to-all-start.3
  657.4 9.7 all-to-all-done.3
  670.6 21.1 %while.107 = (s32[]{:T(128)}, bf16[1024,1,4,64]{0,3,2,1:T(8,128)(2,1)}, f32[1024,1,64]{0,2,1:T(8,128)S(1)}, f32[1024,1,64]{0,2,1:T(8,128)S(1)}, bf16[1024,1,4,64...) while((s32[]{:T(128)}, ...), condition=%wide.region_16.0_spmd.clone.clone, body=%wide.region_13.16_spmd.clone.clone.sunk | while | flops 683082752 | bytes 25170536 | solution.py:202
  671.8 5.8 while.109
  673.8 2.5 fusion.206
  679.4 11.6 while.109
  681.4 2.5 fusion.206
  687.2 2.5 fusion.206
  692.6 3.6 all-to-all-start.5
  696.2 6.8 convolution_convert_fusion.3
  704.1 4.2 all-to-all-start.4
  708.8 9.3 all-to-all-done.4
  721.2 4.9 convolution_convert_fusion
  726.2 16.7 %pad_maximum_fusion = bf16[2048,5120]{1,0:T(8,128)(2,1)} fusion(bf16[2048,2048]{1,0:T(8,128)(2,1)} %convolution_convert_fusion.3, bf16[2048,3072]{1,0:T(8,128)(2,1)S(1)} %convolution_convert_fusion), kind=kLoop, calls=%fused_computation.77 | loop fusion | flops 41943040 | bytes 41943040 | tf_op jit(solution)/shard_map/concatenate | solution.py:331
  743.0 10.3 convert_bitcast_fusion
  753.3 7.2 convolution_convert_fusion.1
  760.5 6.8 convolution_convert_fusion.2
  767.3 320.5 %reduce-scatter.8.cloned.1.call-done = bf16[512,5120]{1,0:T(8,128)(2,1)} async-done(((bf16[2048,5120]{1,0:T(8,128)(2,1)}), bf16[512,5120]{1,0:T(8,128)(2,1)}) %reduce-scatter.8.cloned.1.call-update) | async-done | bytes 5242896 | tf_op jit(solution)/shard_map/reduce_scatter | solution.py:330
  1087.8 2.2 fusion.140
  1090.0 4.8 fusion.139
  1095.9 6.4 fusion.146
  1105.2 43.2 %all-reduce.4 = (f32[2048]{0:T(1024)}, f32[64]{0:T(128)}, f32[64]{0:T(128)}, f32[2048]{0:T(1024)}) all-reduce(f32[2048]{0:T(1024)S(1)} %get-tuple-element.885, f32[64]{0:T(128)S(1)} %get-tuple-element.881, f32[64]{0:T(128)S(1)} %get-tuple-element.887, f32[2048]{0:T(1024)S(1)} %copy-done.29), channel_id=1, replica_groups=mesh['seq'=8,'fsdp'=4] {'seq','fsdp'}, use_global_device_ids=true, to_apply=%region_21.22 | all-reduce | flops 4224 | bytes 33792 | tf_op jit(solution)/shard_map/psum | solution.py:361
  1149.5 311.9 %all-reduce.8.cloned.1.call-done = (bf16[2048,2048]{0,1:T(8,128)(2,1)}, bf16[512,2048]{1,0:T(8,128)(2,1)}, bf16[512,512]{1,0:T(8,128)(2,1)}, bf16[512,512]{1,0:T...) async-done(((bf16[2048,2048]{0,1:T(8,128)(2,1)}, bf16[512,2048]{1,0:T(8,128)(2,1)}, bf16[512,512]{1,0:T(8,128)(2,1)}, ...) | async-done | bytes 30408720 | tf_op jit(solution)/shard_map/psum | solution.py:359
  1461.5 2.3 convert_element_type.262
  1463.8 2.3 convert_element_type.263
  1466.1 2.5 convert_element_type.261
  1468.6 2.5 convert_element_type.264
  1471.1 13.0 copy.121
  1484.2 11.7 convert_element_type.266
  1495.8 11.7 convert_element_type.268
  (224 shorter events, 43.6 us)
Async XLA Ops:
  7.2 50.8 %all-gather.12.cloned.1.call-start = ((), (), s32[]{:S(2)}) async-start(), calls=%async_computation.11 | async-start | bytes 2621440 | tf_op jit(solution)/shard_map/all_gather | solution.py:243
  7.9 96.1 %all-gather.10.cloned.1.call-start = ((), (), s32[]{:S(2)}) async-start(), calls=%async_computation.10 | async-start | bytes 2621440 | tf_op jit(solution)/shard_map/all_gather | solution.py:242
  8.7 245.4 %all-gather.8.cloned.1.call-start = ((), (), s32[]{:S(2)}) async-start(), calls=%async_computation.9 | async-start | bytes 10485760 | tf_op jit(solution)/shard_map/all_gather | solution.py:241
  9.4 97.6 %copy-start.2 = (bf16[1,128,2048]{2,1,0:T(8,128)(2,1)S(1)}, bf16[1,128,2048]{2,1,0:T(8,128)(2,1)}, u32[]{:S(2)}) copy-start(bf16[1,128,2048]{2,1,0:T(8,128)(2,1)} %param.21) | copy-start | bytes 1572868
  9.4 97.6 %copy-start.22 = (f32[2048]{0:T(1024)S(1)}, f32[2048]{0:T(1024)}, u32[]{:S(2)}) copy-start(f32[2048]{0:T(1024)} %param.23) | copy-start | bytes 24580
  9.6 263.0 %copy-start.16 = (f32[128,64]{0,1:T(8,128)}, f32[128,64]{0,1:T(8,128)S(1)}, u32[]{:S(2)}) copy-start(f32[128,64]{0,1:T(8,128)S(1)} %get-tuple-element.1004) | copy-start | bytes 98308
  9.6 263.0 %copy-start.18 = (f32[128,64]{0,1:T(8,128)}, f32[128,64]{0,1:T(8,128)S(1)}, u32[]{:S(2)}) copy-start(f32[128,64]{0,1:T(8,128)S(1)} %get-tuple-element.1005) | copy-start | bytes 98308
  10.9 255.4 %copy-start.32 = (f32[128]{0:T(128)}, f32[128]{0:T(128)S(1)}, u32[]{:S(2)}) copy-start(f32[128]{0:T(128)S(1)} %add_rsqrt_fusion.1) | copy-start | bytes 1540
  60.2 47.6 %copy-start.36 = (f32[64]{0:T(128)S(1)}, f32[64]{0:T(128)}, u32[]{:S(2)}) copy-start(f32[64]{0:T(128)} %param.29) | copy-start | bytes 772
  107.8 0.7 copy-start.9
  107.8 158.5 %copy-start.30 = (f32[128,8]{0,1:T(8,128)}, f32[128,8]{0,1:T(8,128)S(1)}, u32[]{:S(2)}) copy-start(f32[128,8]{0,1:T(8,128)S(1)} %get-tuple-element.1008) | copy-start | bytes 12292
  107.8 158.5 %copy-start.26 = (f32[128,8]{0,1:T(8,128)}, f32[128,8]{0,1:T(8,128)S(1)}, u32[]{:S(2)}) copy-start(f32[128,8]{0,1:T(8,128)S(1)} %fusion.137) | copy-start | bytes 12292
  109.3 165.0 %all-to-all-start.1 = ((bf16[128,8,128]{0,2,1:T(8,128)(2,1)}), bf16[128,8,128]{0,2,1:T(8,128)(2,1)S(1)}, u32[]{:S(2)}, u32[]{:S(2)}) async-start(bf16[128,8,128]{0,2,1:T(8,128)(2,1)} %pad_maximum_fusion.1), calls=%async_computation.1 | async-start | bytes 524288 | tf_op jit(solution)/shard_map/all_to_all | solution.py:262
  266.3 5.9 copy-start.34
  272.2 1.0 copy-start
  272.2 6.3 copy-start.24
  272.2 6.3 copy-start.20
  274.3 13.4 all-to-all-start
  277.9 150.4 %all-gather.14.cloned.1.call-start = ((), (), s32[]{:S(2)}) async-start(), calls=%async_computation.12 | async-start | bytes 10485760 | tf_op jit(solution)/shard_map/all_gather | solution.py:244
  278.5 199.6 %all-gather.16.cloned.1.call-start = ((), (), s32[]{:S(2)}) async-start(), calls=%async_computation.13 | async-start | bytes 2621440 | tf_op jit(solution)/shard_map/all_gather | solution.py:270
  311.6 121.5 %copy-start.6 = (bf16[128,8,256]{0,2,1:T(8,128)(2,1)}, bf16[128,8,256]{0,2,1:T(8,128)(2,1)S(1)}, u32[]{:S(2)}) copy-start(bf16[128,8,256]{0,2,1:T(8,128)(2,1)S(1)} %copy.112) | copy-start | bytes 1572868
  428.4 4.8 copy-start.28
  434.1 89.9 %all-gather.18.cloned.1.call-start = ((), (), s32[]{:S(2)}) async-start(), calls=%async_computation.17 | async-start | bytes 2621440 | tf_op jit(solution)/shard_map/all_gather | solution.py:271
  434.7 163.4 %reduce-scatter.6.cloned.1.call-start = ((), (), s32[]{:S(2)}) async-start(), calls=%async_computation.15 | async-start | bytes 2621440 | tf_op jit(solution)/shard_map/reduce_scatter | solution.py:287
  478.1 10.7 copy-start.38
  537.6 8.5 copy-start.40
  537.6 8.5 copy-start.42
  555.5 88.3 %reduce-scatter.4.cloned.1.call-start = ((), (), s32[]{:S(2)}) async-start(), calls=%async_computation.14 | async-start | bytes 2621440 | tf_op jit(solution)/shard_map/reduce_scatter | solution.py:276
  555.8 88.1 %copy-start.13 = (bf16[1,128,2048]{2,1,0:T(8,128)(2,1)S(1)}, bf16[1,128,2048]{2,1,0:T(8,128)(2,1)}, u32[]{:S(2)}) copy-start(bf16[1,128,2048]{2,1,0:T(8,128)(2,1)} %param.22) | copy-start | bytes 1572868
  646.3 6.7 copy-start.4
  653.8 13.4 all-to-all-start.3
  670.6 25.6 %copy-start.5 = (f32[128,2048]{1,0:T(8,128)S(1)}, f32[128,2048]{1,0:T(8,128)}, u32[]{:S(2)}) copy-start(f32[128,2048]{1,0:T(8,128)} %copy-done.4) | copy-start | bytes 3145732
  692.6 11.5 all-to-all-start.5
  696.2 6.9 copy-start.14
  696.2 12.1 copy-start.19
  703.1 5.4 copy-start.10
  703.1 5.4 copy-start.17
  703.1 5.4 copy-start.27
  703.1 5.4 copy-start.37
  703.1 5.5 copy-start.31
  704.1 14.0 all-to-all-start.4
  708.2 379.6 %reduce-scatter.8.cloned.1.call-start = ((), (), s32[]{:S(2)}) async-start(), calls=%async_computation.16 | async-start | bytes 26214400 | tf_op jit(solution)/shard_map/reduce_scatter | solution.py:330
  708.3 11.1 copy-start.1
  708.3 11.1 copy-start.21
  708.3 11.1 copy-start.35
  719.2 0.9 copy-start.25
  719.3 2.0 copy-start.3
  719.3 2.0 copy-start.23
  719.3 1.9 copy-start.33
  742.9 718.5 %all-reduce.8.cloned.1.call-start = ((), (), s32[]{:S(2)}) async-start(), calls=%async_computation.18 | async-start | bytes 60817408 | tf_op jit(solution)/shard_map/psum | solution.py:359
  743.0 10.4 copy-start.39
  743.0 10.4 copy-start.43
  753.3 7.2 copy-start.41
  1094.9 1.0 copy-start.8
  1095.9 6.5 copy-start.7
  1102.4 1.8 copy-start.15
  1102.4 2.8 copy-start.29
  1461.5 4.6 copy-start.12
  1463.8 4.8 copy-start.11
Sparse Core Ops, SparseCore 0:
  9.6 48.3 all-gather.11
  59.5 44.4 all-gather.9
  105.6 148.4 all-gather.7
  280.0 148.3 all-gather.13
  434.2 43.8 all-gather.15
  479.5 44.4 all-gather.17
  555.7 42.4 reduce-scatter.5
  601.0 42.8 reduce-scatter.3
  743.0 344.7 reduce-scatter.7
  1095.0 366.3 all-reduce.7
where the time goes:
time: 1530 us; the launch traced here: 1510 us
  waiting for transfers between devices  1160 us (76%)
  matrix products  152 us (10%)
  other arithmetic  66.2 us (4%)
  blocking collectives  55.3 us (4%)
  local copies, waits for them, and re-layouts  49.7 us (3%)
  starting transfers between devices  19.8 us (1%)
    reduce_scatter x1, waiting for transfers between devices, per_device(): lax.psum_scatter(jnp.concatenate([inner_rows(normed_in, proj_grads), inne...  320 us
    psum x1, waiting for transfers between devices, per_device(): lax.psum(grad_down.astype(jnp.bfloat16), 'seq').astype(jnp.float32)  312 us
    all_gather x1, waiting for transfers between devices, per_device(): lax.all_gather(query_weight, 'fsdp', axis=0, tiled=True)  141 us
    all_gather x1, waiting for transfers between devices, per_device(): lax.all_gather(output_weight, 'fsdp', axis=0, tiled=True)  117 us
    dot_general x7, matrix products, matmul(): return jnp.dot(left, right, preferred_element_type=jnp.float32)  47.3 us
    all_gather x1, waiting for transfers between devices, per_device(): lax.all_gather(value_weight, 'fsdp', axis=0, tiled=True)  47.1 us
    reduce_scatter x1, waiting for transfers between devices, per_device(): lax.psum_scatter(inner_cols(hidden, down_weight).astype(jnp.bfloat16), 'f...  43.8 us
    all_gather x1, waiting for transfers between devices, per_device(): lax.all_gather(key_weight, 'fsdp', axis=0, tiled=True)  43.7 us
  transfers between devices with their start and end apart: 15, of which 13 were waited for; matrix products, arithmetic and copies ran while one was open for 8% of the time, Pallas kernels for 0%

commit v1 on v0

--- a/solution.py
+++ b/solution.py
@@ -228,93 +228,225 @@
     tokens = inputs.shape[1]
     model = inputs.shape[2]
     width = query_gain.shape[0]
-    heads = query_weight.shape[1] // width
     pair_heads = key_weight.shape[1] // width
     parts = lax.axis_size("seq")
+    planes = lax.axis_size("fsdp")
     copies = max(1, parts // pair_heads)
-    local_pairs = pair_heads * copies // parts
-    local_heads = heads // parts
-    local_groups = local_heads // local_pairs
+    place = lax.axis_index("seq")
+    plane = lax.axis_index("fsdp")
+    core = place % 2
+    chip_bits = [1 << i for i in range(1, parts.bit_length() - 1)]
+    query_cols = model // parts
+    local_groups = query_cols // width
+    shard = query_weight.shape[0]
+    f32, bf16 = jnp.float32, jnp.bfloat16
+
+    def swap(value, bit):
+        return lax.ppermute(value, "seq", [(i, i ^ bit) for i in range(parts)])
+
+    def side(bit):
+        return (place // bit) % 2
+
+    def line_gather(value):
+        ups, downs = [value], [value]
+        for step in range(1, planes):
+            ups.append(
+                lax.ppermute(ups[-1], "fsdp", [(i, i + 1) for i in range(step - 1, planes - 1)])
+            )
+            downs.append(
+                lax.ppermute(downs[-1], "fsdp", [(i, i - 1) for i in range(1, planes - step + 1)])
+            )
+        return [value] + [
+            jnp.where(plane >= k, ups[k], downs[planes - k]) for k in range(1, planes)
+        ]
+
+    def line_scatter(slots):
+        up = down = None
+        for step in range(1, planes):
+            send_up, send_down = slots[step], slots[planes - step]
+            if step > 1:
+                send_up = (send_up.astype(f32) + up.astype(f32)).astype(bf16)
+                send_down = (send_down.astype(f32) + down.astype(f32)).astype(bf16)
+            up = lax.ppermute(send_up, "fsdp", [(i, i + 1) for i in range(step)])
+            down = lax.ppermute(
+                send_down, "fsdp", [(i, i - 1) for i in range(planes - 1, planes - 1 - step, -1)]
+            )
+        return slots[0].astype(f32) + up.astype(f32) + down.astype(f32)
+
+    def plane_gather(value):
+        half = value.shape[0] // 2
+        pieces = {}
+        for color, bits in enumerate((chip_bits, chip_bits[::-1])):
+            held = {0: value[color * half : (color + 1) * half]}
+            for bit in bits:
+                for offset, piece in list(held.items()):
+                    held[offset ^ bit] = swap(piece, bit)
+            for offset, piece in held.items():
+                pieces[(offset, color)] = piece
+                pieces[(offset ^ 1, color)] = swap(piece, 1)
+        return pieces
+
+    def by_place(pieces):
+        (half, columns) = pieces[(0, 0)].shape
+        out = jnp.zeros((parts, 2 * half, columns), pieces[(0, 0)].dtype)
+        for (offset, color), piece in pieces.items():
+            out = lax.dynamic_update_slice(out, piece[None], (place ^ offset, color * half, 0))
+        return out
+
+    def by_plane(slots):
+        out = jnp.zeros((planes,) + slots[0].shape, slots[0].dtype)
+        for k, slot in enumerate(slots):
+            out = lax.dynamic_update_slice(
+                out, slot[None], ((plane - k) % planes,) + (0,) * slot.ndim
+            )
+        return out
+
+    def half_rows(value, bit):
+        rows = value.shape[0] // 2
+        keep = lax.dynamic_slice_in_dim(value, side(bit) * rows, rows, 0)
+        give = lax.dynamic_slice_in_dim(value, (1 - side(bit)) * rows, rows, 0)
+        return keep, give
+
+    def plane_scatter(value):
+        blocks = value.reshape(parts // 2, 2, tokens, value.shape[1])
+        give = lax.dynamic_index_in_dim(blocks, 1 - core, 1, keepdims=False)
+        keep = lax.dynamic_index_in_dim(blocks, core, 1, keepdims=False)
+        keep = (keep.astype(f32) + swap(give, 1).astype(f32)).astype(bf16)
+        keep = keep.reshape(parts // 2 * tokens, value.shape[1])
+        half = value.shape[1] // 2
+        sums = []
+        for color, bits in enumerate((chip_bits[::-1], chip_bits)):
+            current = keep[:, color * half : (color + 1) * half]
+            if color == 1:
+                chips = parts // 2
+                order = current.reshape((2,) * (chips.bit_length() - 1) + (tokens, half))
+                axes = list(range(chips.bit_length() - 1))[::-1]
+                order = order.transpose(axes + [len(axes), len(axes) + 1])
+                current = order.reshape(chips * tokens, half)
+            for position, bit in enumerate(bits):
+                own, other = half_rows(current, bit)
+                current = own.astype(f32) + swap(other, bit).astype(f32)
+                if position < len(bits) - 1:
+                    current = current.astype(bf16)
+            sums.append(current)
+        return jnp.concatenate(sums, axis=1)
+
+    def chip_total(value, bits):
+        start = 0
+        current = value
+        splits = []
+        for bit in bits[:-1]:
+            keep, give = half_rows(current, bit)
+            current = (keep.astype(f32) + swap(give, bit).astype(f32)).astype(bf16)
+            splits.append((bit, start))
+            start = start + side(bit) * current.shape[0]
+        current = (current.astype(f32) + swap(current, bits[-1]).astype(f32)).astype(bf16)
+        pieces = [(start, current)]
+        for bit, base in splits[::-1]:
+            rows = sum(piece.shape[0] for _, piece in pieces)
+            mine = base + side(bit) * rows
+            theirs = base + (1 - side(bit)) * rows
+            pieces = pieces + [
+                (theirs + offset - mine, swap(piece, bit)) for offset, piece in pieces
+            ]
+        return pieces
+
+    def weight_total(value):
+        half = value.shape[0] // 2
+        columns = value.shape[1]
+        out = jnp.zeros((value.shape[0], 2 * columns), f32)
+        for color, bits in enumerate((chip_bits, chip_bits[::-1])):
+            for offset, piece in chip_total(value[color * half : (color + 1) * half], bits):
+                offset = offset + color * half
+                out = lax.dynamic_update_slice(out, piece.astype(f32), (offset, core * columns))
+                out = lax.dynamic_update_slice(
+                    out, swap_rows(piece).astype(f32), (other_core(offset), (1 - core) * columns)
+                )
+        return out
+
+    def swap_rows(piece):
+        return swap(piece, 1)
+
+    def other_core(offset):
+        return offset
+
     rows_in = inputs.reshape(tokens, model)
     cot_rows = cotangent.reshape(tokens, model)
-    full_query, full_key, full_value, full_output = (
-        lax.all_gather(query_weight, "fsdp", axis=0, tiled=True),
-        lax.all_gather(key_weight, "fsdp", axis=0, tiled=True),
-        lax.all_gather(value_weight, "fsdp", axis=0, tiled=True),
-        lax.all_gather(output_weight, "fsdp", axis=0, tiled=True),
-    )
-    source = rows_in.astype(jnp.float32)
+
+    pair_index = place // copies
+    head_weights = jnp.concatenate(
+        [
+            lax.dynamic_slice(query_weight, (0, place * query_cols), (shard, query_cols)),
+            lax.dynamic_slice(key_weight, (0, pair_index * width), (shard, width)),
+            lax.dynamic_slice(value_weight, (0, pair_index * width), (shard, width)),
+        ],
+        axis=1,
+    )
+    source = rows_in.astype(f32)
     first = rms_factor(source)
-    normed_in = (source * first * attention_gain).astype(jnp.bfloat16)
-    query_proj = matmul(normed_in, full_query)
-    key_proj = matmul(normed_in, full_key)
-    values = matmul(normed_in, full_value).astype(jnp.bfloat16)
-    positions = lax.axis_index("seq") * tokens + jnp.arange(tokens, dtype=jnp.int32)
-    cosine, sine = rope_tables(positions, width)
-    queries = prepare(query_proj, query_gain, cosine, sine).astype(jnp.bfloat16)
-    keys = prepare(key_proj, key_gain, cosine, sine).astype(jnp.bfloat16)
-    key_copies = jnp.repeat(keys.reshape(tokens, pair_heads, width), copies, axis=1)
-    value_copies = jnp.repeat(values.reshape(tokens, pair_heads, width), copies, axis=1)
-    pair_send = jnp.concatenate([key_copies, value_copies], axis=2)
-    pair_send = pair_send.reshape(tokens, parts * 2 * local_pairs * width)
-    query_rows, pair_rows = (
-        lax.all_to_all(queries, "seq", split_axis=1, concat_axis=0, tiled=True),
-        lax.all_to_all(pair_send, "seq", split_axis=1, concat_axis=0, tiled=True),
-    )
-    out_rows, log_rows = attend_heads(query_rows, pair_rows, local_groups, width)
+    normed_in = (source * first * attention_gain).astype(bf16)
+    head_full = by_plane(line_gather(head_weights)).reshape(model, -1)
+    normed_all = by_place(plane_gather(normed_in)).reshape(parts * tokens, model)
+
+    proj = matmul(normed_all, head_full)
+    query_proj = proj[:, :query_cols]
+    key_proj = proj[:, query_cols : query_cols + width]
+    values = proj[:, query_cols + width :].astype(bf16)
+    cosine, sine = rope_tables(jnp.arange(parts * tokens, dtype=jnp.int32), width)
+    queries = prepare(query_proj, query_gain, cosine, sine).astype(bf16)
+    keys = prepare(key_proj, key_gain, cosine, sine).astype(bf16)
+    pair_rows = jnp.concatenate([keys, values], axis=1)
+    out_rows, log_rows = attend_heads(queries, pair_rows, local_groups, width)
     attended = lax.all_to_all(out_rows, "seq", split_axis=0, concat_axis=1, tiled=True)
+
+    piece_rows = shard // parts
+    out_piece = lax.dynamic_slice_in_dim(output_weight, place * piece_rows, piece_rows, 0)
+    out_column = by_plane(line_gather(out_piece)).reshape(planes * piece_rows, model)
+    full_output = by_place(plane_gather(out_column)).reshape(parts, planes, piece_rows, model)
+    full_output = full_output.transpose(1, 0, 2, 3).reshape(model, model)
+
     middle = source + matmul(attended, full_output)
     second = rms_factor(middle)
-    normed_mid = (middle * second * feedforward_gain).astype(jnp.bfloat16)
-    mid_all, cot_all = (
-        lax.all_gather(normed_mid, "fsdp", axis=0, tiled=True),
-        lax.all_gather(cot_rows, "fsdp", axis=0, tiled=True),
-    )
-    gate = matmul(mid_all, gate_weight)
-    lifted = matmul(mid_all, up_weight)
+    normed_mid = (middle * second * feedforward_gain).astype(bf16)
+
+    cot_slots = line_gather(cot_rows)
+    cot_all = jnp.concatenate(cot_slots + [swap(slot, 1) for slot in cot_slots], axis=0)
+    mid_slots = line_gather(normed_mid)
+    mid_all = jnp.concatenate(mid_slots + [swap(slot, 1) for slot in mid_slots], axis=0)
+    units = gate_weight.shape[1] // 2
+    gate_half = lax.dynamic_slice_in_dim(gate_weight, core * units, units, 1)
+    up_half = lax.dynamic_slice_in_dim(up_weight, core * units, units, 1)
+    down_half = lax.dynamic_slice_in_dim(down_weight, core * units, units, 1)
+    hidden_grad = matmul(cot_all, down_half)
+    gate = matmul(mid_all, gate_half)
+    lifted = matmul(mid_all, up_half)
     hidden = activate(gate, lifted)
-    block_rows = middle + lax.psum_scatter(
-        inner_cols(hidden, down_weight).astype(jnp.bfloat16),
-        "fsdp",
-        scatter_dimension=0,
-        tiled=True,
-    ).astype(jnp.float32)
-    hidden_grad = matmul(cot_all, down_weight)
     gate_grad, lifted_grad = gate_back(hidden_grad, gate, lifted)
-    grad_gate = inner_rows(mid_all, gate_grad)
-    grad_up = inner_rows(mid_all, lifted_grad)
-    grad_down = inner_rows(cot_all, hidden)
-    mid_grad = lax.psum_scatter(
-        (inner_cols(gate_grad, gate_weight) + inner_cols(lifted_grad, up_weight)).astype(
-            jnp.bfloat16
-        ),
-        "fsdp",
-        scatter_dimension=0,
-        tiled=True,
-    ).astype(jnp.float32)
+    mine = planes * tokens
+
+    grad_down = weight_total(inner_rows(cot_all, hidden).astype(bf16))
+
+    def token_total(term):
+        keep = term[:mine] + swap(term[mine:].astype(bf16), 1).astype(f32)
+        keep = keep.astype(bf16)
+        return line_scatter([keep[k * tokens : (k + 1) * tokens] for k in range(planes)])
+
+    mid_grad = token_total(inner_cols(gate_grad, gate_half) + inner_cols(lifted_grad, up_half))
+    grad_gate = weight_total(inner_rows(mid_all, gate_grad).astype(bf16))
+    grad_up = weight_total(inner_rows(mid_all, lifted_grad).astype(bf16))
+    block_rows = middle + token_total(inner_cols(hidden, down_half))
+
     feedforward_slope = jnp.sum(mid_grad * middle * second, axis=0)
-    middle_grad = cot_rows.astype(jnp.float32) + norm_back(
-        mid_grad, middle, second, feedforward_gain
-    )
-    middle_half = middle_grad.astype(jnp.bfloat16)
-    attended_grad = inner_cols(middle_half, full_output).astype(jnp.bfloat16)
+    middle_grad = cot_rows.astype(f32) + norm_back(mid_grad, middle, second, feedforward_gain)
+    middle_half = middle_grad.astype(bf16)
+    attended_grad = inner_cols(middle_half, full_output).astype(bf16)
     grad_rows = lax.all_to_all(attended_grad, "seq", split_axis=1, concat_axis=0, tiled=True)
-    query_grad_rows, pair_grad_rows = attend_back(
-        query_rows, pair_rows, out_rows, log_rows, grad_rows, local_groups, width
-    )
-    query_back, pair_back = (
-        lax.all_to_all(
-            query_grad_rows.astype(jnp.bfloat16), "seq", split_axis=0, concat_axis=1, tiled=True
-        ).astype(query_grad_rows.dtype),
-        lax.all_to_all(
-            pair_grad_rows.astype(jnp.bfloat16), "seq", split_axis=0, concat_axis=1, tiled=True
-        ).astype(pair_grad_rows.dtype),
-    )
-    pair_back = pair_back.reshape(tokens, parts, 2, local_pairs, width)
-    key_back = pair_back[:, :, 0].reshape(tokens, pair_heads, copies, width).sum(axis=2)
-    value_back = pair_back[:, :, 1].reshape(tokens, pair_heads, copies, width).sum(axis=2)
-    key_back = key_back.reshape(tokens, pair_heads * width)
-    value_back = value_back.reshape(tokens, pair_heads * width)
+    middle_all = by_place(plane_gather(middle_half)).reshape(parts * tokens, model)
+    query_back, pair_back = attend_back(
+        queries, pair_rows, out_rows, log_rows, grad_rows, local_groups, width
+    )
+    key_back = pair_back[:, :width]
+    value_back = pair_back[:, width:]
     _, query_pull = jax.vjp(
         lambda proj_in, gain_in: prepare(proj_in, gain_in, cosine, sine), query_proj, query_gain
     )
@@ -323,45 +455,56 @@
         lambda proj_in, gain_in: prepare(proj_in, gain_in, cosine, sine), key_proj, key_gain
     )
     key_proj_grad, key_slope = key_pull(key_back)
-    query_half = query_proj_grad.astype(jnp.bfloat16)
-    key_half = key_proj_grad.astype(jnp.bfloat16)
-    value_half = value_back.astype(jnp.bfloat16)
-    proj_grads = jnp.concatenate([query_half, key_half, value_half], axis=1)
-    attn_rows_sum = lax.psum_scatter(
-        jnp.concatenate(
-            [inner_rows(normed_in, proj_grads), inner_rows(attended, middle_half)], axis=1
-        ).astype(jnp.bfloat16),
-        "fsdp",
-        scatter_dimension=0,
+    halves = jnp.concatenate([query_proj_grad, key_proj_grad, value_back], axis=1).astype(bf16)
+
+    in_grad = plane_scatter(inner_cols(halves, head_full).astype(bf16))
+    attention_slope = jnp.sum(in_grad * source * first, axis=0)
+    input_rows = (middle_grad + norm_back(in_grad, source, first, attention_gain)).astype(bf16)
+
+    def plane_slots(value, rows):
+        return [
+            lax.dynamic_slice_in_dim(value, ((plane - k) % planes) * rows, rows, 0)
+            for k in range(planes)
+        ]
+
+    head_grad = line_scatter(plane_slots(inner_rows(normed_all, halves).astype(bf16), shard))
+    head_grads = by_place(plane_gather(head_grad.astype(bf16)))
+    grad_query = head_grads[:, :, :query_cols].transpose(1, 0, 2).reshape(shard, -1).astype(f32)
+    grad_pair = head_grads[:, :, query_cols:].astype(f32)
+    grad_pair = grad_pair.reshape(parts // copies, copies, shard, 2, width).sum(axis=1)
+    grad_key = grad_pair[:, :, 0].transpose(1, 0, 2).reshape(shard, -1)
+    grad_value = grad_pair[:, :, 1].transpose(1, 0, 2).reshape(shard, -1)
+
+    out_grad = inner_rows(out_rows, middle_all).astype(bf16)
+    dealt = lax.all_to_all(
+        out_grad.reshape(parts, query_cols // parts, model),
+        "seq",
+        split_axis=0,
+        concat_axis=0,
         tiled=True,
-    ).astype(jnp.float32)
-    pair_width = pair_heads * width
-    grad_query = attn_rows_sum[:, :model]
-    grad_key = attn_rows_sum[:, model : model + pair_width]
-    grad_value = attn_rows_sum[:, model + pair_width : model + 2 * pair_width]
-    grad_output = attn_rows_sum[:, model + 2 * pair_width :]
-    in_grad = (
-        inner_cols(query_half, full_query)
-        + inner_cols(key_half, full_key)
-        + inner_cols(value_half, full_value)
-    )
-    attention_slope = jnp.sum(in_grad * source * first, axis=0)
-    input_rows = (middle_grad + norm_back(in_grad, source, first, attention_gain)).astype(
-        jnp.bfloat16
-    )
-    grad_query, grad_key, grad_value, grad_output, grad_gate, grad_up, grad_down = (
-        lax.psum(grad_query.astype(jnp.bfloat16), "seq").astype(jnp.float32),
-        lax.psum(grad_key.astype(jnp.bfloat16), "seq").astype(jnp.float32),
-        lax.psum(grad_value.astype(jnp.bfloat16), "seq").astype(jnp.float32),
-        lax.psum(grad_output.astype(jnp.bfloat16), "seq").astype(jnp.float32),
-        lax.psum(grad_gate.astype(jnp.bfloat16), "seq").astype(jnp.float32),
-        lax.psum(grad_up.astype(jnp.bfloat16), "seq").astype(jnp.float32),
-        lax.psum(grad_down.astype(jnp.bfloat16), "seq").astype(jnp.float32),
-    )
-    attention_slope, query_slope, key_slope, feedforward_slope = lax.psum(
-        (attention_slope, query_slope, key_slope, feedforward_slope), ("seq", "fsdp")
-    )
-    block_out = block_rows.astype(jnp.bfloat16).reshape(1, tokens, model)
+    )
+    dealt = dealt.reshape(planes, -1, model)
+    out_grad = line_scatter(
+        [lax.dynamic_index_in_dim(dealt, (plane - k) % planes, 0, False) for k in range(planes)]
+    )
+    out_grads = by_place(plane_gather(out_grad.astype(bf16)))
+    grad_output = out_grads.reshape(parts, parts // planes, query_cols // parts, model)
+    grad_output = grad_output.transpose(1, 0, 2, 3).reshape(shard, model).astype(f32)
+
+    slopes = jnp.concatenate([attention_slope, feedforward_slope, query_slope, key_slope])
+    slopes = slopes.reshape(1, -1)
+    for bit in range(parts.bit_length() - 1):
+        slopes = slopes + swap(slopes, 1 << bit)
+    for bit in range(planes.bit_length() - 1):
+        slopes = slopes + lax.ppermute(
+            slopes, "fsdp", [(i, i ^ (1 << bit)) for i in range(planes)]
+        )
+    slopes = slopes.reshape(-1)
+    attention_slope = slopes[:model]
+    feedforward_slope = slopes[model : 2 * model]
+    query_slope = slopes[2 * model : 2 * model + width]
+    key_slope = slopes[2 * model + width :]
+    block_out = block_rows.astype(bf16).reshape(1, tokens, model)
     input_grad = input_rows.reshape(1, tokens, model)
     return (
         block_out,

time: 1530 us -> 963 us (0.63)
  waiting for transfers between devices: 1160 us -> 384 us
  starting transfers between devices: 19.8 us -> 186 us
  local copies, waits for them, and re-layouts: 49.7 us -> 151 us
  blocking collectives: 55.3 us -> 0 us
  other arithmetic: 66.2 us -> 112 us
  matrix products: 152 us -> 118 us
    all_gather x6 -> x0, waiting for transfers between devices: 417 us -> none  [the longest x1 141 us: per_device(): lax.all_gather(query_weight, 'fsdp', axis=0, tiled=True)]
    reduce_scatter x3 -> x0, waiting for transfers between devices: 397 us -> none  [the longest x1 320 us: per_device(): lax.psum_scatter(jnp.concatenate([inner_rows(normed_in, proj_grads), inne...]
    ppermute x0 -> x168, waiting for transfers between devices: none -> 380 us  [the longest x118 264 us: swap(): return lax.ppermute(value, 'seq', [(i, i ^ bit) for i in range(parts)])]
    psum x1 -> x0, waiting for transfers between devices: 312 us -> none  [per_device(): lax.psum(grad_down.astype(jnp.bfloat16), 'seq').astype(jnp.float32)]
    ppermute x0 -> x168, starting transfers between devices: none -> 176 us  [the longest x118 72.6 us: swap(): return lax.ppermute(value, 'seq', [(i, i ^ bit) for i in range(parts)])]
    dynamic_update_slice x0 -> x81, local copies, waits for them, and re-layouts: none -> 62.4 us  [the longest x80 61.4 us: by_place(): lax.dynamic_update_slice(out, piece[None], (place ^ offset, color * half,...]
    dynamic_update_slice x0 -> x31, other arithmetic: none -> 57.2 us  [the longest x12 30.9 us: weight_total(): lax.dynamic_update_slice(out, piece.astype(f32), (offset, core * columns))]
    psum x1 -> x0, blocking collectives: 43.2 us -> none  [per_device(): lax.psum((attention_slope, query_slope, key_slope, feedforward_slope), ('...]
  transfers between devices with their start and end apart: 15 -> 171, of which waited for: 13 -> 51; matrix products, arithmetic and copies ran while one was open for 8% -> 33% of each run, Pallas kernels for 0% -> 0%
where the time goes in v1:
time: 963 us; the launch traced here: 955 us
  waiting for transfers between devices  384 us (40%)
  starting transfers between devices  186 us (19%)
  local copies, waits for them, and re-layouts  151 us (16%)
  matrix products  118 us (12%)
  other arithmetic  112 us (12%)
    ppermute x118, waiting for transfers between devices, swap(): return lax.ppermute(value, 'seq', [(i, i ^ bit) for i in range(parts)])  264 us
    ppermute x12, waiting for transfers between devices, line_gather(): lax.ppermute(downs[-1], 'fsdp', [(i, i - 1) for i in range(1, planes - st...  74.5 us
    ppermute x118, starting transfers between devices, swap(): return lax.ppermute(value, 'seq', [(i, i ^ bit) for i in range(parts)])  72.6 us
    dynamic_update_slice x80, local copies, waits for them, and re-layouts, by_place(): lax.dynamic_update_slice(out, piece[None], (place ^ offset, color * half,...  61.4 us
    ppermute x12, starting transfers between devices, line_scatter(): up = lax.ppermute(send_up, 'fsdp', [(i, i + 1) for i in range(step)])  44.6 us
    dot_general x5, matrix products, inner_cols(): lax.dot_general(left, right, (((1,), (1,)), ((), ())), preferred_element_...  34 us
    dot_general x5, matrix products, matmul(): return jnp.dot(left, right, preferred_element_type=jnp.float32)  33.1 us
    dynamic_update_slice x12, other arithmetic, weight_total(): lax.dynamic_update_slice(out, piece.astype(f32), (offset, core * columns))  30.9 us
  transfers between devices with their start and end apart: 171, of which 51 were waited for; matrix products, arithmetic and copies ran while one was open for 33% of the time, Pallas kernels for 0%

profile of v1, /device:TPU:0, one launch (start us, length us, event | category | flops | bytes accessed | tf_op | source)
XLA Modules:
  0.0 954.9 jit_solution(3629101394279404880)
XLA Ops:
  19.7 3.5 collective-permute-start.20
  31.0 6.3 collective-permute-done.21
  41.4 4.0 collective-permute-done.5
  51.6 6.6 collective-permute-done.23
  64.3 10.5 %collective-permute-start.14 = (bf16[512,384]{1,0:T(8,128)(2,1)S(1)}, bf16[512,384]{1,0:T(8,128)(2,1)S(1)}, u32[]{:S(2)}, u32[]{:S(2)}) collective-permute-start(bf16[512,384]{1,0:T(8,128)(2,1)S(1)} %copy-done.52), channel_id=1, source_target_pairs={{0,1},{1,2},{2,3},{4,5},{5,6},{6,7},{8,9},{9,10},{10,11},{12,13},{... | collective-permute-start | bytes 1179656 | tf_op jit(solution)/shard_map/ppermute | solution.py:254
  83.9 7.5 collective-permute-done.15
  101.5 6.8 collective-permute-done.16
  110.9 16.6 %collective-permute-done.17 = bf16[512,384]{1,0:T(8,128)(2,1)S(1)} collective-permute-done((bf16[512,384]{1,0:T(8,128)(2,1)S(1)}, bf16[512,384]{1,0:T(8,128)(2,1)S(1)}, u32[]{:S(2)}, u32[]{:S(2)}) %collective-permute-start.17) | collective-permute-done | bytes 393248 | tf_op jit(solution)/shard_map/ppermute | solution.py:257
  128.9 4.6 fusion.171
  137.9 9.2 while.105
  141.4 5.0 while.108
  148.4 3.5 all-to-all-start
  157.6 4.5 all-to-all-done
  168.3 8.7 collective-permute-done.31
  178.6 6.1 collective-permute-done.34
  194.8 5.7 collective-permute-done.38
  206.2 8.4 copy.84
  214.6 4.9 multiply_reduce_fusion.4
  222.9 5.6 collective-permute-start.40
  228.5 6.9 collective-permute-done.41
  240.6 9.7 %collective-permute-done.42 = bf16[128,2048]{1,0:T(8,128)(2,1)S(1)} collective-permute-done((bf16[128,2048]{1,0:T(8,128)(2,1)S(1)}, bf16[128,2048]{1,0:T(8,128)(2,1)S(1)}, u32[]{:S(2)}, u32[]{:S(2)}) %collective-permute-start.42) | collective-permute-done | bytes 524320 | tf_op jit(solution)/shard_map/ppermute | solution.py:257
  252.5 11.8 %collective-permute-done.43 = bf16[128,2048]{1,0:T(8,128)(2,1)S(1)} collective-permute-done((bf16[128,2048]{1,0:T(8,128)(2,1)S(1)}, bf16[128,2048]{1,0:T(8,128)(2,1)S(1)}, u32[]{:S(2)}, u32[]{:S(2)}) %collective-permute-start.43) | collective-permute-done | bytes 524320 | tf_op jit(solution)/shard_map/ppermute | solution.py:257
  268.0 7.8 fusion.90
  275.9 6.0 fusion.94
  281.9 9.8 %multiply_convert_fusion = (bf16[1024,1024]{1,0:T(8,128)(2,1)}, bf16[1024,1024]{1,0:T(8,128)(2,1)}, bf16[1024,1024]{1,0:T(8,128)(2,1)}) fusion(f32[1024,1024]{1,0:T(8,128)} %fusion.94, f32[1024,1024]{1,0:T(8,128)S(1)} %fusion.90, bf16[1024,2048]{1,0:T(8,128)(2,1)S(1)} %constant_dynamic-update-slice_fusion.10, bf16[2048,2048]{1,0:T(8,128)(2,1)S(1)} %bitcast.615, ...), kind=kOutput, calls=%fused_computation.86 | convolution fusion | flops 4311744512 | bytes 23068676 | tf_op jit(solution)/shard_map/dot_general | solution.py:34
  291.7 6.6 convolution_convert_fusion.1
  298.3 6.5 fusion.87
  304.9 5.3 convolution_convert_fusion.3
  310.2 9.0 fusion.92
  322.9 5.1 convolution_convert_fusion.2
  333.7 13.2 %convolution_add_fusion = f32[1024,2048]{1,0:T(8,128)} fusion(f32[1024,2048]{1,0:T(8,128)} %fusion.92, bf16[1024,1024]{1,0:T(8,128)(2,1)} %get-tuple-element.944, bf16[2048,2048]{1,0:T(8,128)(2,1)} %param.32, s32[]{:T(128)S(6)} %select_n.578), kind=kOutput, calls=%fused_computation.90 | convolution fusion | flops 4297064448 | bytes 23068676 | tf_op jit(solution)/shard_map/dot_general | solution.py:44
  346.9 3.8 slice.310
  354.3 14.1 %collective-permute-done.138 = bf16[512,1024]{1,0:T(8,128)(2,1)} collective-permute-done((bf16[512,1024]{1,0:T(8,128)(2,1)S(1)}, bf16[512,1024]{1,0:T(8,128)(2,1)}, u32[]{:S(2)}, u32[]{:S(2)}) %collective-permute-start.138) | collective-permute-done | bytes 1048608 | tf_op jit(solution)/shard_map/ppermute | solution.py:245
  370.3 19.7 %collective-permute-done.148 = bf16[512,1024]{1,0:T(8,128)(2,1)} collective-permute-done((bf16[512,1024]{1,0:T(8,128)(2,1)}, bf16[512,1024]{1,0:T(8,128)(2,1)}, u32[]{:S(2)}, u32[]{:S(2)}) %collective-permute-start.148) | collective-permute-done | bytes 1048608 | tf_op jit(solution)/shard_map/ppermute | solution.py:245
  411.9 54.5 %collective-permute-done.149 = bf16[512,1024]{1,0:T(8,128)(2,1)S(1)} collective-permute-done((bf16[512,1024]{1,0:T(8,128)(2,1)S(1)}, bf16[512,1024]{1,0:T(8,128)(2,1)S(1)}, u32[]{:S(2)}, u32[]{:S(2)}) %collective-permute-start.149) | collective-permute-done | bytes 1048608 | tf_op jit(solution)/shard_map/ppermute | solution.py:245
  476.7 8.3 broadcast.287.clone
  488.3 8.3 broadcast.287.clone.2
  509.8 16.3 %collective-permute-done.151 = bf16[512,1024]{1,0:T(8,128)(2,1)} collective-permute-done((bf16[512,1024]{1,0:T(8,128)(2,1)}, bf16[512,1024]{1,0:T(8,128)(2,1)}, u32[]{:S(2)}, u32[]{:S(2)}) %collective-permute-start.151) | collective-permute-done | bytes 1048608 | tf_op jit(solution)/shard_map/ppermute | solution.py:245
  529.0 19.7 %collective-permute-done.141 = bf16[512,1024]{1,0:T(8,128)(2,1)} collective-permute-done((bf16[512,1024]{1,0:T(8,128)(2,1)S(1)}, bf16[512,1024]{1,0:T(8,128)(2,1)}, u32[]{:S(2)}, u32[]{:S(2)}) %collective-permute-start.141) | collective-permute-done | bytes 1048608 | tf_op jit(solution)/shard_map/ppermute | solution.py:245
  556.1 13.1 %collective-permute-start.70 = (bf16[128,2048]{1,0:T(8,128)(2,1)S(1)}, bf16[128,2048]{1,0:T(8,128)(2,1)S(1)}, u32[]{:S(2)}, u32[]{:S(2)}) collective-permute-start(bf16[128,2048]{1,0:T(8,128)(2,1)S(1)} %get-tuple-element.955), channel_id=1, source_target_pairs={{0,1},{1,2},{2,3},{4,5},{5,6},{6,7},{8,9},{9,10},{10,11},{12,13},{... | collective-permute-start | bytes 1572872 | tf_op jit(solution)/shard_map/ppermute | solution.py:270
  571.1 9.6 %collective-permute-start.53 = (bf16[128,2048]{1,0:T(8,128)(2,1)S(1)}, bf16[128,2048]{1,0:T(8,128)(2,1)S(1)}, u32[]{:S(2)}, u32[]{:S(2)}) collective-permute-start(bf16[128,2048]{1,0:T(8,128)(2,1)S(1)} %get-tuple-element.961), channel_id=1, source_target_pairs={{0,1},{1,2},{2,3},{4,5},{5,6},{6,7},{8,9},{9,10},{10,11},{12,13},{... | collective-permute-start | bytes 1572872 | tf_op jit(solution)/shard_map/ppermute | solution.py:270
  589.3 5.2 collective-permute-done.56
  601.1 3.5 all-to-all-start.1
  610.6 16.1 %collective-permute-done.105 = bf16[64,2048]{1,0:T(8,128)(2,1)S(1)} collective-permute-done((bf16[64,2048]{1,0:T(8,128)(2,1)S(1)}, bf16[64,2048]{1,0:T(8,128)(2,1)S(1)}, u32[]{:S(2)}, u32[]{:S(2)}) %collective-permute-start.105) | collective-permute-done | bytes 262176 | tf_op jit(solution)/shard_map/ppermute | solution.py:245
  630.1 25.8 %while.107 = (s32[]{:T(128)}, f32[1024,1,4,64]{0,3,2,1:T(8,128)}, f32[1024,1,64]{0,2,1:T(8,128)S(1)}, f32[1024,1,64]{0,2,1:T(8,128)S(1)}, bf16[1024,1,4,64]{0,3,...) while((s32[]{:T(128)}, f32[1024,1,4,64]{0,3,2,1:T(8,128)}, ...), condition=%wide.region_14.15_spmd.clone.clone, body=%wide.region_11.14_spmd.clone.clone.sunk | while | flops 683082752 | bytes 25236144 | solution.py:202
  631.6 7.0 while.109
  640.9 13.9 %while.109 = (s32[]{:T(128)}, f32[512,1,4,64]{0,3,2,1:T(8,128)S(1)}, f32[1024,1,64]{0,2,1:T(8,128)S(1)}, f32[1024,1,64]{0,2,1:T(8,128)S(1)}, s32[]{:T(128)}, /*i...) while((s32[]{:T(128)}, f32[512,1,4,64]{0,3,2,1:T(8,128)S(1)}, ...), condition=%wide.region_13.13_spmd.clone, body=%wide.region_12.12_spmd.clone.sunk | while | flops 683082752 | bytes 22579488 | solution.py:193
  662.6 4.1 convolution_convert_fusion.4
  683.3 3.7 convert_dynamic-update-slice_fusion.11
  687.0 10.1 %collective-permute-done.144 = bf16[512,1024]{1,0:T(8,128)(2,1)S(1)} collective-permute-done((bf16[512,1024]{1,0:T(8,128)(2,1)S(1)}, bf16[512,1024]{1,0:T(8,128)(2,1)S(1)}, u32[]{:S(2)}, u32[]{:S(2)}) %collective-permute-start.144) | collective-permute-done | bytes 1048608 | tf_op jit(solution)/shard_map/ppermute | solution.py:245
  701.0 3.7 convert_dynamic-update-slice_fusion.3
  708.5 5.0 collective-permute-done.109
  725.7 4.4 collective-permute-start.85
  730.2 4.4 convolution_convert_fusion.5
  734.6 3.6 all-to-all-start.2
  754.8 26.7 %collective-permute-done.146 = bf16[512,1024]{1,0:T(8,128)(2,1)S(1)} collective-permute-done((bf16[512,1024]{1,0:T(8,128)(2,1)}, bf16[512,1024]{1,0:T(8,128)(2,1)S(1)}, u32[]{:S(2)}, u32[]{:S(2)}) %collective-permute-start.146) | collective-permute-done | bytes 1048608 | tf_op jit(solution)/shard_map/ppermute | solution.py:245
  790.7 12.6 %collective-permute-done.166 = bf16[512,1024]{1,0:T(8,128)(2,1)} collective-permute-done((bf16[512,1024]{1,0:T(8,128)(2,1)}, bf16[512,1024]{1,0:T(8,128)(2,1)}, u32[]{:S(2)}, u32[]{:S(2)}) %collective-permute-start.166) | collective-permute-done | bytes 1048608 | tf_op jit(solution)/shard_map/ppermute | solution.py:245
  811.2 11.6 %collective-permute-done.89 = bf16[512,384]{0,1:T(8,128)(2,1)S(1)} collective-permute-done((bf16[512,384]{0,1:T(8,128)(2,1)S(1)}, bf16[512,384]{0,1:T(8,128)(2,1)S(1)}, u32[]{:S(2)}, u32[]{:S(2)}) %collective-permute-start.89) | collective-permute-done | bytes 393248 | tf_op jit(solution)/shard_map/ppermute | solution.py:271
  825.0 4.2 collective-permute-start.120
  844.9 4.5 collective-permute-done.93
  857.3 12.7 %collective-permute-done.123 = bf16[64,2048]{1,0:T(8,128)(2,1)S(1)} collective-permute-done((bf16[64,2048]{1,0:T(8,128)(2,1)S(1)}, bf16[64,2048]{1,0:T(8,128)(2,1)S(1)}, u32[]{:S(2)}, u32[]{:S(2)}) %collective-permute-start.123) | collective-permute-done | bytes 262176 | tf_op jit(solution)/shard_map/ppermute | solution.py:271
  873.5 16.1 %collective-permute-done.102 = bf16[256,384]{0,1:T(8,128)(2,1)S(1)} collective-permute-done((bf16[256,384]{0,1:T(8,128)(2,1)S(1)}, bf16[256,384]{0,1:T(8,128)(2,1)S(1)}, u32[]{:S(2)}, u32[]{:S(2)}) %collective-permute-start.102) | collective-permute-done | bytes 196640 | tf_op jit(solution)/shard_map/ppermute | solution.py:245
  896.8 5.4 copy.90
  920.6 6.2 collective-permute-done.129
  (810 shorter events, 410.3 us)
Async XLA Ops:
  4.1 60.2 %collective-permute-start.8 = (bf16[64,2048]{1,0:T(8,128)(2,1)}, bf16[64,2048]{1,0:T(8,128)(2,1)S(1)}, u32[]{:S(2)}, u32[]{:S(2)}) collective-permute-start(bf16[64,2048]{1,0:T(8,128)(2,1)} %get-tuple-element.980), channel_id=1, source_target_pairs={{0,16},{4,20},{8,24},{12,28},{16,0},{20,4},{24,8},{28,12},{1,17},{... | collective-permute-start | bytes 786440 | tf_op jit(solution)/shard_map/ppermute | solution.py:245
  7.1 67.7 %collective-permute-start.7 = (bf16[64,2048]{1,0:T(8,128)(2,1)}, bf16[64,2048]{1,0:T(8,128)(2,1)}, u32[]{:S(2)}, u32[]{:S(2)}) collective-permute-start(bf16[64,2048]{1,0:T(8,128)(2,1)} %get-tuple-element.980), channel_id=1, source_target_pairs={{0,4},{4,0},{8,12},{12,8},{16,20},{20,16},{24,28},{28,24},{1,5},{5... | collective-permute-start | bytes 786440 | tf_op jit(solution)/shard_map/ppermute | solution.py:245
  40.9 38.4 %collective-permute-start.10 = (bf16[64,2048]{1,0:T(8,128)(2,1)}, bf16[64,2048]{1,0:T(8,128)(2,1)S(1)}, u32[]{:S(2)}, u32[]{:S(2)}) collective-permute-start(bf16[64,2048]{1,0:T(8,128)(2,1)} %get-tuple-element.980), channel_id=1, source_target_pairs={{0,8},{4,12},{8,0},{12,4},{16,24},{20,28},{24,16},{28,20},{1,9},{5... | collective-permute-start | bytes 786440 | tf_op jit(solution)/shard_map/ppermute | solution.py:245
  50.3 43.2 %collective-permute-start.58 = (bf16[128,2048]{1,0:T(8,128)(2,1)S(1)}, bf16[128,2048]{1,0:T(8,128)(2,1)}, u32[]{:S(2)}, u32[]{:S(2)}) collective-permute-start(bf16[128,2048]{1,0:T(8,128)(2,1)S(1)} %bitcast.594), channel_id=1, source_target_pairs={{1,0},{2,1},{3,2},{5,4},{6,5},{7,6},{9,8},{10,9},{11,10},{13,12},{... | collective-permute-start | bytes 1572872 | tf_op jit(solution)/shard_map/ppermute | solution.py:257
  60.6 34.2 %collective-permute-start.57 = (bf16[128,2048]{1,0:T(8,128)(2,1)S(1)}, bf16[128,2048]{1,0:T(8,128)(2,1)}, u32[]{:S(2)}, u32[]{:S(2)}) collective-permute-start(bf16[128,2048]{1,0:T(8,128)(2,1)S(1)} %bitcast.595), channel_id=1, source_target_pairs={{0,1},{1,2},{2,3},{4,5},{5,6},{6,7},{8,9},{9,10},{10,11},{12,13},{... | collective-permute-start | bytes 1572872 | tf_op jit(solution)/shard_map/ppermute | solution.py:254
  93.5 99.0 %collective-permute-start.59 = (bf16[128,2048]{1,0:T(8,128)(2,1)}, bf16[128,2048]{1,0:T(8,128)(2,1)}, u32[]{:S(2)}, u32[]{:S(2)}) collective-permute-start(bf16[128,2048]{1,0:T(8,128)(2,1)} %collective-permute-done.58), channel_id=1, source_target_pairs={{1,0},{2,1},{5,4},{6,5},{9,8},{10,9},{13,12},{14,13},{17,16},{18,1... | collective-permute-start | bytes 1572872 | tf_op jit(solution)/shard_map/ppermute | solution.py:257
  94.8 98.0 %collective-permute-start.61 = (bf16[128,2048]{1,0:T(8,128)(2,1)}, bf16[128,2048]{1,0:T(8,128)(2,1)}, u32[]{:S(2)}, u32[]{:S(2)}) collective-permute-start(bf16[128,2048]{1,0:T(8,128)(2,1)} %collective-permute-done.57), channel_id=1, source_target_pairs={{1,2},{2,3},{5,6},{6,7},{9,10},{10,11},{13,14},{14,15},{17,18},{18... | collective-permute-start | bytes 1572872 | tf_op jit(solution)/shard_map/ppermute | solution.py:254
  99.9 62.5 %collective-permute-start.29 = (bf16[128,2048]{1,0:T(8,128)(2,1)}, bf16[128,2048]{1,0:T(8,128)(2,1)}, u32[]{:S(2)}, u32[]{:S(2)}) collective-permute-start(bf16[128,2048]{1,0:T(8,128)(2,1)} %bitcast.42), channel_id=1, source_target_pairs={{0,16},{4,20},{8,24},{12,28},{16,0},{20,4},{24,8},{28,12},{1,17},{... | collective-permute-start | bytes 1572872 | tf_op jit(solution)/shard_map/ppermute | solution.py:245
  110.3 41.6 %collective-permute-start.27 = (bf16[128,2048]{1,0:T(8,128)(2,1)}, bf16[128,2048]{1,0:T(8,128)(2,1)}, u32[]{:S(2)}, u32[]{:S(2)}) collective-permute-start(bf16[128,2048]{1,0:T(8,128)(2,1)} %bitcast.42), channel_id=1, source_target_pairs={{0,8},{4,12},{8,0},{12,4},{16,24},{20,28},{24,16},{28,20},{1,9},{5... | collective-permute-start | bytes 1572872 | tf_op jit(solution)/shard_map/ppermute | solution.py:245
  128.7 25.2 %collective-permute-start.26 = (bf16[128,2048]{1,0:T(8,128)(2,1)}, bf16[128,2048]{1,0:T(8,128)(2,1)}, u32[]{:S(2)}, u32[]{:S(2)}) collective-permute-start(bf16[128,2048]{1,0:T(8,128)(2,1)} %bitcast.42), channel_id=1, source_target_pairs={{0,4},{4,0},{8,12},{12,8},{16,20},{20,16},{24,28},{28,24},{1,5},{5... | collective-permute-start | bytes 1572872 | tf_op jit(solution)/shard_map/ppermute | solution.py:245
  151.9 42.2 %collective-permute-start.36 = (bf16[128,2048]{1,0:T(8,128)(2,1)}, bf16[128,2048]{1,0:T(8,128)(2,1)}, u32[]{:S(2)}, u32[]{:S(2)}) collective-permute-start(bf16[128,2048]{1,0:T(8,128)(2,1)} %bitcast.600), channel_id=1, source_target_pairs={{0,8},{4,12},{8,0},{12,4},{16,24},{20,28},{24,16},{28,20},{1,9},{5... | collective-permute-start | bytes 1572872 | tf_op jit(solution)/shard_map/ppermute | solution.py:245
  192.5 45.6 %collective-permute-start.63 = (bf16[128,2048]{1,0:T(8,128)(2,1)S(1)}, bf16[128,2048]{1,0:T(8,128)(2,1)S(1)}, u32[]{:S(2)}, u32[]{:S(2)}) collective-permute-start(bf16[128,2048]{1,0:T(8,128)(2,1)S(1)} %bitcast.596), channel_id=1, source_target_pairs={{0,4},{4,0},{8,12},{12,8},{16,20},{20,16},{24,28},{28,24},{1,5},{5... | collective-permute-start | bytes 1572872 | tf_op jit(solution)/shard_map/ppermute | solution.py:245
  192.8 28.2 %collective-permute-start.60 = (bf16[128,2048]{1,0:T(8,128)(2,1)}, bf16[128,2048]{1,0:T(8,128)(2,1)S(1)}, u32[]{:S(2)}, u32[]{:S(2)}) collective-permute-start(bf16[128,2048]{1,0:T(8,128)(2,1)} %collective-permute-done.59), channel_id=1, source_target_pairs={{1,0},{5,4},{9,8},{13,12},{17,16},{21,20},{25,24},{29,28}} | collective-permute-start | bytes 1572872 | tf_op jit(solution)/shard_map/ppermute | solution.py:257
  194.1 28.8 %collective-permute-start.62 = (bf16[128,2048]{1,0:T(8,128)(2,1)}, bf16[128,2048]{1,0:T(8,128)(2,1)S(1)}, u32[]{:S(2)}, u32[]{:S(2)}) collective-permute-start(bf16[128,2048]{1,0:T(8,128)(2,1)} %collective-permute-done.61), channel_id=1, source_target_pairs={{2,3},{6,7},{10,11},{14,15},{18,19},{22,23},{26,27},{30,31}} | collective-permute-start | bytes 1572872 | tf_op jit(solution)/shard_map/ppermute | solution.py:254
  222.4 29.3 %collective-permute-start.65 = (bf16[128,2048]{1,0:T(8,128)(2,1)S(1)}, bf16[128,2048]{1,0:T(8,128)(2,1)S(1)}, u32[]{:S(2)}, u32[]{:S(2)}) collective-permute-start(bf16[128,2048]{1,0:T(8,128)(2,1)S(1)} %get-tuple-element.921), channel_id=1, source_target_pairs={{0,4},{4,0},{8,12},{12,8},{16,20},{20,16},{24,28},{28,24},{1,5},{5... | collective-permute-start | bytes 1572872 | tf_op jit(solution)/shard_map/ppermute | solution.py:245
  222.4 29.1 %collective-permute-start.64 = (bf16[128,2048]{1,0:T(8,128)(2,1)S(1)}, bf16[128,2048]{1,0:T(8,128)(2,1)S(1)}, u32[]{:S(2)}, u32[]{:S(2)}) collective-permute-start(bf16[128,2048]{1,0:T(8,128)(2,1)S(1)} %get-tuple-element.923), channel_id=1, source_target_pairs={{0,4},{4,0},{8,12},{12,8},{16,20},{20,16},{24,28},{28,24},{1,5},{5... | collective-permute-start | bytes 1572872 | tf_op jit(solution)/shard_map/ppermute | solution.py:245
  319.7 31.2 %collective-permute-start.158 = (bf16[512,1024]{1,0:T(8,128)(2,1)S(1)}, bf16[512,1024]{1,0:T(8,128)(2,1)}, u32[]{:S(2)}, u32[]{:S(2)}) collective-permute-start(bf16[512,1024]{1,0:T(8,128)(2,1)S(1)} %constant_dynamic-slice_fusion.5), channel_id=1, source_target_pairs={{0,8},{4,12},{8,0},{12,4},{16,24},{20,28},{24,16},{28,20},{1,9},{5... | collective-permute-start | bytes 3145736 | tf_op jit(solution)/shard_map/ppermute | solution.py:245
  322.6 69.1 %collective-permute-start.163 = (bf16[512,1024]{1,0:T(8,128)(2,1)}, bf16[512,1024]{1,0:T(8,128)(2,1)}, u32[]{:S(2)}, u32[]{:S(2)}) collective-permute-start(bf16[512,1024]{1,0:T(8,128)(2,1)} %constant_dynamic-slice_fusion.4), channel_id=1, source_target_pairs={{0,16},{4,20},{8,24},{12,28},{16,0},{20,4},{24,8},{28,12},{1,17},{... | collective-permute-start | bytes 3145736 | tf_op jit(solution)/shard_map/ppermute | solution.py:245
  330.0 38.4 %collective-permute-start.138 = (bf16[512,1024]{1,0:T(8,128)(2,1)S(1)}, bf16[512,1024]{1,0:T(8,128)(2,1)}, u32[]{:S(2)}, u32[]{:S(2)}) collective-permute-start(bf16[512,1024]{1,0:T(8,128)(2,1)S(1)} %constant_dynamic-slice_fusion.9), channel_id=1, source_target_pairs={{0,8},{4,12},{8,0},{12,4},{16,24},{20,28},{24,16},{28,20},{1,9},{5... | collective-permute-start | bytes 3145736 | tf_op jit(solution)/shard_map/ppermute | solution.py:245
  331.4 58.6 %collective-permute-start.148 = (bf16[512,1024]{1,0:T(8,128)(2,1)}, bf16[512,1024]{1,0:T(8,128)(2,1)}, u32[]{:S(2)}, u32[]{:S(2)}) collective-permute-start(bf16[512,1024]{1,0:T(8,128)(2,1)} %constant_dynamic-slice_fusion.7), channel_id=1, source_target_pairs={{0,8},{4,12},{8,0},{12,4},{16,24},{20,28},{24,16},{28,20},{1,9},{5... | collective-permute-start | bytes 3145736 | tf_op jit(solution)/shard_map/ppermute | solution.py:245
  333.7 68.9 %collective-permute-start.50 = (bf16[512,2048]{1,0:T(8,128)(2,1)}, bf16[512,2048]{1,0:T(8,128)(2,1)}, u32[]{:S(2)}, u32[]{:S(2)}) collective-permute-start(bf16[512,2048]{1,0:T(8,128)(2,1)} %slice.311), channel_id=1, source_target_pairs={{0,4},{4,0},{8,12},{12,8},{16,20},{20,16},{24,28},{28,24},{1,5},{5... | collective-permute-start | bytes 6291464 | tf_op jit(solution)/shard_map/ppermute | solution.py:245
  350.9 43.7 %collective-permute-start.143 = (bf16[512,1024]{1,0:T(8,128)(2,1)S(1)}, bf16[512,1024]{1,0:T(8,128)(2,1)S(1)}, u32[]{:S(2)}, u32[]{:S(2)}) collective-permute-start(bf16[512,1024]{1,0:T(8,128)(2,1)S(1)} %constant_dynamic-slice_fusion.8), channel_id=1, source_target_pairs={{0,16},{4,20},{8,24},{12,28},{16,0},{20,4},{24,8},{28,12},{1,17},{... | collective-permute-start | bytes 3145736 | tf_op jit(solution)/shard_map/ppermute | solution.py:245
  368.4 31.1 %collective-permute-start.153 = (bf16[512,1024]{1,0:T(8,128)(2,1)S(1)}, bf16[512,1024]{1,0:T(8,128)(2,1)S(1)}, u32[]{:S(2)}, u32[]{:S(2)}) collective-permute-start(bf16[512,1024]{1,0:T(8,128)(2,1)S(1)} %constant_dynamic-slice_fusion.6), channel_id=1, source_target_pairs={{0,16},{4,20},{8,24},{12,28},{16,0},{20,4},{24,8},{28,12},{1,17},{... | collective-permute-start | bytes 3145736 | tf_op jit(solution)/shard_map/ppermute | solution.py:245
  391.7 96.6 %collective-permute-start.159 = (bf16[512,1024]{1,0:T(8,128)(2,1)S(1)}, bf16[512,1024]{1,0:T(8,128)(2,1)}, u32[]{:S(2)}, u32[]{:S(2)}) collective-permute-start(bf16[512,1024]{1,0:T(8,128)(2,1)S(1)} %add_convert_fusion.3), channel_id=1, source_target_pairs={{0,16},{4,20},{8,24},{12,28},{16,0},{20,4},{24,8},{28,12},{1,17},{... | collective-permute-start | bytes 3145736 | tf_op jit(solution)/shard_map/ppermute | solution.py:245
  394.7 80.2 %collective-permute-start.139 = (bf16[512,1024]{1,0:T(8,128)(2,1)S(1)}, bf16[512,1024]{1,0:T(8,128)(2,1)}, u32[]{:S(2)}, u32[]{:S(2)}) collective-permute-start(bf16[512,1024]{1,0:T(8,128)(2,1)S(1)} %add_convert_fusion.11), channel_id=1, source_target_pairs={{0,16},{4,20},{8,24},{12,28},{16,0},{20,4},{24,8},{28,12},{1,17},{... | collective-permute-start | bytes 3145736 | tf_op jit(solution)/shard_map/ppermute | solution.py:245
  399.5 66.9 %collective-permute-start.149 = (bf16[512,1024]{1,0:T(8,128)(2,1)S(1)}, bf16[512,1024]{1,0:T(8,128)(2,1)S(1)}, u32[]{:S(2)}, u32[]{:S(2)}) collective-permute-start(bf16[512,1024]{1,0:T(8,128)(2,1)S(1)} %add_convert_fusion.7), channel_id=1, source_target_pairs={{0,16},{4,20},{8,24},{12,28},{16,0},{20,4},{24,8},{28,12},{1,17},{... | collective-permute-start | bytes 3145736 | tf_op jit(solution)/shard_map/ppermute | solution.py:245
  406.4 93.4 %collective-permute-start.51 = (bf16[128,2048]{1,0:T(8,128)(2,1)}, bf16[128,2048]{1,0:T(8,128)(2,1)}, u32[]{:S(2)}, u32[]{:S(2)}) collective-permute-start(bf16[128,2048]{1,0:T(8,128)(2,1)} %get-tuple-element.965), channel_id=1, source_target_pairs={{0,1},{4,5},{8,9},{12,13},{16,17},{20,21},{24,25},{28,29}} | collective-permute-start | bytes 1572872 | tf_op jit(solution)/shard_map/ppermute | solution.py:270
  408.6 92.5 %collective-permute-start.54 = (bf16[128,2048]{1,0:T(8,128)(2,1)}, bf16[128,2048]{1,0:T(8,128)(2,1)}, u32[]{:S(2)}, u32[]{:S(2)}) collective-permute-start(bf16[128,2048]{1,0:T(8,128)(2,1)} %get-tuple-element.966), channel_id=1, source_target_pairs={{3,2},{7,6},{11,10},{15,14},{19,18},{23,22},{27,26},{31,30}} | collective-permute-start | bytes 1572872 | tf_op jit(solution)/shard_map/ppermute | solution.py:271
  467.4 35.5 %collective-permute-start.68 = (bf16[128,2048]{1,0:T(8,128)(2,1)}, bf16[128,2048]{1,0:T(8,128)(2,1)}, u32[]{:S(2)}, u32[]{:S(2)}) collective-permute-start(bf16[128,2048]{1,0:T(8,128)(2,1)} %get-tuple-element.959), channel_id=1, source_target_pairs={{0,1},{4,5},{8,9},{12,13},{16,17},{20,21},{24,25},{28,29}} | collective-permute-start | bytes 1572872 | tf_op jit(solution)/shard_map/ppermute | solution.py:270
  474.9 28.8 %collective-permute-start.71 = (bf16[128,2048]{1,0:T(8,128)(2,1)}, bf16[128,2048]{1,0:T(8,128)(2,1)}, u32[]{:S(2)}, u32[]{:S(2)}) collective-permute-start(bf16[128,2048]{1,0:T(8,128)(2,1)} %get-tuple-element.960), channel_id=1, source_target_pairs={{3,2},{7,6},{11,10},{15,14},{19,18},{23,22},{27,26},{31,30}} | collective-permute-start | bytes 1572872 | tf_op jit(solution)/shard_map/ppermute | solution.py:271
  499.8 26.3 %collective-permute-start.151 = (bf16[512,1024]{1,0:T(8,128)(2,1)}, bf16[512,1024]{1,0:T(8,128)(2,1)}, u32[]{:S(2)}, u32[]{:S(2)}) collective-permute-start(bf16[512,1024]{1,0:T(8,128)(2,1)} %get-tuple-element.905), channel_id=1, source_target_pairs={{0,8},{4,12},{8,0},{12,4},{16,24},{20,28},{24,16},{28,20},{1,9},{5... | collective-permute-start | bytes 3145736 | tf_op jit(solution)/shard_map/ppermute | solution.py:245
  502.9 45.7 %collective-permute-start.141 = (bf16[512,1024]{1,0:T(8,128)(2,1)S(1)}, bf16[512,1024]{1,0:T(8,128)(2,1)}, u32[]{:S(2)}, u32[]{:S(2)}) collective-permute-start(bf16[512,1024]{1,0:T(8,128)(2,1)S(1)} %copy-done.48), channel_id=1, source_target_pairs={{0,8},{4,12},{8,0},{12,4},{16,24},{20,28},{24,16},{28,20},{1,9},{5... | collective-permute-start | bytes 3145736 | tf_op jit(solution)/shard_map/ppermute | solution.py:245
  503.7 48.5 %collective-permute-start.160 = (bf16[512,1024]{1,0:T(8,128)(2,1)S(1)}, bf16[512,1024]{1,0:T(8,128)(2,1)S(1)}, u32[]{:S(2)}, u32[]{:S(2)}) collective-permute-start(bf16[512,1024]{1,0:T(8,128)(2,1)S(1)} %get-tuple-element.901), channel_id=1, source_target_pairs={{0,4},{4,0},{8,12},{12,8},{16,20},{20,16},{24,28},{28,24},{1,5},{5... | collective-permute-start | bytes 3145736 | tf_op jit(solution)/shard_map/ppermute | solution.py:245
  505.2 75.6 %collective-permute-start.161 = (bf16[512,1024]{1,0:T(8,128)(2,1)S(1)}, bf16[512,1024]{1,0:T(8,128)(2,1)S(1)}, u32[]{:S(2)}, u32[]{:S(2)}) collective-permute-start(bf16[512,1024]{1,0:T(8,128)(2,1)S(1)} %get-tuple-element.901), channel_id=1, source_target_pairs={{0,8},{4,12},{8,0},{12,4},{16,24},{20,28},{24,16},{28,20},{1,9},{5... | collective-permute-start | bytes 3145736 | tf_op jit(solution)/shard_map/ppermute | solution.py:245
  506.9 62.3 %collective-permute-start.52 = (bf16[128,2048]{1,0:T(8,128)(2,1)S(1)}, bf16[128,2048]{1,0:T(8,128)(2,1)S(1)}, u32[]{:S(2)}, u32[]{:S(2)}) collective-permute-start(bf16[128,2048]{1,0:T(8,128)(2,1)S(1)} %get-tuple-element.963), channel_id=1, source_target_pairs={{0,1},{1,2},{4,5},{5,6},{8,9},{9,10},{12,13},{13,14},{16,17},{17,1... | collective-permute-start | bytes 1572872 | tf_op jit(solution)/shard_map/ppermute | solution.py:270
  526.1 28.2 %collective-permute-start.69 = (bf16[128,2048]{1,0:T(8,128)(2,1)S(1)}, bf16[128,2048]{1,0:T(8,128)(2,1)S(1)}, u32[]{:S(2)}, u32[]{:S(2)}) collective-permute-start(bf16[128,2048]{1,0:T(8,128)(2,1)S(1)} %get-tuple-element.957), channel_id=1, source_target_pairs={{0,1},{1,2},{4,5},{5,6},{8,9},{9,10},{12,13},{13,14},{16,17},{17,1... | collective-permute-start | bytes 1572872 | tf_op jit(solution)/shard_map/ppermute | solution.py:270
  554.4 146.6 %collective-permute-start.164 = (bf16[512,1024]{1,0:T(8,128)(2,1)}, bf16[512,1024]{1,0:T(8,128)(2,1)}, u32[]{:S(2)}, u32[]{:S(2)}) collective-permute-start(bf16[512,1024]{1,0:T(8,128)(2,1)} %add_convert_fusion.1), channel_id=1, source_target_pairs={{0,8},{4,12},{8,0},{12,4},{16,24},{20,28},{24,16},{28,20},{1,9},{5... | collective-permute-start | bytes 3145736 | tf_op jit(solution)/shard_map/ppermute | solution.py:245
  556.1 27.6 %collective-permute-start.70 = (bf16[128,2048]{1,0:T(8,128)(2,1)S(1)}, bf16[128,2048]{1,0:T(8,128)(2,1)S(1)}, u32[]{:S(2)}, u32[]{:S(2)}) collective-permute-start(bf16[128,2048]{1,0:T(8,128)(2,1)S(1)} %get-tuple-element.955), channel_id=1, source_target_pairs={{0,1},{1,2},{2,3},{4,5},{5,6},{6,7},{8,9},{9,10},{10,11},{12,13},{... | collective-permute-start | bytes 1572872 | tf_op jit(solution)/shard_map/ppermute | solution.py:270
  583.7 98.2 %collective-permute-start.154 = (bf16[512,1024]{1,0:T(8,128)(2,1)}, bf16[512,1024]{1,0:T(8,128)(2,1)}, u32[]{:S(2)}, u32[]{:S(2)}) collective-permute-start(bf16[512,1024]{1,0:T(8,128)(2,1)} %add_convert_fusion.5), channel_id=1, source_target_pairs={{0,8},{4,12},{8,0},{12,4},{16,24},{20,28},{24,16},{28,20},{1,9},{5... | collective-permute-start | bytes 3145736 | tf_op jit(solution)/shard_map/ppermute | solution.py:245
  585.1 85.6 %collective-permute-start.152 = (bf16[512,1024]{1,0:T(8,128)(2,1)}, bf16[512,1024]{1,0:T(8,128)(2,1)}, u32[]{:S(2)}, u32[]{:S(2)}) collective-permute-start(bf16[512,1024]{1,0:T(8,128)(2,1)} %collective-permute-done.151), channel_id=1, source_target_pairs={{0,4},{4,0},{8,12},{12,8},{16,20},{20,16},{24,28},{28,24},{1,5},{5... | collective-permute-start | bytes 3145736 | tf_op jit(solution)/shard_map/ppermute | solution.py:245
  589.3 85.9 %collective-permute-start.142 = (bf16[512,1024]{1,0:T(8,128)(2,1)}, bf16[512,1024]{1,0:T(8,128)(2,1)}, u32[]{:S(2)}, u32[]{:S(2)}) collective-permute-start(bf16[512,1024]{1,0:T(8,128)(2,1)} %collective-permute-done.141), channel_id=1, source_target_pairs={{0,4},{4,0},{8,12},{12,8},{16,20},{20,16},{24,28},{28,24},{1,5},{5... | collective-permute-start | bytes 3145736 | tf_op jit(solution)/shard_map/ppermute | solution.py:245
  601.1 26.4 %all-to-all-start.1 = ((bf16[128,8,256]{2,0,1:T(8,128)(2,1)}), bf16[128,8,256]{2,0,1:T(8,128)(2,1)S(1)}, u32[]{:S(2)}, u32[]{:S(2)}) async-start(bf16[128,8,256]{2,0,1:T(8,128)(2,1)} %bitcast.503), calls=%async_computation.1 | async-start | bytes 1048576 | tf_op jit(solution)/shard_map/all_to_all | solution.py:443
  626.7 52.2 %collective-permute-start.162 = (bf16[512,1024]{1,0:T(8,128)(2,1)}, bf16[512,1024]{1,0:T(8,128)(2,1)}, u32[]{:S(2)}, u32[]{:S(2)}) collective-permute-start(bf16[512,1024]{1,0:T(8,128)(2,1)} %copy-done.44), channel_id=1, source_target_pairs={{0,4},{4,0},{8,12},{12,8},{16,20},{20,16},{24,28},{28,24},{1,5},{5... | collective-permute-start | bytes 3145736 | tf_op jit(solution)/shard_map/ppermute | solution.py:245
  671.0 26.0 %collective-permute-start.144 = (bf16[512,1024]{1,0:T(8,128)(2,1)S(1)}, bf16[512,1024]{1,0:T(8,128)(2,1)S(1)}, u32[]{:S(2)}, u32[]{:S(2)}) collective-permute-start(bf16[512,1024]{1,0:T(8,128)(2,1)S(1)} %copy-done.26), channel_id=1, source_target_pairs={{0,8},{4,12},{8,0},{12,4},{16,24},{20,28},{24,16},{28,20},{1,9},{5... | collective-permute-start | bytes 3145736 | tf_op jit(solution)/shard_map/ppermute | solution.py:245
  675.2 29.5 %collective-permute-start.112 = (bf16[64,2048]{1,0:T(8,128)(2,1)S(1)}, bf16[64,2048]{1,0:T(8,128)(2,1)S(1)}, u32[]{:S(2)}, u32[]{:S(2)}) collective-permute-start(bf16[64,2048]{1,0:T(8,128)(2,1)S(1)} %copy-done.55), channel_id=1, source_target_pairs={{0,16},{4,20},{8,24},{12,28},{16,0},{20,4},{24,8},{28,12},{1,17},{... | collective-permute-start | bytes 786440 | tf_op jit(solution)/shard_map/ppermute | solution.py:245
  678.9 39.3 %collective-permute-start.111 = (bf16[64,2048]{1,0:T(8,128)(2,1)S(1)}, bf16[64,2048]{1,0:T(8,128)(2,1)S(1)}, u32[]{:S(2)}, u32[]{:S(2)}) collective-permute-start(bf16[64,2048]{1,0:T(8,128)(2,1)S(1)} %copy-done.55), channel_id=1, source_target_pairs={{0,4},{4,0},{8,12},{12,8},{16,20},{20,16},{24,28},{28,24},{1,5},{5... | collective-permute-start | bytes 786440 | tf_op jit(solution)/shard_map/ppermute | solution.py:245
  681.9 26.0 %collective-permute-start.114 = (bf16[64,2048]{1,0:T(8,128)(2,1)S(1)}, bf16[64,2048]{1,0:T(8,128)(2,1)S(1)}, u32[]{:S(2)}, u32[]{:S(2)}) collective-permute-start(bf16[64,2048]{1,0:T(8,128)(2,1)S(1)} %copy-done.55), channel_id=1, source_target_pairs={{0,8},{4,12},{8,0},{12,4},{16,24},{20,28},{24,16},{28,20},{1,9},{5... | collective-permute-start | bytes 786440 | tf_op jit(solution)/shard_map/ppermute | solution.py:245
  718.2 111.2 %collective-permute-start.74 = (bf16[4,128,2048]{2,1,0:T(8,128)(2,1)}, bf16[4,128,2048]{2,1,0:T(8,128)(2,1)}, u32[]{:S(2)}, u32[]{:S(2)}) collective-permute-start(bf16[4,128,2048]{2,1,0:T(8,128)(2,1)} %dynamic-slice_bitcast_fusion.1), channel_id=1, source_target_pairs={{0,4},{4,0},{8,12},{12,8},{16,20},{20,16},{24,28},{28,24},{1,5},{5... | collective-permute-start | bytes 6291464 | tf_op jit(solution)/shard_map/ppermute | solution.py:245
  721.6 29.6 %collective-permute-start.156 = (bf16[512,1024]{1,0:T(8,128)(2,1)}, bf16[512,1024]{1,0:T(8,128)(2,1)S(1)}, u32[]{:S(2)}, u32[]{:S(2)}) collective-permute-start(bf16[512,1024]{1,0:T(8,128)(2,1)} %get-tuple-element.903), channel_id=1, source_target_pairs={{0,16},{4,20},{8,24},{12,28},{16,0},{20,4},{24,8},{28,12},{1,17},{... | collective-permute-start | bytes 3145736 | tf_op jit(solution)/shard_map/ppermute | solution.py:245
  734.6 49.5 %all-to-all-start.2 = ((bf16[8,32,2048]{2,1,0:T(8,128)(2,1)}), bf16[8,32,2048]{2,1,0:T(8,128)(2,1)S(1)}, u32[]{:S(2)}, u32[]{:S(2)}) async-start(bf16[8,32,2048]{2,1,0:T(8,128)(2,1)} %bitcast.606), calls=%async_computation.2 | async-start | bytes 2097152 | tf_op jit(solution)/shard_map/all_to_all | solution.py:479
  738.2 43.4 %collective-permute-start.146 = (bf16[512,1024]{1,0:T(8,128)(2,1)}, bf16[512,1024]{1,0:T(8,128)(2,1)S(1)}, u32[]{:S(2)}, u32[]{:S(2)}) collective-permute-start(bf16[512,1024]{1,0:T(8,128)(2,1)} %get-tuple-element.907), channel_id=1, source_target_pairs={{0,16},{4,20},{8,24},{12,28},{16,0},{20,4},{24,8},{28,12},{1,17},{... | collective-permute-start | bytes 3145736 | tf_op jit(solution)/shard_map/ppermute | solution.py:245
  741.9 42.2 %collective-permute-start.165 = (bf16[512,1024]{1,0:T(8,128)(2,1)}, bf16[512,1024]{1,0:T(8,128)(2,1)}, u32[]{:S(2)}, u32[]{:S(2)}) collective-permute-start(bf16[512,1024]{1,0:T(8,128)(2,1)} %get-tuple-element.899), channel_id=1, source_target_pairs={{0,4},{4,0},{8,12},{12,8},{16,20},{20,16},{24,28},{28,24},{1,5},{5... | collective-permute-start | bytes 3145736 | tf_op jit(solution)/shard_map/ppermute | solution.py:245
  744.7 58.5 %collective-permute-start.166 = (bf16[512,1024]{1,0:T(8,128)(2,1)}, bf16[512,1024]{1,0:T(8,128)(2,1)}, u32[]{:S(2)}, u32[]{:S(2)}) collective-permute-start(bf16[512,1024]{1,0:T(8,128)(2,1)} %get-tuple-element.899), channel_id=1, source_target_pairs={{0,16},{4,20},{8,24},{12,28},{16,0},{20,4},{24,8},{28,12},{1,17},{... | collective-permute-start | bytes 3145736 | tf_op jit(solution)/shard_map/ppermute | solution.py:245
  751.2 59.9 %collective-permute-start.86 = (bf16[512,384]{0,1:T(8,128)(2,1)S(1)}, bf16[512,384]{0,1:T(8,128)(2,1)}, u32[]{:S(2)}, u32[]{:S(2)}) collective-permute-start(bf16[512,384]{0,1:T(8,128)(2,1)S(1)} %get-tuple-element.912), channel_id=1, source_target_pairs={{0,1},{1,2},{2,3},{4,5},{5,6},{6,7},{8,9},{9,10},{10,11},{12,13},{... | collective-permute-start | bytes 1179656 | tf_op jit(solution)/shard_map/ppermute | solution.py:270
  788.4 45.8 %collective-permute-start.157 = (bf16[512,1024]{1,0:T(8,128)(2,1)}, bf16[512,1024]{1,0:T(8,128)(2,1)S(1)}, u32[]{:S(2)}, u32[]{:S(2)}) collective-permute-start(bf16[512,1024]{1,0:T(8,128)(2,1)} %copy-done.45), channel_id=1, source_target_pairs={{0,4},{4,0},{8,12},{12,8},{16,20},{20,16},{24,28},{28,24},{1,5},{5... | collective-permute-start | bytes 3145736 | tf_op jit(solution)/shard_map/ppermute | solution.py:245
  807.3 28.4 %collective-permute-start.147 = (bf16[512,1024]{1,0:T(8,128)(2,1)S(1)}, bf16[512,1024]{1,0:T(8,128)(2,1)S(1)}, u32[]{:S(2)}, u32[]{:S(2)}) collective-permute-start(bf16[512,1024]{1,0:T(8,128)(2,1)S(1)} %copy-done.47), channel_id=1, source_target_pairs={{0,4},{4,0},{8,12},{12,8},{16,20},{20,16},{24,28},{28,24},{1,5},{5... | collective-permute-start | bytes 3145736 | tf_op jit(solution)/shard_map/ppermute | solution.py:245
  811.1 27.6 %collective-permute-start.167 = (bf16[512,1024]{1,0:T(8,128)(2,1)}, bf16[512,1024]{1,0:T(8,128)(2,1)S(1)}, u32[]{:S(2)}, u32[]{:S(2)}) collective-permute-start(bf16[512,1024]{1,0:T(8,128)(2,1)} %collective-permute-done.166), channel_id=1, source_target_pairs={{0,4},{4,0},{8,12},{12,8},{16,20},{20,16},{24,28},{28,24},{1,5},{5... | collective-permute-start | bytes 3145736 | tf_op jit(solution)/shard_map/ppermute | solution.py:245
  825.0 31.5 %collective-permute-start.120 = (bf16[64,2048]{1,0:T(8,128)(2,1)S(1)}, bf16[64,2048]{1,0:T(8,128)(2,1)S(1)}, u32[]{:S(2)}, u32[]{:S(2)}) collective-permute-start(bf16[64,2048]{1,0:T(8,128)(2,1)S(1)} %get-tuple-element.910), channel_id=1, source_target_pairs={{0,1},{1,2},{2,3},{4,5},{5,6},{6,7},{8,9},{9,10},{10,11},{12,13},{... | collective-permute-start | bytes 786440 | tf_op jit(solution)/shard_map/ppermute | solution.py:270
  829.3 41.5 %collective-permute-start.98 = (bf16[256,384]{0,1:T(8,128)(2,1)S(1)}, bf16[256,384]{0,1:T(8,128)(2,1)S(1)}, u32[]{:S(2)}, u32[]{:S(2)}) collective-permute-start(bf16[256,384]{0,1:T(8,128)(2,1)S(1)} %get-tuple-element.982), channel_id=1, source_target_pairs={{0,16},{4,20},{8,24},{12,28},{16,0},{20,4},{24,8},{28,12},{1,17},{... | collective-permute-start | bytes 589832 | tf_op jit(solution)/shard_map/ppermute | solution.py:245
  834.1 38.8 %collective-permute-start.97 = (bf16[256,384]{0,1:T(8,128)(2,1)S(1)}, bf16[256,384]{0,1:T(8,128)(2,1)S(1)}, u32[]{:S(2)}, u32[]{:S(2)}) collective-permute-start(bf16[256,384]{0,1:T(8,128)(2,1)S(1)} %get-tuple-element.982), channel_id=1, source_target_pairs={{0,4},{4,0},{8,12},{12,8},{16,20},{20,16},{24,28},{28,24},{1,5},{5... | collective-permute-start | bytes 589832 | tf_op jit(solution)/shard_map/ppermute | solution.py:245
  856.6 51.9 %collective-permute-start.75 = (bf16[256,1024]{1,0:T(8,128)(2,1)}, bf16[256,1024]{1,0:T(8,128)(2,1)}, u32[]{:S(2)}, u32[]{:S(2)}) collective-permute-start(bf16[256,1024]{1,0:T(8,128)(2,1)} %constant_dynamic-slice_fusion.15), channel_id=1, source_target_pairs={{0,16},{4,20},{8,24},{12,28},{16,0},{20,4},{24,8},{28,12},{1,17},{... | collective-permute-start | bytes 1572872 | tf_op jit(solution)/shard_map/ppermute | solution.py:245
  870.9 38.9 %collective-permute-start.77 = (bf16[256,1024]{1,0:T(8,128)(2,1)}, bf16[256,1024]{1,0:T(8,128)(2,1)}, u32[]{:S(2)}, u32[]{:S(2)}) collective-permute-start(bf16[256,1024]{1,0:T(8,128)(2,1)} %constant_dynamic-slice_fusion.13), channel_id=1, source_target_pairs={{0,8},{4,12},{8,0},{12,4},{16,24},{20,28},{24,16},{28,20},{1,9},{5... | collective-permute-start | bytes 1572872 | tf_op jit(solution)/shard_map/ppermute | solution.py:245
  889.7 30.3 %collective-permute-start.132 = (bf16[32,2048]{1,0:T(8,128)(2,1)}, bf16[32,2048]{1,0:T(8,128)(2,1)S(1)}, u32[]{:S(2)}, u32[]{:S(2)}) collective-permute-start(bf16[32,2048]{1,0:T(8,128)(2,1)} %get-tuple-element.984), channel_id=1, source_target_pairs={{0,16},{4,20},{8,24},{12,28},{16,0},{20,4},{24,8},{28,12},{1,17},{... | collective-permute-start | bytes 393224 | tf_op jit(solution)/shard_map/ppermute | solution.py:245
  890.6 52.5 %collective-permute-start.131 = (bf16[32,2048]{1,0:T(8,128)(2,1)}, bf16[32,2048]{1,0:T(8,128)(2,1)}, u32[]{:S(2)}, u32[]{:S(2)}) collective-permute-start(bf16[32,2048]{1,0:T(8,128)(2,1)} %get-tuple-element.984), channel_id=1, source_target_pairs={{0,4},{4,0},{8,12},{12,8},{16,20},{20,16},{24,28},{28,24},{1,5},{5... | collective-permute-start | bytes 393224 | tf_op jit(solution)/shard_map/ppermute | solution.py:245
  (199 other events, 2283.1 us)

commit v2 on v0

--- a/solution.py
+++ b/solution.py
@@ -1,6 +1,10 @@
+import functools
+
 import jax
 import jax.numpy as jnp
 from jax import lax
+from jax.experimental import pallas as pl
+from jax.experimental.pallas import tpu as pltpu
 from jax.sharding import PartitionSpec as P
 
 EPS = 1e-05
@@ -208,6 +212,940 @@
         axis=1,
     )
     return (query_grad.reshape(length, key_heads * groups * width), pair_grad)
+
+
+MESH = pl.DeviceIdType.MESH
+
+
+def flip(index, mask, bits):
+    for bit in bits:
+        if mask & bit:
+            index = index + bit - 2 * bit * ((index // bit) % 2)
+    return index
+
+
+class Place:
+    def __init__(self, parts, planes):
+        self.parts, self.planes = parts, planes
+        self.seat = lax.axis_index("seq")
+        self.plane = lax.axis_index("fsdp")
+        self.core = self.seat % 2
+        self.chip = self.seat // 2
+        self.seat_bits = [1 << i for i in range(parts.bit_length() - 1)]
+        self.chip_bits = self.seat_bits[1:]
+        self.plane_bits = [1 << i for i in range(planes.bit_length() - 1)]
+
+    def at(self, mask):
+        return flip(self.seat, mask, self.seat_bits)
+
+    def side(self, bit):
+        return (self.seat // bit) % 2
+
+    def colors(self):
+        return (self.chip_bits, self.chip_bits[::-1])
+
+    def enter(self, masks=(), line=False, plane_masks=()):
+        barrier = pltpu.get_barrier_semaphore()
+        peers = [{"seq": self.at(mask)} for mask in masks]
+        if line:
+            peers.append({"fsdp": (self.plane + 1) % self.planes})
+            peers.append({"fsdp": (self.plane + self.planes - 1) % self.planes})
+        for mask in plane_masks:
+            peers.append({"fsdp": flip(self.plane, mask, self.plane_bits)})
+        for peer in peers:
+            pl.semaphore_signal(barrier, inc=1, device_id=peer, device_id_type=MESH)
+        pl.semaphore_wait(barrier, len(peers))
+
+
+class Wire:
+    def __init__(self, sends, receives, locals_):
+        self.sends, self.receives, self.locals = sends, receives, locals_
+        self.count = self.local_count = 0
+        self.open = []
+
+    def remote(self, source, target, device):
+        number = self.count
+        self.count += 1
+        return pltpu.make_async_remote_copy(
+            src_ref=source,
+            dst_ref=target,
+            send_sem=self.sends.at[number],
+            recv_sem=self.receives.at[number],
+            device_id=device,
+            device_id_type=MESH,
+        )
+
+    def send(self, source, target, device):
+        copy = self.remote(source, target, device)
+        copy.start()
+        self.open.append(copy)
+        return copy
+
+    def local(self, source, target):
+        number = self.local_count
+        self.local_count += 1
+        copy = pltpu.make_async_copy(source, target, self.locals.at[number])
+        copy.start()
+        return copy
+
+    def close(self):
+        for copy in self.open:
+            copy.wait_send()
+
+
+def add_rows(target, left, right, step=64):
+    rows = target.shape[0]
+    step = min(step, rows)
+
+    def body(index, carry):
+        at = pl.ds(pl.multiple_of(index * step, step), step)
+        total = left[at, :].astype(jnp.float32) + right[at, :].astype(jnp.float32)
+        target[at, :] = total.astype(target.dtype)
+        return carry
+
+    lax.fori_loop(0, rows // step, body, 0)
+
+
+class LineGather:
+    def __init__(self, wire, here, source, target, share=None):
+        self.here = here
+        planes, plane = here.planes, here.plane
+        above = {"fsdp": (plane + 1) % planes}
+        below = {"fsdp": (plane + planes - 1) % planes}
+        self.ups, self.downs = {}, {}
+        for step in range(1, planes):
+            lower = (plane + planes - step + 1) % planes
+            upper = (plane + step - 1) % planes
+            first = step == 1
+            self.ups[step] = wire.remote(
+                source if first else target(lower), target(lower), above
+            )
+            self.downs[step] = wire.remote(
+                source if first else target(upper), target(upper), below
+            )
+        self.shared = {}
+        if share is not None:
+            for step in range(1, planes):
+                for way, shift in ((0, planes - step), (1, step)):
+                    index = (plane + shift) % planes
+                    self.shared[(step, way)] = wire.remote(
+                        target(index), share(index), {"seq": here.at(1)}
+                    )
+
+    def start(self, step):
+        planes, plane = self.here.planes, self.here.plane
+
+        @pl.when((plane >= step - 1) & (plane <= planes - 2))
+        def _():
+            self.ups[step].start()
+
+        @pl.when((plane + step <= planes) & (plane >= 1))
+        def _():
+            self.downs[step].start()
+
+    def arrive(self, step):
+        planes, plane = self.here.planes, self.here.plane
+
+        @pl.when(plane >= step)
+        def _():
+            self.ups[step].wait_recv()
+            if self.shared:
+                self.shared[(step, 0)].start()
+
+        @pl.when(plane + step <= planes - 1)
+        def _():
+            self.downs[step].wait_recv()
+            if self.shared:
+                self.shared[(step, 1)].start()
+
+    def close(self):
+        planes, plane = self.here.planes, self.here.plane
+        for (step, way), copy in self.shared.items():
+
+            @pl.when(plane >= step if way == 0 else plane + step <= planes - 1)
+            def _(copy=copy):
+                copy.wait()
+
+        for step in range(1, planes):
+
+            @pl.when((plane >= step - 1) & (plane <= planes - 2))
+            def _(step=step):
+                self.ups[step].wait_send()
+
+            @pl.when((plane + step <= planes) & (plane >= 1))
+            def _(step=step):
+                self.downs[step].wait_send()
+
+
+class LineScatter:
+    def __init__(self, wire, here, term, landing):
+        self.wire, self.here, self.term, self.landing = wire, here, term, landing
+        planes, plane = here.planes, here.plane
+        above = {"fsdp": (plane + 1) % planes}
+        below = {"fsdp": (plane + planes - 1) % planes}
+        self.ups, self.downs = {}, {}
+        for step in range(1, planes):
+            self.ups[step] = wire.remote(
+                term((plane + planes - step) % planes), landing(0, step - 1), above
+            )
+            self.downs[step] = wire.remote(
+                term((plane + step) % planes), landing(1, step - 1), below
+            )
+
+    def step(self, step):
+        planes, plane = self.here.planes, self.here.plane
+        mirror = planes - 1 - plane
+        for way, (position, copies, dest) in enumerate(
+            (
+                (plane, self.ups, (plane + planes - step) % planes),
+                (mirror, self.downs, (plane + step) % planes),
+            )
+        ):
+            if step > 1:
+
+                @pl.when((position >= 1) & (position <= step - 1))
+                def _(way=way, copies=copies, dest=dest):
+                    copies[step - 1].wait_recv()
+                    term = self.term(dest)
+                    add_rows(term, term, self.landing(way, step - 2))
+
+            @pl.when(position <= step - 1)
+            def _(copies=copies):
+                copies[step].start()
+
+    def finish(self, out):
+        planes, plane = self.here.planes, self.here.plane
+        own = self.term(plane)
+        last = planes - 1
+
+        @pl.when(plane >= 1)
+        def _():
+            self.ups[last].wait_recv()
+
+        @pl.when(plane <= planes - 2)
+        def _():
+            self.downs[last].wait_recv()
+
+        @pl.when(plane == 0)
+        def _():
+            add_rows(out, own, self.landing(1, last - 1))
+
+        @pl.when(plane == planes - 1)
+        def _():
+            add_rows(out, own, self.landing(0, last - 1))
+
+        @pl.when((plane >= 1) & (plane <= planes - 2))
+        def _():
+            add_rows(own, own, self.landing(0, last - 1))
+            add_rows(out, own, self.landing(1, last - 1))
+
+    def close(self):
+        planes, plane = self.here.planes, self.here.plane
+        mirror = planes - 1 - plane
+        for step in range(1, planes):
+
+            @pl.when(plane <= step - 1)
+            def _(step=step):
+                self.ups[step].wait_send()
+
+            @pl.when(mirror <= step - 1)
+            def _(step=step):
+                self.downs[step].wait_send()
+
+
+class PlaneGather:
+    def __init__(self, wire, here, source, target):
+        self.wire, self.here, self.source, self.target = wire, here, source, target
+        self.incoming = {}
+
+    def _send(self, mask, color, bit):
+        here = self.here
+        target = self.target(here.at(mask), color)
+        source = self.source(color) if mask == 0 else target
+        self.incoming[(mask ^ bit, color)] = self.wire.send(
+            source, target, {"seq": here.at(bit)}
+        )
+
+    def start(self):
+        for position in range(len(self.here.chip_bits)):
+            for color, bits in enumerate(self.here.colors()):
+                self._send(0, color, bits[position])
+        for color in (0, 1):
+            self._send(0, color, 1)
+
+    def forward(self):
+        here = self.here
+        chips = here.parts // 2
+        masks = sorted(
+            (mask * 2 for mask in range(1, chips)), key=lambda mask: bin(mask).count("1")
+        )
+        for mask in masks:
+            for color, bits in enumerate(here.colors()):
+                self.incoming[(mask, color)].wait_recv()
+                last = max(i for i, bit in enumerate(bits) if mask & bit)
+                for bit in bits[last + 1 :]:
+                    self._send(mask, color, bit)
+                self._send(mask, color, 1)
+
+    def finish(self):
+        for mask in range(1, self.here.parts, 2):
+            for color in (0, 1):
+                self.incoming[(mask, color)].wait_recv()
+
+
+class PlaneScatter:
+    def __init__(self, wire, here, product, give, take, current, landing, model):
+        self.wire, self.here, self.product = wire, here, product
+        self.give, self.take, self.current, self.landing = give, take, current, landing
+        self.model = model
+
+    def start(self):
+        here = self.here
+        chips = here.parts // 2
+        self.swaps = {}
+        tokens = self.give.shape[1]
+        seats = [2 * flip(here.chip, mask, [b // 2 for b in here.chip_bits]) for mask in range(chips)]
+        for part in range(self.model // 512):
+            columns = slice(part * 512, (part + 1) * 512)
+            rows = self.product([seat + 1 - here.core for seat in seats], columns)
+            for mask in range(chips):
+                self.give[mask, :, columns] = rows[mask * tokens : (mask + 1) * tokens].astype(
+                    self.give.dtype
+                )
+        for mask in range(chips)[::-1]:
+            self.swaps[mask] = self.wire.send(
+                self.give.at[mask], self.take.at[mask], {"seq": here.at(1)}
+            )
+        half = self.model // 2
+        for part in range(self.model // 512):
+            columns = slice(part * 512, (part + 1) * 512)
+            rows = self.product([seat + here.core for seat in seats], columns)
+            color, inside = divmod(part * 512, half)
+            for mask in range(chips):
+                self.current[color, mask, :, inside : inside + 512] = rows[
+                    mask * tokens : (mask + 1) * tokens
+                ].astype(self.current.dtype)
+
+    def join(self):
+        half = self.model // 2
+        chips = self.here.parts // 2
+        for mask in range(chips)[::-1]:
+            self.swaps[mask].wait_recv()
+            for color in (0, 1):
+                mine = self.current.at[color, mask]
+                add_rows(mine, mine, self.take.at[mask, :, pl.ds(color * half, half)])
+
+    def stage(self, position):
+        here = self.here
+        self.moved = {}
+        for color, bits in enumerate(here.colors()):
+            bit = bits[position]
+            done = sum(bits[:position])
+            for mask in range(here.parts // 2):
+                if mask * 2 & bit and not mask * 2 & done:
+                    low = mask ^ (bit // 2)
+                    self.moved[(color, low)] = self.wire.send(
+                        self.current.at[color, mask],
+                        self.landing.at[position, color, low],
+                        {"seq": here.at(bit)},
+                    )
+
+    def settle(self, position, out):
+        half = self.model // 2
+        last = position == len(self.here.chip_bits) - 1
+        for (color, low), copy in self.moved.items():
+            copy.wait_recv()
+            mine = self.current.at[color, low]
+            if last:
+                target = out.at[:, pl.ds(color * half, half)]
+            else:
+                target = mine
+            add_rows(target, mine, self.landing.at[position, color, low])
+
+
+def head_weights_kernel(parts, planes, x, w, o, x_all, w_all, o_slice, o_all, *sems):
+    here = Place(parts, planes)
+    wire = Wire(*sems)
+    tokens, shard, rows = x.shape[0], w.shape[0], o.shape[0]
+    half = tokens // 2
+    chips = parts // 2
+    chip_masks = [mask * 2 for mask in range(1, chips)]
+    here.enter(chip_masks + [1], line=True)
+    weights = LineGather(
+        wire, here, w, lambda index: w_all.at[pl.ds(pl.multiple_of(index * shard, shard), shard)]
+    )
+    weights.start(1)
+    plane_rows = PlaneGather(
+        wire,
+        here,
+        lambda color: x.at[pl.ds(color * half, half)],
+        lambda seat, color: x_all.at[pl.ds(pl.multiple_of(seat * tokens + color * half, half), half)],
+    )
+    plane_rows.start()
+    kept = [
+        wire.local(x, x_all.at[pl.ds(pl.multiple_of(here.seat * tokens, tokens), tokens)]),
+        wire.local(w, w_all.at[pl.ds(pl.multiple_of(here.plane * shard, shard), shard)]),
+        wire.local(o, o_all.at[here.plane]),
+    ]
+    outer = LineGather(wire, here, o, lambda index: o_all.at[index])
+    weights.arrive(1)
+    if planes > 2:
+        weights.start(2)
+    outer.start(1)
+    plane_rows.forward()
+    for step in range(2, planes):
+        weights.arrive(step)
+        if step + 1 < planes:
+            weights.start(step + 1)
+        outer.arrive(step - 1)
+        outer.start(step)
+    outer.arrive(planes - 1)
+    plane_rows.finish()
+    for copy in kept:
+        copy.wait()
+    dealt = []
+    spot = o_slice.at[pl.ds(pl.multiple_of(here.chip * rows, rows), rows)]
+    for mask in chip_masks:
+        chip = here.at(mask) // 2
+        dealt.append(wire.send(o_all.at[chip], spot, {"seq": here.at(mask)}))
+    own = wire.local(o_all.at[here.chip], spot)
+    own.wait()
+    for copy in dealt:
+        copy.wait_recv()
+    wire.close()
+    weights.close()
+    outer.close()
+
+
+def out_rows_kernel(
+    parts, planes, a, w, c, out, c_all, give, take, current, landing, *sems
+):
+    here = Place(parts, planes)
+    wire = Wire(*sems)
+    tokens, model = c.shape
+    here.enter([mask for mask in here.seat_bits], line=True)
+
+    def product(seats, columns):
+        rows = [a[pl.ds(pl.multiple_of(seat * tokens, tokens), tokens), :] for seat in seats]
+        return jnp.dot(
+            jnp.concatenate(rows, axis=0), w[:, columns], preferred_element_type=jnp.float32
+        )
+
+    mine, theirs = here.core * planes, (1 - here.core) * planes
+    cots = LineGather(
+        wire,
+        here,
+        c,
+        lambda index: c_all.at[mine + index],
+        lambda index: c_all.at[mine + index],
+    )
+    cots.start(1)
+    own = wire.local(c, c_all.at[mine + here.plane])
+    across = wire.send(c, c_all.at[mine + here.plane], {"seq": here.at(1)})
+    rows = PlaneScatter(wire, here, product, give, take, current, landing, model)
+    rows.start()
+    rows.join()
+    stages = len(here.chip_bits)
+    for stage in range(stages):
+        rows.stage(stage)
+        if stage + 1 < planes:
+            cots.arrive(stage + 1)
+            if stage + 2 < planes:
+                cots.start(stage + 2)
+        rows.settle(stage, out)
+    for step in range(stages + 1, planes):
+        cots.arrive(step)
+        if step + 1 < planes:
+            cots.start(step + 1)
+    own.wait()
+    across.wait_recv()
+    wire.close()
+    cots.close()
+
+
+def mid_rows_kernel(parts, planes, m, m_all, *sems):
+    here = Place(parts, planes)
+    wire = Wire(*sems)
+    here.enter([1], line=True)
+    mine = here.core * planes
+    mids = LineGather(
+        wire,
+        here,
+        m,
+        lambda index: m_all.at[mine + index],
+        lambda index: m_all.at[mine + index],
+    )
+    mids.start(1)
+    own = wire.local(m, m_all.at[mine + here.plane])
+    across = wire.send(m, m_all.at[mine + here.plane], {"seq": here.at(1)})
+    for step in range(1, planes):
+        mids.arrive(step)
+        if step + 1 < planes:
+            mids.start(step + 1)
+    own.wait()
+    across.wait_recv()
+    wire.close()
+    mids.close()
+
+
+def halve_kernel(parts, planes, p_a, p_b, p_c, part, s_down, s_first, s_second, mid, keep, *rest):
+    here = Place(parts, planes)
+    stages = len(here.chip_bits) - 1
+    landings, rest = rest[:stages], rest[stages:]
+    current, take, line_landing, *sems = rest
+    wire = Wire(*sems)
+    here.enter(here.seat_bits, line=True)
+    tokens = mid.shape[0]
+    model = p_a.shape[0]
+    swaps = TokenSum(wire, here, part, current, take, line_landing)
+    swaps.start()
+    terms = (p_a, p_b, p_c)
+    moved, kept = {}, {}
+    rows = model // 4
+    for number, term in enumerate(terms):
+        for color, bits in enumerate(here.colors()):
+            base = color * (model // 2)
+            away = pl.multiple_of(base + (1 - here.side(bits[0])) * rows, rows)
+            stay = pl.multiple_of(base + here.side(bits[0]) * rows, rows)
+            moved[(number, color)] = wire.send(
+                term.at[pl.ds(away, rows)],
+                landings[0].at[number, color],
+                {"seq": here.at(bits[0])},
+            )
+            kept[(number, color)] = wire.local(
+                term.at[pl.ds(stay, rows)], keep.at[number, color]
+            )
+    swaps.join()
+    steps = list(range(1, planes))
+    done = 0
+    starts = {(number, color): 0 for number in range(3) for color in (0, 1)}
+    for stage in range(stages):
+        last = stage == stages - 1
+        for number in range(3):
+            take_steps = len(steps) * (stage * 3 + number + 1) // (stages * 3) - done
+            for step in steps[done : done + take_steps]:
+                swaps.step(step)
+            done += take_steps
+            for color, bits in enumerate(here.colors()):
+                moved[(number, color)].wait_recv()
+                if stage == 0:
+                    kept[(number, color)].wait()
+                begin = starts[(number, color)]
+                mine = keep.at[number, color, pl.ds(begin, rows)]
+                if last:
+                    target = (
+                        s_down.at[color]
+                        if number == 0
+                        else (s_first, s_second)[color].at[number - 1]
+                    )
+                    add_rows(target, mine, landings[stage].at[number, color])
+                else:
+                    add_rows(mine, mine, landings[stage].at[number, color])
+                    bit = bits[stage + 1]
+                    half = rows // 2
+                    away = pl.multiple_of(begin + (1 - here.side(bit)) * half, half)
+                    moved[(number, color)] = wire.send(
+                        keep.at[number, color, pl.ds(away, half)],
+                        landings[stage + 1].at[number, color],
+                        {"seq": here.at(bit)},
+                    )
+                    starts[(number, color)] = pl.multiple_of(begin + here.side(bit) * half, half)
+        rows //= 2
+    swaps.finish(mid)
+    wire.close()
+    swaps.close()
+
+
+class TokenSum:
+    def __init__(self, wire, here, part, current, take, landing):
+        self.wire, self.here, self.part = wire, here, part
+        self.current, self.take = current, take
+        self.line = LineScatter(
+            wire, here, lambda index: current.at[index], lambda way, step: landing.at[way, step]
+        )
+
+    def start(self):
+        here, planes = self.here, self.here.planes
+        self.across = self.wire.send(
+            self.part.at[pl.ds((1 - here.core) * planes, planes)], self.take, {"seq": here.at(1)}
+        )
+        self.own = self.wire.local(self.part.at[pl.ds(here.core * planes, planes)], self.current)
+
+    def join(self):
+        self.own.wait()
+        self.across.wait_recv()
+
+        def body(index, carry):
+            row = self.current.at[index]
+            add_rows(row, row, self.take.at[index])
+            return carry
+
+        lax.fori_loop(0, self.here.planes, body, 0)
+
+    def step(self, step):
+        self.line.step(step)
+
+    def finish(self, out):
+        self.line.finish(out)
+
+    def close(self):
+        self.line.close()
+
+
+def spread_kernel(parts, planes, h, s, part, h_all, t, block, current, take, line_landing, *sems):
+    here = Place(parts, planes)
+    wire = Wire(*sems)
+    here.enter(here.seat_bits, line=True)
+    tokens = h.shape[0]
+    half = tokens // 2
+    rows = PlaneGather(
+        wire,
+        here,
+        lambda color: h.at[pl.ds(color * half, half)],
+        lambda seat, color: h_all.at[pl.ds(pl.multiple_of(seat * tokens + color * half, half), half)],
+    )
+    swaps = TokenSum(wire, here, part, current, take, line_landing)
+    rows.start()
+    own = wire.local(h, h_all.at[pl.ds(pl.multiple_of(here.seat * tokens, tokens), tokens)])
+    swaps.start()
+    moved = [
+        wire.send(s.at[color], t.at[color], {"seq": here.at(bits[-1])})
+        for color, bits in enumerate(here.colors())
+    ]
+    rows.forward()
+    swaps.join()
+    for step in range(1, planes):
+        swaps.step(step)
+    rows.finish()
+    for color in (0, 1):
+        moved[color].wait_recv()
+        add_rows(t.at[color], t.at[color], s.at[color])
+    own.wait()
+    swaps.finish(block)
+    wire.close()
+    swaps.close()
+
+
+def in_rows_kernel(
+    parts,
+    planes,
+    a,
+    w,
+    head_part,
+    out_part,
+    out,
+    head_sum,
+    out_sum,
+    give,
+    take,
+    current,
+    landing,
+    head_current,
+    head_landing,
+    dealt,
+    out_landing,
+    *sems,
+):
+    here = Place(parts, planes)
+    wire = Wire(*sems)
+    tokens, model = out.shape
+    shard = head_sum.shape[0]
+    rows_out = out_sum.shape[0]
+    chips = parts // 2
+    chip_masks = [mask * 2 for mask in range(1, chips)]
+    here.enter(chip_masks + [1], line=True)
+    head_own = wire.local(head_part, head_current)
+    deals = []
+    for mask in chip_masks:
+        chip = here.at(mask) // 2
+        deals.append(
+            wire.send(
+                out_part.at[pl.ds(pl.multiple_of(chip * rows_out, rows_out), rows_out)],
+                dealt.at[here.chip],
+                {"seq": here.at(mask)},
+            )
+        )
+    deal_own = wire.local(
+        out_part.at[pl.ds(pl.multiple_of(here.chip * rows_out, rows_out), rows_out)],
+        dealt.at[here.chip],
+    )
+
+    def product(seats, columns):
+        rows = [a[pl.ds(pl.multiple_of(seat * tokens, tokens), tokens), :] for seat in seats]
+        return lax.dot_general(
+            jnp.concatenate(rows, axis=0),
+            w[columns, :],
+            (((1,), (1,)), ((), ())),
+            preferred_element_type=jnp.float32,
+        )
+
+    heads = LineScatter(
+        wire, here, lambda index: head_current.at[index], lambda way, step: head_landing.at[way, step]
+    )
+    outer = LineScatter(
+        wire, here, lambda index: dealt.at[index], lambda way, step: out_landing.at[way, step]
+    )
+    head_own.wait()
+    heads.step(1)
+    rows = PlaneScatter(wire, here, product, give, take, current, landing, model)
+    rows.start()
+    deal_own.wait()
+    for copy in deals:
+        copy.wait_recv()
+    outer.step(1)
+    rows.join()
+    stages = len(here.chip_bits)
+    for stage in range(stages):
+        rows.stage(stage)
+        if stage + 2 < planes:
+            heads.step(stage + 2)
+            outer.step(stage + 2)
+        rows.settle(stage, out)
+    for step in range(stages + 2, planes):
+        heads.step(step)
+        outer.step(step)
+    heads.finish(head_sum)
+    outer.finish(out_sum)
+    wire.close()
+    heads.close()
+    outer.close()
+
+
+def collect_kernel(
+    parts,
+    planes,
+    t_down,
+    t_first,
+    t_second,
+    head,
+    outer,
+    slope,
+    grad_down,
+    grad_gate,
+    grad_up,
+    head_all,
+    outer_all,
+    slope_out,
+    near,
+    far,
+    stage_rows,
+    slope_sums,
+    slope_landing,
+    *sems,
+):
+    here = Place(parts, planes)
+    wire = Wire(*sems)
+    here.enter(here.seat_bits, plane_masks=here.plane_bits)
+    shard, rows_out = head.shape[0], outer.shape[0]
+    chips = parts // 2
+
+    bits = [("seq", bit) for bit in here.seat_bits] + [("fsdp", bit) for bit in here.plane_bits]
+    slope_copies = []
+
+    def slope_send(number):
+        axis, bit = bits[number]
+        index = here.at(bit) if axis == "seq" else flip(here.plane, bit, here.plane_bits)
+        source = slope if number == 0 else slope_sums.at[number - 1]
+        slope_copies.append(wire.send(source, slope_landing.at[number], {axis: index}))
+
+    def slope_add(number):
+        slope_copies[number].wait_recv()
+        source = slope if number == 0 else slope_sums.at[number - 1]
+        target = slope_out if number == len(bits) - 1 else slope_sums.at[number]
+        target[...] = source[...] + slope_landing[number]
+
+    slope_send(0)
+    half = shard // 2
+    heads = PlaneGather(
+        wire,
+        here,
+        lambda color: head.at[pl.ds(color * half, half)],
+        lambda seat, color: head_all.at[seat, pl.ds(color * half, half)],
+    )
+    half_out = rows_out // 2
+
+    def outer_target(seat, color):
+        start = ((seat % 2) * chips + seat // 2) * rows_out + color * half_out
+        return outer_all.at[pl.ds(pl.multiple_of(start, half_out), half_out)]
+
+    outers = PlaneGather(
+        wire, here, lambda color: outer.at[pl.ds(color * half_out, half_out)], outer_target
+    )
+    heads.start()
+    outers.start()
+    own_start = (here.core * chips + here.chip) * rows_out
+    own = [
+        wire.local(head, head_all.at[here.seat]),
+        wire.local(
+            outer, outer_all.at[pl.ds(pl.multiple_of(own_start, rows_out), rows_out)]
+        ),
+    ]
+
+    model = near.shape[1]
+    units = near.shape[2]
+    size = t_down.shape[1]
+    outs = (grad_down, grad_gate, grad_up)
+    sources = {}
+    incoming = {}
+    swaps = {}
+
+    def final(number, color):
+        if number == 0:
+            return t_down.at[color]
+        return (t_first, t_second)[color].at[number - 1]
+
+    def rows_at(start):
+        return pl.ds(pl.multiple_of(start, size), size)
+
+    starts = {}
+    for color, order in enumerate(here.colors()):
+        start = color * (model // 2)
+        rows = model // 2
+        for bit in order[:-1]:
+            rows //= 2
+            start = start + here.side(bit) * rows
+        starts[color] = start
+
+    def pass_on(number, color, start, source, bit, rows):
+        incoming_start = start + rows - 2 * rows * here.side(bit)
+        copy = wire.send(
+            source, near.at[number, rows_at(start)], {"seq": here.at(bit)}
+        )
+        return incoming_start, copy
+
+    def swap_core(number, start, source):
+        return wire.send(source, far.at[number, rows_at(start)], {"seq": here.at(1)})
+
+    held = {}
+    for number in range(3):
+        for color, order in enumerate(here.colors()):
+            rest = order[:-1]
+            source = final(number, color)
+            pieces = [(starts[color], source, None)]
+            rows = size
+            if rest:
+                pieces.append(
+                    _pending(
+                        pass_on(number, color, starts[color], source, rest[-1], rows),
+                        near,
+                        number,
+                        rows_at,
+                    )
+                )
+            swaps[(number, color)] = [(starts[color], swap_core(number, starts[color], source))]
+            held[(number, color)] = pieces
+
+    blocks = []
+    count = [0]
+
+    def write(number, start, source, column):
+        step = stage_rows.shape[1]
+        for part in range(size // step):
+            slot = count[0] % stage_rows.shape[0]
+            if count[0] >= stage_rows.shape[0]:
+                blocks[count[0] - stage_rows.shape[0]].wait()
+            count[0] += 1
+
+            def body(index, carry):
+                at = pl.ds(pl.multiple_of(index * 32, 32), 32)
+                from_ = pl.ds(pl.multiple_of(part * step + index * 32, 32), 32)
+                stage_rows[slot, at, :] = source[from_, :].astype(jnp.float32)
+                return carry
+
+            lax.fori_loop(0, step // 32, body, 0)
+            blocks.append(
+                wire.local(
+                    stage_rows.at[slot],
+                    outs[number].at[
+                        pl.ds(pl.multiple_of(start + part * step, step), step),
+                        pl.ds(pl.multiple_of(column * units, units), units),
+                    ],
+                )
+            )
+
+    slope_add(0)
+    if len(bits) > 1:
+        slope_send(1)
+    heads.forward()
+    outers.forward()
+    for number in range(1, len(bits)):
+        slope_add(number)
+        if number + 1 < len(bits):
+            slope_send(number + 1)
+        if number == 1:
+            for color in (0, 1):
+                write(0, starts[color], final(0, color), here.core)
+    for number in range(3):
+        if number > 0:
+            for color in (0, 1):
+                write(number, starts[color], final(number, color), here.core)
+        for color, order in enumerate(here.colors()):
+            rest = order[:-1]
+            pieces = held[(number, color)]
+            position = len(rest) - 1
+            rows = size
+            while position >= 0:
+                fresh = [piece for piece in pieces if piece[2] is not None]
+                for piece in fresh:
+                    piece[2].wait_recv()
+                    swaps[(number, color)].append(
+                        (piece[0], swap_core(number, piece[0], piece[1]))
+                    )
+                    write(number, piece[0], piece[1], here.core)
+                pieces = [(start, source, None) for start, source, _ in pieces]
+                position -= 1
+                rows *= 2
+                if position >= 0:
+                    bit = rest[position]
+                    pieces = pieces + [
+                        _pending(
+                            pass_on(number, color, start, source, bit, rows), near, number, rows_at
+                        )
+                        for start, source, _ in pieces
+                    ]
+        for color in (0, 1):
+            for start, copy in swaps[(number, color)]:
+                copy.wait_recv()
+                write(number, start, far.at[number, rows_at(start)], 1 - here.core)
+    heads.finish()
+    outers.finish()
+    for copy in own:
+        copy.wait()
+    for copy in blocks[-stage_rows.shape[0] :]:
+        copy.wait()
+    wire.close()
+
+
+def _pending(passed, near, number, rows_at):
+    start, copy = passed
+    return (start, near.at[number, rows_at(start)], copy)
+
+
+SENDS, LOCALS = 128, 96
+
+
+def call(kernel, mesh_sizes, number, inputs, in_vmem, outputs, scratch, out_vmem=None):
+    vmem = pl.BlockSpec(memory_space=pltpu.VMEM)
+    anywhere = pl.BlockSpec(memory_space=pl.ANY)
+    out_vmem = out_vmem or [True] * len(outputs)
+    semaphores = [
+        pltpu.SemaphoreType.DMA((SENDS,)),
+        pltpu.SemaphoreType.DMA((SENDS,)),
+        pltpu.SemaphoreType.DMA((LOCALS,)),
+    ]
+    return pl.pallas_call(
+        functools.partial(kernel, *mesh_sizes),
+        out_shape=[jax.ShapeDtypeStruct(shape, kind) for shape, kind in outputs],
+        in_specs=[vmem if inside else anywhere for inside in in_vmem],
+        out_specs=[vmem if inside else anywhere for inside in out_vmem],
+        scratch_shapes=[pltpu.VMEM(shape, kind) for shape, kind in scratch] + semaphores,
+        compiler_params=pltpu.CompilerParams(
+            collective_id=number, has_side_effects=True, vmem_limit_bytes=VMEM_BYTES
+        ),
+    )(*inputs)
+
+
+VMEM_BYTES = 62 * 1024 * 1024
 
 
 def per_device(
@@ -228,93 +1166,158 @@
     tokens = inputs.shape[1]
     model = inputs.shape[2]
     width = query_gain.shape[0]
-    heads = query_weight.shape[1] // width
     pair_heads = key_weight.shape[1] // width
     parts = lax.axis_size("seq")
+    planes = lax.axis_size("fsdp")
+    sizes = (parts, planes)
+    chips = parts // 2
     copies = max(1, parts // pair_heads)
-    local_pairs = pair_heads * copies // parts
-    local_heads = heads // parts
-    local_groups = local_heads // local_pairs
+    place = lax.axis_index("seq")
+    plane = lax.axis_index("fsdp")
+    core = place % 2
+    query_cols = model // parts
+    head_cols = query_cols + 2 * width
+    local_groups = query_cols // width
+    shard = query_weight.shape[0]
+    piece_rows = shard // parts
+    length = parts * tokens
+    units = gate_weight.shape[1] // 2
+    f32, bf16 = jnp.float32, jnp.bfloat16
+    halvings = chips.bit_length() - 2
+    last_rows = model // 2 >> halvings
     rows_in = inputs.reshape(tokens, model)
     cot_rows = cotangent.reshape(tokens, model)
-    full_query, full_key, full_value, full_output = (
-        lax.all_gather(query_weight, "fsdp", axis=0, tiled=True),
-        lax.all_gather(key_weight, "fsdp", axis=0, tiled=True),
-        lax.all_gather(value_weight, "fsdp", axis=0, tiled=True),
-        lax.all_gather(output_weight, "fsdp", axis=0, tiled=True),
-    )
-    source = rows_in.astype(jnp.float32)
+
+    pair_index = place // copies
+    head_weights = jnp.concatenate(
+        [
+            lax.dynamic_slice(query_weight, (0, place * query_cols), (shard, query_cols)),
+            lax.dynamic_slice(key_weight, (0, pair_index * width), (shard, width)),
+            lax.dynamic_slice(value_weight, (0, pair_index * width), (shard, width)),
+        ],
+        axis=1,
+    )
+    piece_index = core * chips + place // 2
+    out_piece = lax.dynamic_slice_in_dim(output_weight, piece_index * piece_rows, piece_rows, 0)
+    source = rows_in.astype(f32)
     first = rms_factor(source)
-    normed_in = (source * first * attention_gain).astype(jnp.bfloat16)
-    query_proj = matmul(normed_in, full_query)
-    key_proj = matmul(normed_in, full_key)
-    values = matmul(normed_in, full_value).astype(jnp.bfloat16)
-    positions = lax.axis_index("seq") * tokens + jnp.arange(tokens, dtype=jnp.int32)
-    cosine, sine = rope_tables(positions, width)
-    queries = prepare(query_proj, query_gain, cosine, sine).astype(jnp.bfloat16)
-    keys = prepare(key_proj, key_gain, cosine, sine).astype(jnp.bfloat16)
-    key_copies = jnp.repeat(keys.reshape(tokens, pair_heads, width), copies, axis=1)
-    value_copies = jnp.repeat(values.reshape(tokens, pair_heads, width), copies, axis=1)
-    pair_send = jnp.concatenate([key_copies, value_copies], axis=2)
-    pair_send = pair_send.reshape(tokens, parts * 2 * local_pairs * width)
-    query_rows, pair_rows = (
-        lax.all_to_all(queries, "seq", split_axis=1, concat_axis=0, tiled=True),
-        lax.all_to_all(pair_send, "seq", split_axis=1, concat_axis=0, tiled=True),
-    )
-    out_rows, log_rows = attend_heads(query_rows, pair_rows, local_groups, width)
-    attended = lax.all_to_all(out_rows, "seq", split_axis=0, concat_axis=1, tiled=True)
-    middle = source + matmul(attended, full_output)
+    normed_in = (source * first * attention_gain).astype(bf16)
+    normed_all, head_full, out_slice = call(
+        head_weights_kernel,
+        sizes,
+        0,
+        (normed_in, head_weights, out_piece),
+        (True, True, True),
+        [((length, model), bf16), ((model, head_cols), bf16), ((query_cols, model), bf16)],
+        [((planes, piece_rows, model), bf16)],
+    )
+
+    proj = matmul(normed_all, head_full)
+    query_proj = proj[:, :query_cols]
+    key_proj = proj[:, query_cols : query_cols + width]
+    values = proj[:, query_cols + width :].astype(bf16)
+    cosine, sine = rope_tables(jnp.arange(length, dtype=jnp.int32), width)
+    queries = prepare(query_proj, query_gain, cosine, sine).astype(bf16)
+    keys = prepare(key_proj, key_gain, cosine, sine).astype(bf16)
+    pair_rows = jnp.concatenate([keys, values], axis=1)
+    out_rows, log_rows = attend_heads(queries, pair_rows, local_groups, width)
+
+    half = model // 2
+    scatter_scratch = [
+        ((chips, tokens, model), bf16),
+        ((chips, tokens, model), bf16),
+        ((2, chips, tokens, half), bf16),
+        ((halvings + 1, 2, chips, tokens, half), bf16),
+    ]
+    out_sum, cot_all = call(
+        out_rows_kernel,
+        sizes,
+        1,
+        (out_rows, out_slice, cot_rows),
+        (True, True, True),
+        [((tokens, model), f32), ((2 * planes, tokens, model), bf16)],
+        scatter_scratch,
+    )
+    middle = source + out_sum
     second = rms_factor(middle)
-    normed_mid = (middle * second * feedforward_gain).astype(jnp.bfloat16)
-    mid_all, cot_all = (
-        lax.all_gather(normed_mid, "fsdp", axis=0, tiled=True),
-        lax.all_gather(cot_rows, "fsdp", axis=0, tiled=True),
-    )
-    gate = matmul(mid_all, gate_weight)
-    lifted = matmul(mid_all, up_weight)
+    normed_mid = (middle * second * feedforward_gain).astype(bf16)
+    (mid_all,) = call(
+        mid_rows_kernel,
+        sizes,
+        2,
+        (normed_mid,),
+        (True,),
+        [((2 * planes, tokens, model), bf16)],
+        [],
+    )
+    cot_all = cot_all.reshape(-1, model)
+    mid_all = mid_all.reshape(-1, model)
+    gate_half = lax.dynamic_slice_in_dim(gate_weight, core * units, units, 1)
+    up_half = lax.dynamic_slice_in_dim(up_weight, core * units, units, 1)
+    down_half = lax.dynamic_slice_in_dim(down_weight, core * units, units, 1)
+    hidden_grad = matmul(cot_all, down_half)
+    gate = matmul(mid_all, gate_half)
+    lifted = matmul(mid_all, up_half)
     hidden = activate(gate, lifted)
-    block_rows = middle + lax.psum_scatter(
-        inner_cols(hidden, down_weight).astype(jnp.bfloat16),
-        "fsdp",
-        scatter_dimension=0,
-        tiled=True,
-    ).astype(jnp.float32)
-    hidden_grad = matmul(cot_all, down_weight)
     gate_grad, lifted_grad = gate_back(hidden_grad, gate, lifted)
-    grad_gate = inner_rows(mid_all, gate_grad)
-    grad_up = inner_rows(mid_all, lifted_grad)
-    grad_down = inner_rows(cot_all, hidden)
-    mid_grad = lax.psum_scatter(
-        (inner_cols(gate_grad, gate_weight) + inner_cols(lifted_grad, up_weight)).astype(
-            jnp.bfloat16
-        ),
-        "fsdp",
-        scatter_dimension=0,
-        tiled=True,
-    ).astype(jnp.float32)
+
+    mid_part = inner_cols(gate_grad, gate_half) + inner_cols(lifted_grad, up_half)
+    mid_part = mid_part.astype(bf16).reshape(2 * planes, tokens, model)
+    down_part = inner_cols(hidden, down_half).astype(bf16).reshape(2 * planes, tokens, model)
+    part_down = inner_rows(cot_all, hidden).astype(bf16)
+    part_gate = inner_rows(mid_all, gate_grad).astype(bf16)
+    part_up = inner_rows(mid_all, lifted_grad).astype(bf16)
+
+    line_scratch = [
+        ((planes, tokens, model), bf16),
+        ((planes, tokens, model), bf16),
+        ((2, planes - 1, tokens, model), bf16),
+    ]
+    quarter = model // 4
+    s_down, s_first, s_second, mid_grad = call(
+        halve_kernel,
+        sizes,
+        3,
+        (part_down, part_gate, part_up, mid_part),
+        (False, False, False, False),
+        [
+            ((2, last_rows, units), bf16),
+            ((2, last_rows, units), bf16),
+            ((2, last_rows, units), bf16),
+            ((tokens, model), f32),
+        ],
+        [((3, 2, quarter, units), bf16)]
+        + [((3, 2, quarter >> stage, units), bf16) for stage in range(halvings)]
+        + line_scratch,
+    )
+
     feedforward_slope = jnp.sum(mid_grad * middle * second, axis=0)
-    middle_grad = cot_rows.astype(jnp.float32) + norm_back(
-        mid_grad, middle, second, feedforward_gain
-    )
-    middle_half = middle_grad.astype(jnp.bfloat16)
-    attended_grad = inner_cols(middle_half, full_output).astype(jnp.bfloat16)
-    grad_rows = lax.all_to_all(attended_grad, "seq", split_axis=1, concat_axis=0, tiled=True)
-    query_grad_rows, pair_grad_rows = attend_back(
-        query_rows, pair_rows, out_rows, log_rows, grad_rows, local_groups, width
-    )
-    query_back, pair_back = (
-        lax.all_to_all(
-            query_grad_rows.astype(jnp.bfloat16), "seq", split_axis=0, concat_axis=1, tiled=True
-        ).astype(query_grad_rows.dtype),
-        lax.all_to_all(
-            pair_grad_rows.astype(jnp.bfloat16), "seq", split_axis=0, concat_axis=1, tiled=True
-        ).astype(pair_grad_rows.dtype),
-    )
-    pair_back = pair_back.reshape(tokens, parts, 2, local_pairs, width)
-    key_back = pair_back[:, :, 0].reshape(tokens, pair_heads, copies, width).sum(axis=2)
-    value_back = pair_back[:, :, 1].reshape(tokens, pair_heads, copies, width).sum(axis=2)
-    key_back = key_back.reshape(tokens, pair_heads * width)
-    value_back = value_back.reshape(tokens, pair_heads * width)
+    middle_grad = cot_rows.astype(f32) + norm_back(mid_grad, middle, second, feedforward_gain)
+    middle_half = middle_grad.astype(bf16)
+    middle_all, t_down, down_sum = call(
+        spread_kernel,
+        sizes,
+        4,
+        (middle_half, s_down, down_part),
+        (True, True, False),
+        [((length, model), bf16), ((2, last_rows, units), bf16), ((tokens, model), f32)],
+        line_scratch,
+    )
+    block_rows = middle + down_sum
+
+    def trade(value, bit):
+        other = lax.ppermute(value, "seq", [(i, i ^ bit) for i in range(parts)])
+        return (value.astype(f32) + other.astype(f32)).astype(bf16)
+
+    t_first = trade(s_first, parts // 2)
+    t_second = trade(s_second, 2)
+
+    attended_grad = inner_cols(middle_all, out_slice).astype(bf16)
+    query_back, pair_back = attend_back(
+        queries, pair_rows, out_rows, log_rows, attended_grad, local_groups, width
+    )
+    key_back = pair_back[:, :width]
+    value_back = pair_back[:, width:]
     _, query_pull = jax.vjp(
         lambda proj_in, gain_in: prepare(proj_in, gain_in, cosine, sine), query_proj, query_gain
     )
@@ -323,45 +1326,67 @@
         lambda proj_in, gain_in: prepare(proj_in, gain_in, cosine, sine), key_proj, key_gain
     )
     key_proj_grad, key_slope = key_pull(key_back)
-    query_half = query_proj_grad.astype(jnp.bfloat16)
-    key_half = key_proj_grad.astype(jnp.bfloat16)
-    value_half = value_back.astype(jnp.bfloat16)
-    proj_grads = jnp.concatenate([query_half, key_half, value_half], axis=1)
-    attn_rows_sum = lax.psum_scatter(
-        jnp.concatenate(
-            [inner_rows(normed_in, proj_grads), inner_rows(attended, middle_half)], axis=1
-        ).astype(jnp.bfloat16),
-        "fsdp",
-        scatter_dimension=0,
-        tiled=True,
-    ).astype(jnp.float32)
-    pair_width = pair_heads * width
-    grad_query = attn_rows_sum[:, :model]
-    grad_key = attn_rows_sum[:, model : model + pair_width]
-    grad_value = attn_rows_sum[:, model + pair_width : model + 2 * pair_width]
-    grad_output = attn_rows_sum[:, model + 2 * pair_width :]
-    in_grad = (
-        inner_cols(query_half, full_query)
-        + inner_cols(key_half, full_key)
-        + inner_cols(value_half, full_value)
+    halves = jnp.concatenate([query_proj_grad, key_proj_grad, value_back], axis=1).astype(bf16)
+    head_part = inner_rows(normed_all, halves).astype(bf16).reshape(planes, shard, head_cols)
+    out_part = inner_rows(out_rows, middle_all).astype(bf16)
+
+    in_grad, head_sum, outer_sum = call(
+        in_rows_kernel,
+        sizes,
+        5,
+        (halves, head_full, head_part, out_part),
+        (True, True, False, False),
+        [((tokens, model), f32), ((shard, head_cols), bf16), ((piece_rows, model), bf16)],
+        scatter_scratch
+        + [
+            ((planes, shard, head_cols), bf16),
+            ((2, planes - 1, shard, head_cols), bf16),
+            ((planes, piece_rows, model), bf16),
+            ((2, planes - 1, piece_rows, model), bf16),
+        ],
     )
     attention_slope = jnp.sum(in_grad * source * first, axis=0)
-    input_rows = (middle_grad + norm_back(in_grad, source, first, attention_gain)).astype(
-        jnp.bfloat16
-    )
-    grad_query, grad_key, grad_value, grad_output, grad_gate, grad_up, grad_down = (
-        lax.psum(grad_query.astype(jnp.bfloat16), "seq").astype(jnp.float32),
-        lax.psum(grad_key.astype(jnp.bfloat16), "seq").astype(jnp.float32),
-        lax.psum(grad_value.astype(jnp.bfloat16), "seq").astype(jnp.float32),
-        lax.psum(grad_output.astype(jnp.bfloat16), "seq").astype(jnp.float32),
-        lax.psum(grad_gate.astype(jnp.bfloat16), "seq").astype(jnp.float32),
-        lax.psum(grad_up.astype(jnp.bfloat16), "seq").astype(jnp.float32),
-        lax.psum(grad_down.astype(jnp.bfloat16), "seq").astype(jnp.float32),
-    )
-    attention_slope, query_slope, key_slope, feedforward_slope = lax.psum(
-        (attention_slope, query_slope, key_slope, feedforward_slope), ("seq", "fsdp")
-    )
-    block_out = block_rows.astype(jnp.bfloat16).reshape(1, tokens, model)
+    input_rows = (middle_grad + norm_back(in_grad, source, first, attention_gain)).astype(bf16)
+
+    slopes = jnp.concatenate([attention_slope, feedforward_slope, query_slope, key_slope])
+    slope_cols = -(-slopes.shape[0] // 1024) * 128
+    slopes = jnp.pad(slopes, (0, 8 * slope_cols - slopes.shape[0])).reshape(8, slope_cols)
+    rounds = (parts * planes).bit_length() - 1
+    grad_down, grad_gate, grad_up, head_all, outer_all, slopes = call(
+        collect_kernel,
+        sizes,
+        6,
+        (t_down, t_first, t_second, head_sum, outer_sum, slopes),
+        (True,) * 6,
+        [
+            ((model, 2 * units), f32),
+            ((model, 2 * units), f32),
+            ((model, 2 * units), f32),
+            ((parts, shard, head_cols), bf16),
+            ((shard, model), bf16),
+            ((8, slope_cols), f32),
+        ],
+        [
+            ((3, model, units), bf16),
+            ((3, model, units), bf16),
+            ((4, 256, units), f32),
+            ((rounds, 8, slope_cols), f32),
+            ((rounds, 8, slope_cols), f32),
+        ],
+        [False, False, False, True, True, True],
+    )
+    grad_query = head_all[:, :, :query_cols].transpose(1, 0, 2).reshape(shard, -1).astype(f32)
+    grad_pair = head_all[:, :, query_cols:].astype(f32)
+    grad_pair = grad_pair.reshape(parts // copies, copies, shard, 2, width).sum(axis=1)
+    grad_key = grad_pair[:, :, 0].transpose(1, 0, 2).reshape(shard, -1)
+    grad_value = grad_pair[:, :, 1].transpose(1, 0, 2).reshape(shard, -1)
+    grad_output = outer_all.astype(f32)
+    slopes = slopes.reshape(-1)
+    attention_slope = slopes[:model]
+    feedforward_slope = slopes[model : 2 * model]
+    query_slope = slopes[2 * model : 2 * model + width]
+    key_slope = slopes[2 * model + width : 2 * model + 2 * width]
+    block_out = block_rows.astype(bf16).reshape(1, tokens, model)
     input_grad = input_rows.reshape(1, tokens, model)
     return (
         block_out,

time: 1530 us -> 787 us (0.51)
  waiting for transfers between devices: 1160 us -> 0.01 us
  Pallas kernels: 0 us -> 534 us
  blocking collectives: 55.3 us -> 0 us
  matrix products: 152 us -> 123 us
  starting transfers between devices: 19.8 us -> 1.81 us
  local copies, waits for them, and re-layouts: 49.7 us -> 65.1 us
    pallas_call x0 -> x7, Pallas kernels: none -> 534 us  [call(): pl.pallas_call(functools.partial(kernel, *mesh_sizes), out_shape=[jax.Sha...]
    all_gather x6 -> x0, waiting for transfers between devices: 417 us -> none  [the longest x1 141 us: per_device(): lax.all_gather(query_weight, 'fsdp', axis=0, tiled=True)]
    reduce_scatter x3 -> x0, waiting for transfers between devices: 397 us -> none  [the longest x1 320 us: per_device(): lax.psum_scatter(jnp.concatenate([inner_rows(normed_in, proj_grads), inne...]
    psum x1 -> x0, waiting for transfers between devices: 312 us -> none  [per_device(): lax.psum(grad_down.astype(jnp.bfloat16), 'seq').astype(jnp.float32)]
    psum x1 -> x0, blocking collectives: 43.2 us -> none  [per_device(): lax.psum((attention_slope, query_slope, key_slope, feedforward_slope), ('...]
    all_to_all x5 -> x0, waiting for transfers between devices: 26.8 us -> none  [the longest x1 9.71 us: per_device(): lax.all_to_all(attended_grad, 'seq', split_axis=1, concat_axis=0, tiled=T...]
    unnamed x94 -> x138, local copies, waits for them, and re-layouts: 17.3 us -> 44.1 us
    all_to_all x5 -> x0, starting transfers between devices: 18.8 us -> none  [the longest x1 4.17 us: per_device(): lax.all_to_all(query_grad_rows.astype(jnp.bfloat16), 'seq', split_axis=0,...]
  transfers between devices with their start and end apart: 15 -> 2, of which waited for: 13 -> 0; matrix products, arithmetic and copies ran while one was open for 8% -> 8% of each run, Pallas kernels for 0% -> 22%
where the time goes in v2:
time: 787 us; the launch traced here: 781 us
  Pallas kernels  534 us (68%)
  matrix products  123 us (16%)
  local copies, waits for them, and re-layouts  65.1 us (8%)
  other arithmetic  54.6 us (7%)
    pallas_call x7, Pallas kernels, call(): pl.pallas_call(functools.partial(kernel, *mesh_sizes), out_shape=[jax.Sha...  534 us
    unnamed x138, local copies, waits for them, and re-layouts  44.1 us
    dot_general x5, matrix products, inner_rows(): lax.dot_general(left, right, (((0,), (0,)), ((), ())), preferred_element_...  40.1 us
    dot_general x4, matrix products, matmul(): return jnp.dot(left, right, preferred_element_type=jnp.float32)  34.7 us
    dot_general x4, matrix products, inner_cols(): lax.dot_general(left, right, (((1,), (1,)), ((), ())), preferred_element_...  27.9 us
  transfers between devices with their start and end apart: 2, of which 0 were waited for; matrix products, arithmetic and copies ran while one was open for 8% of the time, Pallas kernels for 22%

profile of v2, /device:TPU:0, one launch (start us, length us, event | category | flops | bytes accessed | tf_op | source)
XLA Modules:
  0.0 781.3 jit_solution(6055908805959901236)
XLA Ops:
  0.7 1.2 fusion.101
  1.9 1.7 constant_dynamic-slice_fusion.4.o
  4.6 2.0 fusion.94.x
  8.6 69.0 %shard_map.228 = (bf16[1024,2048]{1,0:T(8,128)(2,1)}, bf16[2048,384]{1,0:T(8,128)(2,1)}, bf16[256,2048]{1,0:T(8,128)(2,1)}) custom-call(bf16[128,2048]{1,0:T(8,128)(2,1)} %fusion.94.x, bf16[512,384]{1,0:T(8,128)(2,1)} %pad_maximum_fusion.3.w, bf16[64,2048]{1,0:T(8,128)(2,1)} %constant_dynamic-slice_fusion.4.o), custom_call_target="tpu_custom_call" | custom-call | tf_op jit(solution)/shard_map/pallas_call | solution.py:1136
  77.6 4.5 fusion.139
  84.2 3.2 fusion.119
  87.5 1.2 copy.47
  92.5 1.2 fusion.134
  93.7 8.1 %while.105 = (s32[]{:T(128)}, bf16[1024,256]{0,1:T(8,128)(2,1)S(1)}, f32[1,4,1024]{2,1,0:T(4,128)S(1)}, bf16[1024,1,4,64]{0,3,2,1:T(8,128)(2,1)S(1)}, bf16[1024,...) while((s32[]{:T(128)}, bf16[1024,256]{0,1:T(8,128)(2,1)S(1)}, ...), condition=%wide.region_7.8_spmd.clone.clone, body=%wide.region_3.7_spmd.clone.clone.sunk | while | flops 275383296 | bytes 13054458 | solution.py:130
  93.8 2.5 while.108
  94.1 1.3 fusion.196
  96.6 5.1 while.108
  96.9 1.3 fusion.196
  99.4 1.3 fusion.196
  103.6 45.4 %shard_map.229 = (f32[128,2048]{1,0:T(8,128)}, bf16[8,128,2048]{2,1,0:T(8,128)(2,1)}) custom-call(bf16[1024,256]{1,0:T(8,128)(2,1)} %copy.50.a, bf16[256,2048]{1,0:T(8,128)(2,1)} %get-tuple-element.627.w, bf16[128,2048]{1,0:T(8,128)(2,1)} %bitcast.344), custom_call_target="tpu_custom_call" | custom-call | tf_op jit(solution)/shard_map/pallas_call | solution.py:1136
  149.0 1.6 multiply_reduce_fusion.4
  151.8 47.5 %shard_map.230 = bf16[8,128,2048]{2,1,0:T(8,128)(2,1)} custom-call(bf16[128,2048]{1,0:T(8,128)(2,1)} %multiply_convert_fusion.3.m), custom_call_target="tpu_custom_call" | custom-call | tf_op jit(solution)/shard_map/pallas_call | solution.py:1136
  199.3 10.1 %fusion.86 = f32[1024,1024]{1,0:T(8,128)} fusion(bf16[1024,2048]{1,0:T(8,128)(2,1)} %bitcast.345, bf16[2048,2048]{1,0:T(8,128)(2,1)} %param.32, s32[]{:T(128)S(6)} %select_n.79), kind=kOutput, calls=%fused_computation.93 | convolution fusion | flops 4294967296 | bytes 12582916 | tf_op jit(solution)/shard_map/dot_general | solution.py:38
  209.4 8.4 %fusion.90 = f32[1024,1024]{1,0:T(8,128)} fusion(bf16[1024,2048]{1,0:T(8,128)(2,1)S(1)} %bitcast.346, bf16[2048,2048]{1,0:T(8,128)(2,1)} %param.31, s32[]{:T(128)S(6)} %select_n.79), kind=kOutput, calls=%fused_computation.97 | convolution fusion | flops 4294967296 | bytes 12582916 | tf_op jit(solution)/shard_map/dot_general | solution.py:38
  217.9 11.7 %multiply_convert_fusion = (bf16[1024,1024]{1,0:T(8,128)(2,1)}, bf16[1024,1024]{1,0:T(8,128)(2,1)}, bf16[1024,1024]{1,0:T(8,128)(2,1)}) fusion(f32[1024,1024]{1,0:T(8,128)} %fusion.90, f32[1024,1024]{1,0:T(8,128)} %fusion.86, bf16[1024,2048]{1,0:T(8,128)(2,1)} %bitcast.367, bf16[2048,2048]{1,0:T(8,128)(2,1)S(1)} %bitcast.366, s32[]{:T(128)S(6)} %select_n.79), kind=kOutput, calls=%fused_computation.81 | convolution fusion | flops 4311744512 | bytes 23068676 | tf_op jit(solution)/shard_map/dot_general | solution.py:38
  229.6 8.6 %fusion.88 = f32[1024,2048]{1,0:T(8,128)} fusion(bf16[1024,1024]{1,0:T(8,128)(2,1)} %get-tuple-element.936, bf16[2048,2048]{1,0:T(8,128)(2,1)S(1)} %bitcast.362, s32[]{:T(128)S(6)} %select_n.79), kind=kOutput, calls=%fused_computation.95 | convolution fusion | flops 4294967296 | bytes 14680068 | tf_op jit(solution)/shard_map/dot_general | solution.py:48
  238.2 17.4 %convolution_convert_fusion.2.p_b = bf16[2048,1024]{1,0:T(8,128)(2,1)} fusion(bf16[1024,2048]{1,0:T(8,128)(2,1)S(1)} %bitcast.347, bf16[1024,1024]{1,0:T(8,128)(2,1)S(1)} %copy-done.48), kind=kOutput, calls=%fused_computation.87 | convolution fusion | flops 4297064448 | bytes 10485760 | tf_op jit(solution)/shard_map/dot_general | solution.py:42
  255.6 6.2 convolution_convert_fusion.1.p_c
  261.8 8.5 %add_convert_fusion = bf16[1024,2048]{1,0:T(8,128)(2,1)} fusion(f32[1024,2048]{1,0:T(8,128)} %fusion.88, bf16[1024,1024]{1,0:T(8,128)(2,1)S(1)} %copy-done.49, bf16[2048,2048]{1,0:T(8,128)(2,1)S(1)} %bitcast.364, s32[]{:T(128)S(6)} %select_n.79), kind=kOutput, calls=%fused_computation.77 | convolution fusion | flops 4299161600 | bytes 18874372 | tf_op jit(solution)/shard_map/dot_general | solution.py:48
  270.3 6.2 convolution_convert_fusion.3.p_a
  276.6 78.0 %shard_map.231 = (bf16[2,512,1024]{2,1,0:T(8,128)(2,1)}, bf16[2,512,1024]{2,1,0:T(8,128)(2,1)}, bf16[2,512,1024]{2,1,0:T(8,128)(2,1)}, f32[128,2048]{1,0:T(8,128)}) custom-call(bf16[2048,1024]{1,0:T(8,128)(2,1)} %convolution_convert_fusion.3.p_a, bf16[2048,1024]{1,0:T(8,128)(2,1)} %convolution_convert_fusion.2.p_b, ...), custom_call_target="tpu_custom_call" | custom-call | tf_op jit(solution)/shard_map/pallas_call | solution.py:1136
  354.6 1.6 collective-permute-start.1
  356.4 9.5 %convolution_convert_fusion = bf16[1024,2048]{1,0:T(8,128)(2,1)} fusion(bf16[1024,1024]{1,0:T(8,128)(2,1)} %get-tuple-element.937, bf16[2048,2048]{1,0:T(8,128)(2,1)} %param.33, s32[]{:T(128)S(6)} %select_n.79), kind=kOutput, calls=%fused_computation.85 | convolution fusion | flops 4297064448 | bytes 10485764 | tf_op jit(solution)/shard_map/dot_general | solution.py:48
  366.8 1.2 fusion.131.h
  368.0 115.6 %shard_map.232 = (bf16[1024,2048]{1,0:T(8,128)(2,1)}, bf16[2,512,1024]{2,1,0:T(8,128)(2,1)}, f32[128,2048]{1,0:T(8,128)}) custom-call(bf16[128,2048]{1,0:T(8,128)(2,1)} %fusion.131.h, bf16[2,512,1024]{2,1,0:T(8,128)(2,1)} %get-tuple-element.631.s, bf16[8,128,2048]{2,1,0:T(8,128)(2,1)} %bitcast.350), custom_call_target="tpu_custom_call" | custom-call | tf_op jit(solution)/shard_map/pallas_call | solution.py:1136
  483.7 4.6 convolution_convert_fusion.5.out_part
  488.2 1.3 convolution_convert_fusion.6
  490.9 16.8 %while.107 = (s32[]{:T(128)}, f32[1024,1,4,64]{0,3,2,1:T(8,128)}, f32[1024,1,64]{0,2,1:T(8,128)S(1)}, f32[1024,1,64]{0,2,1:T(8,128)S(1)}, bf16[1024,1,4,64]{0,3,...) while((s32[]{:T(128)}, f32[1024,1,4,64]{0,3,2,1:T(8,128)}, ...), condition=%wide.region_14.15_spmd.clone.clone, body=%wide.region_11.14_spmd.clone.clone.sunk | while | flops 683082752 | bytes 25170536 | solution.py:206
  491.0 4.9 while.109
  492.0 1.7 fusion.190
  497.0 9.9 %while.109 = (s32[]{:T(128)}, f32[512,1,4,64]{0,3,2,1:T(8,128)S(1)}, f32[1024,1,64]{0,2,1:T(8,128)S(1)}, f32[1024,1,64]{0,2,1:T(8,128)S(1)}, s32[]{:T(128)}, /*i...) while((s32[]{:T(128)}, f32[512,1,4,64]{0,3,2,1:T(8,128)S(1)}, ...), condition=%wide.region_13.13_spmd.clone, body=%wide.region_12.12_spmd.clone.sunk | while | flops 683082752 | bytes 22513896 | solution.py:197
  498.0 1.7 fusion.190
  502.9 1.7 fusion.190
  507.7 1.5 bitcast_multiply_fusion.1
  509.8 2.8 multiply_reduce_fusion
  512.8 3.1 sine_multiply_fusion
  517.2 3.7 fusion.115
  522.7 5.7 convolution_convert_fusion.4
  528.5 52.4 %shard_map.233 = (f32[128,2048]{1,0:T(8,128)}, bf16[512,384]{1,0:T(8,128)(2,1)}, bf16[64,2048]{1,0:T(8,128)(2,1)}) custom-call(bf16[1024,384]{1,0:T(8,128)(2,1)} %copy-done.14, bf16[2048,384]{1,0:T(8,128)(2,1)} %get-tuple-element.625.w, bf16[4,512,384]{2,1,0:T(8,128)(2,1)} %bitcast.355, bf16[256,2048]{1,0:T(8,128)(2,1)} %convolution_convert_fusion.5.out_part), custom_call_target="tpu_custom_call" | custom-call | tf_op jit(solution)/shard_map/pallas_call | solution.py:1136
  580.9 1.5 fusion.104
  583.1 3.7 fusion.111
  586.8 4.0 add_convert_fusion.1.t_second
  590.9 3.9 add_convert_fusion.2.t_first
  594.7 126.1 %shard_map.234 = (f32[2048,2048]{1,0:T(8,128)}, f32[2048,2048]{1,0:T(8,128)}, f32[2048,2048]{1,0:T(8,128)}, bf16[8,512,384]{2,1,0:T(8,128)(2,1)}, bf16[512,2048]{1,0:T(8,128)(2,1)}, /*index=5*/f32[8,640]{1,0:T(8,128)}) custom-call(bf16[2,512,1024]{2,1,0:T(8,128)(2,1)} %get-tuple-element.639.t_down, bf16[2,512,1024]{2,1,0:T(8,128)(2,1)} %add_convert_fusion.2.t_first, ...), custom_call_target="tpu_custom_call" | custom-call | tf_op jit(solution)/shard_map/pallas_call | solution.py:1136
  720.8 4.0 convert_bitcast_fusion
  724.8 1.4 slice_convert_fusion
  727.4 5.3 copy.56
  732.7 5.3 copy.58
  738.1 1.8 copy.57
  739.9 1.8 fusion.133
  741.7 1.3 copy.59
  743.0 1.3 copy.60
  744.3 4.3 convert_element_type.211
  748.6 13.6 %copy.123 = f32[2048,2048]{1,0:T(8,128)} copy(f32[2048,2048]{1,0:T(8,128)} %get-tuple-element.1484) | data formatting | bytes 33554432
  762.2 1.7 slice-done.7
  763.9 8.5 %copy.124 = f32[2048,2048]{1,0:T(8,128)} copy(f32[2048,2048]{1,0:T(8,128)S(1)} %bitcast.337) | data formatting | bytes 33554432
  772.4 1.4 slice-done.2
  773.8 1.2 slice-done.3
  775.0 6.2 copy.125
  (242 shorter events, 35.4 us)
Async XLA Ops:
  1.9 75.7 %copy-start.42 = (f32[128]{0:T(128)}, f32[128]{0:T(128)S(1)}, u32[]{:S(2)}) copy-start(f32[128]{0:T(128)S(1)} %add_rsqrt_fusion.1) | copy-start | bytes 1540
  77.6 5.2 copy-start.36
  82.1 10.3 %copy-start.2 = (f32[1024,384]{0,1:T(8,128)}, f32[1024,384]{0,1:T(8,128)S(1)}, u32[]{:S(2)}) copy-start(f32[1024,384]{0,1:T(8,128)S(1)} %fusion.139) | copy-start | bytes 4718596
  82.3 6.4 copy-start.25
  82.5 6.2 copy-start.4
  82.8 6.0 copy-start.32
  82.8 5.9 copy-start.29
  82.8 6.0 copy-start.38
  88.7 4.9 copy-start.17
  88.8 4.9 copy-start.23
  90.1 3.5 copy-start.15
  101.8 48.8 %copy-start.27 = (f32[2048]{0:T(1024)S(1)}, f32[2048]{0:T(1024)}, u32[]{:S(2)}) copy-start(f32[2048]{0:T(1024)} %param.30) | copy-start | bytes 24580
  150.6 216.2 %copy-start = (f32[128,2048]{1,0:T(8,128)}, f32[128,2048]{1,0:T(8,128)S(1)}, u32[]{:S(2)}) copy-start(f32[128,2048]{1,0:T(8,128)S(1)} %get-tuple-element.926) | copy-start | bytes 3145732
  150.6 216.2 %copy-start.40 = (f32[128]{0:T(128)}, f32[128]{0:T(128)S(1)}, u32[]{:S(2)}) copy-start(f32[128]{0:T(128)S(1)} %add_rsqrt_fusion) | copy-start | bytes 1540
  199.3 10.1 %copy-start.11 = (bf16[8,128,2048]{2,1,0:T(8,128)(2,1)S(1)}, bf16[8,128,2048]{2,1,0:T(8,128)(2,1)}, u32[]{:S(2)}) copy-start(bf16[8,128,2048]{2,1,0:T(8,128)(2,1)} %shard_map.230) | copy-start | bytes 12582916
  199.3 18.6 %slice-start.12 = ((s8[8388608]{0:T(1024)(128)(4,1)}), s8[4194304]{0:T(1024)(128)(4,1)S(1)}, s32[]{:S(2)}) async-start(s8[8388608]{0:T(1024)(128)(4,1)} %bitcast.365), calls=%async_computation.12 | async-start | bytes 8388608
  209.4 8.4 %slice-start.13 = ((s8[8388608]{0:T(1024)(128)(4,1)}), s8[4194304]{0:T(1024)(128)(4,1)S(1)}, s32[]{:S(2)}) async-start(s8[8388608]{0:T(1024)(128)(4,1)} %bitcast.365), calls=%async_computation.13 | async-start | bytes 8388608
  209.4 20.1 %slice-start.8 = ((s8[8388608]{0:T(1024)(128)(4,1)}), s8[4194304]{0:T(1024)(128)(4,1)S(1)}, s32[]{:S(2)}) async-start(s8[8388608]{0:T(1024)(128)(4,1)} %bitcast.361), calls=%async_computation.8 | async-start | bytes 8388608
  217.9 11.7 %slice-start.9 = ((s8[8388608]{0:T(1024)(128)(4,1)}), s8[4194304]{0:T(1024)(128)(4,1)S(1)}, s32[]{:S(2)}) async-start(s8[8388608]{0:T(1024)(128)(4,1)} %bitcast.361), calls=%async_computation.9 | async-start | bytes 8388608
  229.6 8.6 %copy-start.48 = (bf16[1024,1024]{1,0:T(8,128)(2,1)S(1)}, bf16[1024,1024]{1,0:T(8,128)(2,1)}, u32[]{:S(2)}) copy-start(bf16[1024,1024]{1,0:T(8,128)(2,1)} %get-tuple-element.936) | copy-start | bytes 6291460
  238.2 17.4 %copy-start.49 = (bf16[1024,1024]{1,0:T(8,128)(2,1)S(1)}, bf16[1024,1024]{1,0:T(8,128)(2,1)}, u32[]{:S(2)}) copy-start(bf16[1024,1024]{1,0:T(8,128)(2,1)} %get-tuple-element.935) | copy-start | bytes 6291460
  238.2 23.6 %slice-start.10 = ((s8[8388608]{0:T(1024)(128)(4,1)}), s8[4194304]{0:T(1024)(128)(4,1)S(1)}, s32[]{:S(2)}) async-start(s8[8388608]{0:T(1024)(128)(4,1)} %bitcast.363), calls=%async_computation.10 | async-start | bytes 8388608
  255.6 6.2 slice-start.11
  261.8 8.5 %copy-start.46 = (bf16[8,128,2048]{2,1,0:T(8,128)(2,1)S(1)}, bf16[8,128,2048]{2,1,0:T(8,128)(2,1)}, u32[]{:S(2)}) copy-start(bf16[8,128,2048]{2,1,0:T(8,128)(2,1)} %get-tuple-element.629) | copy-start | bytes 12582916
  261.8 8.5 %copy-start.50 = (bf16[1024,1024]{1,0:T(8,128)(2,1)S(1)}, bf16[1024,1024]{1,0:T(8,128)(2,1)}, u32[]{:S(2)}) copy-start(bf16[1024,1024]{1,0:T(8,128)(2,1)} %get-tuple-element.937) | copy-start | bytes 6291460
  354.6 232.3 %collective-permute-start.1 = (bf16[2,512,1024]{2,1,0:T(8,128)(2,1)}, bf16[2,512,1024]{2,1,0:T(8,128)(2,1)}, u32[]{:S(2)}, u32[]{:S(2)}) collective-permute-start(bf16[2,512,1024]{2,1,0:T(8,128)(2,1)} %get-tuple-element.641), channel_id=1, source_target_pairs={{0,8},{4,12},{8,0},{12,4},{16,24},{20,28},{24,16},{28,20},{1,9},{5... | collective-permute-start | bytes 6291464 | tf_op jit(solution)/shard_map/ppermute | solution.py:1309
  356.1 9.7 %copy-start.7 = (f32[128,2048]{1,0:T(8,128)S(1)}, f32[128,2048]{1,0:T(8,128)}, u32[]{:S(2)}) copy-start(f32[128,2048]{1,0:T(8,128)} %get-tuple-element.630) | copy-start | bytes 3145732
  356.2 10.6 %copy-start.10 = (bf16[1,128,2048]{2,1,0:T(8,128)(2,1)S(1)}, bf16[1,128,2048]{2,1,0:T(8,128)(2,1)}, u32[]{:S(2)}) copy-start(bf16[1,128,2048]{2,1,0:T(8,128)(2,1)} %param.22) | copy-start | bytes 1572868
  356.2 234.7 %collective-permute-start = (bf16[2,512,1024]{2,1,0:T(8,128)(2,1)}, bf16[2,512,1024]{2,1,0:T(8,128)(2,1)}, u32[]{:S(2)}, u32[]{:S(2)}) collective-permute-start(bf16[2,512,1024]{2,1,0:T(8,128)(2,1)} %get-tuple-element.640), channel_id=1, source_target_pairs={{0,16},{4,20},{8,24},{12,28},{16,0},{20,4},{24,8},{28,12},{1,17},{... | collective-permute-start | bytes 6291464 | tf_op jit(solution)/shard_map/ppermute | solution.py:1309
  366.8 116.8 %copy-start.44 = (f32[128]{0:T(128)}, f32[128]{0:T(128)S(1)}, u32[]{:S(2)}) copy-start(f32[128]{0:T(128)S(1)} %broadcast_multiply_fusion.2) | copy-start | bytes 1540
  368.0 115.7 %copy-start.9 = (bf16[1024,256]{0,1:T(8,128)(2,1)S(1)}, bf16[1024,256]{0,1:T(8,128)(2,1)}, u32[]{:S(2)}) copy-start(bf16[1024,256]{0,1:T(8,128)(2,1)} %copy-done.8) | copy-start | bytes 1572868
  483.6 4.6 copy-start.22
  483.6 4.6 copy-start.47
  490.9 16.9 %copy-start.18 = (f32[1024,64]{0,1:T(8,128)S(1)}, f32[1024,64]{0,1:T(8,128)}, u32[]{:S(2)}) copy-start(f32[1024,64]{0,1:T(8,128)} %copy-done.17) | copy-start | bytes 786436
  507.7 2.0 copy-start.12
  507.7 2.0 copy-start.16
  507.7 2.0 copy-start.24
  507.7 2.0 copy-start.39
  509.2 3.4 copy-start.26
  512.5 4.7 copy-start.5
  512.6 4.7 copy-start.30
  512.6 4.7 copy-start.37
  512.8 3.3 copy-start.13
  515.9 5.0 copy-start.33
  517.2 4.0 copy-start.21
  528.4 52.4 %copy-start.6 = (bf16[1,128,2048]{2,1,0:T(8,128)(2,1)S(1)}, bf16[1,128,2048]{2,1,0:T(8,128)(2,1)}, u32[]{:S(2)}) copy-start(bf16[1,128,2048]{2,1,0:T(8,128)(2,1)} %param.21) | copy-start | bytes 1572868
  528.4 52.4 %copy-start.31 = (f32[2048]{0:T(1024)S(1)}, f32[2048]{0:T(1024)}, u32[]{:S(2)}) copy-start(f32[2048]{0:T(1024)} %param.23) | copy-start | bytes 24580
  528.4 52.4 %copy-start.43 = (f32[128]{0:T(128)S(1)}, f32[128]{0:T(128)}, u32[]{:S(2)}) copy-start(f32[128]{0:T(128)} %copy-done.42) | copy-start | bytes 1540
  528.4 54.0 %copy-start.34 = (f32[2048]{0:T(1024)S(1)}, f32[2048]{0:T(1024)}, u32[]{:S(2)}) copy-start(f32[2048]{0:T(1024)} %get-tuple-element.839) | copy-start | bytes 24580
  528.4 54.7 %copy-start.1 = (f32[128,2048]{1,0:T(8,128)S(1)}, f32[128,2048]{1,0:T(8,128)}, u32[]{:S(2)}) copy-start(f32[128,2048]{1,0:T(8,128)} %copy-done) | copy-start | bytes 3145732
  528.5 54.7 %copy-start.28 = (f32[2048]{0:T(1024)S(1)}, f32[2048]{0:T(1024)}, u32[]{:S(2)}) copy-start(f32[2048]{0:T(1024)} %param.30) | copy-start | bytes 24580
  528.5 54.7 %copy-start.41 = (f32[128]{0:T(128)S(1)}, f32[128]{0:T(128)}, u32[]{:S(2)}) copy-start(f32[128]{0:T(128)} %copy-done.40) | copy-start | bytes 1540
  528.5 54.7 %copy-start.45 = (f32[128]{0:T(128)S(1)}, f32[128]{0:T(128)}, u32[]{:S(2)}) copy-start(f32[128]{0:T(128)} %copy-done.44) | copy-start | bytes 1540
  583.1 3.7 copy-start.20
  586.8 4.0 copy-start.19
  720.8 5.4 copy-start.35
  744.3 17.9 %slice-start.4 = ((s8[16777216]{0:T(1024)(128)(4,1)}), s8[4194304]{0:T(1024)(128)(4,1)S(1)}, s32[]{:S(2)}) async-start(s8[16777216]{0:T(1024)(128)(4,1)} %bitcast.336), calls=%async_computation.4 | async-start | bytes 8388608
  748.6 13.6 %slice-start.5 = ((s8[16777216]{0:T(1024)(128)(4,1)}), s8[4194304]{0:T(1024)(128)(4,1)S(1)}, s32[]{:S(2)}) async-start(s8[16777216]{0:T(1024)(128)(4,1)} %bitcast.336), calls=%async_computation.5 | async-start | bytes 8388608
  748.6 13.6 %slice-start.6 = ((s8[16777216]{0:T(1024)(128)(4,1)}), s8[4194304]{0:T(1024)(128)(4,1)S(1)}, s32[]{:S(2)}) async-start(s8[16777216]{0:T(1024)(128)(4,1)} %bitcast.336), calls=%async_computation.6 | async-start | bytes 8388608
  748.6 15.3 %slice-start.7 = ((s8[16777216]{0:T(1024)(128)(4,1)}), s8[4194304]{0:T(1024)(128)(4,1)S(1)}, s32[]{:S(2)}) async-start(s8[16777216]{0:T(1024)(128)(4,1)} %bitcast.336), calls=%async_computation.7 | async-start | bytes 8388608
  748.6 23.8 %slice-start = ((s8[16777216]{0:T(1024)(128)(4,1)}), s8[4194304]{0:T(1024)(128)(4,1)S(1)}, s32[]{:S(2)}) async-start(s8[16777216]{0:T(1024)(128)(4,1)} %bitcast.334), calls=%async_computation | async-start | bytes 8388608
  748.6 23.8 %slice-start.1 = ((s8[16777216]{0:T(1024)(128)(4,1)}), s8[4194304]{0:T(1024)(128)(4,1)S(1)}, s32[]{:S(2)}) async-start(s8[16777216]{0:T(1024)(128)(4,1)} %bitcast.334), calls=%async_computation.1 | async-start | bytes 8388608
  763.9 9.9 %slice-start.2 = ((s8[16777216]{0:T(1024)(128)(4,1)}), s8[4194304]{0:T(1024)(128)(4,1)S(1)}, s32[]{:S(2)}) async-start(s8[16777216]{0:T(1024)(128)(4,1)} %bitcast.334), calls=%async_computation.2 | async-start | bytes 8388608
  763.9 11.1 %slice-start.3 = ((s8[16777216]{0:T(1024)(128)(4,1)}), s8[4194304]{0:T(1024)(128)(4,1)S(1)}, s32[]{:S(2)}) async-start(s8[16777216]{0:T(1024)(128)(4,1)} %bitcast.334), calls=%async_computation.3 | async-start | bytes 8388608
  (3 other events, 3.4 us)

commit v3 on v2

--- a/solution.py
+++ b/solution.py
@@ -833,9 +833,16 @@
     w,
     head_part,
     out_part,
+    t_down,
+    t_first,
+    t_second,
     out,
     head_sum,
     out_sum,
+    near_down,
+    far_down,
+    near_gate,
+    far_gate,
     give,
     take,
     current,
@@ -887,6 +894,10 @@
     )
     head_own.wait()
     heads.step(1)
+    weights = [
+        WeightGather(wire, here, (t_down.at[0], t_down.at[1]), near_down, far_down),
+        WeightGather(wire, here, (t_first.at[0], t_second.at[0]), near_gate, far_gate),
+    ]
     rows = PlaneScatter(wire, here, product, give, take, current, landing, model)
     rows.start()
     deal_own.wait()
@@ -897,6 +908,8 @@
     stages = len(here.chip_bits)
     for stage in range(stages):
         rows.stage(stage)
+        if stage < 2:
+            weights[stage].start()
         if stage + 2 < planes:
             heads.step(stage + 2)
             outer.step(stage + 2)
@@ -904,31 +917,112 @@
     for step in range(stages + 2, planes):
         heads.step(step)
         outer.step(step)
+    for weight in weights:
+        weight.own()
+    for weight in weights:
+        weight.forward()
     heads.finish(head_sum)
     outer.finish(out_sum)
+    for weight in weights:
+        weight.finish()
     wire.close()
     heads.close()
     outer.close()
 
 
+class WeightGather:
+    def __init__(self, wire, here, finals, near, far):
+        self.wire, self.here, self.near, self.far = wire, here, near, far
+        self.size = finals[0].shape[0]
+        model = near.shape[0]
+        self.finals = finals
+        self.starts = []
+        for color, order in enumerate(here.colors()):
+            start = color * (model // 2)
+            rows = model // 2
+            for bit in order[:-1]:
+                rows //= 2
+                start = start + here.side(bit) * rows
+            self.starts.append(start)
+        self.swaps, self.kept = [], []
+
+    def _rows(self, start):
+        return pl.ds(pl.multiple_of(start, self.size), self.size)
+
+    def _pass(self, start, source, bit, rows):
+        copy = self.wire.send(
+            source, self.near.at[self._rows(start)], {"seq": self.here.at(bit)}
+        )
+        start = start + rows - 2 * rows * self.here.side(bit)
+        return (start, self.near.at[self._rows(start)], copy)
+
+    def _swap(self, start, source):
+        self.swaps.append(
+            self.wire.send(source, self.far.at[self._rows(start)], {"seq": self.here.at(1)})
+        )
+
+    def start(self):
+        self.held = []
+        for color, order in enumerate(self.here.colors()):
+            source, start = self.finals[color], self.starts[color]
+            pieces = [(start, source, None)]
+            if order[:-1]:
+                pieces.append(self._pass(start, source, order[-2], self.size))
+            self.held.append(pieces)
+
+    def own(self):
+        for color in (0, 1):
+            source, start = self.finals[color], self.starts[color]
+            self._swap(start, source)
+            self.kept.append(self.wire.local(source, self.near.at[self._rows(start)]))
+
+    def forward(self):
+        for color, order in enumerate(self.here.colors()):
+            rest = order[:-1]
+            pieces = self.held[color]
+            rows = self.size
+            for position in range(len(rest) - 1, -1, -1):
+                for start, source, copy in pieces:
+                    if copy is not None:
+                        copy.wait_recv()
+                        self._swap(start, source)
+                pieces = [(start, source, None) for start, source, _ in pieces]
+                rows *= 2
+                if position > 0:
+                    pieces = pieces + [
+                        self._pass(start, source, rest[position - 1], rows)
+                        for start, source, _ in pieces
+                    ]
+
+    def finish(self):
+        for copy in self.swaps:
+            copy.wait_recv()
+        for copy in self.kept:
+            copy.wait()
+
+
+def widen_kernel(near, far, out):
+    core = lax.axis_index("seq") % 2
+    units = near.shape[1]
+    out[:, pl.ds(pl.multiple_of(core * units, units), units)] = near[...].astype(out.dtype)
+    out[:, pl.ds(pl.multiple_of((1 - core) * units, units), units)] = far[...].astype(out.dtype)
+
+
 def collect_kernel(
     parts,
     planes,
-    t_down,
     t_first,
     t_second,
-    head,
+    query,
+    pair,
     outer,
     slope,
-    grad_down,
-    grad_gate,
-    grad_up,
-    head_all,
+    near,
+    far,
+    query_all,
+    pair_all,
     outer_all,
     slope_out,
-    near,
-    far,
-    stage_rows,
     slope_sums,
     slope_landing,
     *sems,
@@ -936,7 +1030,7 @@
     here = Place(parts, planes)
     wire = Wire(*sems)
     here.enter(here.seat_bits, plane_masks=here.plane_bits)
-    shard, rows_out = head.shape[0], outer.shape[0]
+    shard, rows_out = query.shape[0], outer.shape[0]
     chips = parts // 2
 
     bits = [("seq", bit) for bit in here.seat_bits] + [("fsdp", bit) for bit in here.plane_bits]
@@ -954,171 +1048,61 @@
         target = slope_out if number == len(bits) - 1 else slope_sums.at[number]
         target[...] = source[...] + slope_landing[number]
 
+    def row_gather(source, target):
+        return PlaneGather(wire, here, source, target)
+
     slope_send(0)
-    half = shard // 2
-    heads = PlaneGather(
-        wire,
-        here,
-        lambda color: head.at[pl.ds(color * half, half)],
-        lambda seat, color: head_all.at[seat, pl.ds(color * half, half)],
-    )
-    half_out = rows_out // 2
-
-    def outer_target(seat, color):
-        start = ((seat % 2) * chips + seat // 2) * rows_out + color * half_out
-        return outer_all.at[pl.ds(pl.multiple_of(start, half_out), half_out)]
-
-    outers = PlaneGather(
-        wire, here, lambda color: outer.at[pl.ds(color * half_out, half_out)], outer_target
-    )
-    heads.start()
-    outers.start()
+    half, half_out = shard // 2, rows_out // 2
+    columns = query.shape[1]
     own_start = (here.core * chips + here.chip) * rows_out
-    own = [
-        wire.local(head, head_all.at[here.seat]),
-        wire.local(
-            outer, outer_all.at[pl.ds(pl.multiple_of(own_start, rows_out), rows_out)]
+    gathers = [
+        row_gather(
+            lambda color: query.at[pl.ds(color * half, half)],
+            lambda seat, color: query_all.at[
+                pl.ds(color * half, half), pl.ds(pl.multiple_of(seat * columns, columns), columns)
+            ],
+        ),
+        row_gather(
+            lambda color: pair.at[pl.ds(color * half, half)],
+            lambda seat, color: pair_all.at[seat, pl.ds(color * half, half)],
+        ),
+        row_gather(
+            lambda color: outer.at[pl.ds(color * half_out, half_out)],
+            lambda seat, color: outer_all.at[
+                pl.ds(
+                    pl.multiple_of(
+                        ((seat % 2) * chips + seat // 2) * rows_out + color * half_out, half_out
+                    ),
+                    half_out,
+                )
+            ],
         ),
     ]
-
-    model = near.shape[1]
-    units = near.shape[2]
-    size = t_down.shape[1]
-    outs = (grad_down, grad_gate, grad_up)
-    sources = {}
-    incoming = {}
-    swaps = {}
-
-    def final(number, color):
-        if number == 0:
-            return t_down.at[color]
-        return (t_first, t_second)[color].at[number - 1]
-
-    def rows_at(start):
-        return pl.ds(pl.multiple_of(start, size), size)
-
-    starts = {}
-    for color, order in enumerate(here.colors()):
-        start = color * (model // 2)
-        rows = model // 2
-        for bit in order[:-1]:
-            rows //= 2
-            start = start + here.side(bit) * rows
-        starts[color] = start
-
-    def pass_on(number, color, start, source, bit, rows):
-        incoming_start = start + rows - 2 * rows * here.side(bit)
-        copy = wire.send(
-            source, near.at[number, rows_at(start)], {"seq": here.at(bit)}
-        )
-        return incoming_start, copy
-
-    def swap_core(number, start, source):
-        return wire.send(source, far.at[number, rows_at(start)], {"seq": here.at(1)})
-
-    held = {}
-    for number in range(3):
-        for color, order in enumerate(here.colors()):
-            rest = order[:-1]
-            source = final(number, color)
-            pieces = [(starts[color], source, None)]
-            rows = size
-            if rest:
-                pieces.append(
-                    _pending(
-                        pass_on(number, color, starts[color], source, rest[-1], rows),
-                        near,
-                        number,
-                        rows_at,
-                    )
-                )
-            swaps[(number, color)] = [(starts[color], swap_core(number, starts[color], source))]
-            held[(number, color)] = pieces
-
-    blocks = []
-    count = [0]
-
-    def write(number, start, source, column):
-        step = stage_rows.shape[1]
-        for part in range(size // step):
-            slot = count[0] % stage_rows.shape[0]
-            if count[0] >= stage_rows.shape[0]:
-                blocks[count[0] - stage_rows.shape[0]].wait()
-            count[0] += 1
-
-            def body(index, carry):
-                at = pl.ds(pl.multiple_of(index * 32, 32), 32)
-                from_ = pl.ds(pl.multiple_of(part * step + index * 32, 32), 32)
-                stage_rows[slot, at, :] = source[from_, :].astype(jnp.float32)
-                return carry
-
-            lax.fori_loop(0, step // 32, body, 0)
-            blocks.append(
-                wire.local(
-                    stage_rows.at[slot],
-                    outs[number].at[
-                        pl.ds(pl.multiple_of(start + part * step, step), step),
-                        pl.ds(pl.multiple_of(column * units, units), units),
-                    ],
-                )
-            )
-
+    for gather in gathers:
+        gather.start()
+    weight = WeightGather(wire, here, (t_first.at[1], t_second.at[1]), near, far)
+    weight.start()
+    own = [
+        wire.local(query, query_all.at[:, pl.ds(pl.multiple_of(here.seat * columns, columns), columns)]),
+        wire.local(pair, pair_all.at[here.seat]),
+        wire.local(outer, outer_all.at[pl.ds(pl.multiple_of(own_start, rows_out), rows_out)]),
+    ]
     slope_add(0)
-    if len(bits) > 1:
-        slope_send(1)
-    heads.forward()
-    outers.forward()
+    slope_send(1)
+    for gather in gathers:
+        gather.forward()
+    weight.own()
     for number in range(1, len(bits)):
         slope_add(number)
         if number + 1 < len(bits):
             slope_send(number + 1)
-        if number == 1:
-            for color in (0, 1):
-                write(0, starts[color], final(0, color), here.core)
-    for number in range(3):
-        if number > 0:
-            for color in (0, 1):
-                write(number, starts[color], final(number, color), here.core)
-        for color, order in enumerate(here.colors()):
-            rest = order[:-1]
-            pieces = held[(number, color)]
-            position = len(rest) - 1
-            rows = size
-            while position >= 0:
-                fresh = [piece for piece in pieces if piece[2] is not None]
-                for piece in fresh:
-                    piece[2].wait_recv()
-                    swaps[(number, color)].append(
-                        (piece[0], swap_core(number, piece[0], piece[1]))
-                    )
-                    write(number, piece[0], piece[1], here.core)
-                pieces = [(start, source, None) for start, source, _ in pieces]
-                position -= 1
-                rows *= 2
-                if position >= 0:
-                    bit = rest[position]
-                    pieces = pieces + [
-                        _pending(
-                            pass_on(number, color, start, source, bit, rows), near, number, rows_at
-                        )
-                        for start, source, _ in pieces
-                    ]
-        for color in (0, 1):
-            for start, copy in swaps[(number, color)]:
-                copy.wait_recv()
-                write(number, start, far.at[number, rows_at(start)], 1 - here.core)
-    heads.finish()
-    outers.finish()
+    weight.forward()
+    for gather in gathers:
+        gather.finish()
+    weight.finish()
     for copy in own:
         copy.wait()
-    for copy in blocks[-stage_rows.shape[0] :]:
-        copy.wait()
     wire.close()
-
-
-def _pending(passed, near, number, rows_at):
-    start, copy = passed
-    return (start, near.at[number, rows_at(start)], copy)
 
 
 SENDS, LOCALS = 128, 96
@@ -1143,6 +1127,21 @@
             collective_id=number, has_side_effects=True, vmem_limit_bytes=VMEM_BYTES
         ),
     )(*inputs)
+
+
+def widen(near, far):
+    rows, units = near.shape
+    step = min(256, rows)
+    return pl.pallas_call(
+        widen_kernel,
+        grid=(rows // step,),
+        out_shape=jax.ShapeDtypeStruct((rows, 2 * units), jnp.float32),
+        in_specs=[pl.BlockSpec((step, units), lambda index: (index, 0))] * 2,
+        out_specs=pl.BlockSpec((step, 2 * units), lambda index: (index, 0)),
+        cost_estimate=pl.CostEstimate(
+            flops=0, transcendentals=0, bytes_accessed=12 * rows * units
+        ),
+    )(near, far)
 
 
 VMEM_BYTES = 62 * 1024 * 1024
@@ -1309,6 +1308,7 @@
         other = lax.ppermute(value, "seq", [(i, i ^ bit) for i in range(parts)])
         return (value.astype(f32) + other.astype(f32)).astype(bf16)
 
+    s_first, s_second, middle_all = lax.optimization_barrier((s_first, s_second, middle_all))
     t_first = trade(s_first, parts // 2)
     t_second = trade(s_second, 2)
 
@@ -1330,13 +1330,15 @@
     head_part = inner_rows(normed_all, halves).astype(bf16).reshape(planes, shard, head_cols)
     out_part = inner_rows(out_rows, middle_all).astype(bf16)
 
-    in_grad, head_sum, outer_sum = call(
+    side = ((model, units), bf16)
+    in_grad, head_sum, outer_sum, near_down, far_down, near_gate, far_gate = call(
         in_rows_kernel,
         sizes,
         5,
-        (halves, head_full, head_part, out_part),
-        (True, True, False, False),
-        [((tokens, model), f32), ((shard, head_cols), bf16), ((piece_rows, model), bf16)],
+        (halves, head_full, head_part, out_part, t_down, t_first, t_second),
+        (True, True, False, False, False, False, False),
+        [((tokens, model), f32), ((shard, head_cols), bf16), ((piece_rows, model), bf16)]
+        + [side] * 4,
         scatter_scratch
         + [
             ((planes, shard, head_cols), bf16),
@@ -1344,6 +1346,7 @@
             ((planes, piece_rows, model), bf16),
             ((2, planes - 1, piece_rows, model), bf16),
         ],
+        [True] * 3 + [False] * 4,
     )
     attention_slope = jnp.sum(in_grad * source * first, axis=0)
     input_rows = (middle_grad + norm_back(in_grad, source, first, attention_gain)).astype(bf16)
@@ -1352,31 +1355,35 @@
     slope_cols = -(-slopes.shape[0] // 1024) * 128
     slopes = jnp.pad(slopes, (0, 8 * slope_cols - slopes.shape[0])).reshape(8, slope_cols)
     rounds = (parts * planes).bit_length() - 1
-    grad_down, grad_gate, grad_up, head_all, outer_all, slopes = call(
+    near_up, far_up, query_all, pair_all, outer_all, slopes = call(
         collect_kernel,
         sizes,
         6,
-        (t_down, t_first, t_second, head_sum, outer_sum, slopes),
-        (True,) * 6,
+        (
+            t_first,
+            t_second,
+            head_sum[:, :query_cols],
+            head_sum[:, query_cols:],
+            outer_sum,
+            slopes,
+        ),
+        (False, False, True, True, True, True),
         [
-            ((model, 2 * units), f32),
-            ((model, 2 * units), f32),
-            ((model, 2 * units), f32),
-            ((parts, shard, head_cols), bf16),
+            side,
+            side,
+            ((shard, model), bf16),
+            ((parts, shard, 2 * width), bf16),
             ((shard, model), bf16),
             ((8, slope_cols), f32),
         ],
-        [
-            ((3, model, units), bf16),
-            ((3, model, units), bf16),
-            ((4, 256, units), f32),
-            ((rounds, 8, slope_cols), f32),
-            ((rounds, 8, slope_cols), f32),
-        ],
-        [False, False, False, True, True, True],
-    )
-    grad_query = head_all[:, :, :query_cols].transpose(1, 0, 2).reshape(shard, -1).astype(f32)
-    grad_pair = head_all[:, :, query_cols:].astype(f32)
+        [((rounds, 8, slope_cols), f32), ((rounds, 8, slope_cols), f32)],
+        [False, False, True, True, True, True],
+    )
+    grad_down = widen(near_down, far_down)
+    grad_gate = widen(near_gate, far_gate)
+    grad_up = widen(near_up, far_up)
+    grad_query = query_all.astype(f32)
+    grad_pair = pair_all.astype(f32)
     grad_pair = grad_pair.reshape(parts // copies, copies, shard, 2, width).sum(axis=1)
     grad_key = grad_pair[:, :, 0].transpose(1, 0, 2).reshape(shard, -1)
     grad_value = grad_pair[:, :, 1].transpose(1, 0, 2).reshape(shard, -1)

time: 787 us -> 879 us (1.12)
  Pallas kernels: 534 us -> 669 us
  local copies, waits for them, and re-layouts: 65.1 us -> 28.9 us
  matrix products: 123 us -> 112 us
    pallas_call x7, Pallas kernels: 534 us -> 638 us  [call(): pl.pallas_call(functools.partial(kernel, *mesh_sizes), out_shape=[jax.Sha...]
    unnamed x138 -> x122, local copies, waits for them, and re-layouts: 44.1 us -> 3.71 us
    pallas_call x0 -> x3, Pallas kernels: none -> 30.8 us  [widen(): pl.pallas_call(widen_kernel, grid=(rows // step,), out_shape=jax.ShapeDty...]
    dot_general x5, matrix products: 40.1 us -> 25 us  [inner_rows(): lax.dot_general(left, right, (((0,), (0,)), ((), ())), preferred_element_...]
  transfers between devices with their start and end apart: 2 -> 2, of which waited for: 0 -> 0; matrix products, arithmetic and copies ran while one was open for 8% -> 6% of each run, Pallas kernels for 22% -> 0%
where the time goes in v3:
time: 879 us; the launch traced here: 869 us
  Pallas kernels  669 us (76%)
  matrix products  112 us (13%)
  other arithmetic  53.8 us (6%)
  local copies, waits for them, and re-layouts  28.9 us (3%)
    pallas_call x7, Pallas kernels, call(): pl.pallas_call(functools.partial(kernel, *mesh_sizes), out_shape=[jax.Sha...  638 us
    dot_general x4, matrix products, matmul(): return jnp.dot(left, right, preferred_element_type=jnp.float32)  34.7 us
    pallas_call x3, Pallas kernels, widen(): pl.pallas_call(widen_kernel, grid=(rows // step,), out_shape=jax.ShapeDty...  30.8 us
    dot_general x4, matrix products, inner_cols(): lax.dot_general(left, right, (((1,), (1,)), ((), ())), preferred_element_...  26.9 us
    dot_general x5, matrix products, inner_rows(): lax.dot_general(left, right, (((0,), (0,)), ((), ())), preferred_element_...  25 us
  transfers between devices with their start and end apart: 2, of which 0 were waited for; matrix products, arithmetic and copies ran while one was open for 6% of the time, Pallas kernels for 0%

profile of v3, /device:TPU:0, one launch (start us, length us, event | category | flops | bytes accessed | tf_op | source)
XLA Modules:
  0.0 868.5 jit_solution(5283533548162495092)
XLA Ops:
  1.9 1.7 constant_dynamic-slice_fusion.4.o
  4.6 2.0 fusion.94.x
  8.6 69.1 %shard_map.228 = (bf16[1024,2048]{1,0:T(8,128)(2,1)}, bf16[2048,384]{1,0:T(8,128)(2,1)}, bf16[256,2048]{1,0:T(8,128)(2,1)}) custom-call(bf16[128,2048]{1,0:T(8,128)(2,1)} %fusion.94.x, bf16[512,384]{1,0:T(8,128)(2,1)} %pad_maximum_fusion.3.w, bf16[64,2048]{1,0:T(8,128)(2,1)} %constant_dynamic-slice_fusion.4.o), custom_call_target="tpu_custom_call" | custom-call | tf_op jit(solution)/shard_map/pallas_call | solution.py:1120
  77.7 4.5 fusion.139
  84.3 3.2 fusion.119
  90.7 1.3 maximum_multiply_fusion
  92.0 1.3 fusion.134
  93.4 10.1 %while.105 = (s32[]{:T(128)}, bf16[1024,256]{0,1:T(8,128)(2,1)S(1)}, f32[1,4,1024]{2,1,0:T(4,128)S(1)}, bf16[1024,1,4,64]{0,3,2,1:T(8,128)(2,1)}, bf16[1024,1,64...) while((s32[]{:T(128)}, bf16[1024,256]{0,1:T(8,128)(2,1)S(1)}, ...), condition=%wide.region_7.8_spmd.clone.clone, body=%wide.region_3.7_spmd.clone.clone.sunk | while | flops 275383296 | bytes 13054458 | solution.py:130
  94.6 2.5 while.108
  94.8 1.3 fusion.196
  98.3 5.1 while.108
  98.6 1.3 fusion.196
  101.1 1.3 fusion.196
  104.5 45.3 %shard_map.229 = (f32[128,2048]{1,0:T(8,128)}, bf16[8,128,2048]{2,1,0:T(8,128)(2,1)}) custom-call(bf16[1024,256]{1,0:T(8,128)(2,1)} %copy.50.a, bf16[256,2048]{1,0:T(8,128)(2,1)} %get-tuple-element.634.w, bf16[128,2048]{1,0:T(8,128)(2,1)} %bitcast.335), custom_call_target="tpu_custom_call" | custom-call | tf_op jit(solution)/shard_map/pallas_call | solution.py:1120
  149.8 1.4 multiply_reduce_fusion.4
  152.4 47.5 %shard_map.230 = bf16[8,128,2048]{2,1,0:T(8,128)(2,1)} custom-call(bf16[128,2048]{1,0:T(8,128)(2,1)} %multiply_convert_fusion.3.m), custom_call_target="tpu_custom_call" | custom-call | tf_op jit(solution)/shard_map/pallas_call | solution.py:1120
  200.0 10.1 %fusion.86 = f32[1024,1024]{1,0:T(8,128)} fusion(bf16[1024,2048]{1,0:T(8,128)(2,1)} %bitcast.336, bf16[2048,2048]{1,0:T(8,128)(2,1)} %param.32, s32[]{:T(128)S(6)} %select_n.79), kind=kOutput, calls=%fused_computation.92 | convolution fusion | flops 4294967296 | bytes 12582916 | tf_op jit(solution)/shard_map/dot_general | solution.py:38
  210.1 8.4 fusion.90
  218.5 11.7 %multiply_convert_fusion = (bf16[1024,1024]{1,0:T(8,128)(2,1)}, bf16[1024,1024]{1,0:T(8,128)(2,1)}, bf16[1024,1024]{1,0:T(8,128)(2,1)}) fusion(f32[1024,1024]{1,0:T(8,128)} %fusion.90, f32[1024,1024]{1,0:T(8,128)} %fusion.86, bf16[1024,2048]{1,0:T(8,128)(2,1)} %bitcast.358, bf16[2048,2048]{1,0:T(8,128)(2,1)S(1)} %bitcast.355, s32[]{:T(128)S(6)} %select_n.79), kind=kOutput, calls=%fused_computation.80 | convolution fusion | flops 4311744512 | bytes 23068676 | tf_op jit(solution)/shard_map/dot_general | solution.py:38
  230.2 8.6 fusion.88
  238.9 6.7 convolution_convert_fusion.2.p_b
  245.6 6.2 convolution_convert_fusion.3.p_a
  251.8 6.1 convolution_convert_fusion
  258.0 6.2 convolution_convert_fusion.1.p_c
  264.2 8.3 add_convert_fusion
  272.6 78.1 %shard_map.231 = (bf16[2,512,1024]{2,1,0:T(8,128)(2,1)}, bf16[2,512,1024]{2,1,0:T(8,128)(2,1)}, bf16[2,512,1024]{2,1,0:T(8,128)(2,1)}, f32[128,2048]{1,0:T(8,128)}) custom-call(bf16[2048,1024]{1,0:T(8,128)(2,1)} %convolution_convert_fusion.3.p_a, bf16[2048,1024]{1,0:T(8,128)(2,1)} %convolution_convert_fusion.2.p_b, ...), custom_call_target="tpu_custom_call" | custom-call | tf_op jit(solution)/shard_map/pallas_call | solution.py:1120
  350.7 2.1 multiply_reduce_fusion.1
  352.8 2.4 fusion.131.h
  355.2 85.7 %shard_map.232 = (bf16[1024,2048]{1,0:T(8,128)(2,1)}, bf16[2,512,1024]{2,1,0:T(8,128)(2,1)}, f32[128,2048]{1,0:T(8,128)}) custom-call(bf16[128,2048]{1,0:T(8,128)(2,1)} %fusion.131.h, bf16[2,512,1024]{2,1,0:T(8,128)(2,1)} %get-tuple-element.638.s, bf16[8,128,2048]{2,1,0:T(8,128)(2,1)} %bitcast.341), custom_call_target="tpu_custom_call" | custom-call | tf_op jit(solution)/shard_map/pallas_call | solution.py:1120
  441.5 1.5 collective-permute-start
  443.0 3.8 convolution_convert_fusion.6
  447.8 21.8 %while.107 = (s32[]{:T(128)}, f32[1024,1,4,64]{0,3,2,1:T(8,128)S(1)}, f32[1024,1,64]{0,2,1:T(8,128)S(1)}, f32[1024,1,64]{0,2,1:T(8,128)}, bf16[1024,1,4,64]{0,3,...) while((s32[]{:T(128)}, ...), condition=%wide.region_14.15_spmd.clone.clone, body=%wide.region_11.14_spmd.clone.clone.sunk | while | flops 683082752 | bytes 25170536 | solution.py:206
  449.0 6.5 while.109
  449.9 1.7 fusion.190
  452.9 2.6 fusion.193
  456.6 13.0 %while.109 = (s32[]{:T(128)}, f32[512,1,4,64]{0,3,2,1:T(8,128)S(1)}, f32[1024,1,64]{0,2,1:T(8,128)S(1)}, f32[1024,1,64]{0,2,1:T(8,128)}, s32[]{:T(128)}, /*index...) while((s32[]{:T(128)}, f32[512,1,4,64]{0,3,2,1:T(8,128)S(1)}, ...), condition=%wide.region_13.13_spmd.clone, body=%wide.region_12.12_spmd.clone.sunk | while | flops 683082752 | bytes 22513896 | solution.py:197
  457.6 1.7 fusion.190
  460.6 2.6 fusion.193
  464.1 1.7 fusion.190
  467.1 2.6 fusion.193
  471.5 1.6 multiply_reduce_fusion
  473.4 2.3 fusion.100
  475.7 2.9 sine_multiply_fusion
  478.6 2.0 copy.55
  482.1 3.7 fusion.115
  486.3 2.3 convolution_convert_fusion.5.out_part
  488.7 3.6 convolution_convert_fusion.4
  492.3 4.0 add_convert_fusion.1.t_second
  496.3 3.9 add_convert_fusion.2.t_first
  500.2 190.6 %shard_map.233 = (f32[128,2048]{1,0:T(8,128)}, bf16[512,384]{1,0:T(8,128)(2,1)}, bf16[64,2048]{1,0:T(8,128)(2,1)}, bf16[2048,1024]{1,0:T(8,128)(2,1)}, bf16[2048...) custom-call(bf16[1024,384]{1,0:T(8,128)(2,1)} %copy-done.15, ...), custom_call_target="tpu_custom_call" | custom-call | tf_op jit(solution)/shard_map/pallas_call | solution.py:1120
  690.9 1.7 slice.53.query
  692.5 1.6 slice.54.pair
  694.1 1.5 fusion.104
  696.3 122.0 %shard_map.234 = (bf16[2048,1024]{1,0:T(8,128)(2,1)}, bf16[2048,1024]{1,0:T(8,128)(2,1)}, bf16[512,2048]{1,0:T(8,128)(2,1)}, bf16[8,512,128]{2,1,0:T(8,128)(2,1)...) custom-call(bf16[2,512,1024]{2,1,0:T(8,128)(2,1)} %add_convert_fusion.2.t_first, ...), custom_call_target="tpu_custom_call" | custom-call | tf_op jit(solution)/shard_map/pallas_call | solution.py:1120
  820.2 2.6 copy.56
  822.8 1.8 fusion.133
  824.6 1.3 copy.57
  825.9 1.3 copy.58
  827.2 4.3 convert_element_type.202
  831.5 2.5 convert_element_type.203
  834.0 10.2 %shard_map.237 = f32[2048,2048]{1,0:T(8,128)} custom-call(bf16[2048,1024]{1,0:T(8,128)(2,1)} %get-tuple-element.662.near, bf16[2048,1024]{1,0:T(8,128)(2,1)} %get-tuple-element.663.far), custom_call_target="tpu_custom_call" | custom-call | bytes 25165824 | tf_op jit(solution)/shard_map/pallas_call | solution.py:1135
  844.2 10.2 %shard_map.236 = f32[2048,2048]{1,0:T(8,128)} custom-call(bf16[2048,1024]{1,0:T(8,128)(2,1)} %get-tuple-element.660.near, bf16[2048,1024]{1,0:T(8,128)(2,1)} %get-tuple-element.661.far), custom_call_target="tpu_custom_call" | custom-call | bytes 25165824 | tf_op jit(solution)/shard_map/pallas_call | solution.py:1135
  854.5 10.4 %shard_map.235 = f32[2048,2048]{1,0:T(8,128)} custom-call(bf16[2048,1024]{1,0:T(8,128)(2,1)} %get-tuple-element.658.near, bf16[2048,1024]{1,0:T(8,128)(2,1)} %get-tuple-element.659.far), custom_call_target="tpu_custom_call" | custom-call | bytes 25165824 | tf_op jit(solution)/shard_map/pallas_call | solution.py:1135
  864.9 3.2 fusion.111
  (227 shorter events, 34.4 us)
Async XLA Ops:
  1.9 2.7 copy-start.42
  77.7 5.2 copy-start.36
  82.2 9.7 %copy-start.2 = (f32[1024,384]{0,1:T(8,128)}, f32[1024,384]{0,1:T(8,128)S(1)}, u32[]{:S(2)}) copy-start(f32[1024,384]{0,1:T(8,128)S(1)} %fusion.139) | copy-start | bytes 4718596
  82.4 6.4 copy-start.26
  82.6 6.2 copy-start.4
  82.9 6.0 copy-start.33
  82.9 5.9 copy-start.30
  82.9 6.0 copy-start.38
  88.8 4.5 copy-start.18
  88.9 4.5 copy-start.24
  88.9 1.7 copy-start.23
  90.4 3.0 copy-start.16
  93.4 56.4 %copy-start.6 = (bf16[1,128,2048]{2,1,0:T(8,128)(2,1)S(1)}, bf16[1,128,2048]{2,1,0:T(8,128)(2,1)}, u32[]{:S(2)}) copy-start(bf16[1,128,2048]{2,1,0:T(8,128)(2,1)} %param.21) | copy-start | bytes 1572868
  103.5 46.3 %copy-start.9 = (bf16[1024,256]{0,1:T(8,128)(2,1)}, bf16[1024,256]{0,1:T(8,128)(2,1)S(1)}, u32[]{:S(2)}) copy-start(bf16[1024,256]{0,1:T(8,128)(2,1)S(1)} %get-tuple-element.633) | copy-start | bytes 1572868
  103.5 47.8 %copy-start.28 = (f32[2048]{0:T(1024)S(1)}, f32[2048]{0:T(1024)}, u32[]{:S(2)}) copy-start(f32[2048]{0:T(1024)} %param.30) | copy-start | bytes 24580
  151.3 201.5 %copy-start = (f32[128,2048]{1,0:T(8,128)}, f32[128,2048]{1,0:T(8,128)S(1)}, u32[]{:S(2)}) copy-start(f32[128,2048]{1,0:T(8,128)S(1)} %get-tuple-element.940) | copy-start | bytes 3145732
  151.3 201.5 %copy-start.40 = (f32[128]{0:T(128)}, f32[128]{0:T(128)S(1)}, u32[]{:S(2)}) copy-start(f32[128]{0:T(128)S(1)} %add_rsqrt_fusion) | copy-start | bytes 1540
  200.0 10.1 %copy-start.13 = (bf16[8,128,2048]{2,1,0:T(8,128)(2,1)S(1)}, bf16[8,128,2048]{2,1,0:T(8,128)(2,1)}, u32[]{:S(2)}) copy-start(bf16[8,128,2048]{2,1,0:T(8,128)(2,1)} %shard_map.230) | copy-start | bytes 12582916
  200.0 18.6 %slice-start.2 = ((s8[8388608]{0:T(1024)(128)(4,1)}), s8[4194304]{0:T(1024)(128)(4,1)S(1)}, s32[]{:S(2)}) async-start(s8[8388608]{0:T(1024)(128)(4,1)} %bitcast.354), calls=%async_computation.2 | async-start | bytes 8388608
  210.1 8.4 slice-start.3
  210.1 20.1 %slice-start = ((s8[8388608]{0:T(1024)(128)(4,1)}), s8[4194304]{0:T(1024)(128)(4,1)S(1)}, s32[]{:S(2)}) async-start(s8[8388608]{0:T(1024)(128)(4,1)} %bitcast.352), calls=%async_computation | async-start | bytes 8388608
  218.5 11.7 %slice-start.1 = ((s8[8388608]{0:T(1024)(128)(4,1)}), s8[4194304]{0:T(1024)(128)(4,1)S(1)}, s32[]{:S(2)}) async-start(s8[8388608]{0:T(1024)(128)(4,1)} %bitcast.352), calls=%async_computation.1 | async-start | bytes 8388608
  230.2 8.6 copy-start.49
  238.9 6.7 copy-start.48
  238.9 6.7 copy-start.52
  251.8 6.2 copy-start.50
  251.8 12.4 %slice-start.4 = ((s8[8388608]{0:T(1024)(128)(4,1)}), s8[4194304]{0:T(1024)(128)(4,1)S(1)}, s32[]{:S(2)}) async-start(s8[8388608]{0:T(1024)(128)(4,1)} %bitcast.356), calls=%async_computation.4 | async-start | bytes 8388608
  258.0 6.3 slice-start.5
  258.0 6.3 copy-start.51
  272.6 80.2 %copy-start.12 = (bf16[1,128,2048]{2,1,0:T(8,128)(2,1)S(1)}, bf16[1,128,2048]{2,1,0:T(8,128)(2,1)}, u32[]{:S(2)}) copy-start(bf16[1,128,2048]{2,1,0:T(8,128)(2,1)} %param.22) | copy-start | bytes 1572868
  352.8 2.4 copy-start.44
  440.9 5.9 copy-start.10
  440.9 51.4 %collective-permute-start.1 = (bf16[2,512,1024]{2,1,0:T(8,128)(2,1)}, bf16[2,512,1024]{2,1,0:T(8,128)(2,1)}, u32[]{:S(2)}, u32[]{:S(2)}) collective-permute-start(bf16[2,512,1024]{2,1,0:T(8,128)(2,1)} %get-tuple-element.650), channel_id=1, source_target_pairs={{0,8},{4,12},{8,0},{12,4},{16,24},{20,28},{24,16},{28,20},{1,9},{5... | collective-permute-start | bytes 6291464 | tf_op jit(solution)/shard_map/ppermute | solution.py:1308
  441.5 54.9 %collective-permute-start = (bf16[2,512,1024]{2,1,0:T(8,128)(2,1)}, bf16[2,512,1024]{2,1,0:T(8,128)(2,1)}, u32[]{:S(2)}, u32[]{:S(2)}) collective-permute-start(bf16[2,512,1024]{2,1,0:T(8,128)(2,1)} %get-tuple-element.649), channel_id=1, source_target_pairs={{0,16},{4,20},{8,24},{12,28},{16,0},{20,4},{24,8},{28,12},{1,17},{... | collective-permute-start | bytes 6291464 | tf_op jit(solution)/shard_map/ppermute | solution.py:1308
  469.7 1.5 copy-start.3
  469.7 1.8 copy-start.14
  469.7 1.8 copy-start.17
  469.7 1.8 copy-start.25
  469.7 1.8 copy-start.39
  471.0 2.2 copy-start.27
  473.1 8.9 %copy-start.5 = (f32[1024,64]{1,0:T(8,128)S(1)}, f32[1024,64]{1,0:T(8,128)}, u32[]{:S(2)}) copy-start(f32[1024,64]{1,0:T(8,128)} %copy-done.4) | copy-start | bytes 786436
  473.2 8.9 %copy-start.31 = (f32[1024]{0:T(1024)S(1)}, f32[1024]{0:T(1024)}, u32[]{:S(2)}) copy-start(f32[1024]{0:T(1024)} %copy-done.30) | copy-start | bytes 12292
  473.2 8.9 %copy-start.37 = (f32[64]{0:T(128)S(1)}, f32[64]{0:T(128)}, u32[]{:S(2)}) copy-start(f32[64]{0:T(128)} %param.29) | copy-start | bytes 772
  475.7 10.1 %copy-start.34 = (f32[1024]{0:T(1024)S(1)}, f32[1024]{0:T(1024)}, u32[]{:S(2)}) copy-start(f32[1024]{0:T(1024)} %copy-done.33) | copy-start | bytes 12292
  481.8 4.3 copy-start.22
  481.8 4.5 copy-start.11
  481.8 4.5 copy-start.47
  486.1 2.6 copy-start.46
  486.3 6.0 copy-start.15
  488.7 3.6 copy-start.20
  492.3 4.0 copy-start.19
  500.2 193.9 %copy-start.7 = (bf16[1,128,2048]{2,1,0:T(8,128)(2,1)S(1)}, bf16[1,128,2048]{2,1,0:T(8,128)(2,1)}, u32[]{:S(2)}) copy-start(bf16[1,128,2048]{2,1,0:T(8,128)(2,1)} %param.21) | copy-start | bytes 1572868
  500.2 193.9 %copy-start.32 = (f32[2048]{0:T(1024)S(1)}, f32[2048]{0:T(1024)}, u32[]{:S(2)}) copy-start(f32[2048]{0:T(1024)} %param.23) | copy-start | bytes 24580
  500.2 193.9 %copy-start.43 = (f32[128]{0:T(128)S(1)}, f32[128]{0:T(128)}, u32[]{:S(2)}) copy-start(f32[128]{0:T(128)} %copy-done.42) | copy-start | bytes 1540
  500.2 195.4 %copy-start.35 = (f32[2048]{0:T(1024)S(1)}, f32[2048]{0:T(1024)}, u32[]{:S(2)}) copy-start(f32[2048]{0:T(1024)} %get-tuple-element.853) | copy-start | bytes 24580
  827.2 4.3 copy-start.21
  854.4 10.4 %copy-start.1 = (f32[128,2048]{1,0:T(8,128)S(1)}, f32[128,2048]{1,0:T(8,128)}, u32[]{:S(2)}) copy-start(f32[128,2048]{1,0:T(8,128)} %copy-done) | copy-start | bytes 3145732
  854.5 10.4 %copy-start.8 = (f32[128,2048]{1,0:T(8,128)S(1)}, f32[128,2048]{1,0:T(8,128)}, u32[]{:S(2)}) copy-start(f32[128,2048]{1,0:T(8,128)} %get-tuple-element.637) | copy-start | bytes 3145732
  854.5 10.4 %copy-start.29 = (f32[2048]{0:T(1024)S(1)}, f32[2048]{0:T(1024)}, u32[]{:S(2)}) copy-start(f32[2048]{0:T(1024)} %param.30) | copy-start | bytes 24580
  854.5 10.4 %copy-start.41 = (f32[128]{0:T(128)S(1)}, f32[128]{0:T(128)}, u32[]{:S(2)}) copy-start(f32[128]{0:T(128)} %copy-done.40) | copy-start | bytes 1540
  854.5 10.4 %copy-start.45 = (f32[128]{0:T(128)S(1)}, f32[128]{0:T(128)}, u32[]{:S(2)}) copy-start(f32[128]{0:T(128)} %copy-done.44) | copy-start | bytes 1540

commit v4 on v3

--- a/solution.py
+++ b/solution.py
@@ -287,6 +287,10 @@
         copy = pltpu.make_async_copy(source, target, self.locals.at[number])
         copy.start()
         return copy
+
+    def sent(self, copy):
+        copy.wait_send()
+        self.open = [other for other in self.open if other is not copy]
 
     def close(self):
         for copy in self.open:
@@ -358,13 +362,15 @@
             if self.shared:
                 self.shared[(step, 1)].start()
 
-    def close(self):
+    def close(self, shared_taken=False):
         planes, plane = self.here.planes, self.here.plane
         for (step, way), copy in self.shared.items():
 
             @pl.when(plane >= step if way == 0 else plane + step <= planes - 1)
             def _(copy=copy):
-                copy.wait()
+                copy.wait_send()
+                if not shared_taken:
+                    copy.wait_recv()
 
         for step in range(1, planes):
 
@@ -375,6 +381,46 @@
             @pl.when((plane + step <= planes) & (plane >= 1))
             def _(step=step):
                 self.downs[step].wait_send()
+
+
+class Lines:
+    def __init__(self, members):
+        self.members = members
+
+    def start(self, step):
+        for member in self.members:
+            member.start(step)
+
+    def pass_on(self, step):
+        for member in self.members:
+            member.arrive(step)
+            if step + 1 < member.here.planes:
+                member.start(step + 1)
+
+    def step(self, step):
+        for member in self.members:
+            member.step(step)
+
+    def close(self, *options):
+        for member in self.members:
+            member.close(*options)
+
+
+def gather_lines(wire, here, source, target, share=None, cuts=2):
+    rows = source.shape[0] // cuts
+    members = []
+    for cut in range(cuts):
+        at = pl.ds(cut * rows, rows)
+        members.append(
+            LineGather(
+                wire,
+                here,
+                source.at[at],
+                lambda index, at=at: target(index).at[at],
+                None if share is None else lambda index, at=at: share(index).at[at],
+            )
+        )
+    return Lines(members)
 
 
 class LineScatter:
@@ -473,19 +519,22 @@
         for color in (0, 1):
             self._send(0, color, 1)
 
-    def forward(self):
+    def hop(self, hops):
         here = self.here
         chips = here.parts // 2
-        masks = sorted(
-            (mask * 2 for mask in range(1, chips)), key=lambda mask: bin(mask).count("1")
-        )
-        for mask in masks:
+        for mask in (mask * 2 for mask in range(1, chips)):
+            if bin(mask).count("1") != hops:
+                continue
             for color, bits in enumerate(here.colors()):
                 self.incoming[(mask, color)].wait_recv()
                 last = max(i for i, bit in enumerate(bits) if mask & bit)
                 for bit in bits[last + 1 :]:
                     self._send(mask, color, bit)
                 self._send(mask, color, 1)
+
+    def hops(self, first=1):
+        for hops in range(first, len(self.here.chip_bits) + 1):
+            self.hop(hops)
 
     def finish(self):
         for mask in range(1, self.here.parts, 2):
@@ -571,7 +620,7 @@
     chips = parts // 2
     chip_masks = [mask * 2 for mask in range(1, chips)]
     here.enter(chip_masks + [1], line=True)
-    weights = LineGather(
+    weights = gather_lines(
         wire, here, w, lambda index: w_all.at[pl.ds(pl.multiple_of(index * shard, shard), shard)]
     )
     weights.start(1)
@@ -587,19 +636,20 @@
         wire.local(w, w_all.at[pl.ds(pl.multiple_of(here.plane * shard, shard), shard)]),
         wire.local(o, o_all.at[here.plane]),
     ]
-    outer = LineGather(wire, here, o, lambda index: o_all.at[index])
-    weights.arrive(1)
+    outer = gather_lines(wire, here, o, lambda index: o_all.at[index])
+    weights.members[0].arrive(1)
     if planes > 2:
-        weights.start(2)
+        weights.members[0].start(2)
+    plane_rows.hop(1)
+    weights.members[1].arrive(1)
+    if planes > 2:
+        weights.members[1].start(2)
     outer.start(1)
-    plane_rows.forward()
+    plane_rows.hops(2)
     for step in range(2, planes):
-        weights.arrive(step)
-        if step + 1 < planes:
-            weights.start(step + 1)
-        outer.arrive(step - 1)
-        outer.start(step)
-    outer.arrive(planes - 1)
+        weights.pass_on(step)
+        outer.pass_on(step - 1)
+    outer.pass_on(planes - 1)
     plane_rows.finish()
     for copy in kept:
         copy.wait()
@@ -631,148 +681,275 @@
             jnp.concatenate(rows, axis=0), w[:, columns], preferred_element_type=jnp.float32
         )
 
-    mine, theirs = here.core * planes, (1 - here.core) * planes
-    cots = LineGather(
-        wire,
-        here,
-        c,
-        lambda index: c_all.at[mine + index],
-        lambda index: c_all.at[mine + index],
-    )
+    def spot(index):
+        return c_all.at[index, here.core]
+
+    cots = gather_lines(wire, here, c, spot, spot)
     cots.start(1)
-    own = wire.local(c, c_all.at[mine + here.plane])
-    across = wire.send(c, c_all.at[mine + here.plane], {"seq": here.at(1)})
+    own = wire.local(c, spot(here.plane))
     rows = PlaneScatter(wire, here, product, give, take, current, landing, model)
     rows.start()
+    across = wire.send(c, spot(here.plane), {"seq": here.at(1)})
     rows.join()
+    rows.stage(0)
     stages = len(here.chip_bits)
     for stage in range(stages):
-        rows.stage(stage)
         if stage + 1 < planes:
-            cots.arrive(stage + 1)
-            if stage + 2 < planes:
-                cots.start(stage + 2)
+            cots.pass_on(stage + 1)
         rows.settle(stage, out)
+        if stage + 1 < stages:
+            rows.stage(stage + 1)
     for step in range(stages + 1, planes):
-        cots.arrive(step)
-        if step + 1 < planes:
-            cots.start(step + 1)
+        cots.pass_on(step)
     own.wait()
     across.wait_recv()
     wire.close()
     cots.close()
 
 
-def mid_rows_kernel(parts, planes, m, m_all, *sems):
-    here = Place(parts, planes)
-    wire = Wire(*sems)
-    here.enter([1], line=True)
-    mine = here.core * planes
-    mids = LineGather(
-        wire,
-        here,
-        m,
-        lambda index: m_all.at[mine + index],
-        lambda index: m_all.at[mine + index],
-    )
-    mids.start(1)
-    own = wire.local(m, m_all.at[mine + here.plane])
-    across = wire.send(m, m_all.at[mine + here.plane], {"seq": here.at(1)})
-    for step in range(1, planes):
-        mids.arrive(step)
-        if step + 1 < planes:
-            mids.start(step + 1)
-    own.wait()
-    across.wait_recv()
-    wire.close()
-    mids.close()
-
-
-def halve_kernel(parts, planes, p_a, p_b, p_c, part, s_down, s_first, s_second, mid, keep, *rest):
+def feed_kernel(
+    parts,
+    planes,
+    m,
+    cots,
+    gate_weight,
+    up_weight,
+    down_weight,
+    s_down,
+    s_first,
+    s_second,
+    mid,
+    down_give,
+    down_keep,
+    gate_half,
+    up_half,
+    down_half,
+    mids,
+    hidden,
+    gate_grads,
+    lifted_grads,
+    away,
+    *rest,
+):
     here = Place(parts, planes)
     stages = len(here.chip_bits) - 1
     landings, rest = rest[:stages], rest[stages:]
-    current, take, line_landing, *sems = rest
+    give, take, current, line_landing, *sems = rest
     wire = Wire(*sems)
+    tokens, model = m.shape
+    units = gate_half.shape[1]
+    own_units = pl.ds(pl.multiple_of(here.core * units, units), units)
+    loads = [
+        wire.local(whole.at[:, own_units], part)
+        for whole, part in (
+            (gate_weight, gate_half),
+            (up_weight, up_half),
+            (down_weight, down_half),
+        )
+    ]
     here.enter(here.seat_bits, line=True)
-    tokens = mid.shape[0]
-    model = p_a.shape[0]
-    swaps = TokenSum(wire, here, part, current, take, line_landing)
-    swaps.start()
-    terms = (p_a, p_b, p_c)
-    moved, kept = {}, {}
-    rows = model // 4
-    for number, term in enumerate(terms):
+
+    def spot(index):
+        return mids.at[index, here.core]
+
+    lines = gather_lines(wire, here, m, spot, spot)
+    lines.start(1)
+    across = wire.send(m, spot(here.plane), {"seq": here.at(1)})
+    own = wire.local(m, spot(here.plane))
+
+    def block(index):
+        rows = pl.ds(pl.multiple_of(index * 2 * tokens, 2 * tokens), 2 * tokens)
+        mid_rows = mids[index].reshape(2 * tokens, model)
+        cot_rows = cots[rows, :]
+
+        def part(number, carry):
+            at = pl.ds(pl.multiple_of(number * 256, 256), 256)
+            gate = jnp.dot(mid_rows, gate_half[:, at], preferred_element_type=jnp.float32)
+            lifted = jnp.dot(mid_rows, up_half[:, at], preferred_element_type=jnp.float32)
+            hidden_grad = jnp.dot(cot_rows, down_half[:, at], preferred_element_type=jnp.float32)
+            sigma = 1.0 / (1.0 + jnp.exp(-gate))
+            active = gate * sigma
+            hidden[rows, at] = (active * lifted).astype(hidden.dtype)
+            lifted_grads[rows, at] = (hidden_grad * active).astype(hidden.dtype)
+            gate_grads[rows, at] = (
+                hidden_grad * lifted * sigma * (1.0 + gate * (1.0 - sigma))
+            ).astype(hidden.dtype)
+            return carry
+
+        lax.fori_loop(0, units // 256, part, 0)
+
+    for load in loads:
+        load.wait()
+    own.wait()
+    across.wait_recv()
+    plane = here.plane
+    block(plane)
+    for step in range(1, planes):
+        lines.pass_on(step)
+        ups = jnp.where(plane >= step, 1, 0)
+        downs = jnp.where(plane + step <= planes - 1, 1, 0)
+
+        def arrived(number, carry, step=step, ups=ups):
+            from_up = (number == 0) & (ups == 1)
+            for way, chosen in ((0, from_up), (1, jnp.logical_not(from_up))):
+
+                @pl.when(chosen)
+                def _(way=way):
+                    for line in lines.members:
+                        line.shared[(step, way)].wait_recv()
+
+            block(jnp.where(from_up, plane + planes - step, plane + step) % planes)
+            return carry
+
+        lax.fori_loop(0, ups + downs, arrived, 0)
+
+    flat_mids = mids.reshape(2 * planes * tokens, model)
+    pairs = ((cots, hidden), (flat_mids, gate_grads), (flat_mids, lifted_grads))
+    quarter = model // 4
+    moved = {}
+
+    def gradient(target, pair, start):
+        left, right = pair
+
+        def part(number, carry):
+            at = pl.ds(pl.multiple_of(start + number * 256, 256), 256)
+            target[pl.ds(pl.multiple_of(number * 256, 256), 256), :] = lax.dot_general(
+                left[:, at],
+                right[...],
+                (((0,), (0,)), ((), ())),
+                preferred_element_type=jnp.float32,
+            ).astype(target.dtype)
+            return carry
+
+        lax.fori_loop(0, quarter // 256, part, 0)
+
+    def first_half(color, mine):
+        bit = here.colors()[color][0]
+        side = here.side(bit) if mine else 1 - here.side(bit)
+        return pl.multiple_of(color * (model // 2) + side * quarter, quarter)
+
+    def send_away(number):
         for color, bits in enumerate(here.colors()):
-            base = color * (model // 2)
-            away = pl.multiple_of(base + (1 - here.side(bits[0])) * rows, rows)
-            stay = pl.multiple_of(base + here.side(bits[0]) * rows, rows)
+            gradient(away.at[number, color], pairs[number], first_half(color, False))
             moved[(number, color)] = wire.send(
-                term.at[pl.ds(away, rows)],
-                landings[0].at[number, color],
-                {"seq": here.at(bits[0])},
-            )
-            kept[(number, color)] = wire.local(
-                term.at[pl.ds(stay, rows)], keep.at[number, color]
-            )
+                away.at[number, color], landings[0].at[number, color], {"seq": here.at(bits[0])}
+            )
+
+    def mid_term(target, core):
+        rows = [pl.ds(pl.multiple_of((2 * p + core) * tokens, tokens), tokens) for p in range(planes)]
+        gates = jnp.concatenate([gate_grads[at, :] for at in rows], axis=0)
+        lifts = jnp.concatenate([lifted_grads[at, :] for at in rows], axis=0)
+
+        def part(number, carry):
+            at = pl.ds(pl.multiple_of(number * 256, 256), 256)
+            term = lax.dot_general(
+                gates, gate_half[at, :], (((1,), (1,)), ((), ())), preferred_element_type=jnp.float32
+            ) + lax.dot_general(
+                lifts, up_half[at, :], (((1,), (1,)), ((), ())), preferred_element_type=jnp.float32
+            )
+            target[:, :, at] = term.reshape(planes, tokens, 256).astype(target.dtype)
+            return carry
+
+        lax.fori_loop(0, model // 256, part, 0)
+
+    def down_term(target, core):
+        rows = [pl.ds(pl.multiple_of((2 * p + core) * tokens, tokens), tokens) for p in range(planes)]
+        hiddens = jnp.concatenate([hidden[at, :] for at in rows], axis=0)
+
+        def part(number, carry):
+            at = pl.ds(pl.multiple_of(number * 256, 256), 256)
+            term = lax.dot_general(
+                hiddens, down_half[at, :], (((1,), (1,)), ((), ())), preferred_element_type=jnp.float32
+            )
+            target[:, :, at] = term.reshape(planes, tokens, 256).astype(target.dtype)
+            return carry
+
+        lax.fori_loop(0, model // 256, part, 0)
+
+    send_away(0)
+    swaps = TokenSum(wire, here, current, take, line_landing)
+    mid_term(give, 1 - here.core)
+    swaps.start(give)
+    send_away(1)
+    mid_term(current, here.core)
     swaps.join()
-    steps = list(range(1, planes))
-    done = 0
-    starts = {(number, color): 0 for number in range(3) for color in (0, 1)}
+    swaps.step(1)
+    send_away(2)
+    for step in range(2, planes):
+        swaps.step(step)
+
+    def final(number, color):
+        if number == 0:
+            return s_down.at[color]
+        return (s_first, s_second)[color].at[number - 1]
+
+    wire.sent(swaps.across)
+    down_term(give, 1 - here.core)
+    down_term(take, here.core)
+    handed = [wire.local(give, down_give), wire.local(take, down_keep)]
+    rows = quarter
+    keeps = {}
+    for number in range(3):
+        for color in (0, 1):
+            keep = final(number, color) if stages == 1 else away.at[number, color]
+            if stages > 1:
+                wire.sent(moved[(number, color)])
+            gradient(keep, pairs[number], first_half(color, True))
+            keeps[(number, color)] = (keep, 0)
+    swaps.finish(mid)
     for stage in range(stages):
         last = stage == stages - 1
         for number in range(3):
-            take_steps = len(steps) * (stage * 3 + number + 1) // (stages * 3) - done
-            for step in steps[done : done + take_steps]:
-                swaps.step(step)
-            done += take_steps
             for color, bits in enumerate(here.colors()):
+                keep, begin = keeps[(number, color)]
                 moved[(number, color)].wait_recv()
-                if stage == 0:
-                    kept[(number, color)].wait()
-                begin = starts[(number, color)]
-                mine = keep.at[number, color, pl.ds(begin, rows)]
+                mine = keep.at[pl.ds(begin, rows)]
                 if last:
-                    target = (
-                        s_down.at[color]
-                        if number == 0
-                        else (s_first, s_second)[color].at[number - 1]
-                    )
-                    add_rows(target, mine, landings[stage].at[number, color])
+                    add_rows(final(number, color), mine, landings[stage].at[number, color])
                 else:
                     add_rows(mine, mine, landings[stage].at[number, color])
                     bit = bits[stage + 1]
                     half = rows // 2
-                    away = pl.multiple_of(begin + (1 - here.side(bit)) * half, half)
+                    gone = pl.multiple_of(begin + (1 - here.side(bit)) * half, half)
                     moved[(number, color)] = wire.send(
-                        keep.at[number, color, pl.ds(away, half)],
+                        keep.at[pl.ds(gone, half)],
                         landings[stage + 1].at[number, color],
                         {"seq": here.at(bit)},
                     )
-                    starts[(number, color)] = pl.multiple_of(begin + here.side(bit) * half, half)
+                    keeps[(number, color)] = (
+                        keep,
+                        pl.multiple_of(begin + here.side(bit) * half, half),
+                    )
         rows //= 2
-    swaps.finish(mid)
+    for copy in handed:
+        copy.wait()
     wire.close()
+    lines.close(True)
     swaps.close()
 
 
 class TokenSum:
-    def __init__(self, wire, here, part, current, take, landing):
-        self.wire, self.here, self.part = wire, here, part
+    def __init__(self, wire, here, current, take, landing):
+        self.wire, self.here = wire, here
         self.current, self.take = current, take
-        self.line = LineScatter(
-            wire, here, lambda index: current.at[index], lambda way, step: landing.at[way, step]
-        )
-
-    def start(self):
-        here, planes = self.here, self.here.planes
-        self.across = self.wire.send(
-            self.part.at[pl.ds((1 - here.core) * planes, planes)], self.take, {"seq": here.at(1)}
-        )
-        self.own = self.wire.local(self.part.at[pl.ds(here.core * planes, planes)], self.current)
+        self.cuts = 2
+        rows = current.shape[1] // self.cuts
+        self.lines = []
+        for cut in range(self.cuts):
+            at = pl.ds(cut * rows, rows)
+            self.lines.append(
+                LineScatter(
+                    wire,
+                    here,
+                    lambda index, at=at: current.at[index, at],
+                    lambda way, step, at=at: landing.at[way, step, at],
+                )
+            )
+
+    def start(self, give):
+        self.across = self.wire.send(give, self.take, {"seq": self.here.at(1)})
 
     def join(self):
-        self.own.wait()
         self.across.wait_recv()
 
         def body(index, carry):
@@ -783,16 +960,22 @@
         lax.fori_loop(0, self.here.planes, body, 0)
 
     def step(self, step):
-        self.line.step(step)
+        for line in self.lines:
+            line.step(step)
 
     def finish(self, out):
-        self.line.finish(out)
+        rows = out.shape[0] // self.cuts
+        for cut, line in enumerate(self.lines):
+            line.finish(out.at[pl.ds(cut * rows, rows)])
 
     def close(self):
-        self.line.close()
-
-
-def spread_kernel(parts, planes, h, s, part, h_all, t, block, current, take, line_landing, *sems):
+        for line in self.lines:
+            line.close()
+
+
+def spread_kernel(
+    parts, planes, h, s, give, keep, h_all, t, block, current, take, line_landing, *sems
+):
     here = Place(parts, planes)
     wire = Wire(*sems)
     here.enter(here.seat_bits, line=True)
@@ -804,18 +987,25 @@
         lambda color: h.at[pl.ds(color * half, half)],
         lambda seat, color: h_all.at[pl.ds(pl.multiple_of(seat * tokens + color * half, half), half)],
     )
-    swaps = TokenSum(wire, here, part, current, take, line_landing)
+    swaps = TokenSum(wire, here, current, take, line_landing)
+    swaps.start(give)
+    kept = wire.local(keep, current)
     rows.start()
     own = wire.local(h, h_all.at[pl.ds(pl.multiple_of(here.seat * tokens, tokens), tokens)])
-    swaps.start()
+    kept.wait()
+    swaps.join()
+    swaps.step(1)
+    rows.hop(1)
     moved = [
         wire.send(s.at[color], t.at[color], {"seq": here.at(bits[-1])})
         for color, bits in enumerate(here.colors())
     ]
-    rows.forward()
-    swaps.join()
-    for step in range(1, planes):
+    for step in range(2, planes):
+        if step == 3:
+            rows.hops(2)
         swaps.step(step)
+    if planes <= 3:
+        rows.hops(2)
     rows.finish()
     for color in (0, 1):
         moved[color].wait_recv()
@@ -898,31 +1088,38 @@
         WeightGather(wire, here, (t_down.at[0], t_down.at[1]), near_down, far_down),
         WeightGather(wire, here, (t_first.at[0], t_second.at[0]), near_gate, far_gate),
     ]
+    weights[0].start()
     rows = PlaneScatter(wire, here, product, give, take, current, landing, model)
     rows.start()
+    weights[0].own()
+    heads.step(2)
+    rows.join()
+    rows.stage(0)
     deal_own.wait()
     for copy in deals:
         copy.wait_recv()
     outer.step(1)
-    rows.join()
     stages = len(here.chip_bits)
     for stage in range(stages):
-        rows.stage(stage)
-        if stage < 2:
-            weights[stage].start()
+        if stage + 3 < planes:
+            heads.step(stage + 3)
         if stage + 2 < planes:
-            heads.step(stage + 2)
             outer.step(stage + 2)
+        if stage == 0:
+            weights[0].forward()
         rows.settle(stage, out)
+        if stage + 1 < stages:
+            rows.stage(stage + 1)
+        if stage == 0:
+            weights[1].start()
+            weights[1].own()
+    for step in range(stages + 3, planes):
+        heads.step(step)
     for step in range(stages + 2, planes):
-        heads.step(step)
         outer.step(step)
-    for weight in weights:
-        weight.own()
-    for weight in weights:
-        weight.forward()
     heads.finish(head_sum)
     outer.finish(out_sum)
+    weights[1].forward()
     for weight in weights:
         weight.finish()
     wire.close()
@@ -1081,7 +1278,6 @@
     for gather in gathers:
         gather.start()
     weight = WeightGather(wire, here, (t_first.at[1], t_second.at[1]), near, far)
-    weight.start()
     own = [
         wire.local(query, query_all.at[:, pl.ds(pl.multiple_of(here.seat * columns, columns), columns)]),
         wire.local(pair, pair_all.at[here.seat]),
@@ -1090,12 +1286,16 @@
     slope_add(0)
     slope_send(1)
     for gather in gathers:
-        gather.forward()
+        gather.hop(1)
+    weight.start()
     weight.own()
     for number in range(1, len(bits)):
         slope_add(number)
         if number + 1 < len(bits):
             slope_send(number + 1)
+        if number == 2:
+            for gather in gathers:
+                gather.hops(2)
     weight.forward()
     for gather in gathers:
         gather.finish()
@@ -1144,7 +1344,7 @@
     )(near, far)
 
 
-VMEM_BYTES = 62 * 1024 * 1024
+VMEM_BYTES = 67_000_000
 
 
 def per_device(
@@ -1234,60 +1434,42 @@
         1,
         (out_rows, out_slice, cot_rows),
         (True, True, True),
-        [((tokens, model), f32), ((2 * planes, tokens, model), bf16)],
+        [((tokens, model), f32), ((planes, 2, tokens, model), bf16)],
         scatter_scratch,
     )
     middle = source + out_sum
     second = rms_factor(middle)
     normed_mid = (middle * second * feedforward_gain).astype(bf16)
-    (mid_all,) = call(
-        mid_rows_kernel,
+    quarter = model // 4
+    rows_shape = (planes, tokens, model)
+    line_scratch = [
+        (rows_shape, bf16),
+        (rows_shape, bf16),
+        ((2, planes - 1, tokens, model), bf16),
+    ]
+    acts = (2 * planes * tokens, units)
+    s_down, s_first, s_second, mid_grad, down_give, down_keep = call(
+        feed_kernel,
         sizes,
         2,
-        (normed_mid,),
-        (True,),
-        [((2 * planes, tokens, model), bf16)],
-        [],
-    )
-    cot_all = cot_all.reshape(-1, model)
-    mid_all = mid_all.reshape(-1, model)
-    gate_half = lax.dynamic_slice_in_dim(gate_weight, core * units, units, 1)
-    up_half = lax.dynamic_slice_in_dim(up_weight, core * units, units, 1)
-    down_half = lax.dynamic_slice_in_dim(down_weight, core * units, units, 1)
-    hidden_grad = matmul(cot_all, down_half)
-    gate = matmul(mid_all, gate_half)
-    lifted = matmul(mid_all, up_half)
-    hidden = activate(gate, lifted)
-    gate_grad, lifted_grad = gate_back(hidden_grad, gate, lifted)
-
-    mid_part = inner_cols(gate_grad, gate_half) + inner_cols(lifted_grad, up_half)
-    mid_part = mid_part.astype(bf16).reshape(2 * planes, tokens, model)
-    down_part = inner_cols(hidden, down_half).astype(bf16).reshape(2 * planes, tokens, model)
-    part_down = inner_rows(cot_all, hidden).astype(bf16)
-    part_gate = inner_rows(mid_all, gate_grad).astype(bf16)
-    part_up = inner_rows(mid_all, lifted_grad).astype(bf16)
-
-    line_scratch = [
-        ((planes, tokens, model), bf16),
-        ((planes, tokens, model), bf16),
-        ((2, planes - 1, tokens, model), bf16),
-    ]
-    quarter = model // 4
-    s_down, s_first, s_second, mid_grad = call(
-        halve_kernel,
-        sizes,
-        3,
-        (part_down, part_gate, part_up, mid_part),
-        (False, False, False, False),
+        (normed_mid, cot_all.reshape(-1, model), gate_weight, up_weight, down_weight),
+        (True, True, False, False, False),
         [
             ((2, last_rows, units), bf16),
             ((2, last_rows, units), bf16),
             ((2, last_rows, units), bf16),
             ((tokens, model), f32),
+            (rows_shape, bf16),
+            (rows_shape, bf16),
         ],
-        [((3, 2, quarter, units), bf16)]
+        [((model, units), bf16)] * 3
+        + [((planes, 2, tokens, model), bf16)]
+        + [(acts, bf16)] * 3
+        + [((3, 2, quarter, units), bf16)]
         + [((3, 2, quarter >> stage, units), bf16) for stage in range(halvings)]
+        + [(rows_shape, bf16)]
         + line_scratch,
+        [True] * 4 + [False] * 2,
     )
 
     feedforward_slope = jnp.sum(mid_grad * middle * second, axis=0)
@@ -1297,8 +1479,8 @@
         spread_kernel,
         sizes,
         4,
-        (middle_half, s_down, down_part),
-        (True, True, False),
+        (middle_half, s_down, down_give, down_keep),
+        (True, True, False, False),
         [((length, model), bf16), ((2, last_rows, units), bf16), ((tokens, model), f32)],
         line_scratch,
     )
@@ -1336,7 +1518,7 @@
         sizes,
         5,
         (halves, head_full, head_part, out_part, t_down, t_first, t_second),
-        (True, True, False, False, False, False, False),
+        (True, True, False, False, True, True, True),
         [((tokens, model), f32), ((shard, head_cols), bf16), ((piece_rows, model), bf16)]
         + [side] * 4,
         scatter_scratch
@@ -1367,7 +1549,7 @@
             outer_sum,
             slopes,
         ),
-        (False, False, True, True, True, True),
+        (True, True, True, True, True, True),
         [
             side,
             side,

time: 879 us -> 615 us (0.70)
  Pallas kernels: 669 us -> 471 us
  matrix products: 112 us -> 47.4 us
    pallas_call x7 -> x6, Pallas kernels: 638 us -> 440 us  [call(): pl.pallas_call(functools.partial(kernel, *mesh_sizes), out_shape=[jax.Sha...]
    dot_general x4 -> x1, matrix products: 34.7 us -> 4.51 us  [matmul(): return jnp.dot(left, right, preferred_element_type=jnp.float32)]
    dot_general x4 -> x1, matrix products: 26.9 us -> 3.77 us  [inner_cols(): lax.dot_general(left, right, (((1,), (1,)), ((), ())), preferred_element_...]
    dot_general x5 -> x2, matrix products: 25 us -> 5.83 us  [inner_rows(): lax.dot_general(left, right, (((0,), (0,)), ((), ())), preferred_element_...]
  transfers between devices with their start and end apart: 2 -> 2, of which waited for: 0 -> 0; matrix products, arithmetic and copies ran while one was open for 6% -> 8% of each run, Pallas kernels for 0% -> 0%
where the time goes in v4:
time: 615 us; the launch traced here: 604 us
  Pallas kernels  471 us (77%)
  other arithmetic  50.6 us (8%)
  matrix products  47.4 us (8%)
  local copies, waits for them, and re-layouts  30.1 us (5%)
    pallas_call x6, Pallas kernels, call(): pl.pallas_call(functools.partial(kernel, *mesh_sizes), out_shape=[jax.Sha...  440 us
    pallas_call x3, Pallas kernels, widen(): pl.pallas_call(widen_kernel, grid=(rows // step,), out_shape=jax.ShapeDty...  30.9 us
  transfers between devices with their start and end apart: 2, of which 0 were waited for; matrix products, arithmetic and copies ran while one was open for 8% of the time, Pallas kernels for 0%

profile of v4, /device:TPU:0, one launch (start us, length us, event | category | flops | bytes accessed | tf_op | source)
XLA Modules:
  0.0 603.8 jit_solution(4439980126883343408)
XLA Ops:
  0.7 1.2 fusion.91
  1.9 1.7 constant_dynamic-slice_fusion.4.o
  4.6 2.0 fusion.84.x
  6.6 1.1 constant_dynamic-slice_fusion.5
  8.6 67.3 %shard_map.228 = (bf16[1024,2048]{1,0:T(8,128)(2,1)}, bf16[2048,384]{1,0:T(8,128)(2,1)}, bf16[256,2048]{1,0:T(8,128)(2,1)}) custom-call(bf16[128,2048]{1,0:T(8,128)(2,1)} %fusion.84.x, bf16[512,384]{1,0:T(8,128)(2,1)} %pad_maximum_fusion.3.w, bf16[64,2048]{1,0:T(8,128)(2,1)} %constant_dynamic-slice_fusion.4.o), custom_call_target="tpu_custom_call" | custom-call | tf_op jit(solution)/shard_map/pallas_call | solution.py:1320
  75.9 4.5 fusion.123
  83.3 3.2 fusion.109
  88.9 1.1 maximum_multiply_fusion
  90.1 1.3 fusion.118
  91.5 15.0 %while.105 = (s32[]{:T(128)}, bf16[1024,256]{0,1:T(8,128)(2,1)S(1)}, f32[1,4,1024]{2,1,0:T(4,128)S(1)}, bf16[1024,1,4,64]{0,3,2,1:T(8,128)(2,1)}, bf16[1024,1,64...) while((s32[]{:T(128)}, bf16[1024,256]{0,1:T(8,128)(2,1)S(1)}, ...), condition=%wide.region_7.8_spmd.clone.clone, body=%wide.region_3.7_spmd.clone.clone.sunk | while | flops 275383296 | bytes 13054458 | solution.py:130
  92.6 4.2 while.108
  92.9 2.1 fusion.168
  95.0 1.8 fusion.169
  98.0 8.4 %while.108 = (s32[]{:T(128)}, f32[1,4,512,64]{2,3,1,0:T(8,128)S(1)}, f32[1,4,512]{2,1,0:T(4,128)S(1)}, s32[]{:T(128)}, s32[]{:T(128)}, /*index=5*/s32[512]{0:T(5...) while((s32[]{:T(128)}, f32[1,4,512,64]{2,3,1,0:T(8,128)S(1)}, ...), condition=%wide.region_6.6_spmd.clone, body=%wide.region_4.5_spmd.clone.sunk | while | flops 275121152 | bytes 10660027 | solution.py:119
  98.3 2.1 fusion.168
  100.4 1.8 fusion.169
  102.5 2.1 fusion.168
  104.6 1.8 fusion.169
  108.4 42.2 %shard_map.229 = (f32[128,2048]{1,0:T(8,128)}, bf16[4,2,128,2048]{3,2,1,0:T(8,128)(2,1)}) custom-call(bf16[1024,256]{1,0:T(8,128)(2,1)} %copy.50.a, bf16[256,2048]{1,0:T(8,128)(2,1)} %get-tuple-element.636.w, bf16[128,2048]{1,0:T(8,128)(2,1)} %bitcast.320), custom_call_target="tpu_custom_call" | custom-call | tf_op jit(solution)/shard_map/pallas_call | solution.py:1320
  150.6 1.6 multiply_reduce_fusion.4
  154.1 124.1 %shard_map.230 = (bf16[2,512,1024]{2,1,0:T(8,128)(2,1)}, bf16[2,512,1024]{2,1,0:T(8,128)(2,1)}, bf16[2,512,1024]{2,1,0:T(8,128)(2,1)}, f32[128,2048]{1,0:T(8,128...) custom-call(bf16[128,2048]{1,0:T(8,128)(2,1)} %multiply_convert_fusion.m, bf16[1024,2048]{1,0:T(8,128)(2,1)} %bitcast.321, ...), custom_call_target="tpu_custom_call" | custom-call | tf_op jit(solution)/shard_map/pallas_call | solution.py:1320
  278.2 2.4 multiply_reduce_fusion.1
  280.6 2.8 fusion.115.h
  283.4 52.4 %shard_map.231 = (bf16[1024,2048]{1,0:T(8,128)(2,1)}, bf16[2,512,1024]{2,1,0:T(8,128)(2,1)}, f32[128,2048]{1,0:T(8,128)}) custom-call(bf16[128,2048]{1,0:T(8,128)(2,1)} %fusion.115.h, bf16[2,512,1024]{2,1,0:T(8,128)(2,1)} %get-tuple-element.640.s, bf16[4,128,2048]{2,1,0:T(8,128)(2,1)} %get-tuple-element.641.give, bf16[4,128,2048]{2,1,0:T(8,128)(2,1)} %get-tuple-element.642.keep), custom_call_target="tpu_custom_call" | custom-call | tf_op jit(solution)/shard_map/pallas_call | solution.py:1320
  335.8 1.4 collective-permute-start.1
  337.9 3.8 convolution_convert_fusion.2
  342.1 25.2 %while.107 = (s32[]{:T(128)}, f32[1024,1,4,64]{0,3,2,1:T(8,128)S(1)}, f32[1024,1,64]{0,2,1:T(8,128)S(1)}, f32[1024,1,64]{0,2,1:T(8,128)S(1)}, bf16[1024,1,4,64]{...) while((s32[]{:T(128)}, ...), condition=%wide.region_14.15_spmd.clone.clone, body=%wide.region_11.14_spmd.clone.clone.sunk | while | flops 683082752 | bytes 25170536 | solution.py:206
  343.6 7.5 %while.109 = (s32[]{:T(128)}, f32[512,1,4,64]{0,3,2,1:T(8,128)S(1)}, f32[1024,1,64]{0,2,1:T(8,128)S(1)}, f32[1024,1,64]{0,2,1:T(8,128)S(1)}, s32[]{:T(128)}, /*i...) while((s32[]{:T(128)}, f32[512,1,4,64]{0,3,2,1:T(8,128)S(1)}, ...), condition=%wide.region_13.13_spmd.clone, body=%wide.region_12.12_spmd.clone.sunk | while | flops 683082752 | bytes 22513896 | solution.py:197
  343.6 1.6 fusion.161
  345.4 2.5 fusion.162
  348.0 1.3 fusion.163
  351.2 1.0 constant_dynamic-slice_fusion.12
  352.3 14.9 %while.109 = (s32[]{:T(128)}, f32[512,1,4,64]{0,3,2,1:T(8,128)S(1)}, f32[1024,1,64]{0,2,1:T(8,128)S(1)}, f32[1024,1,64]{0,2,1:T(8,128)S(1)}, s32[]{:T(128)}, /*i...) while((s32[]{:T(128)}, f32[512,1,4,64]{0,3,2,1:T(8,128)S(1)}, ...), condition=%wide.region_13.13_spmd.clone, body=%wide.region_12.12_spmd.clone.sunk | while | flops 683082752 | bytes 22513896 | solution.py:197
  352.3 1.6 fusion.161
  354.1 2.5 fusion.162
  356.6 1.3 fusion.163
  359.8 1.6 fusion.161
  361.6 2.5 fusion.162
  364.1 1.3 fusion.163
  369.1 1.6 multiply_reduce_fusion
  371.0 2.3 fusion.90
  373.3 1.9 sine_multiply_fusion
  375.2 1.2 copy.55
  376.5 1.1 copy.54
  377.8 2.5 fusion.105
  380.9 2.3 convolution_convert_fusion.1.out_part
  383.3 3.6 convolution_convert_fusion
  386.8 4.0 add_convert_fusion.t_second
  390.9 3.9 add_convert_fusion.1.t_first
  394.7 88.1 %shard_map.232 = (f32[128,2048]{1,0:T(8,128)}, bf16[512,384]{1,0:T(8,128)(2,1)}, bf16[64,2048]{1,0:T(8,128)(2,1)}, bf16[2048,1024]{1,0:T(8,128)(2,1)}, bf16[2048...) custom-call(bf16[1024,384]{1,0:T(8,128)(2,1)} %copy-done.14, ...), custom_call_target="tpu_custom_call" | custom-call | tf_op jit(solution)/shard_map/pallas_call | solution.py:1320
  482.9 1.7 slice.53.query
  484.6 1.6 slice.54.pair
  486.1 1.6 fusion.94
  488.5 65.9 %shard_map.233 = (bf16[2048,1024]{1,0:T(8,128)(2,1)}, bf16[2048,1024]{1,0:T(8,128)(2,1)}, bf16[512,2048]{1,0:T(8,128)(2,1)}, bf16[8,512,128]{2,1,0:T(8,128)(2,1)...) custom-call(bf16[2,512,1024]{2,1,0:T(8,128)(2,1)} %add_convert_fusion.1.t_first, ...), custom_call_target="tpu_custom_call" | custom-call | tf_op jit(solution)/shard_map/pallas_call | solution.py:1320
  556.3 1.5 copy.56
  557.8 1.2 fusion.117
  559.0 2.5 copy.57
  561.6 1.3 copy.58
  562.9 4.1 convert_element_type.170
  567.0 2.5 convert_element_type.171
  569.6 10.2 %shard_map.236 = f32[2048,2048]{1,0:T(8,128)} custom-call(bf16[2048,1024]{1,0:T(8,128)(2,1)} %get-tuple-element.666.near, bf16[2048,1024]{1,0:T(8,128)(2,1)} %get-tuple-element.667.far), custom_call_target="tpu_custom_call" | custom-call | bytes 25165824 | tf_op jit(solution)/shard_map/pallas_call | solution.py:1335
  579.8 10.2 %shard_map.235 = f32[2048,2048]{1,0:T(8,128)} custom-call(bf16[2048,1024]{1,0:T(8,128)(2,1)} %get-tuple-element.664.near, bf16[2048,1024]{1,0:T(8,128)(2,1)} %get-tuple-element.665.far), custom_call_target="tpu_custom_call" | custom-call | bytes 25165824 | tf_op jit(solution)/shard_map/pallas_call | solution.py:1335
  590.0 10.5 %shard_map.234 = f32[2048,2048]{1,0:T(8,128)} custom-call(bf16[2048,1024]{1,0:T(8,128)(2,1)} %get-tuple-element.662.near, bf16[2048,1024]{1,0:T(8,128)(2,1)} %get-tuple-element.663.far), custom_call_target="tpu_custom_call" | custom-call | bytes 25165824 | tf_op jit(solution)/shard_map/pallas_call | solution.py:1335
  600.5 3.1 fusion.101
  (192 shorter events, 27.5 us)
Async XLA Ops:
  1.9 2.7 copy-start.42
  75.9 6.0 copy-start.36
  80.4 9.7 %copy-start.2 = (f32[1024,384]{0,1:T(8,128)}, f32[1024,384]{0,1:T(8,128)S(1)}, u32[]{:S(2)}) copy-start(f32[1024,384]{0,1:T(8,128)S(1)} %fusion.123) | copy-start | bytes 4718596
  80.6 6.1 %copy-start.26 = (f32[1024,4]{0,1:T(4,128)}, f32[1024,4]{0,1:T(4,128)S(1)}, u32[]{:S(2)}) copy-start(f32[1024,4]{0,1:T(4,128)S(1)} %multiply_reduce_fusion.5) | copy-start | bytes 49156
  81.6 5.1 copy-start.4
  81.8 4.6 copy-start.33
  81.8 4.6 copy-start.30
  81.9 4.8 copy-start.38
  86.7 4.8 copy-start.17
  86.7 4.7 copy-start.24
  86.7 1.4 copy-start.22
  88.1 3.5 copy-start.15
  106.6 0.8 copy-start.8
  106.6 46.6 %copy-start.28 = (f32[2048]{0:T(1024)S(1)}, f32[2048]{0:T(1024)}, u32[]{:S(2)}) copy-start(f32[2048]{0:T(1024)} %param.30) | copy-start | bytes 24580
  152.2 1.0 copy-start
  152.2 128.4 %copy-start.40 = (f32[128]{0:T(128)}, f32[128]{0:T(128)S(1)}, u32[]{:S(2)}) copy-start(f32[128]{0:T(128)S(1)} %add_rsqrt_fusion) | copy-start | bytes 1540
  280.6 2.8 copy-start.44
  335.8 5.9 copy-start.9
  335.8 51.0 %collective-permute-start.1 = (bf16[2,512,1024]{2,1,0:T(8,128)(2,1)}, bf16[2,512,1024]{2,1,0:T(8,128)(2,1)}, u32[]{:S(2)}, u32[]{:S(2)}) collective-permute-start(bf16[2,512,1024]{2,1,0:T(8,128)(2,1)} %get-tuple-element.654), channel_id=1, source_target_pairs={{0,8},{4,12},{8,0},{12,4},{16,24},{20,28},{24,16},{28,20},{1,9},{5... | collective-permute-start | bytes 6291464 | tf_op jit(solution)/shard_map/ppermute | solution.py:1490
  337.2 53.6 %collective-permute-start = (bf16[2,512,1024]{2,1,0:T(8,128)(2,1)}, bf16[2,512,1024]{2,1,0:T(8,128)(2,1)}, u32[]{:S(2)}, u32[]{:S(2)}) collective-permute-start(bf16[2,512,1024]{2,1,0:T(8,128)(2,1)} %get-tuple-element.653), channel_id=1, source_target_pairs={{0,16},{4,20},{8,24},{12,28},{16,0},{20,4},{24,8},{28,12},{1,17},{... | collective-permute-start | bytes 6291464 | tf_op jit(solution)/shard_map/ppermute | solution.py:1490
  342.1 25.3 %copy-start.18 = (f32[1024,64]{0,1:T(8,128)S(1)}, f32[1024,64]{0,1:T(8,128)}, u32[]{:S(2)}) copy-start(f32[1024,64]{0,1:T(8,128)} %copy-done.17) | copy-start | bytes 786436
  367.3 0.7 copy-start.23
  367.3 1.5 copy-start.3
  367.3 1.8 copy-start.13
  367.3 1.8 copy-start.16
  367.3 1.8 copy-start.25
  367.3 1.8 copy-start.39
  367.5 3.2 copy-start.27
  369.1 4.2 copy-start.12
  370.8 7.0 %copy-start.5 = (f32[1024,64]{1,0:T(8,128)S(1)}, f32[1024,64]{1,0:T(8,128)}, u32[]{:S(2)}) copy-start(f32[1024,64]{1,0:T(8,128)} %copy-done.4) | copy-start | bytes 786436
  370.8 7.0 %copy-start.31 = (f32[1024]{0:T(1024)S(1)}, f32[1024]{0:T(1024)}, u32[]{:S(2)}) copy-start(f32[1024]{0:T(1024)} %copy-done.30) | copy-start | bytes 12292
  370.8 7.0 %copy-start.37 = (f32[64]{0:T(128)S(1)}, f32[64]{0:T(128)}, u32[]{:S(2)}) copy-start(f32[64]{0:T(128)} %param.29) | copy-start | bytes 772
  373.3 7.0 %copy-start.34 = (f32[1024]{0:T(1024)S(1)}, f32[1024]{0:T(1024)}, u32[]{:S(2)}) copy-start(f32[1024]{0:T(1024)} %copy-done.33) | copy-start | bytes 12292
  377.6 3.3 copy-start.10
  377.6 3.3 copy-start.47
  380.7 2.6 copy-start.46
  380.9 6.0 copy-start.14
  383.3 3.6 copy-start.20
  386.8 4.0 copy-start.19
  394.7 91.4 %copy-start.32 = (f32[2048]{0:T(1024)S(1)}, f32[2048]{0:T(1024)}, u32[]{:S(2)}) copy-start(f32[2048]{0:T(1024)} %param.23) | copy-start | bytes 24580
  394.7 91.4 %copy-start.43 = (f32[128]{0:T(128)S(1)}, f32[128]{0:T(128)}, u32[]{:S(2)}) copy-start(f32[128]{0:T(128)} %copy-done.42) | copy-start | bytes 1540
  394.7 93.0 %copy-start.35 = (f32[2048]{0:T(1024)S(1)}, f32[2048]{0:T(1024)}, u32[]{:S(2)}) copy-start(f32[2048]{0:T(1024)} %get-tuple-element.857) | copy-start | bytes 24580
  561.6 5.4 copy-start.21
  590.0 10.5 %copy-start.1 = (f32[128,2048]{1,0:T(8,128)S(1)}, f32[128,2048]{1,0:T(8,128)}, u32[]{:S(2)}) copy-start(f32[128,2048]{1,0:T(8,128)} %copy-done) | copy-start | bytes 3145732
  590.0 10.5 %copy-start.6 = (bf16[1,128,2048]{2,1,0:T(8,128)(2,1)S(1)}, bf16[1,128,2048]{2,1,0:T(8,128)(2,1)}, u32[]{:S(2)}) copy-start(bf16[1,128,2048]{2,1,0:T(8,128)(2,1)} %param.21) | copy-start | bytes 1572868
  590.0 10.5 %copy-start.7 = (f32[128,2048]{1,0:T(8,128)S(1)}, f32[128,2048]{1,0:T(8,128)}, u32[]{:S(2)}) copy-start(f32[128,2048]{1,0:T(8,128)} %get-tuple-element.639) | copy-start | bytes 3145732
  590.0 10.5 %copy-start.11 = (bf16[1,128,2048]{2,1,0:T(8,128)(2,1)S(1)}, bf16[1,128,2048]{2,1,0:T(8,128)(2,1)}, u32[]{:S(2)}) copy-start(bf16[1,128,2048]{2,1,0:T(8,128)(2,1)} %param.22) | copy-start | bytes 1572868
  590.0 10.5 %copy-start.29 = (f32[2048]{0:T(1024)S(1)}, f32[2048]{0:T(1024)}, u32[]{:S(2)}) copy-start(f32[2048]{0:T(1024)} %param.30) | copy-start | bytes 24580
  590.0 10.5 %copy-start.41 = (f32[128]{0:T(128)S(1)}, f32[128]{0:T(128)}, u32[]{:S(2)}) copy-start(f32[128]{0:T(128)} %copy-done.40) | copy-start | bytes 1540
  590.0 10.5 %copy-start.45 = (f32[128]{0:T(128)S(1)}, f32[128]{0:T(128)}, u32[]{:S(2)}) copy-start(f32[128]{0:T(128)} %copy-done.44) | copy-start | bytes 1540

commit v5 on v4

--- a/solution.py
+++ b/solution.py
@@ -281,10 +281,13 @@
         self.open.append(copy)
         return copy
 
-    def local(self, source, target):
+    def quiet(self, source, target):
         number = self.local_count
         self.local_count += 1
-        copy = pltpu.make_async_copy(source, target, self.locals.at[number])
+        return pltpu.make_async_copy(source, target, self.locals.at[number])
+
+    def local(self, source, target):
+        copy = self.quiet(source, target)
         copy.start()
         return copy
 
@@ -612,7 +615,100 @@
             add_rows(target, mine, self.landing.at[position, color, low])
 
 
-def head_weights_kernel(parts, planes, x, w, o, x_all, w_all, o_slice, o_all, *sems):
+def pick_lanes(low, high, width):
+    lane = lax.broadcasted_iota(jnp.int32, low.shape, low.ndim - 1)
+    return jnp.where(lane % (2 * width) < width, low, high)
+
+
+def group_mean(values, group, width):
+    high = values.astype(jnp.bfloat16)
+    low = (values - high.astype(jnp.float32)).astype(jnp.bfloat16)
+    total = jnp.dot(high, group, preferred_element_type=jnp.float32) + jnp.dot(
+        low, group, preferred_element_type=jnp.float32
+    )
+    return total * (1.0 / width)
+
+
+def turn(values, width):
+    lanes = values.shape[1]
+    half = width // 2
+    return pick_lanes(
+        pltpu.roll(values, lanes - half, 1), pltpu.roll(values, half, 1), half
+    )
+
+
+def attend_block(index, block, width, heads, queries, pair, twin, left, right, out_rows, logs):
+    rows = pl.ds(index * block, block)
+    before = index * block
+    columns = 2 * width
+    row = lax.broadcasted_iota(jnp.int32, (block, block), 0)
+    column = lax.broadcasted_iota(jnp.int32, (block, block), 1)
+    allowed = row >= column
+    contract = (((1,), (1,)), ((), ()))
+    totals = []
+    for number in range(heads // 2):
+        at = pl.ds(number * columns, columns)
+        both = queries[rows, at]
+        both = (both.astype(jnp.float32) * width**-0.5).astype(both.dtype)
+        zero = jnp.zeros_like(both)
+        result = None
+        for side, values in ((0, left), (1, right)):
+            mine = pick_lanes(both, zero, width) if side == 0 else pick_lanes(zero, both, width)
+            scores = lax.dot_general(
+                mine, twin[rows, :], contract, preferred_element_type=jnp.float32
+            )
+            weights = jnp.where(allowed, jnp.exp(scores), 0.0)
+            total = jnp.sum(weights, axis=1, keepdims=True)
+            summed = jnp.dot(
+                weights.astype(jnp.bfloat16), values[rows, :], preferred_element_type=jnp.float32
+            )
+            if before:
+                scores = lax.dot_general(
+                    mine, twin[0:before, :], contract, preferred_element_type=jnp.float32
+                )
+                weights = jnp.exp(scores)
+                total = total + jnp.sum(weights, axis=1, keepdims=True)
+                summed = summed + jnp.dot(
+                    weights.astype(jnp.bfloat16),
+                    values[0:before, :],
+                    preferred_element_type=jnp.float32,
+                )
+            totals.append(total)
+            part = summed / total
+            result = part if result is None else result + part
+        out_rows[rows, at] = result.astype(out_rows.dtype)
+    lane = lax.broadcasted_iota(jnp.int32, (block, 128), 1)
+    table = jnp.ones((block, 128), jnp.float32)
+    for number, total in enumerate(totals):
+        table = jnp.where(lane == number, total, table)
+    logs[:, rows] = jnp.log(table).T[0 : logs.shape[0], :]
+
+
+def front_kernel(
+    width,
+    parts,
+    planes,
+    x,
+    w,
+    o,
+    gain,
+    cosine,
+    sine,
+    group,
+    x_all,
+    w_all,
+    o_slice,
+    proj,
+    queries,
+    pair,
+    out_rows,
+    logs,
+    o_all,
+    twin,
+    left,
+    right,
+    *sems,
+):
     here = Place(parts, planes)
     wire = Wire(*sems)
     tokens, shard, rows = x.shape[0], w.shape[0], o.shape[0]
@@ -646,22 +742,70 @@
         weights.members[1].start(2)
     outer.start(1)
     plane_rows.hops(2)
+    spot = o_slice.at[pl.ds(pl.multiple_of(here.chip * rows, rows), rows)]
+    deals = []
+    for mask in chip_masks:
+        chip = here.at(mask) // 2
+        deals.append((chip, wire.remote(o_all.at[chip], spot, {"seq": here.at(mask)})))
+    keep_own = wire.quiet(o_all.at[here.chip], spot)
+
+    def deal(step):
+        for chip, copy in deals + [(here.chip, keep_own)]:
+
+            @pl.when((chip == here.plane + step) | (chip + step == here.plane))
+            def _(copy=copy):
+                copy.start()
+
+    kept[2].wait()
+    deal(0)
     for step in range(2, planes):
         weights.pass_on(step)
-        outer.pass_on(step - 1)
-    outer.pass_on(planes - 1)
     plane_rows.finish()
-    for copy in kept:
+    for copy in kept[:2]:
         copy.wait()
-    dealt = []
-    spot = o_slice.at[pl.ds(pl.multiple_of(here.chip * rows, rows), rows)]
-    for mask in chip_masks:
-        chip = here.at(mask) // 2
-        dealt.append(wire.send(o_all.at[chip], spot, {"seq": here.at(mask)}))
-    own = wire.local(o_all.at[here.chip], spot)
-    own.wait()
-    for copy in dealt:
-        copy.wait_recv()
+    length = x_all.shape[0]
+    block = min(256, length)
+    blocks = length // block
+    query_cols = queries.shape[1]
+    heads = query_cols // width
+
+    def project(index, carry):
+        at = pl.ds(pl.multiple_of(index * block, block), block)
+        value = jnp.dot(x_all[at, :], w_all[...], preferred_element_type=jnp.float32)
+        proj[at, :] = value
+        factor = lax.rsqrt(group_mean(value * value, group[...], width) + EPS)
+        normed = value * factor * gain[...]
+        repeat = value.shape[1] // cosine.shape[1]
+        cosines = jnp.concatenate([cosine[at, :]] * repeat, axis=1)
+        sines = jnp.concatenate([sine[at, :]] * repeat, axis=1)
+        turned = normed * cosines + turn(normed, width) * sines
+        queries[at, :] = turned[:, :query_cols].astype(queries.dtype)
+        keys, values = turned[:, query_cols:], value[:, query_cols:]
+        both = pick_lanes(keys, values, width)
+        pair[at, :] = both.astype(pair.dtype)
+        swapped = pltpu.roll(both, width, 1)
+        twin[at, :] = pick_lanes(both, swapped, width).astype(twin.dtype)
+        zero = jnp.zeros_like(both)
+        left[at, :] = pick_lanes(swapped, zero, width).astype(left.dtype)
+        right[at, :] = pick_lanes(zero, both, width).astype(right.dtype)
+        return carry
+
+    lax.fori_loop(0, blocks, project, 0)
+    waits = list(range(1, planes))
+    for index in range(blocks):
+        while waits and waits[0] * blocks <= (index + 1) * planes:
+            step = waits.pop(0)
+            outer.pass_on(step)
+            deal(step)
+        attend_block(
+            index, block, width, heads, queries, pair, twin, left, right, out_rows, logs
+        )
+    for step in waits:
+        outer.pass_on(step)
+        deal(step)
+    keep_own.wait()
+    for _, copy in deals:
+        copy.wait()
     wire.close()
     weights.close()
     outer.close()
@@ -716,8 +860,10 @@
     up_weight,
     down_weight,
     s_down,
-    s_first,
-    s_second,
+    s_gate_a,
+    s_gate_b,
+    s_up_a,
+    s_up_b,
     mid,
     down_give,
     down_keep,
@@ -881,7 +1027,7 @@
     def final(number, color):
         if number == 0:
             return s_down.at[color]
-        return (s_first, s_second)[color].at[number - 1]
+        return ((s_gate_a, s_gate_b), (s_up_a, s_up_b))[number - 1][color]
 
     wire.sent(swaps.across)
     down_term(give, 1 - here.core)
@@ -1016,7 +1162,7 @@
     swaps.close()
 
 
-def in_rows_kernel(
+def final_kernel(
     parts,
     planes,
     a,
@@ -1024,33 +1170,45 @@
     head_part,
     out_part,
     t_down,
-    t_first,
-    t_second,
-    out,
-    head_sum,
-    out_sum,
-    near_down,
-    far_down,
-    near_gate,
-    far_gate,
-    give,
-    take,
-    current,
-    landing,
-    head_current,
-    head_landing,
-    dealt,
-    out_landing,
-    *sems,
+    source,
+    factor,
+    slope,
+    *rest,
 ):
+    sent, rest = rest[:4], rest[4:]
+    came, rest = rest[:4], rest[4:]
+    out, near, far, query_all, pair_all, outer_all, slope_out, *rest = rest
+    joined, rest = rest[:4], rest[4:]
+    (
+        give,
+        take,
+        current,
+        landing,
+        head_current,
+        head_landing,
+        dealt,
+        out_landing,
+        head_sum,
+        out_sum,
+        left,
+        right,
+        slope_sums,
+        slope_landing,
+        *sems,
+    ) = rest
     here = Place(parts, planes)
     wire = Wire(*sems)
     tokens, model = out.shape
     shard = head_sum.shape[0]
+    columns = query_all.shape[1] // parts
     rows_out = out_sum.shape[0]
     chips = parts // 2
     chip_masks = [mask * 2 for mask in range(1, chips)]
-    here.enter(chip_masks + [1], line=True)
+    here.enter(chip_masks + [1], line=True, plane_masks=here.plane_bits)
+    weights = [
+        WeightGather(wire, here, (t_down.at[0], t_down.at[1]), near, far, cut, 2)
+        for cut in range(2)
+    ]
     head_own = wire.local(head_part, head_current)
     deals = []
     for mask in chip_masks:
@@ -1084,55 +1242,157 @@
     )
     head_own.wait()
     heads.step(1)
-    weights = [
-        WeightGather(wire, here, (t_down.at[0], t_down.at[1]), near_down, far_down),
-        WeightGather(wire, here, (t_first.at[0], t_second.at[0]), near_gate, far_gate),
-    ]
-    weights[0].start()
     rows = PlaneScatter(wire, here, product, give, take, current, landing, model)
     rows.start()
-    weights[0].own()
+    loads = []
+    for number in range(4):
+        loads.append(
+            (
+                wire.local(sent[number], left.at[number]),
+                wire.local(came[number], right.at[number]),
+            )
+        )
     heads.step(2)
     rows.join()
     rows.stage(0)
+    weights[0].start()
+    weights[0].own()
     deal_own.wait()
     for copy in deals:
         copy.wait_recv()
     outer.step(1)
+
+    stores = []
+
+    def join(number):
+        for load in loads[number]:
+            load.wait()
+        add_rows(left.at[number], left.at[number], right.at[number])
+        stores.append(wire.local(left.at[number], joined[number]))
+
     stages = len(here.chip_bits)
-    for stage in range(stages):
-        if stage + 3 < planes:
-            heads.step(stage + 3)
-        if stage + 2 < planes:
-            outer.step(stage + 2)
-        if stage == 0:
-            weights[0].forward()
-        rows.settle(stage, out)
+    for step in range(3, planes):
+        heads.step(step)
+    rows.settle(0, out)
+    for stage in range(1, stages):
+        rows.stage(stage)
+        if stage + 1 < planes:
+            outer.step(stage + 1)
+        if stage == 1:
+            heads.finish(head_sum)
         if stage + 1 < stages:
-            rows.stage(stage + 1)
-        if stage == 0:
-            weights[1].start()
-            weights[1].own()
-    for step in range(stages + 3, planes):
-        heads.step(step)
-    for step in range(stages + 2, planes):
+            rows.settle(stage, out)
+    half, half_out = shard // 2, rows_out // 2
+
+    def seat_columns(seat):
+        return pl.ds(pl.multiple_of(seat * columns, columns), columns)
+
+    gathers = [
+        PlaneGather(
+            wire,
+            here,
+            lambda color: head_sum.at[pl.ds(color * half, half), pl.ds(0, columns)],
+            lambda seat, color: query_all.at[pl.ds(color * half, half), seat_columns(seat)],
+        ),
+        PlaneGather(
+            wire,
+            here,
+            lambda color: head_sum.at[
+                pl.ds(color * half, half), pl.ds(columns, pair_all.shape[2])
+            ],
+            lambda seat, color: pair_all.at[seat, pl.ds(color * half, half)],
+        ),
+        PlaneGather(
+            wire,
+            here,
+            lambda color: out_sum.at[pl.ds(color * half_out, half_out)],
+            lambda seat, color: outer_all.at[
+                pl.ds(
+                    pl.multiple_of(
+                        ((seat % 2) * chips + seat // 2) * rows_out + color * half_out, half_out
+                    ),
+                    half_out,
+                )
+            ],
+        ),
+    ]
+    own = []
+    for gather in gathers[:2]:
+        gather.start()
+    own.append(
+        wire.local(head_sum.at[:, pl.ds(0, columns)], query_all.at[:, seat_columns(here.seat)])
+    )
+    own.append(
+        wire.local(
+            head_sum.at[:, pl.ds(columns, pair_all.shape[2])], pair_all.at[here.seat]
+        )
+    )
+
+    weights[1].start()
+    weights[1].own()
+    rows.settle(stages - 1, out)
+    slope_sums[0] = slope[...]
+    slope_sums[0, 0:1, :] = jnp.sum(out[...] * source[...].astype(jnp.float32) * factor[...], axis=0, keepdims=True)
+    bits = [("seq", bit) for bit in here.seat_bits] + [("fsdp", bit) for bit in here.plane_bits]
+    slope_copies = []
+
+    def slope_send(number):
+        axis, bit = bits[number]
+        index = here.at(bit) if axis == "seq" else flip(here.plane, bit, here.plane_bits)
+        slope_copies.append(
+            wire.send(slope_sums.at[number], slope_landing.at[number], {axis: index})
+        )
+
+    def slope_add(number):
+        slope_copies[number].wait_recv()
+        target = slope_out if number == len(bits) - 1 else slope_sums.at[number + 1]
+        target[...] = slope_sums[number] + slope_landing[number]
+
+    slope_send(0)
+    for step in range(stages + 1, planes):
         outer.step(step)
-    heads.finish(head_sum)
+    join(0)
+    gathers[0].hop(1)
+    gathers[1].hop(1)
+    slope_add(0)
+    slope_send(1)
     outer.finish(out_sum)
+    gathers[2].start()
+    weights[0].forward()
+    own_start = (here.core * chips + here.chip) * rows_out
+    own.append(
+        wire.local(out_sum, outer_all.at[pl.ds(pl.multiple_of(own_start, rows_out), rows_out)])
+    )
+    join(1)
+    for number in range(1, len(bits)):
+        slope_add(number)
+        if number + 1 < len(bits):
+            slope_send(number + 1)
+        if number < 3:
+            join(number + 1)
+    gathers[2].hop(1)
+    for gather in gathers:
+        gather.hops(2)
     weights[1].forward()
+    for gather in gathers:
+        gather.finish()
     for weight in weights:
         weight.finish()
+    for copy in own + stores:
+        copy.wait()
     wire.close()
     heads.close()
     outer.close()
 
 
 class WeightGather:
-    def __init__(self, wire, here, finals, near, far):
+    def __init__(self, wire, here, finals, near, far, cut=0, cuts=1):
         self.wire, self.here, self.near, self.far = wire, here, near, far
         self.size = finals[0].shape[0]
+        self.rows = self.size // cuts
+        self.shift = cut * self.rows
         model = near.shape[0]
-        self.finals = finals
+        self.finals = [final.at[pl.ds(self.shift, self.rows)] for final in finals]
         self.starts = []
         for color, order in enumerate(here.colors()):
             start = color * (model // 2)
@@ -1144,7 +1404,7 @@
         self.swaps, self.kept = [], []
 
     def _rows(self, start):
-        return pl.ds(pl.multiple_of(start, self.size), self.size)
+        return pl.ds(pl.multiple_of(start + self.shift, self.rows), self.rows)
 
     def _pass(self, start, source, bit, rows):
         copy = self.wire.send(
@@ -1205,104 +1465,19 @@
     out[:, pl.ds(pl.multiple_of((1 - core) * units, units), units)] = far[...].astype(out.dtype)
 
 
-def collect_kernel(
-    parts,
-    planes,
-    t_first,
-    t_second,
-    query,
-    pair,
-    outer,
-    slope,
-    near,
-    far,
-    query_all,
-    pair_all,
-    outer_all,
-    slope_out,
-    slope_sums,
-    slope_landing,
-    *sems,
-):
-    here = Place(parts, planes)
-    wire = Wire(*sems)
-    here.enter(here.seat_bits, plane_masks=here.plane_bits)
-    shard, rows_out = query.shape[0], outer.shape[0]
-    chips = parts // 2
-
-    bits = [("seq", bit) for bit in here.seat_bits] + [("fsdp", bit) for bit in here.plane_bits]
-    slope_copies = []
-
-    def slope_send(number):
-        axis, bit = bits[number]
-        index = here.at(bit) if axis == "seq" else flip(here.plane, bit, here.plane_bits)
-        source = slope if number == 0 else slope_sums.at[number - 1]
-        slope_copies.append(wire.send(source, slope_landing.at[number], {axis: index}))
-
-    def slope_add(number):
-        slope_copies[number].wait_recv()
-        source = slope if number == 0 else slope_sums.at[number - 1]
-        target = slope_out if number == len(bits) - 1 else slope_sums.at[number]
-        target[...] = source[...] + slope_landing[number]
-
-    def row_gather(source, target):
-        return PlaneGather(wire, here, source, target)
-
-    slope_send(0)
-    half, half_out = shard // 2, rows_out // 2
-    columns = query.shape[1]
-    own_start = (here.core * chips + here.chip) * rows_out
-    gathers = [
-        row_gather(
-            lambda color: query.at[pl.ds(color * half, half)],
-            lambda seat, color: query_all.at[
-                pl.ds(color * half, half), pl.ds(pl.multiple_of(seat * columns, columns), columns)
-            ],
-        ),
-        row_gather(
-            lambda color: pair.at[pl.ds(color * half, half)],
-            lambda seat, color: pair_all.at[seat, pl.ds(color * half, half)],
-        ),
-        row_gather(
-            lambda color: outer.at[pl.ds(color * half_out, half_out)],
-            lambda seat, color: outer_all.at[
-                pl.ds(
-                    pl.multiple_of(
-                        ((seat % 2) * chips + seat // 2) * rows_out + color * half_out, half_out
-                    ),
-                    half_out,
-                )
-            ],
-        ),
-    ]
-    for gather in gathers:
-        gather.start()
-    weight = WeightGather(wire, here, (t_first.at[1], t_second.at[1]), near, far)
-    own = [
-        wire.local(query, query_all.at[:, pl.ds(pl.multiple_of(here.seat * columns, columns), columns)]),
-        wire.local(pair, pair_all.at[here.seat]),
-        wire.local(outer, outer_all.at[pl.ds(pl.multiple_of(own_start, rows_out), rows_out)]),
-    ]
-    slope_add(0)
-    slope_send(1)
-    for gather in gathers:
-        gather.hop(1)
-    weight.start()
-    weight.own()
-    for number in range(1, len(bits)):
-        slope_add(number)
-        if number + 1 < len(bits):
-            slope_send(number + 1)
-        if number == 2:
-            for gather in gathers:
-                gather.hops(2)
-    weight.forward()
-    for gather in gathers:
-        gather.finish()
-    weight.finish()
-    for copy in own:
-        copy.wait()
-    wire.close()
+def widen_pieces_kernel(count, steps, starts, *refs):
+    nears, fars, out = refs[:count], refs[count : 2 * count], refs[2 * count]
+    core = lax.axis_index("seq") % 2
+    units = nears[0].shape[1]
+    index = pl.program_id(0)
+    for number in range(count):
+
+        @pl.when(index // steps == number)
+        def _(near=nears[number], far=fars[number]):
+            own = pl.ds(pl.multiple_of(core * units, units), units)
+            other = pl.ds(pl.multiple_of((1 - core) * units, units), units)
+            out[:, own] = near[...].astype(out.dtype)
+            out[:, other] = far[...].astype(out.dtype)
 
 
 SENDS, LOCALS = 128, 96
@@ -1342,6 +1517,36 @@
             flops=0, transcendentals=0, bytes_accessed=12 * rows * units
         ),
     )(near, far)
+
+
+def widen_pieces(pieces, fars):
+    rows, units = fars[0].shape
+    count = len(fars)
+    step = min(256, rows)
+    steps = rows // step
+    starts = jnp.stack([jnp.asarray(start, jnp.int32) // step for start, _ in pieces])
+
+    def block(number):
+        return pl.BlockSpec(
+            (step, units),
+            lambda index, starts: (jnp.clip(index - number * steps, 0, steps - 1), 0),
+        )
+
+    return pl.pallas_call(
+        functools.partial(widen_pieces_kernel, count, steps),
+        out_shape=jax.ShapeDtypeStruct((count * rows, 2 * units), jnp.float32),
+        grid_spec=pltpu.PrefetchScalarGridSpec(
+            num_scalar_prefetch=1,
+            grid=(count * steps,),
+            in_specs=[block(number) for number in range(count)] * 2,
+            out_specs=pl.BlockSpec(
+                (step, 2 * units), lambda index, starts: (starts[index // steps] + index % steps, 0)
+            ),
+        ),
+        cost_estimate=pl.CostEstimate(
+            flops=0, transcendentals=0, bytes_accessed=12 * count * rows * units
+        ),
+    )(starts, *[value for _, value in pieces], *fars)
 
 
 VMEM_BYTES = 67_000_000
@@ -1401,25 +1606,42 @@
     source = rows_in.astype(f32)
     first = rms_factor(source)
     normed_in = (source * first * attention_gain).astype(bf16)
-    normed_all, head_full, out_slice = call(
-        head_weights_kernel,
+    cosine, sine = rope_tables(jnp.arange(length, dtype=jnp.int32), width)
+    lanes = jnp.arange(2 * width)
+    signed = jnp.where(lanes % width < width // 2, -1.0, 1.0) * jnp.concatenate([sine, sine], axis=1)
+    heads_of = jnp.arange(head_cols) // width
+    group = (heads_of[:, None] == heads_of[None, :]).astype(bf16)
+    gain_row = jnp.concatenate([jnp.tile(query_gain, local_groups), key_gain, key_gain])[None, :]
+    log_rows_count = -(-local_groups // 8) * 8
+    normed_all, head_full, out_slice, proj, queries, pair_rows, out_rows, log_rows = call(
+        functools.partial(front_kernel, width),
         sizes,
         0,
-        (normed_in, head_weights, out_piece),
-        (True, True, True),
-        [((length, model), bf16), ((model, head_cols), bf16), ((query_cols, model), bf16)],
-        [((planes, piece_rows, model), bf16)],
-    )
-
-    proj = matmul(normed_all, head_full)
+        (
+            normed_in,
+            head_weights,
+            out_piece,
+            gain_row,
+            jnp.concatenate([cosine, cosine], axis=1),
+            signed,
+            group,
+        ),
+        (True,) * 7,
+        [
+            ((length, model), bf16),
+            ((model, head_cols), bf16),
+            ((query_cols, model), bf16),
+            ((length, head_cols), f32),
+            ((length, query_cols), bf16),
+            ((length, 2 * width), bf16),
+            ((length, query_cols), bf16),
+            ((log_rows_count, length), f32),
+        ],
+        [((planes, piece_rows, model), bf16)] + [((length, 2 * width), bf16)] * 3,
+    )
     query_proj = proj[:, :query_cols]
     key_proj = proj[:, query_cols : query_cols + width]
-    values = proj[:, query_cols + width :].astype(bf16)
-    cosine, sine = rope_tables(jnp.arange(length, dtype=jnp.int32), width)
-    queries = prepare(query_proj, query_gain, cosine, sine).astype(bf16)
-    keys = prepare(key_proj, key_gain, cosine, sine).astype(bf16)
-    pair_rows = jnp.concatenate([keys, values], axis=1)
-    out_rows, log_rows = attend_heads(queries, pair_rows, local_groups, width)
+    log_rows = log_rows[:local_groups][None]
 
     half = model // 2
     scatter_scratch = [
@@ -1448,16 +1670,15 @@
         ((2, planes - 1, tokens, model), bf16),
     ]
     acts = (2 * planes * tokens, units)
-    s_down, s_first, s_second, mid_grad, down_give, down_keep = call(
+    s_down, s_gate_a, s_gate_b, s_up_a, s_up_b, mid_grad, down_give, down_keep = call(
         feed_kernel,
         sizes,
         2,
         (normed_mid, cot_all.reshape(-1, model), gate_weight, up_weight, down_weight),
         (True, True, False, False, False),
-        [
-            ((2, last_rows, units), bf16),
-            ((2, last_rows, units), bf16),
-            ((2, last_rows, units), bf16),
+        [((2, last_rows, units), bf16)]
+        + [((last_rows, units), bf16)] * 4
+        + [
             ((tokens, model), f32),
             (rows_shape, bf16),
             (rows_shape, bf16),
@@ -1469,7 +1690,7 @@
         + [((3, 2, quarter >> stage, units), bf16) for stage in range(halvings)]
         + [(rows_shape, bf16)]
         + line_scratch,
-        [True] * 4 + [False] * 2,
+        [True] * 6 + [False] * 2,
     )
 
     feedforward_slope = jnp.sum(mid_grad * middle * second, axis=0)
@@ -1486,13 +1707,12 @@
     )
     block_rows = middle + down_sum
 
-    def trade(value, bit):
-        other = lax.ppermute(value, "seq", [(i, i ^ bit) for i in range(parts)])
-        return (value.astype(f32) + other.astype(f32)).astype(bf16)
-
-    s_first, s_second, middle_all = lax.optimization_barrier((s_first, s_second, middle_all))
-    t_first = trade(s_first, parts // 2)
-    t_second = trade(s_second, 2)
+    def swap(value, bit):
+        return lax.ppermute(value, "seq", [(i, i ^ bit) for i in range(parts)])
+
+    *sent, middle_all = lax.optimization_barrier((s_gate_a, s_gate_b, s_up_a, s_up_b, middle_all))
+    bit_orders = ([2 << i for i in range(halvings + 1)], [chips >> i for i in range(halvings + 1)])
+    came = [swap(piece, bit_orders[number % 2][-1]) for number, piece in enumerate(sent)]
 
     attended_grad = inner_cols(middle_all, out_slice).astype(bf16)
     query_back, pair_back = attend_back(
@@ -1512,69 +1732,86 @@
     head_part = inner_rows(normed_all, halves).astype(bf16).reshape(planes, shard, head_cols)
     out_part = inner_rows(out_rows, middle_all).astype(bf16)
 
+    gains = jnp.concatenate([query_slope, key_slope])
+    gains = jnp.pad(gains, (0, model - gains.shape[0]))
+    slopes = jnp.stack([feedforward_slope, gains])
+    slopes = jnp.pad(slopes, ((1, 5), (0, 0)))
+    rounds = (parts * planes).bit_length() - 1
     side = ((model, units), bf16)
-    in_grad, head_sum, outer_sum, near_down, far_down, near_gate, far_gate = call(
-        in_rows_kernel,
+    piece = ((last_rows, units), bf16)
+    in_grad, near_down, far_down, query_all, pair_all, outer_all, slopes, *pieces = call(
+        final_kernel,
         sizes,
         5,
-        (halves, head_full, head_part, out_part, t_down, t_first, t_second),
-        (True, True, False, False, True, True, True),
-        [((tokens, model), f32), ((shard, head_cols), bf16), ((piece_rows, model), bf16)]
-        + [side] * 4,
+        (halves, head_full, head_part, out_part, t_down, rows_in, first, slopes, *sent, *came),
+        (True, True, False, False, True, True, True, True) + (False,) * 8,
+        [
+            ((tokens, model), f32),
+            side,
+            side,
+            ((shard, model), bf16),
+            ((parts, shard, 2 * width), bf16),
+            ((shard, model), bf16),
+            ((8, model), f32),
+        ]
+        + [piece] * 4,
         scatter_scratch
         + [
             ((planes, shard, head_cols), bf16),
             ((2, planes - 1, shard, head_cols), bf16),
             ((planes, piece_rows, model), bf16),
             ((2, planes - 1, piece_rows, model), bf16),
+            ((shard, head_cols), bf16),
+            ((piece_rows, model), bf16),
+            ((4, last_rows, units), bf16),
+            ((4, last_rows, units), bf16),
+            ((rounds, 8, model), f32),
+            ((rounds, 8, model), f32),
         ],
-        [True] * 3 + [False] * 4,
-    )
-    attention_slope = jnp.sum(in_grad * source * first, axis=0)
+        [True, False, False] + [True] * 4 + [False] * 4,
+    )
+    pieces, near_down, far_down, in_grad = lax.optimization_barrier(
+        (pieces, near_down, far_down, in_grad)
+    )
     input_rows = (middle_grad + norm_back(in_grad, source, first, attention_gain)).astype(bf16)
 
-    slopes = jnp.concatenate([attention_slope, feedforward_slope, query_slope, key_slope])
-    slope_cols = -(-slopes.shape[0] // 1024) * 128
-    slopes = jnp.pad(slopes, (0, 8 * slope_cols - slopes.shape[0])).reshape(8, slope_cols)
-    rounds = (parts * planes).bit_length() - 1
-    near_up, far_up, query_all, pair_all, outer_all, slopes = call(
-        collect_kernel,
-        sizes,
-        6,
-        (
-            t_first,
-            t_second,
-            head_sum[:, :query_cols],
-            head_sum[:, query_cols:],
-            outer_sum,
-            slopes,
-        ),
-        (True, True, True, True, True, True),
-        [
-            side,
-            side,
-            ((shard, model), bf16),
-            ((parts, shard, 2 * width), bf16),
-            ((shard, model), bf16),
-            ((8, slope_cols), f32),
-        ],
-        [((rounds, 8, slope_cols), f32), ((rounds, 8, slope_cols), f32)],
-        [False, False, True, True, True, True],
-    )
+    def plane_pieces(values):
+        whole = []
+        for color, order in enumerate(bit_orders):
+            start, rows = color * (model // 2), model // 2
+            for bit in order[:-1]:
+                rows //= 2
+                start = start + (place // bit) % 2 * rows
+            held = [(start, values[color])]
+            rows = last_rows
+            for bit in order[-2::-1]:
+                held = held + [
+                    (start + rows - 2 * rows * ((place // bit) % 2), swap(value, bit))
+                    for start, value in held
+                ]
+                rows *= 2
+            whole = whole + held
+        return whole
+
+    gate_pieces = plane_pieces(pieces[:2])
     grad_down = widen(near_down, far_down)
-    grad_gate = widen(near_gate, far_gate)
-    grad_up = widen(near_up, far_up)
     grad_query = query_all.astype(f32)
     grad_pair = pair_all.astype(f32)
     grad_pair = grad_pair.reshape(parts // copies, copies, shard, 2, width).sum(axis=1)
     grad_key = grad_pair[:, :, 0].transpose(1, 0, 2).reshape(shard, -1)
     grad_value = grad_pair[:, :, 1].transpose(1, 0, 2).reshape(shard, -1)
     grad_output = outer_all.astype(f32)
-    slopes = slopes.reshape(-1)
-    attention_slope = slopes[:model]
-    feedforward_slope = slopes[model : 2 * model]
-    query_slope = slopes[2 * model : 2 * model + width]
-    key_slope = slopes[2 * model + width : 2 * model + 2 * width]
+    pieces[2:], gate_pieces, grad_down, grad_query, grad_output, input_rows = (
+        lax.optimization_barrier(
+            (pieces[2:], gate_pieces, grad_down, grad_query, grad_output, input_rows)
+        )
+    )
+    up_pieces = plane_pieces(pieces[2:])
+    grad_gate = widen_pieces(gate_pieces, [swap(value, 1) for _, value in gate_pieces])
+    up_pieces, grad_gate = lax.optimization_barrier((up_pieces, grad_gate))
+    grad_up = widen_pieces(up_pieces, [swap(value, 1) for _, value in up_pieces])
+    attention_slope, feedforward_slope = slopes[0], slopes[1]
+    query_slope, key_slope = slopes[2, :width], slopes[2, width : 2 * width]
     block_out = block_rows.astype(bf16).reshape(1, tokens, model)
     input_grad = input_rows.reshape(1, tokens, model)
     return (

time: 615 us -> 562 us (0.914)
  Pallas kernels: 471 us -> 416 us
  matrix products: 47.4 us -> 30.6 us
  waiting for transfers between devices: 0.01 us -> 14.3 us
  starting transfers between devices: 2.09 us -> 9.84 us
    pallas_call x6 -> x5, Pallas kernels: 440 us -> 382 us  [call(): pl.pallas_call(functools.partial(kernel, *mesh_sizes), out_shape=[jax.Sha...]
    pallas_call x0 -> x2, Pallas kernels: none -> 24.1 us  [widen_pieces(): pl.pallas_call(functools.partial(widen_pieces_kernel, count, steps), out_...]
    pallas_call x3 -> x1, Pallas kernels: 30.9 us -> 10.5 us  [widen(): pl.pallas_call(widen_kernel, grid=(rows // step,), out_shape=jax.ShapeDty...]
    ppermute x2 -> x16, waiting for transfers between devices: 0.01 us -> 14.3 us  [swap(): return lax.ppermute(value, 'seq', [(i, i ^ bit) for i in range(parts)])]
    dot_general x4 -> x0, matrix products: 9.96 us -> none  [the longest x3 5.45 us: key_step(): jnp.einsum('hgqs,shd->hgqd', weights.astype(jnp.bfloat16), value_block, p...]
    dot_general x6 -> x3, matrix products: 11 us -> 2.19 us  [key_step(): jnp.einsum('qhgd,shd->hgqs', query_block, key_block, preferred_element_ty...]
    ppermute x2 -> x16, starting transfers between devices: 2.09 us -> 9.84 us  [swap(): return lax.ppermute(value, 'seq', [(i, i ^ bit) for i in range(parts)])]
    convert_element_type x5 -> x2, other arithmetic: 11.2 us -> 3.91 us  [the longest x1 3.08 us: per_device(): (middle_grad + norm_back(in_grad, source, first, attention_gain)).astype(...]
  transfers between devices with their start and end apart: 2 -> 16, of which waited for: 0 -> 7; matrix products, arithmetic and copies ran while one was open for 8% -> 16% of each run, Pallas kernels for 0% -> 4%
where the time goes in v5:
time: 562 us; the launch traced here: 556 us
  Pallas kernels  416 us (74%)
  other arithmetic  48 us (9%)
  local copies, waits for them, and re-layouts  34.9 us (6%)
  matrix products  30.6 us (5%)
  waiting for transfers between devices  14.3 us (3%)
  starting transfers between devices  9.84 us (2%)
    pallas_call x5, Pallas kernels, call(): pl.pallas_call(functools.partial(kernel, *mesh_sizes), out_shape=[jax.Sha...  382 us
    pallas_call x2, Pallas kernels, widen_pieces(): pl.pallas_call(functools.partial(widen_pieces_kernel, count, steps), out_...  24.1 us
    ppermute x16, waiting for transfers between devices, swap(): return lax.ppermute(value, 'seq', [(i, i ^ bit) for i in range(parts)])  14.3 us
  transfers between devices with their start and end apart: 16, of which 7 were waited for; matrix products, arithmetic and copies ran while one was open for 16% of the time, Pallas kernels for 4%

profile of v5, /device:TPU:0, one launch (start us, length us, event | category | flops | bytes accessed | tf_op | source)
XLA Modules:
  0.0 555.7 jit_solution(2717834971968060817)
XLA Ops:
  0.7 1.0 fusion.75
  1.7 2.2 fusion.72
  4.0 1.6 fusion.65
  9.0 1.7 constant_dynamic-slice_fusion.3.o
  12.7 1.1 constant_dynamic-slice_fusion.4
  14.7 1.3 pad_maximum_fusion.2
  16.0 62.3 %shard_map.228 = (bf16[1024,2048]{1,0:T(8,128)(2,1)}, bf16[2048,384]{1,0:T(8,128)(2,1)}, bf16[256,2048]{1,0:T(8,128)(2,1)}, f32[1024,384]{1,0:T(8,128)}, bf16[10...) custom-call(bf16[128,2048]{1,0:T(8,128)(2,1)} %fusion.58.x, ...), custom_call_target="tpu_custom_call" | custom-call | tf_op jit(solution)/shard_map/pallas_call | solution.py:1495
  78.3 43.9 %shard_map.229 = (f32[128,2048]{1,0:T(8,128)}, bf16[4,2,128,2048]{3,2,1,0:T(8,128)(2,1)}) custom-call(bf16[1024,256]{1,0:T(8,128)(2,1)} %get-tuple-element.430.a, bf16[256,2048]{1,0:T(8,128)(2,1)} %get-tuple-element.431.w, bf16[128,2048]{1,0:T(8,128)(2,1)} %bitcast.246), custom_call_target="tpu_custom_call" | custom-call | tf_op jit(solution)/shard_map/pallas_call | solution.py:1495
  122.2 1.6 multiply_reduce_fusion.6
  125.7 126.5 %shard_map.230 = (bf16[2,512,1024]{2,1,0:T(8,128)(2,1)}, bf16[512,1024]{1,0:T(8,128)(2,1)}, bf16[512,1024]{1,0:T(8,128)(2,1)}, bf16[512,1024]{1,0:T(8,128)(2,1)}...) custom-call(bf16[128,2048]{1,0:T(8,128)(2,1)} %multiply_convert_fusi, ...), custom_call_target="tpu_custom_call" | custom-call | tf_op jit(solution)/shard_map/pallas_call | solution.py:1495
  252.2 2.4 multiply_reduce_fusion.1
  254.6 2.8 fusion.83.h
  257.4 52.7 %shard_map.231 = (bf16[1024,2048]{1,0:T(8,128)(2,1)}, bf16[2,512,1024]{2,1,0:T(8,128)(2,1)}, f32[128,2048]{1,0:T(8,128)}) custom-call(bf16[128,2048]{1,0:T(8,128)(2,1)} %fusion.83.h, bf16[2,512,1024]{2,1,0:T(8,128)(2,1)} %get-tuple-element.435.s, bf16[4,128,2048]{2,1,0:T(8,128)(2,1)} %get-tuple-element.436.give, bf16[4,128,2048]{2,1,0:T(8,128)(2,1)} %get-tuple-element.437.keep), custom_call_target="tpu_custom_call" | custom-call | tf_op jit(solution)/shard_map/pallas_call | solution.py:1495
  310.2 2.0 collective-permute-start
  312.2 1.9 collective-permute-start.2
  314.3 1.2 copy.49
  315.5 1.9 copy.52
  317.5 1.9 copy.53
  319.4 2.3 slice.36
  321.6 1.9 multiply_reduce_fusion.7
  323.5 3.5 convolution_convert_fusion.2
  330.6 24.0 %while.55 = (s32[]{:T(128)}, f32[1024,1,4,64]{0,3,2,1:T(8,128)S(1)}, f32[1024,1,64]{0,2,1:T(8,128)S(1)}, f32[1024,1,64]{0,2,1:T(8,128)}, bf16[1024,1,4,64]{0,3,2...) while((s32[]{:T(128)}, ...), condition=%wide.region_7.8_spmd.clone.clone, body=%wide.region_4.7_spmd.clone.clone.sunk | while | flops 683082752 | bytes 25727648 | solution.py:206
  331.4 1.3 dynamic-slice_bitcast_fusion.2
  332.7 6.6 %while.56 = (s32[]{:T(128)}, f32[512,1,4,64]{0,3,2,1:T(8,128)S(1)}, f32[1024,1,64]{0,2,1:T(8,128)S(1)}, f32[1024,1,64]{0,2,1:T(8,128)}, s32[]{:T(128)}, /*index=...) while((s32[]{:T(128)}, f32[512,1,4,64]{0,3,2,1:T(8,128)S(1)}, ...), condition=%wide.region_6.6_spmd.clone, body=%wide.region_5.5_spmd.clone.sunk | while | flops 683082752 | bytes 23071008 | solution.py:197
  333.7 1.7 fusion.121
  336.7 2.6 fusion.124
  340.1 1.3 dynamic-slice_bitcast_fusion.2
  341.5 13.1 %while.56 = (s32[]{:T(128)}, f32[512,1,4,64]{0,3,2,1:T(8,128)S(1)}, f32[1024,1,64]{0,2,1:T(8,128)S(1)}, f32[1024,1,64]{0,2,1:T(8,128)}, s32[]{:T(128)}, /*index=...) while((s32[]{:T(128)}, f32[512,1,4,64]{0,3,2,1:T(8,128)S(1)}, ...), condition=%wide.region_6.6_spmd.clone, body=%wide.region_5.5_spmd.clone.sunk | while | flops 683082752 | bytes 23071008 | solution.py:197
  342.5 1.7 fusion.121
  345.4 2.6 fusion.124
  349.0 1.7 fusion.121
  351.9 2.6 fusion.124
  354.6 1.1 bitcast_multiply_fusion.1
  355.7 1.0 fusion.86
  356.8 1.6 copy.54
  358.7 1.9 sine_multiply_fusion
  360.6 1.1 fusion.87
  361.8 1.8 multiply_reduce_fusion
  363.6 1.1 fusion.64
  364.7 1.3 copy.58
  366.0 3.8 fusion.70
  369.9 1.1 copy.57
  372.5 1.4 fusion.74
  374.1 4.8 convolution_convert_fusion.1.out_part
  378.9 3.6 convolution_convert_fusion
  382.5 96.3 %shard_map.232 = (f32[128,2048]{1,0:T(8,128)}, bf16[2048,1024]{1,0:T(8,128)(2,1)}, bf16[2048,1024]{1,0:T(8,128)(2,1)}, bf16[512,2048]{1,0:T(8,128)(2,1)}, bf16[8...) custom-call(bf16[1024,384]{1,0:T(8,128)(2,1)} %copy-done.9, ...), custom_call_target="tpu_custom_call" | custom-call | tf_op jit(solution)/shard_map/pallas_call | solution.py:1495
  478.8 1.3 collective-permute-start.4
  480.9 4.1 convert_element_type.121
  485.1 2.5 convert_element_type.122
  487.7 10.5 %shard_map.233 = f32[2048,2048]{1,0:T(8,128)} custom-call(bf16[2048,1024]{1,0:T(8,128)(2,1)} %get-tuple-element.470.near, bf16[2048,1024]{1,0:T(8,128)(2,1)} %get-tuple-element.471.far), custom_call_target="tpu_custom_call" | custom-call | bytes 25165824 | tf_op jit(solution)/shard_map/pallas_call | solution.py:1510
  498.2 1.5 fusion.66
  499.8 3.1 fusion.63
  502.9 1.9 collective-permute-done.4.refs_1_
  509.2 1.5 copy.60
  511.5 1.5 collective-permute-done.9.refs_5_
  513.0 12.0 %shard_map.234 = f32[2048,2048]{1,0:T(8,128)} custom-call(s32[4]{0:T(128)} %pad_add_fusion.starts, bf16[512,1024]{1,0:T(8,128)(2,1)} %get-tuple-element.486.refs_0_, bf16[512,1024]{1,0:T(8,128)(2,1)} %collective-permute-done.4.refs_1_, bf16[512,1024]{1,0:T(8,128)(2,1)} %get-tuple-element.488.refs_2_, bf16[512,1024]{1,0:T(8,128)(2,1)} %collective-permute-done.5.refs_3_, ...), custom_call_target="tpu_custom_call" | custom-call | bytes 25165824 | tf_op jit(solution)/shard_map/pallas_call | solution.py:1535
  525.1 7.1 %collective-permute-done.6.refs_1_ = bf16[512,1024]{1,0:T(8,128)(2,1)} collective-permute-done((bf16[512,1024]{1,0:T(8,128)(2,1)}, bf16[512,1024]{1,0:T(8,128)(2,1)}, u32[]{:S(2)}, u32[]{:S(2)}) %collective-permute-start.6) | collective-permute-done | bytes 1048608 | tf_op jit(solution)/shard_map/ppermute | solution.py:1711
  532.2 1.8 collective-permute-done.7.refs_3_
  534.9 1.2 fusion.85
  536.2 2.5 copy.61
  538.7 1.3 copy.62
  540.0 1.3 slice_bitcast_fusion.3
  541.4 1.5 fusion.88
  543.5 12.0 %shard_map.235 = f32[2048,2048]{1,0:T(8,128)} custom-call(s32[4]{0:T(128)} %pad_add_fusion.1.starts, bf16[512,1024]{1,0:T(8,128)(2,1)} %get-tuple-element.495.refs_0_, bf16[512,1024]{1,0:T(8,128)(2,1)} %collective-permute-done.6.refs_1_, bf16[512,1024]{1,0:T(8,128)(2,1)} %get-tuple-element.497.refs_2_, bf16[512,1024]{1,0:T(8,128)(2,1)} %collective-permute-done.7.refs_3_, ...), custom_call_target="tpu_custom_call" | custom-call | bytes 25165824 | tf_op jit(solution)/shard_map/pallas_call | solution.py:1535
  (168 shorter events, 30.0 us)
Async XLA Ops:
  0.6 11.0 %copy-start.2 = (bf16[1,128,2048]{2,1,0:T(8,128)(2,1)S(1)}, bf16[1,128,2048]{2,1,0:T(8,128)(2,1)}, u32[]{:S(2)}) copy-start(bf16[1,128,2048]{2,1,0:T(8,128)(2,1)} %param.17) | copy-start | bytes 1572868
  0.7 11.0 %copy-start.21 = (f32[2048]{0:T(1024)S(1)}, f32[2048]{0:T(1024)}, u32[]{:S(2)}) copy-start(f32[2048]{0:T(1024)} %param.19) | copy-start | bytes 24580
  3.9 10.7 %copy-start.5 = (f32[1024,64]{1,0:T(8,128)}, f32[1024,64]{1,0:T(8,128)S(1)}, u32[]{:S(2)}) copy-start(f32[1024,64]{1,0:T(8,128)S(1)} %get-tuple-element.687) | copy-start | bytes 786436
  3.9 12.0 %copy-start.6 = (f32[1024,64]{1,0:T(8,128)}, f32[1024,64]{1,0:T(8,128)S(1)}, u32[]{:S(2)}) copy-start(f32[1024,64]{1,0:T(8,128)S(1)} %get-tuple-element.686) | copy-start | bytes 786436
  6.1 9.9 %copy-start.30 = (f32[128]{0:T(128)}, f32[128]{0:T(128)S(1)}, u32[]{:S(2)}) copy-start(f32[128]{0:T(128)S(1)} %get-tuple-element.697) | copy-start | bytes 1540
  14.7 110.1 %copy-start.18 = (f32[2048]{0:T(1024)S(1)}, f32[2048]{0:T(1024)}, u32[]{:S(2)}) copy-start(f32[2048]{0:T(1024)} %param.26) | copy-start | bytes 24580
  123.7 1.0 copy-start
  123.8 130.9 %copy-start.26 = (f32[128]{0:T(128)}, f32[128]{0:T(128)S(1)}, u32[]{:S(2)}) copy-start(f32[128]{0:T(128)S(1)} %add_rsqrt_fusion) | copy-start | bytes 1540
  254.6 2.8 copy-start.32
  310.1 13.4 %copy-start.14 = (bf16[256,2048]{1,0:T(8,128)(2,1)S(1)}, bf16[256,2048]{1,0:T(8,128)(2,1)}, u32[]{:S(2)}) copy-start(bf16[256,2048]{1,0:T(8,128)(2,1)} %get-tuple-element.431.w) | copy-start | bytes 3145732
  310.2 72.3 %collective-permute-start = (bf16[512,1024]{1,0:T(8,128)(2,1)}, bf16[512,1024]{1,0:T(8,128)(2,1)}, u32[]{:S(2)}, u32[]{:S(2)}) collective-permute-start(bf16[512,1024]{1,0:T(8,128)(2,1)} %get-tuple-element.455.rest_0_), channel_id=1, source_target_pairs={{0,16},{4,20},{8,24},{12,28},{16,0},{20,4},{24,8},{28,12},{1,17},{... | collective-permute-start | bytes 3145736 | tf_op jit(solution)/shard_map/ppermute | solution.py:1711
  312.1 70.4 %collective-permute-start.1 = (bf16[512,1024]{1,0:T(8,128)(2,1)}, bf16[512,1024]{1,0:T(8,128)(2,1)}, u32[]{:S(2)}, u32[]{:S(2)}) collective-permute-start(bf16[512,1024]{1,0:T(8,128)(2,1)} %get-tuple-element.456.rest_1_), channel_id=1, source_target_pairs={{0,8},{4,12},{8,0},{12,4},{16,24},{20,28},{24,16},{28,20},{1,9},{5... | collective-permute-start | bytes 3145736 | tf_op jit(solution)/shard_map/ppermute | solution.py:1711
  312.2 70.2 %collective-permute-start.2 = (bf16[512,1024]{1,0:T(8,128)(2,1)}, bf16[512,1024]{1,0:T(8,128)(2,1)}, u32[]{:S(2)}, u32[]{:S(2)}) collective-permute-start(bf16[512,1024]{1,0:T(8,128)(2,1)} %get-tuple-element.457.rest_2_), channel_id=1, source_target_pairs={{0,16},{4,20},{8,24},{12,28},{16,0},{20,4},{24,8},{28,12},{1,17},{... | collective-permute-start | bytes 3145736 | tf_op jit(solution)/shard_map/ppermute | solution.py:1711
  314.1 68.4 %collective-permute-start.3 = (bf16[512,1024]{1,0:T(8,128)(2,1)}, bf16[512,1024]{1,0:T(8,128)(2,1)}, u32[]{:S(2)}, u32[]{:S(2)}) collective-permute-start(bf16[512,1024]{1,0:T(8,128)(2,1)} %get-tuple-element.458.rest_3_), channel_id=1, source_target_pairs={{0,8},{4,12},{8,0},{12,4},{16,24},{20,28},{24,16},{28,20},{1,9},{5... | collective-permute-start | bytes 3145736 | tf_op jit(solution)/shard_map/ppermute | solution.py:1711
  321.6 5.4 copy-start.15
  323.5 4.6 copy-start.16
  323.5 4.8 copy-start.25
  332.7 1.0 copy-start.17
  332.8 1.0 copy-start.20
  341.5 1.0 copy-start.17
  341.5 1.0 copy-start.20
  348.0 1.0 copy-start.17
  348.0 1.0 copy-start.20
  354.6 4.1 copy-start.8
  356.8 5.0 copy-start.23
  356.8 5.0 copy-start.28
  361.8 4.3 copy-start.29
  363.6 7.4 %copy-start.34 = (f32[128,1]{0,1:T(1,128)S(1)}, f32[128,1]{0,1:T(1,128)}, u32[]{:S(2)}) copy-start(f32[128,1]{0,1:T(1,128)} %get-tuple-element.696) | copy-start | bytes 1540
  363.6 8.2 %copy-start.24 = (f32[2048]{0:T(1024)S(1)}, f32[2048]{0:T(1024)}, u32[]{:S(2)}) copy-start(f32[2048]{0:T(1024)} %get-tuple-element.618) | copy-start | bytes 24580
  364.7 9.3 %copy-start.11 = (bf16[1024,256]{1,0:T(8,128)(2,1)S(1)}, bf16[1024,256]{1,0:T(8,128)(2,1)}, u32[]{:S(2)}) copy-start(bf16[1024,256]{1,0:T(8,128)(2,1)} %get-tuple-element.430.a) | copy-start | bytes 1572868
  373.9 5.0 copy-start.35
  374.1 8.4 %copy-start.9 = (bf16[1024,384]{1,0:T(8,128)(2,1)}, bf16[1024,384]{1,0:T(8,128)(2,1)S(1)}, u32[]{:S(2)}) copy-start(bf16[1024,384]{1,0:T(8,128)(2,1)S(1)} %pad_maximum_fusion.a) | copy-start | bytes 2359300
  478.8 6.2 %copy-start.10 = (bf16[512,2048]{1,0:T(8,128)(2,1)S(1)}, bf16[512,2048]{1,0:T(8,128)(2,1)}, u32[]{:S(2)}) copy-start(bf16[512,2048]{1,0:T(8,128)(2,1)} %get-tuple-element.473) | copy-start | bytes 6291460
  478.8 25.9 %collective-permute-start.4 = (bf16[512,1024]{1,0:T(8,128)(2,1)}, bf16[512,1024]{1,0:T(8,128)(2,1)}, u32[]{:S(2)}, u32[]{:S(2)}) collective-permute-start(bf16[512,1024]{1,0:T(8,128)(2,1)} %get-tuple-element.486.refs_0_), channel_id=1, source_target_pairs={{0,8},{4,12},{8,0},{12,4},{16,24},{20,28},{24,16},{28,20},{1,9},{5... | collective-permute-start | bytes 3145736 | tf_op jit(solution)/shard_map/ppermute | solution.py:1711
  480.1 25.6 %collective-permute-start.5 = (bf16[512,1024]{1,0:T(8,128)(2,1)}, bf16[512,1024]{1,0:T(8,128)(2,1)}, u32[]{:S(2)}, u32[]{:S(2)}) collective-permute-start(bf16[512,1024]{1,0:T(8,128)(2,1)} %get-tuple-element.488.refs_2_), channel_id=1, source_target_pairs={{0,16},{4,20},{8,24},{12,28},{16,0},{20,4},{24,8},{28,12},{1,17},{... | collective-permute-start | bytes 3145736 | tf_op jit(solution)/shard_map/ppermute | solution.py:1711
  487.6 10.5 %copy-start.3 = (bf16[1,128,2048]{2,1,0:T(8,128)(2,1)S(1)}, bf16[1,128,2048]{2,1,0:T(8,128)(2,1)}, u32[]{:S(2)}) copy-start(bf16[1,128,2048]{2,1,0:T(8,128)(2,1)} %param.17) | copy-start | bytes 1572868
  487.6 10.5 %copy-start.22 = (f32[2048]{0:T(1024)S(1)}, f32[2048]{0:T(1024)}, u32[]{:S(2)}) copy-start(f32[2048]{0:T(1024)} %param.19) | copy-start | bytes 24580
  487.6 12.1 %copy-start.1 = (f32[128,2048]{1,0:T(8,128)S(1)}, f32[128,2048]{1,0:T(8,128)}, u32[]{:S(2)}) copy-start(f32[128,2048]{1,0:T(8,128)} %copy-done) | copy-start | bytes 3145732
  487.6 12.1 %copy-start.4 = (f32[128,2048]{1,0:T(8,128)S(1)}, f32[128,2048]{1,0:T(8,128)}, u32[]{:S(2)}) copy-start(f32[128,2048]{1,0:T(8,128)} %get-tuple-element.434) | copy-start | bytes 3145732
  487.6 12.1 %copy-start.7 = (bf16[1,128,2048]{2,1,0:T(8,128)(2,1)S(1)}, bf16[1,128,2048]{2,1,0:T(8,128)(2,1)}, u32[]{:S(2)}) copy-start(bf16[1,128,2048]{2,1,0:T(8,128)(2,1)} %param.18) | copy-start | bytes 1572868
  487.6 12.1 %copy-start.19 = (f32[2048]{0:T(1024)S(1)}, f32[2048]{0:T(1024)}, u32[]{:S(2)}) copy-start(f32[2048]{0:T(1024)} %param.26) | copy-start | bytes 24580
  487.6 12.1 %copy-start.27 = (f32[128]{0:T(128)S(1)}, f32[128]{0:T(128)}, u32[]{:S(2)}) copy-start(f32[128]{0:T(128)} %copy-done.26) | copy-start | bytes 1540
  487.7 12.1 %copy-start.31 = (f32[128]{0:T(128)S(1)}, f32[128]{0:T(128)}, u32[]{:S(2)}) copy-start(f32[128]{0:T(128)} %copy-done.30) | copy-start | bytes 1540
  487.7 12.1 %copy-start.33 = (f32[128]{0:T(128)S(1)}, f32[128]{0:T(128)}, u32[]{:S(2)}) copy-start(f32[128]{0:T(128)} %copy-done.32) | copy-start | bytes 1540
  498.2 7.6 %copy-start.12 = (bf16[512,1024]{1,0:T(8,128)(2,1)S(1)}, bf16[512,1024]{1,0:T(8,128)(2,1)}, u32[]{:S(2)}) copy-start(bf16[512,1024]{1,0:T(8,128)(2,1)} %get-tuple-element.488.refs_2_) | copy-start | bytes 3145732
  505.7 2.7 collective-permute-start.10
  505.7 5.6 %collective-permute-start.11 = (bf16[512,1024]{1,0:T(8,128)(2,1)}, bf16[512,1024]{1,0:T(8,128)(2,1)}, u32[]{:S(2)}, u32[]{:S(2)}) collective-permute-start(bf16[512,1024]{1,0:T(8,128)(2,1)} %collective-permute-done.5.refs_3_), channel_id=1, source_target_pairs={{0,4},{4,0},{8,12},{12,8},{16,20},{20,16},{24,28},{28,24},{1,5},{5... | collective-permute-start | bytes 3145736 | tf_op jit(solution)/shard_map/ppermute | solution.py:1711
  506.3 5.3 collective-permute-start.8
  506.3 6.8 %collective-permute-start.9 = (bf16[512,1024]{1,0:T(8,128)(2,1)}, bf16[512,1024]{1,0:T(8,128)(2,1)}, u32[]{:S(2)}, u32[]{:S(2)}) collective-permute-start(bf16[512,1024]{1,0:T(8,128)(2,1)} %collective-permute-done.4.refs_1_), channel_id=1, source_target_pairs={{0,4},{4,0},{8,12},{12,8},{16,20},{20,16},{24,28},{28,24},{1,5},{5... | collective-permute-start | bytes 3145736 | tf_op jit(solution)/shard_map/ppermute | solution.py:1711
  506.8 25.4 %collective-permute-start.6 = (bf16[512,1024]{1,0:T(8,128)(2,1)}, bf16[512,1024]{1,0:T(8,128)(2,1)}, u32[]{:S(2)}, u32[]{:S(2)}) collective-permute-start(bf16[512,1024]{1,0:T(8,128)(2,1)} %get-tuple-element.495.refs_0_), channel_id=1, source_target_pairs={{0,8},{4,12},{8,0},{12,4},{16,24},{20,28},{24,16},{28,20},{1,9},{5... | collective-permute-start | bytes 3145736 | tf_op jit(solution)/shard_map/ppermute | solution.py:1711
  508.4 4.6 copy-start.13
  508.4 25.5 %collective-permute-start.7 = (bf16[512,1024]{1,0:T(8,128)(2,1)}, bf16[512,1024]{1,0:T(8,128)(2,1)}, u32[]{:S(2)}, u32[]{:S(2)}) collective-permute-start(bf16[512,1024]{1,0:T(8,128)(2,1)} %get-tuple-element.497.refs_2_), channel_id=1, source_target_pairs={{0,16},{4,20},{8,24},{12,28},{16,0},{20,4},{24,8},{28,12},{1,17},{... | collective-permute-start | bytes 3145736 | tf_op jit(solution)/shard_map/ppermute | solution.py:1711
  533.9 9.5 %collective-permute-start.12 = (bf16[512,1024]{1,0:T(8,128)(2,1)}, bf16[512,1024]{1,0:T(8,128)(2,1)}, u32[]{:S(2)}, u32[]{:S(2)}) collective-permute-start(bf16[512,1024]{1,0:T(8,128)(2,1)} %get-tuple-element.495.refs_0_), channel_id=1, source_target_pairs={{0,4},{4,0},{8,12},{12,8},{16,20},{20,16},{24,28},{28,24},{1,5},{5... | collective-permute-start | bytes 3145736 | tf_op jit(solution)/shard_map/ppermute | solution.py:1711
  533.9 9.5 %collective-permute-start.13 = (bf16[512,1024]{1,0:T(8,128)(2,1)}, bf16[512,1024]{1,0:T(8,128)(2,1)}, u32[]{:S(2)}, u32[]{:S(2)}) collective-permute-start(bf16[512,1024]{1,0:T(8,128)(2,1)} %collective-permute-done.6.refs_1_), channel_id=1, source_target_pairs={{0,4},{4,0},{8,12},{12,8},{16,20},{20,16},{24,28},{28,24},{1,5},{5... | collective-permute-start | bytes 3145736 | tf_op jit(solution)/shard_map/ppermute | solution.py:1711
  534.4 9.0 %collective-permute-start.14 = (bf16[512,1024]{1,0:T(8,128)(2,1)}, bf16[512,1024]{1,0:T(8,128)(2,1)}, u32[]{:S(2)}, u32[]{:S(2)}) collective-permute-start(bf16[512,1024]{1,0:T(8,128)(2,1)} %get-tuple-element.497.refs_2_), channel_id=1, source_target_pairs={{0,4},{4,0},{8,12},{12,8},{16,20},{20,16},{24,28},{28,24},{1,5},{5... | collective-permute-start | bytes 3145736 | tf_op jit(solution)/shard_map/ppermute | solution.py:1711
  534.4 9.0 %collective-permute-start.15 = (bf16[512,1024]{1,0:T(8,128)(2,1)}, bf16[512,1024]{1,0:T(8,128)(2,1)}, u32[]{:S(2)}, u32[]{:S(2)}) collective-permute-start(bf16[512,1024]{1,0:T(8,128)(2,1)} %collective-permute-done.7.refs_3_), channel_id=1, source_target_pairs={{0,4},{4,0},{8,12},{12,8},{16,20},{20,16},{24,28},{28,24},{1,5},{5... | collective-permute-start | bytes 3145736 | tf_op jit(solution)/shard_map/ppermute | solution.py:1711

commit v6 on v5

--- a/solution.py
+++ b/solution.py
@@ -681,7 +681,169 @@
     table = jnp.ones((block, 128), jnp.float32)
     for number, total in enumerate(totals):
         table = jnp.where(lane == number, total, table)
-    logs[:, rows] = jnp.log(table).T[0 : logs.shape[0], :]
+    logs[rows, :] = jnp.log(table)
+
+
+def back_block(
+    index, block, width, heads, queries, grads, outs, logs, keys, values, query_back, key_back, value_back
+):
+    rows = pl.ds(index * block, block)
+    before = index * block
+    scale = width**-0.5
+    row = lax.broadcasted_iota(jnp.int32, (block, block), 0)
+    column = lax.broadcasted_iota(jnp.int32, (block, block), 1)
+    allowed = row >= column
+    across = (((1,), (1,)), ((), ()))
+    down = (((0,), (0,)), ((), ()))
+    f32 = jnp.float32
+    spans = [(rows, True)] + ([(slice(0, before), False)] if before else [])
+    for number in range(heads // 2):
+        at = pl.ds(number * 2 * width, 2 * width)
+        both, both_grad = queries[rows, at], grads[rows, at]
+        product = both_grad.astype(f32) * outs[rows, at].astype(f32)
+        zero = jnp.zeros_like(both)
+        total = None
+        for side in (0, 1):
+            pick = (
+                (lambda value, nothing: pick_lanes(value, nothing, width))
+                if side == 0
+                else (lambda value, nothing: pick_lanes(nothing, value, width))
+            )
+            query, grad = pick(both, zero), pick(both_grad, zero)
+            scaled = (query.astype(f32) * scale).astype(query.dtype)
+            shift = jnp.sum(pick(product, jnp.zeros_like(product)), axis=1, keepdims=True)
+            head = 2 * number + side
+            log = logs[rows, head : head + 1]
+            for span, masked in spans:
+                scores = lax.dot_general(
+                    scaled, keys[0][span, :], across, preferred_element_type=f32
+                )
+                weights = jnp.exp(scores - log)
+                if masked:
+                    weights = jnp.where(allowed, weights, 0.0)
+                prob_grad = lax.dot_general(
+                    grad, values[0][span, :], across, preferred_element_type=f32
+                )
+                score_grad = (weights * (prob_grad - shift) * scale).astype(query.dtype)
+                part = jnp.dot(score_grad, keys[1 + side][span, :], preferred_element_type=f32)
+                total = part if total is None else total + part
+                key_back[span, :] += lax.dot_general(
+                    score_grad, query, down, preferred_element_type=f32
+                )
+                value_back[span, :] += lax.dot_general(
+                    weights.astype(query.dtype), grad, down, preferred_element_type=f32
+                )
+        query_back[rows, at] = total
+
+
+def back_kernel(
+    width,
+    normed,
+    middle,
+    out_slice,
+    outs,
+    logs,
+    queries,
+    pair,
+    proj,
+    gain,
+    cosine,
+    sine,
+    group,
+    halves,
+    head_part,
+    out_part,
+    slopes,
+    grads,
+    query_back,
+    key_back,
+    value_back,
+    *twins,
+):
+    length = normed.shape[0]
+    block = min(256, length)
+    blocks = length // block
+    query_cols = queries.shape[1]
+    heads = query_cols // width
+    keys, values = twins[:3], twins[3:]
+    f32 = jnp.float32
+    key_back[...] = jnp.zeros_like(key_back)
+    value_back[...] = jnp.zeros_like(value_back)
+
+    def ready(index, carry):
+        at = pl.ds(pl.multiple_of(index * block, block), block)
+        grads[at, :] = lax.dot_general(
+            middle[at, :], out_slice[...], (((1,), (1,)), ((), ())), preferred_element_type=f32
+        ).astype(grads.dtype)
+        both = pair[at, :].astype(f32)
+        swapped = pltpu.roll(both, width, 1)
+        zero = jnp.zeros_like(both)
+        for refs, low, high in (
+            (keys, both, swapped),
+            (values, swapped, both),
+        ):
+            refs[0][at, :] = pick_lanes(low, high, width).astype(refs[0].dtype)
+            refs[1][at, :] = pick_lanes(low, zero, width).astype(refs[0].dtype)
+            refs[2][at, :] = pick_lanes(zero, high, width).astype(refs[0].dtype)
+        return carry
+
+    lax.fori_loop(0, blocks, ready, 0)
+    for index in range(blocks):
+        back_block(
+            index,
+            block,
+            width,
+            heads,
+            queries,
+            grads,
+            outs,
+            logs,
+            keys,
+            values,
+            query_back,
+            key_back,
+            value_back,
+        )
+
+    def norms(index, slope):
+        at = pl.ds(pl.multiple_of(index * block, block), block)
+        key_sum, value_sum = key_back[at, :], value_back[at, :]
+        key_sum = key_sum + pltpu.roll(key_sum, width, 1)
+        value_sum = value_sum + pltpu.roll(value_sum, width, 1)
+        back = jnp.concatenate(
+            [query_back[at, :], pick_lanes(key_sum, value_sum, width)], axis=1
+        )
+        value = proj[at, :]
+        factor = lax.rsqrt(group_mean(value * value, group[...], width) + EPS)
+        repeat = value.shape[1] // cosine.shape[1]
+        cosines = jnp.concatenate([cosine[at, :]] * repeat, axis=1)
+        sines = jnp.concatenate([sine[at, :]] * repeat, axis=1)
+        turned = back * cosines + turn(back * sines, width)
+        slope = slope + jnp.sum(turned * value * factor, axis=0, keepdims=True)
+        scaled = turned * gain[...]
+        result = factor * (
+            scaled - value * factor * factor * group_mean(scaled * value, group[...], width)
+        )
+        lane = lax.broadcasted_iota(jnp.int32, back.shape, 1)
+        result = jnp.where(lane >= query_cols + width, back, result)
+        halves[at, :] = result.astype(halves.dtype)
+        return slope
+
+    slope = lax.fori_loop(0, blocks, norms, jnp.zeros((1, proj.shape[1]), f32))
+    slopes[...] = jnp.broadcast_to(slope, slopes.shape)
+
+    def terms(number, carry):
+        at = pl.ds(pl.multiple_of(number * 256, 256), 256)
+        down = (((0,), (0,)), ((), ()))
+        head_part[at, :] = lax.dot_general(
+            normed[:, at], halves[...], down, preferred_element_type=f32
+        ).astype(head_part.dtype)
+        out_part[:, at] = lax.dot_general(
+            outs[...], middle[:, at], down, preferred_element_type=f32
+        ).astype(out_part.dtype)
+        return carry
+
+    lax.fori_loop(0, normed.shape[1] // 256, terms, 0)
 
 
 def front_kernel(
@@ -1612,20 +1774,12 @@
     heads_of = jnp.arange(head_cols) // width
     group = (heads_of[:, None] == heads_of[None, :]).astype(bf16)
     gain_row = jnp.concatenate([jnp.tile(query_gain, local_groups), key_gain, key_gain])[None, :]
-    log_rows_count = -(-local_groups // 8) * 8
+    tables = (gain_row, jnp.concatenate([cosine, cosine], axis=1), signed, group)
     normed_all, head_full, out_slice, proj, queries, pair_rows, out_rows, log_rows = call(
         functools.partial(front_kernel, width),
         sizes,
         0,
-        (
-            normed_in,
-            head_weights,
-            out_piece,
-            gain_row,
-            jnp.concatenate([cosine, cosine], axis=1),
-            signed,
-            group,
-        ),
+        (normed_in, head_weights, out_piece, *tables),
         (True,) * 7,
         [
             ((length, model), bf16),
@@ -1635,13 +1789,10 @@
             ((length, query_cols), bf16),
             ((length, 2 * width), bf16),
             ((length, query_cols), bf16),
-            ((log_rows_count, length), f32),
+            ((length, 128), f32),
         ],
         [((planes, piece_rows, model), bf16)] + [((length, 2 * width), bf16)] * 3,
     )
-    query_proj = proj[:, :query_cols]
-    key_proj = proj[:, query_cols : query_cols + width]
-    log_rows = log_rows[:local_groups][None]
 
     half = model // 2
     scatter_scratch = [
@@ -1714,23 +1865,44 @@
     bit_orders = ([2 << i for i in range(halvings + 1)], [chips >> i for i in range(halvings + 1)])
     came = [swap(piece, bit_orders[number % 2][-1]) for number, piece in enumerate(sent)]
 
-    attended_grad = inner_cols(middle_all, out_slice).astype(bf16)
-    query_back, pair_back = attend_back(
-        queries, pair_rows, out_rows, log_rows, attended_grad, local_groups, width
-    )
-    key_back = pair_back[:, :width]
-    value_back = pair_back[:, width:]
-    _, query_pull = jax.vjp(
-        lambda proj_in, gain_in: prepare(proj_in, gain_in, cosine, sine), query_proj, query_gain
-    )
-    query_proj_grad, query_slope = query_pull(query_back)
-    _, key_pull = jax.vjp(
-        lambda proj_in, gain_in: prepare(proj_in, gain_in, cosine, sine), key_proj, key_gain
-    )
-    key_proj_grad, key_slope = key_pull(key_back)
-    halves = jnp.concatenate([query_proj_grad, key_proj_grad, value_back], axis=1).astype(bf16)
-    head_part = inner_rows(normed_all, halves).astype(bf16).reshape(planes, shard, head_cols)
-    out_part = inner_rows(out_rows, middle_all).astype(bf16)
+    vmem = pl.BlockSpec(memory_space=pltpu.VMEM)
+    halves, head_part, out_part, head_slopes = pl.pallas_call(
+        functools.partial(back_kernel, width),
+        out_shape=[
+            jax.ShapeDtypeStruct((length, head_cols), bf16),
+            jax.ShapeDtypeStruct((model, head_cols), bf16),
+            jax.ShapeDtypeStruct((query_cols, model), bf16),
+            jax.ShapeDtypeStruct((8, head_cols), f32),
+        ],
+        in_specs=[vmem] * 12,
+        out_specs=[vmem] * 4,
+        scratch_shapes=[
+            pltpu.VMEM((length, query_cols), bf16),
+            pltpu.VMEM((length, query_cols), f32),
+            pltpu.VMEM((length, 2 * width), f32),
+            pltpu.VMEM((length, 2 * width), f32),
+        ]
+        + [pltpu.VMEM((length, 2 * width), bf16)] * 6,
+        compiler_params=pltpu.CompilerParams(vmem_limit_bytes=VMEM_BYTES),
+        cost_estimate=pl.CostEstimate(
+            flops=10 * length * model * head_cols,
+            transcendentals=length * length * local_groups,
+            bytes_accessed=16 * length * model,
+        ),
+    )(
+        normed_all,
+        middle_all,
+        out_slice,
+        out_rows,
+        log_rows,
+        queries,
+        pair_rows,
+        proj,
+        *tables,
+    )
+    head_part = head_part.reshape(planes, shard, head_cols)
+    query_slope = head_slopes[0, :query_cols].reshape(local_groups, width).sum(axis=0)
+    key_slope = head_slopes[0, query_cols : query_cols + width]
 
     gains = jnp.concatenate([query_slope, key_slope])
     gains = jnp.pad(gains, (0, model - gains.shape[0]))
@@ -1801,11 +1973,9 @@
     grad_key = grad_pair[:, :, 0].transpose(1, 0, 2).reshape(shard, -1)
     grad_value = grad_pair[:, :, 1].transpose(1, 0, 2).reshape(shard, -1)
     grad_output = outer_all.astype(f32)
-    pieces[2:], gate_pieces, grad_down, grad_query, grad_output, input_rows = (
-        lax.optimization_barrier(
-            (pieces[2:], gate_pieces, grad_down, grad_query, grad_output, input_rows)
-        )
-    )
+    written = (grad_down, grad_query, grad_key, grad_value, grad_output, input_rows)
+    pieces[2:], gate_pieces, written = lax.optimization_barrier((pieces[2:], gate_pieces, written))
+    grad_down, grad_query, grad_key, grad_value, grad_output, input_rows = written
     up_pieces = plane_pieces(pieces[2:])
     grad_gate = widen_pieces(gate_pieces, [swap(value, 1) for _, value in gate_pieces])
     up_pieces, grad_gate = lax.optimization_barrier((up_pieces, grad_gate))

time: 562 us -> 534 us (0.950)
  matrix products: 30.6 us -> 0 us
  Pallas kernels: 416 us -> 442 us
  other arithmetic: 48 us -> 28.7 us
  local copies, waits for them, and re-layouts: 34.9 us -> 18 us
  waiting for transfers between devices: 14.3 us -> 29.4 us
    dot_general x18 -> x0, matrix products: 30.6 us -> none  [the longest x2 8.39 us: inner_rows(): lax.dot_general(left, right, (((0,), (0,)), ((), ())), preferred_element_...]
    pallas_call x0 -> x1, Pallas kernels: none -> 27.7 us  [per_device(): pl.pallas_call(functools.partial(back_kernel, width), out_shape=[jax.Shap...]
    ppermute x16, waiting for transfers between devices: 14.3 us -> 29.4 us  [swap(): return lax.ppermute(value, 'seq', [(i, i ^ bit) for i in range(parts)])]
    reduce_sum x5 -> x1, other arithmetic: 8.41 us -> 0.02 us  [per_device(): head_slopes[0, :query_cols].reshape(local_groups, width).sum(axis=0)]
  transfers between devices with their start and end apart: 16 -> 16, of which waited for: 7 -> 10; matrix products, arithmetic and copies ran while one was open for 16% -> 4% of each run, Pallas kernels for 4% -> 9%
where the time goes in v6:
time: 534 us; the launch traced here: 529 us
  Pallas kernels  442 us (83%)
  waiting for transfers between devices  29.4 us (6%)
  other arithmetic  28.7 us (5%)
  local copies, waits for them, and re-layouts  18 us (3%)
  starting transfers between devices  9.19 us (2%)
    pallas_call x5, Pallas kernels, call(): pl.pallas_call(functools.partial(kernel, *mesh_sizes), out_shape=[jax.Sha...  380 us
    ppermute x16, waiting for transfers between devices, swap(): return lax.ppermute(value, 'seq', [(i, i ^ bit) for i in range(parts)])  29.4 us
    pallas_call x1, Pallas kernels, per_device(): pl.pallas_call(functools.partial(back_kernel, width), out_shape=[jax.Shap...  27.7 us
    pallas_call x2, Pallas kernels, widen_pieces(): pl.pallas_call(functools.partial(widen_pieces_kernel, count, steps), out_...  24 us
  transfers between devices with their start and end apart: 16, of which 10 were waited for; matrix products, arithmetic and copies ran while one was open for 4% of the time, Pallas kernels for 9%

profile of v6, /device:TPU:0, one launch (start us, length us, event | category | flops | bytes accessed | tf_op | source)
XLA Modules:
  0.0 529.0 jit_solution(12193391041791368251)
XLA Ops:
  0.7 1.3 fusion.8
  2.0 0.7 tile.4
  2.8 0.8 pad_maximum_fusion.3
  3.6 0.6 broadcast_in_dim.10.gain
  4.1 0.8 compare_convert_fusion.group
  5.2 2.2 fusion.11
  7.4 1.0 constant_dynamic-slice_fusion.3
  8.4 1.7 constant_dynamic-slice_fusion.o
  10.1 1.0 fusion.2.x
  11.0 1.1 constant_dynamic-slice_fusion.1
  12.2 0.9 pad_maximum_fusion.2.w
  13.0 1.3 pad_maximum_fusion.1
  14.3 62.4 %shard_map.228 = (bf16[1024,2048]{1,0:T(8,128)(2,1)}, bf16[2048,384]{1,0:T(8,128)(2,1)}, bf16[256,2048]{1,0:T(8,128)(2,1)}, f32[1024,384]{1,0:T(8,128)}, bf16[10...) custom-call(bf16[128,2048]{1,0:T(8,128)(2,1)} %fusion.2.x, ...), custom_call_target="tpu_custom_call" | custom-call | tf_op jit(solution)/shard_map/pallas_call | solution.py:1657
  76.7 43.9 %shard_map.229 = (f32[128,2048]{1,0:T(8,128)}, bf16[4,2,128,2048]{3,2,1,0:T(8,128)(2,1)}) custom-call(bf16[1024,256]{1,0:T(8,128)(2,1)} %get-tuple-element.86.a.outs, bf16[256,2048]{1,0:T(8,128)(2,1)} %get-tuple-element.87.w.out_slice, bf16[128,2048]{1,0:T(8,128)(2,1)} %bitcast.51), custom_call_target="tpu_custom_call" | custom-call | tf_op jit(solution)/shard_map/pallas_call | solution.py:1657
  120.6 1.6 multiply_reduce_fusion.2
  122.2 1.0 copy-done
  123.1 1.0 multiply_convert_fusion.m
  124.1 126.5 %shard_map.230 = (bf16[2,512,1024]{2,1,0:T(8,128)(2,1)}, bf16[512,1024]{1,0:T(8,128)(2,1)}, bf16[512,1024]{1,0:T(8,128)(2,1)}, bf16[512,1024]{1,0:T(8,128)(2,1)}...) custom-call(bf16[128,2048]{1,0:T(8,128)(2,1)} %multiply_convert_fusi, ...), custom_call_target="tpu_custom_call" | custom-call | tf_op jit(solution)/shard_map/pallas_call | solution.py:1657
  250.6 2.0 multiply_reduce_fusion
  252.8 2.2 fusion.18.h
  255.0 52.7 %shard_map.231 = (bf16[1024,2048]{1,0:T(8,128)(2,1)}, bf16[2,512,1024]{2,1,0:T(8,128)(2,1)}, f32[128,2048]{1,0:T(8,128)}) custom-call(bf16[128,2048]{1,0:T(8,128)(2,1)} %fusion.18.h, bf16[2,512,1024]{2,1,0:T(8,128)(2,1)} %get-tuple-element.91.s, bf16[4,128,2048]{2,1,0:T(8,128)(2,1)} %get-tuple-element.92.give, bf16[4,128,2048]{2,1,0:T(8,128)(2,1)} %get-tuple-element.93.keep), custom_call_target="tpu_custom_call" | custom-call | tf_op jit(solution)/shard_map/pallas_call | solution.py:1657
  307.7 1.9 collective-permute-start
  309.8 1.9 collective-permute-start.2
  311.8 27.7 %shard_map.232 = (bf16[1024,384]{1,0:T(8,128)(2,1)}, bf16[2048,384]{1,0:T(8,128)(2,1)}, bf16[256,2048]{1,0:T(8,128)(2,1)}, f32[8,384]{1,0:T(8,128)}) custom-call(bf16[1024,2048]{1,0:T(8,128)(2,1)} %get-tuple-element.95.normed, bf16[1024,2048]{1,0:T(8,128)(2,1)} %get-tuple-element.101.middle, bf16[256,2048]{1,0:T(8,128)(2,1)} %get-tuple-element.87.w.out_slice, ...), custom_call_target="tpu_custom_call" | custom-call | flops 8053063680 | bytes 33554432 | tf_op jit(solution)/shard_map/pallas_call | solution.py:1869
  339.5 0.7 copy.29.factor
  340.3 0.7 slice_reduce_fusion
  341.1 0.7 slice_bitcast_fusion.2
  341.9 0.7 select_maximum_fusion.slope
  342.5 12.5 %collective-permute-done.2.rest_6_ = bf16[512,1024]{1,0:T(8,128)(2,1)} collective-permute-done((bf16[512,1024]{1,0:T(8,128)(2,1)}, bf16[512,1024]{1,0:T(8,128)(2,1)}, u32[]{:S(2)}, u32[]{:S(2)}) %collective-permute-start.2) | collective-permute-done | bytes 1048608 | tf_op jit(solution)/shard_map/ppermute | solution.py:1862
  355.0 1.5 collective-permute-done.3.rest_7_
  356.5 95.0 %shard_map.233 = (f32[128,2048]{1,0:T(8,128)}, bf16[2048,1024]{1,0:T(8,128)(2,1)}, bf16[2048,1024]{1,0:T(8,128)(2,1)}, bf16[512,2048]{1,0:T(8,128)(2,1)}, bf16[8...) custom-call(bf16[1024,384]{1,0:T(8,128)(2,1)} %get-tuple-element.106, ...), custom_call_target="tpu_custom_call" | custom-call | tf_op jit(solution)/shard_map/pallas_call | solution.py:1657
  451.5 1.7 fusion.9
  453.1 1.3 collective-permute-start.4
  454.5 0.6 collective-permute-start.5
  455.1 0.5 copy.30
  455.6 4.3 convert_element_type.64
  459.9 2.5 convert_element_type.65
  462.5 10.2 %shard_map.234 = f32[2048,2048]{1,0:T(8,128)} custom-call(bf16[2048,1024]{1,0:T(8,128)(2,1)} %get-tuple-element.127.near, bf16[2048,1024]{1,0:T(8,128)(2,1)} %get-tuple-element.128.far), custom_call_target="tpu_custom_call" | custom-call | bytes 25165824 | tf_op jit(solution)/shard_map/pallas_call | solution.py:1672
  472.7 1.2 fusion.19
  473.9 0.5 copy-done.4
  474.4 0.3 copy-done.6
  474.9 0.3 copy-done.9
  475.2 3.0 fusion.7
  478.2 0.9 collective-permute-done.4.refs_1_
  479.1 1.0 collective-permute-done.5.refs_3_
  480.1 0.8 collective-permute-start.6
  481.1 0.3 collective-permute-start.10
  481.6 1.2 collective-permute-done.8.refs_4_
  482.7 1.0 copy-done.13
  483.7 0.6 collective-permute-start.7
  484.3 0.6 pad_add_fusion.starts
  484.9 1.0 collective-permute-done.10.refs_6_
  485.9 1.5 collective-permute-done.11.refs_7_
  487.4 12.0 %shard_map.235 = f32[2048,2048]{1,0:T(8,128)} custom-call(s32[4]{0:T(128)} %pad_add_fusion.starts, bf16[512,1024]{1,0:T(8,128)(2,1)} %get-tuple-element.145.refs_0_, bf16[512,1024]{1,0:T(8,128)(2,1)} %collective-permute-done.4.refs_1_, bf16[512,1024]{1,0:T(8,128)(2,1)} %get-tuple-element.147.refs_2_, bf16[512,1024]{1,0:T(8,128)(2,1)} %collective-permute-done.5.refs_3_, ...), custom_call_target="tpu_custom_call" | custom-call | bytes 25165824 | tf_op jit(solution)/shard_map/pallas_call | solution.py:1697
  499.4 6.4 %collective-permute-done.6.refs_1_ = bf16[512,1024]{1,0:T(8,128)(2,1)} collective-permute-done((bf16[512,1024]{1,0:T(8,128)(2,1)S(1)}, bf16[512,1024]{1,0:T(8,128)(2,1)}, u32[]{:S(2)}, u32[]{:S(2)}) %collective-permute-start.6) | collective-permute-done | bytes 1048608 | tf_op jit(solution)/shard_map/ppermute | solution.py:1862
  505.8 3.5 collective-permute-done.7.refs_3_
  509.2 0.5 collective-permute-start.13
  509.7 0.5 collective-permute-start.15
  510.2 1.3 slice_bitcast_fusion
  511.6 1.5 fusion.20
  513.1 1.3 copy.31
  514.4 1.3 copy.32
  515.7 0.7 pad_add_fusion.1.starts
  516.5 12.0 %shard_map.236 = f32[2048,2048]{1,0:T(8,128)} custom-call(s32[4]{0:T(128)} %pad_add_fusion.1.starts, bf16[512,1024]{1,0:T(8,128)(2,1)} %get-tuple-element.154.refs_0_, bf16[512,1024]{1,0:T(8,128)(2,1)} %collective-permute-done.6.refs_1_, bf16[512,1024]{1,0:T(8,128)(2,1)} %get-tuple-element.156.refs_2_, bf16[512,1024]{1,0:T(8,128)(2,1)} %collective-permute-done.7.refs_3_, ...), custom_call_target="tpu_custom_call" | custom-call | bytes 25165824 | tf_op jit(solution)/shard_map/pallas_call | solution.py:1697
  (56 shorter events, 1.6 us)
Async XLA Ops:
  0.6 9.4 %copy-start.3 = (bf16[1,128,2048]{2,1,0:T(8,128)(2,1)S(1)}, bf16[1,128,2048]{2,1,0:T(8,128)(2,1)}, u32[]{:S(2)}) copy-start(bf16[1,128,2048]{2,1,0:T(8,128)(2,1)} %param.13) | copy-start | bytes 1572868
  0.7 9.4 %copy-start.16 = (f32[2048]{0:T(1024)S(1)}, f32[2048]{0:T(1024)}, u32[]{:S(2)}) copy-start(f32[2048]{0:T(1024)} %param.15) | copy-start | bytes 24580
  76.7 46.5 %copy-start.15 = (f32[2048]{0:T(1024)S(1)}, f32[2048]{0:T(1024)}, u32[]{:S(2)}) copy-start(f32[2048]{0:T(1024)} %param.22) | copy-start | bytes 24580
  122.1 1.0 copy-start
  250.6 2.0 copy-start.1
  250.6 2.2 copy-start.5
  307.7 34.8 %collective-permute-start = (bf16[512,1024]{1,0:T(8,128)(2,1)}, bf16[512,1024]{1,0:T(8,128)(2,1)}, u32[]{:S(2)}, u32[]{:S(2)}) collective-permute-start(bf16[512,1024]{1,0:T(8,128)(2,1)} %get-tuple-element.112.rest_0_), channel_id=1, source_target_pairs={{0,16},{4,20},{8,24},{12,28},{16,0},{20,4},{24,8},{28,12},{1,17},{... | collective-permute-start | bytes 3145736 | tf_op jit(solution)/shard_map/ppermute | solution.py:1862
  309.6 32.9 %collective-permute-start.1 = (bf16[512,1024]{1,0:T(8,128)(2,1)}, bf16[512,1024]{1,0:T(8,128)(2,1)}, u32[]{:S(2)}, u32[]{:S(2)}) collective-permute-start(bf16[512,1024]{1,0:T(8,128)(2,1)} %get-tuple-element.113.rest_1_), channel_id=1, source_target_pairs={{0,8},{4,12},{8,0},{12,4},{16,24},{20,28},{24,16},{28,20},{1,9},{5... | collective-permute-start | bytes 3145736 | tf_op jit(solution)/shard_map/ppermute | solution.py:1862
  309.8 45.2 %collective-permute-start.2 = (bf16[512,1024]{1,0:T(8,128)(2,1)}, bf16[512,1024]{1,0:T(8,128)(2,1)}, u32[]{:S(2)}, u32[]{:S(2)}) collective-permute-start(bf16[512,1024]{1,0:T(8,128)(2,1)} %get-tuple-element.114.rest_2_), channel_id=1, source_target_pairs={{0,16},{4,20},{8,24},{12,28},{16,0},{20,4},{24,8},{28,12},{1,17},{... | collective-permute-start | bytes 3145736 | tf_op jit(solution)/shard_map/ppermute | solution.py:1862
  311.6 44.8 %collective-permute-start.3 = (bf16[512,1024]{1,0:T(8,128)(2,1)}, bf16[512,1024]{1,0:T(8,128)(2,1)}, u32[]{:S(2)}, u32[]{:S(2)}) collective-permute-start(bf16[512,1024]{1,0:T(8,128)(2,1)} %get-tuple-element.115.rest_3_), channel_id=1, source_target_pairs={{0,8},{4,12},{8,0},{12,4},{16,24},{20,28},{24,16},{28,20},{1,9},{5... | collective-permute-start | bytes 3145736 | tf_op jit(solution)/shard_map/ppermute | solution.py:1862
  451.5 3.6 copy-start.14
  453.1 25.9 %collective-permute-start.4 = (bf16[512,1024]{1,0:T(8,128)(2,1)}, bf16[512,1024]{1,0:T(8,128)(2,1)}, u32[]{:S(2)}, u32[]{:S(2)}) collective-permute-start(bf16[512,1024]{1,0:T(8,128)(2,1)} %get-tuple-element.145.refs_0_), channel_id=1, source_target_pairs={{0,8},{4,12},{8,0},{12,4},{16,24},{20,28},{24,16},{28,20},{1,9},{5... | collective-permute-start | bytes 3145736 | tf_op jit(solution)/shard_map/ppermute | solution.py:1862
  454.5 25.6 %collective-permute-start.5 = (bf16[512,1024]{1,0:T(8,128)(2,1)}, bf16[512,1024]{1,0:T(8,128)(2,1)}, u32[]{:S(2)}, u32[]{:S(2)}) collective-permute-start(bf16[512,1024]{1,0:T(8,128)(2,1)} %get-tuple-element.147.refs_2_), channel_id=1, source_target_pairs={{0,16},{4,20},{8,24},{12,28},{16,0},{20,4},{24,8},{28,12},{1,17},{... | collective-permute-start | bytes 3145736 | tf_op jit(solution)/shard_map/ppermute | solution.py:1862
  455.6 4.3 copy-start.10
  472.7 1.3 copy-start.2
  472.7 1.7 copy-start.4
  472.7 2.1 copy-start.6
  472.7 2.2 copy-start.7
  472.7 2.5 copy-start.9
  475.2 4.9 copy-start.12
  475.2 4.9 copy-start.11
  480.1 2.7 collective-permute-start.8
  480.1 25.7 %collective-permute-start.6 = (bf16[512,1024]{1,0:T(8,128)(2,1)S(1)}, bf16[512,1024]{1,0:T(8,128)(2,1)}, u32[]{:S(2)}, u32[]{:S(2)}) collective-permute-start(bf16[512,1024]{1,0:T(8,128)(2,1)S(1)} %copy-done.11), channel_id=1, source_target_pairs={{0,8},{4,12},{8,0},{12,4},{16,24},{20,28},{24,16},{28,20},{1,9},{5... | collective-permute-start | bytes 3145736 | tf_op jit(solution)/shard_map/ppermute | solution.py:1862
  480.9 4.0 collective-permute-start.9
  481.1 4.8 collective-permute-start.10
  481.4 6.0 %collective-permute-start.11 = (bf16[512,1024]{1,0:T(8,128)(2,1)}, bf16[512,1024]{1,0:T(8,128)(2,1)}, u32[]{:S(2)}, u32[]{:S(2)}) collective-permute-start(bf16[512,1024]{1,0:T(8,128)(2,1)} %collective-permute-done.5.refs_3_), channel_id=1, source_target_pairs={{0,4},{4,0},{8,12},{12,8},{16,20},{20,16},{24,28},{28,24},{1,5},{5... | collective-permute-start | bytes 3145736 | tf_op jit(solution)/shard_map/ppermute | solution.py:1862
  482.7 1.0 copy-start.13
  483.7 25.5 %collective-permute-start.7 = (bf16[512,1024]{1,0:T(8,128)(2,1)}, bf16[512,1024]{1,0:T(8,128)(2,1)}, u32[]{:S(2)}, u32[]{:S(2)}) collective-permute-start(bf16[512,1024]{1,0:T(8,128)(2,1)} %get-tuple-element.156.refs_2_), channel_id=1, source_target_pairs={{0,16},{4,20},{8,24},{12,28},{16,0},{20,4},{24,8},{28,12},{1,17},{... | collective-permute-start | bytes 3145736 | tf_op jit(solution)/shard_map/ppermute | solution.py:1862
  484.9 28.2 %copy-start.8 = (f32[8,512,1,64]{1,3,2,0:T(8,128)S(1)}, f32[8,512,1,64]{1,3,2,0:T(8,128)}, u32[]{:S(2)}) copy-start(f32[8,512,1,64]{1,3,2,0:T(8,128)} %get-tuple-element.177) | copy-start | bytes 3145732
  509.2 7.2 %collective-permute-start.12 = (bf16[512,1024]{1,0:T(8,128)(2,1)S(1)}, bf16[512,1024]{1,0:T(8,128)(2,1)}, u32[]{:S(2)}, u32[]{:S(2)}) collective-permute-start(bf16[512,1024]{1,0:T(8,128)(2,1)S(1)} %copy-done.11), channel_id=1, source_target_pairs={{0,4},{4,0},{8,12},{12,8},{16,20},{20,16},{24,28},{28,24},{1,5},{5... | collective-permute-start | bytes 3145736 | tf_op jit(solution)/shard_map/ppermute | solution.py:1862
  509.2 7.2 %collective-permute-start.13 = (bf16[512,1024]{1,0:T(8,128)(2,1)}, bf16[512,1024]{1,0:T(8,128)(2,1)}, u32[]{:S(2)}, u32[]{:S(2)}) collective-permute-start(bf16[512,1024]{1,0:T(8,128)(2,1)} %collective-permute-done.6.refs_1_), channel_id=1, source_target_pairs={{0,4},{4,0},{8,12},{12,8},{16,20},{20,16},{24,28},{28,24},{1,5},{5... | collective-permute-start | bytes 3145736 | tf_op jit(solution)/shard_map/ppermute | solution.py:1862
  509.7 6.7 %collective-permute-start.14 = (bf16[512,1024]{1,0:T(8,128)(2,1)}, bf16[512,1024]{1,0:T(8,128)(2,1)}, u32[]{:S(2)}, u32[]{:S(2)}) collective-permute-start(bf16[512,1024]{1,0:T(8,128)(2,1)} %get-tuple-element.156.refs_2_), channel_id=1, source_target_pairs={{0,4},{4,0},{8,12},{12,8},{16,20},{20,16},{24,28},{28,24},{1,5},{5... | collective-permute-start | bytes 3145736 | tf_op jit(solution)/shard_map/ppermute | solution.py:1862
  509.7 6.8 %collective-permute-start.15 = (bf16[512,1024]{1,0:T(8,128)(2,1)}, bf16[512,1024]{1,0:T(8,128)(2,1)}, u32[]{:S(2)}, u32[]{:S(2)}) collective-permute-start(bf16[512,1024]{1,0:T(8,128)(2,1)} %collective-permute-done.7.refs_3_), channel_id=1, source_target_pairs={{0,4},{4,0},{8,12},{12,8},{16,20},{20,16},{24,28},{28,24},{1,5},{5... | collective-permute-start | bytes 3145736 | tf_op jit(solution)/shard_map/ppermute | solution.py:1862

commit v7 on v6

--- a/solution.py
+++ b/solution.py
@@ -846,17 +846,29 @@
     lax.fori_loop(0, normed.shape[1] // 256, terms, 0)
 
 
+def row_blocks(rows, step, work):
+    def body(index, carry):
+        work(pl.ds(pl.multiple_of(index * step, step), step))
+        return carry
+
+    lax.fori_loop(0, rows // step, body, 0)
+
+
 def front_kernel(
     width,
+    copies,
     parts,
     planes,
     x,
-    w,
-    o,
+    c,
+    query_weight,
+    key_weight,
+    value_weight,
+    output_weight,
+    in_gain,
+    mid_gain,
     gain,
-    cosine,
-    sine,
-    group,
+    rates,
     x_all,
     w_all,
     o_slice,
@@ -865,36 +877,106 @@
     pair,
     out_rows,
     logs,
+    cosine,
+    sine,
+    group,
+    middle,
+    mid,
+    c_all,
     o_all,
     twin,
     left,
     right,
+    key_block,
+    value_block,
+    give,
+    take,
+    current,
+    landing,
     *sems,
 ):
     here = Place(parts, planes)
     wire = Wire(*sems)
-    tokens, shard, rows = x.shape[0], w.shape[0], o.shape[0]
+    tokens, model = x.shape
+    shard = query_weight.shape[0]
+    query_cols = queries.shape[1]
+    rows = o_all.shape[1]
     half = tokens // 2
     chips = parts // 2
+    f32 = jnp.float32
     chip_masks = [mask * 2 for mask in range(1, chips)]
+    pair_head = here.seat // copies
+    own_shard = pl.ds(pl.multiple_of(here.plane * shard, shard), shard)
+    head_block = pl.ds(pl.multiple_of(pair_head // 2 * 2 * width, 2 * width), 2 * width)
+    loads = [
+        wire.local(key_weight.at[:, head_block], key_block),
+        wire.local(value_weight.at[:, head_block], value_block),
+        wire.local(
+            query_weight.at[:, pl.ds(pl.multiple_of(here.seat * query_cols, query_cols), query_cols)],
+            w_all.at[own_shard, pl.ds(0, query_cols)],
+        ),
+    ]
+    piece = (here.core * chips + here.chip) * rows
+    o = output_weight.at[pl.ds(pl.multiple_of(piece, rows), rows)]
     here.enter(chip_masks + [1], line=True)
+    o_own = wire.local(o, o_all.at[here.plane])
+    for load in loads[:2]:
+        load.wait()
+    upper = (pair_head % 2) * jnp.ones((1, 1), jnp.int32)
+    keys, values = key_block[...].astype(f32), value_block[...].astype(f32)
+    keys = jnp.where(upper == 1, pltpu.roll(keys, width, 1), keys)
+    values = jnp.where(upper == 1, values, pltpu.roll(values, width, 1))
+    w_all[own_shard, query_cols:] = pick_lanes(keys, values, width).astype(w_all.dtype)
+    loads[2].wait()
     weights = gather_lines(
-        wire, here, w, lambda index: w_all.at[pl.ds(pl.multiple_of(index * shard, shard), shard)]
-    )
-    weights.start(1)
-    plane_rows = PlaneGather(
         wire,
         here,
-        lambda color: x.at[pl.ds(color * half, half)],
-        lambda seat, color: x_all.at[pl.ds(pl.multiple_of(seat * tokens + color * half, half), half)],
+        w_all.at[own_shard],
+        lambda index: w_all.at[pl.ds(pl.multiple_of(index * shard, shard), shard)],
+    )
+    weights.start(1)
+
+    def norm_rows(at):
+        value = x[at, :].astype(f32)
+        factor = lax.rsqrt(jnp.mean(value * value, axis=-1, keepdims=True) + EPS)
+        own_at = pl.ds(pl.multiple_of(here.seat * tokens + at.start, 32), 32)
+        x_all[own_at, :] = (value * factor * in_gain[...]).astype(x_all.dtype)
+
+    row_blocks(tokens, 32, norm_rows)
+
+    def seat_rows(seat, color):
+        return x_all.at[pl.ds(pl.multiple_of(seat * tokens + color * half, half), half)]
+
+    plane_rows = PlaneGather(
+        wire, here, lambda color: seat_rows(here.seat, color), seat_rows
     )
     plane_rows.start()
-    kept = [
-        wire.local(x, x_all.at[pl.ds(pl.multiple_of(here.seat * tokens, tokens), tokens)]),
-        wire.local(w, w_all.at[pl.ds(pl.multiple_of(here.plane * shard, shard), shard)]),
-        wire.local(o, o_all.at[here.plane]),
-    ]
     outer = gather_lines(wire, here, o, lambda index: o_all.at[index])
+
+    def c_spot(index):
+        return c_all.at[index, here.core]
+
+    cots = gather_lines(wire, here, c, c_spot, c_spot)
+    c_own = wire.local(c, c_spot(here.plane))
+
+    lane = lax.broadcasted_iota(jnp.int32, (32, 2 * width), 1)
+    row = lax.broadcasted_iota(jnp.int32, (32, 2 * width), 0)
+    sign = jnp.where(lane % width < width // 2, -1.0, 1.0)
+
+    def table_rows(at):
+        angle = (row + at.start).astype(f32) * rates[...]
+        cosine[at, :] = jnp.cos(angle)
+        sine[at, :] = jnp.sin(angle) * sign
+
+    columns = group.shape[0]
+    group[...] = jnp.where(
+        lax.broadcasted_iota(jnp.int32, (columns, columns), 0) // width
+        == lax.broadcasted_iota(jnp.int32, (columns, columns), 1) // width,
+        1.0,
+        0.0,
+    ).astype(group.dtype)
+    length = x_all.shape[0]
+    row_blocks(length // 2, 32, table_rows)
     weights.members[0].arrive(1)
     if planes > 2:
         weights.members[0].start(2)
@@ -903,6 +985,9 @@
     if planes > 2:
         weights.members[1].start(2)
     outer.start(1)
+    row_blocks(
+        length // 2, 32, lambda at: table_rows(pl.ds(at.start + length // 2, at.size))
+    )
     plane_rows.hops(2)
     spot = o_slice.at[pl.ds(pl.multiple_of(here.chip * rows, rows), rows)]
     deals = []
@@ -918,22 +1003,18 @@
             def _(copy=copy):
                 copy.start()
 
-    kept[2].wait()
+    o_own.wait()
     deal(0)
     for step in range(2, planes):
         weights.pass_on(step)
     plane_rows.finish()
-    for copy in kept[:2]:
-        copy.wait()
-    length = x_all.shape[0]
     block = min(256, length)
     blocks = length // block
-    query_cols = queries.shape[1]
     heads = query_cols // width
 
     def project(index, carry):
         at = pl.ds(pl.multiple_of(index * block, block), block)
-        value = jnp.dot(x_all[at, :], w_all[...], preferred_element_type=jnp.float32)
+        value = jnp.dot(x_all[at, :], w_all[...], preferred_element_type=f32)
         proj[at, :] = value
         factor = lax.rsqrt(group_mean(value * value, group[...], width) + EPS)
         normed = value * factor * gain[...]
@@ -953,63 +1034,62 @@
         return carry
 
     lax.fori_loop(0, blocks, project, 0)
+    across = wire.send(c, c_spot(here.plane), {"seq": here.at(1)})
     waits = list(range(1, planes))
+    cot_waits = list(range(1, planes))
     for index in range(blocks):
         while waits and waits[0] * blocks <= (index + 1) * planes:
             step = waits.pop(0)
             outer.pass_on(step)
             deal(step)
+            if not waits or (step == 2 and planes > 3):
+                if len(waits) == planes - 3 or planes <= 3:
+                    cots.start(1)
         attend_block(
             index, block, width, heads, queries, pair, twin, left, right, out_rows, logs
         )
     for step in waits:
         outer.pass_on(step)
         deal(step)
+    cots.pass_on(cot_waits.pop(0))
     keep_own.wait()
     for _, copy in deals:
         copy.wait()
+
+    def product(seats, at):
+        chosen = [
+            out_rows[pl.ds(pl.multiple_of(seat * tokens, tokens), tokens), :] for seat in seats
+        ]
+        return jnp.dot(
+            jnp.concatenate(chosen, axis=0), o_slice[:, at], preferred_element_type=f32
+        )
+
+    sums = PlaneScatter(wire, here, product, give, take, current, landing, model)
+    sums.start()
+    sums.join()
+    sums.stage(0)
+    stages = len(here.chip_bits)
+    for stage in range(stages):
+        if cot_waits:
+            cots.pass_on(cot_waits.pop(0))
+        sums.settle(stage, middle)
+        if stage + 1 < stages:
+            sums.stage(stage + 1)
+
+    def mid_rows(at):
+        value = x[at, :].astype(f32) + middle[at, :]
+        middle[at, :] = value
+        factor = lax.rsqrt(jnp.mean(value * value, axis=-1, keepdims=True) + EPS)
+        mid[at, :] = (value * factor * mid_gain[...]).astype(mid.dtype)
+
+    row_blocks(tokens, 32, mid_rows)
+    for step in cot_waits:
+        cots.pass_on(step)
+    c_own.wait()
+    across.wait_recv()
     wire.close()
     weights.close()
     outer.close()
-
-
-def out_rows_kernel(
-    parts, planes, a, w, c, out, c_all, give, take, current, landing, *sems
-):
-    here = Place(parts, planes)
-    wire = Wire(*sems)
-    tokens, model = c.shape
-    here.enter([mask for mask in here.seat_bits], line=True)
-
-    def product(seats, columns):
-        rows = [a[pl.ds(pl.multiple_of(seat * tokens, tokens), tokens), :] for seat in seats]
-        return jnp.dot(
-            jnp.concatenate(rows, axis=0), w[:, columns], preferred_element_type=jnp.float32
-        )
-
-    def spot(index):
-        return c_all.at[index, here.core]
-
-    cots = gather_lines(wire, here, c, spot, spot)
-    cots.start(1)
-    own = wire.local(c, spot(here.plane))
-    rows = PlaneScatter(wire, here, product, give, take, current, landing, model)
-    rows.start()
-    across = wire.send(c, spot(here.plane), {"seq": here.at(1)})
-    rows.join()
-    rows.stage(0)
-    stages = len(here.chip_bits)
-    for stage in range(stages):
-        if stage + 1 < planes:
-            cots.pass_on(stage + 1)
-        rows.settle(stage, out)
-        if stage + 1 < stages:
-            rows.stage(stage + 1)
-    for step in range(stages + 1, planes):
-        cots.pass_on(step)
-    own.wait()
-    across.wait_recv()
-    wire.close()
     cots.close()
 
 
@@ -1018,6 +1098,8 @@
     planes,
     m,
     cots,
+    middle,
+    mid_gain,
     gate_weight,
     up_weight,
     down_weight,
@@ -1027,6 +1109,8 @@
     s_up_a,
     s_up_b,
     mid,
+    mid_half,
+    mid_slope,
     down_give,
     down_keep,
     gate_half,
@@ -1205,6 +1289,26 @@
             gradient(keep, pairs[number], first_half(color, True))
             keeps[(number, color)] = (keep, 0)
     swaps.finish(mid)
+    f32 = jnp.float32
+
+    def norm_back_rows(index, slope):
+        at = pl.ds(pl.multiple_of(index * 32, 32), 32)
+        own_cots = (here.plane * 2 + here.core) * tokens + index * 32
+        grad, value = mid[at, :], middle[at, :]
+        factor = lax.rsqrt(jnp.mean(value * value, axis=-1, keepdims=True) + EPS)
+        scaled = grad * mid_gain[...]
+        back = factor * (
+            scaled
+            - value * factor * factor * jnp.mean(scaled * value, axis=-1, keepdims=True)
+        )
+        result = cots[pl.ds(pl.multiple_of(own_cots, 32), 32), :].astype(f32) + back
+        mid[at, :] = result
+        mid_half[at, :] = result.astype(mid_half.dtype)
+        return slope + jnp.sum(grad * value * factor, axis=0, keepdims=True)
+
+    mid_slope[...] = lax.fori_loop(
+        0, tokens // 32, norm_back_rows, jnp.zeros((1, model), f32)
+    )
     for stage in range(stages):
         last = stage == stages - 1
         for number in range(3):
@@ -1333,7 +1437,6 @@
     out_part,
     t_down,
     source,
-    factor,
     slope,
     *rest,
 ):
@@ -1494,7 +1597,9 @@
     weights[1].own()
     rows.settle(stages - 1, out)
     slope_sums[0] = slope[...]
-    slope_sums[0, 0:1, :] = jnp.sum(out[...] * source[...].astype(jnp.float32) * factor[...], axis=0, keepdims=True)
+    value = source[...].astype(jnp.float32)
+    factor = lax.rsqrt(jnp.mean(value * value, axis=-1, keepdims=True) + EPS)
+    slope_sums[0, 0:1, :] = jnp.sum(out[...] * value * factor, axis=0, keepdims=True)
     bits = [("seq", bit) for bit in here.seat_bits] + [("fsdp", bit) for bit in here.plane_bits]
     slope_copies = []
 
@@ -1642,7 +1747,7 @@
             out[:, other] = far[...].astype(out.dtype)
 
 
-SENDS, LOCALS = 128, 96
+SENDS, LOCALS = 192, 32
 
 
 def call(kernel, mesh_sizes, number, inputs, in_vmem, outputs, scratch, out_vmem=None):
@@ -1754,33 +1859,50 @@
     rows_in = inputs.reshape(tokens, model)
     cot_rows = cotangent.reshape(tokens, model)
 
-    pair_index = place // copies
-    head_weights = jnp.concatenate(
-        [
-            lax.dynamic_slice(query_weight, (0, place * query_cols), (shard, query_cols)),
-            lax.dynamic_slice(key_weight, (0, pair_index * width), (shard, width)),
-            lax.dynamic_slice(value_weight, (0, pair_index * width), (shard, width)),
-        ],
-        axis=1,
-    )
-    piece_index = core * chips + place // 2
-    out_piece = lax.dynamic_slice_in_dim(output_weight, piece_index * piece_rows, piece_rows, 0)
-    source = rows_in.astype(f32)
-    first = rms_factor(source)
-    normed_in = (source * first * attention_gain).astype(bf16)
-    cosine, sine = rope_tables(jnp.arange(length, dtype=jnp.int32), width)
-    lanes = jnp.arange(2 * width)
-    signed = jnp.where(lanes % width < width // 2, -1.0, 1.0) * jnp.concatenate([sine, sine], axis=1)
-    heads_of = jnp.arange(head_cols) // width
-    group = (heads_of[:, None] == heads_of[None, :]).astype(bf16)
-    gain_row = jnp.concatenate([jnp.tile(query_gain, local_groups), key_gain, key_gain])[None, :]
-    tables = (gain_row, jnp.concatenate([cosine, cosine], axis=1), signed, group)
-    normed_all, head_full, out_slice, proj, queries, pair_rows, out_rows, log_rows = call(
-        functools.partial(front_kernel, width),
+    exponents = jnp.arange(width // 2).astype(f32) * 2.0 / width
+    rates = jnp.power(jnp.float32(THETA), -exponents)
+    rates = jnp.concatenate([rates] * 4)[None, :]
+    gain_row = jnp.concatenate([query_gain] * local_groups + [key_gain] * 2)[None, :]
+    half = model // 2
+    scatter_scratch = [
+        ((chips, tokens, model), bf16),
+        ((chips, tokens, model), bf16),
+        ((2, chips, tokens, half), bf16),
+        ((halvings + 1, 2, chips, tokens, half), bf16),
+    ]
+    mid_gain = feedforward_gain[None, :]
+    (
+        normed_all,
+        head_full,
+        out_slice,
+        proj,
+        queries,
+        pair_rows,
+        out_rows,
+        log_rows,
+        cosine,
+        sine,
+        group,
+        middle,
+        normed_mid,
+        cot_all,
+    ) = call(
+        functools.partial(front_kernel, width, copies),
         sizes,
         0,
-        (normed_in, head_weights, out_piece, *tables),
-        (True,) * 7,
+        (
+            rows_in,
+            cot_rows,
+            query_weight,
+            key_weight,
+            value_weight,
+            output_weight,
+            attention_gain[None, :],
+            mid_gain,
+            gain_row,
+            rates,
+        ),
+        (True, True, False, False, False, False, True, True, True, True),
         [
             ((length, model), bf16),
             ((model, head_cols), bf16),
@@ -1790,29 +1912,20 @@
             ((length, 2 * width), bf16),
             ((length, query_cols), bf16),
             ((length, 128), f32),
+            ((length, 2 * width), f32),
+            ((length, 2 * width), f32),
+            ((head_cols, head_cols), bf16),
+            ((tokens, model), f32),
+            ((tokens, model), bf16),
+            ((planes, 2, tokens, model), bf16),
         ],
-        [((planes, piece_rows, model), bf16)] + [((length, 2 * width), bf16)] * 3,
-    )
-
-    half = model // 2
-    scatter_scratch = [
-        ((chips, tokens, model), bf16),
-        ((chips, tokens, model), bf16),
-        ((2, chips, tokens, half), bf16),
-        ((halvings + 1, 2, chips, tokens, half), bf16),
-    ]
-    out_sum, cot_all = call(
-        out_rows_kernel,
-        sizes,
-        1,
-        (out_rows, out_slice, cot_rows),
-        (True, True, True),
-        [((tokens, model), f32), ((planes, 2, tokens, model), bf16)],
-        scatter_scratch,
-    )
-    middle = source + out_sum
-    second = rms_factor(middle)
-    normed_mid = (middle * second * feedforward_gain).astype(bf16)
+        [((planes, piece_rows, model), bf16)]
+        + [((length, 2 * width), bf16)] * 3
+        + [((shard, 2 * width), bf16)] * 2
+        + scatter_scratch,
+    )
+    tables = (gain_row, cosine, sine, group)
+
     quarter = model // 4
     rows_shape = (planes, tokens, model)
     line_scratch = [
@@ -1821,16 +1934,37 @@
         ((2, planes - 1, tokens, model), bf16),
     ]
     acts = (2 * planes * tokens, units)
-    s_down, s_gate_a, s_gate_b, s_up_a, s_up_b, mid_grad, down_give, down_keep = call(
+    (
+        s_down,
+        s_gate_a,
+        s_gate_b,
+        s_up_a,
+        s_up_b,
+        middle_grad,
+        middle_half,
+        mid_slope,
+        down_give,
+        down_keep,
+    ) = call(
         feed_kernel,
         sizes,
         2,
-        (normed_mid, cot_all.reshape(-1, model), gate_weight, up_weight, down_weight),
-        (True, True, False, False, False),
+        (
+            normed_mid,
+            cot_all.reshape(-1, model),
+            middle,
+            mid_gain,
+            gate_weight,
+            up_weight,
+            down_weight,
+        ),
+        (True, True, True, True, False, False, False),
         [((2, last_rows, units), bf16)]
         + [((last_rows, units), bf16)] * 4
         + [
             ((tokens, model), f32),
+            ((tokens, model), bf16),
+            ((1, model), f32),
             (rows_shape, bf16),
             (rows_shape, bf16),
         ],
@@ -1841,12 +1975,9 @@
         + [((3, 2, quarter >> stage, units), bf16) for stage in range(halvings)]
         + [(rows_shape, bf16)]
         + line_scratch,
-        [True] * 6 + [False] * 2,
-    )
-
-    feedforward_slope = jnp.sum(mid_grad * middle * second, axis=0)
-    middle_grad = cot_rows.astype(f32) + norm_back(mid_grad, middle, second, feedforward_gain)
-    middle_half = middle_grad.astype(bf16)
+        [True] * 8 + [False] * 2,
+    )
+
     middle_all, t_down, down_sum = call(
         spread_kernel,
         sizes,
@@ -1906,8 +2037,8 @@
 
     gains = jnp.concatenate([query_slope, key_slope])
     gains = jnp.pad(gains, (0, model - gains.shape[0]))
-    slopes = jnp.stack([feedforward_slope, gains])
-    slopes = jnp.pad(slopes, ((1, 5), (0, 0)))
+    slopes = jnp.concatenate([jnp.zeros_like(mid_slope), mid_slope, gains[None, :]], axis=0)
+    slopes = jnp.pad(slopes, ((0, 5), (0, 0)))
     rounds = (parts * planes).bit_length() - 1
     side = ((model, units), bf16)
     piece = ((last_rows, units), bf16)
@@ -1915,8 +2046,8 @@
         final_kernel,
         sizes,
         5,
-        (halves, head_full, head_part, out_part, t_down, rows_in, first, slopes, *sent, *came),
-        (True, True, False, False, True, True, True, True) + (False,) * 8,
+        (halves, head_full, head_part, out_part, t_down, rows_in, slopes, *sent, *came),
+        (True, True, False, False, True, True, True) + (False,) * 8,
         [
             ((tokens, model), f32),
             side,
@@ -1945,6 +2076,8 @@
     pieces, near_down, far_down, in_grad = lax.optimization_barrier(
         (pieces, near_down, far_down, in_grad)
     )
+    source = rows_in.astype(f32)
+    first = rms_factor(source)
     input_rows = (middle_grad + norm_back(in_grad, source, first, attention_gain)).astype(bf16)
 
     def plane_pieces(values):

time: 534 us -> 512 us (0.959)
  other arithmetic: 28.7 us -> 13.8 us
  Pallas kernels: 442 us -> 435 us
    pallas_call x5 -> x4, Pallas kernels: 380 us -> 373 us  [call(): pl.pallas_call(functools.partial(kernel, *mesh_sizes), out_shape=[jax.Sha...]
  transfers between devices with their start and end apart: 16 -> 16, of which waited for: 10 -> 9; matrix products, arithmetic and copies ran while one was open for 4% -> 4% of each run, Pallas kernels for 9% -> 10%
where the time goes in v7:
time: 512 us; the launch traced here: 503 us
  Pallas kernels  435 us (85%)
  waiting for transfers between devices  28.4 us (6%)
  other arithmetic  13.8 us (3%)
  local copies, waits for them, and re-layouts  13.6 us (3%)
  starting transfers between devices  11.1 us (2%)
    pallas_call x4, Pallas kernels, call(): pl.pallas_call(functools.partial(kernel, *mesh_sizes), out_shape=[jax.Sha...  373 us
    ppermute x16, waiting for transfers between devices, swap(): return lax.ppermute(value, 'seq', [(i, i ^ bit) for i in range(parts)])  28.4 us
    pallas_call x1, Pallas kernels, per_device(): pl.pallas_call(functools.partial(back_kernel, width), out_shape=[jax.Shap...  27.8 us
    pallas_call x2, Pallas kernels, widen_pieces(): pl.pallas_call(functools.partial(widen_pieces_kernel, count, steps), out_...  24.1 us
    ppermute x16, starting transfers between devices, swap(): return lax.ppermute(value, 'seq', [(i, i ^ bit) for i in range(parts)])  11.1 us
  transfers between devices with their start and end apart: 16, of which 9 were waited for; matrix products, arithmetic and copies ran while one was open for 4% of the time, Pallas kernels for 10%

profile of v7, /device:TPU:0, one launch (start us, length us, event | category | flops | bytes accessed | tf_op | source)
XLA Modules:
  0.0 502.6 jit_solution(16061875833530131437)
XLA Ops:
  0.7 0.6 maximum_bitcast_fusion.rates
  1.2 0.9 concatenate.12
  2.1 0.6 broadcast_in_dim.23.gain
  2.7 94.0 %shard_map.228 = (bf16[1024,2048]{1,0:T(8,128)(2,1)}, bf16[2048,384]{1,0:T(8,128)(2,1)}, bf16[256,2048]{1,0:T(8,128)(2,1)}, f32[1024,384]{1,0:T(8,128)}, bf16[10...) custom-call(bf16[128,2048]{1,0:T(8,128)(2,1)} %bitcast.44, ...), custom_call_target="tpu_custom_call" | custom-call | tf_op jit(solution)/shard_map/pallas_call | solution.py:1762
  96.7 126.1 %shard_map.229 = (bf16[2,512,1024]{2,1,0:T(8,128)(2,1)}, bf16[512,1024]{1,0:T(8,128)(2,1)}, bf16[512,1024]{1,0:T(8,128)(2,1)}, bf16[512,1024]{1,0:T(8,128)(2,1)}...) custom-call(bf16[128,2048]{1,0:T(8,128)(2,1)} %get-tuple-element.93., ...), custom_call_target="tpu_custom_call" | custom-call | tf_op jit(solution)/shard_map/pallas_call | solution.py:1762
  222.8 55.7 %shard_map.230 = (bf16[1024,2048]{1,0:T(8,128)(2,1)}, bf16[2,512,1024]{2,1,0:T(8,128)(2,1)}, f32[128,2048]{1,0:T(8,128)}) custom-call(bf16[128,2048]{1,0:T(8,128)(2,1)} %get-tuple-element.95.h, bf16[2,512,1024]{2,1,0:T(8,128)(2,1)} %get-tuple-element.96.s, bf16[4,128,2048]{2,1,0:T(8,128)(2,1)} %get-tuple-element.97.give, ...), custom_call_target="tpu_custom_call" | custom-call | tf_op jit(solution)/shard_map/pallas_call | solution.py:1762
  278.4 1.1 collective-permute-start
  279.5 1.0 collective-permute-start.1
  280.5 0.9 collective-permute-start.2
  281.5 1.1 collective-permute-start.3
  282.6 27.8 %shard_map.231 = (bf16[1024,384]{1,0:T(8,128)(2,1)}, bf16[2048,384]{1,0:T(8,128)(2,1)}, bf16[256,2048]{1,0:T(8,128)(2,1)}, f32[8,384]{1,0:T(8,128)}) custom-call(bf16[1024,2048]{1,0:T(8,128)(2,1)} %get-tuple-element.100.normed, bf16[1024,2048]{1,0:T(8,128)(2,1)} %get-tuple-element.106.middle, bf16[256,2048]{1,0:T(8,128)(2,1)} %get-tuple-element.107.out_slice, ...), custom_call_target="tpu_custom_call" | custom-call | flops 8053063680 | bytes 33554432 | tf_op jit(solution)/shard_map/pallas_call | solution.py:2000
  310.3 0.7 slice_reduce_fusion
  311.1 0.1 reshape_squeeze.3
  311.2 0.7 slice_bitcast_fusion.2
  311.9 0.1 select_maximum_fusion
  311.9 0.1 pad_maximum_fusion
  312.0 0.6 pad.9.slope
  312.6 0.0 collective-permute-done.rest_4_
  312.6 0.0 collective-permute-done.1.rest_5_
  312.7 13.1 %collective-permute-done.2.rest_6_ = bf16[512,1024]{1,0:T(8,128)(2,1)} collective-permute-done((bf16[512,1024]{1,0:T(8,128)(2,1)}, bf16[512,1024]{1,0:T(8,128)(2,1)}, u32[]{:S(2)}, u32[]{:S(2)}) %collective-permute-start.2) | collective-permute-done | bytes 1048608 | tf_op jit(solution)/shard_map/ppermute | solution.py:1993
  325.7 1.5 collective-permute-done.3.rest_7_
  327.2 96.9 %shard_map.232 = (f32[128,2048]{1,0:T(8,128)}, bf16[2048,1024]{1,0:T(8,128)(2,1)}, bf16[2048,1024]{1,0:T(8,128)(2,1)}, bf16[512,2048]{1,0:T(8,128)(2,1)}, bf16[8...) custom-call(bf16[1024,384]{1,0:T(8,128)(2,1)} %get-tuple-element.116, ...), custom_call_target="tpu_custom_call" | custom-call | tf_op jit(solution)/shard_map/pallas_call | solution.py:1762
  424.1 1.7 fusion
  425.7 0.1 collective-permute-start.4
  425.8 1.9 collective-permute-start.5
  427.7 1.5 copy.28
  429.2 4.3 convert_element_type.31
  433.5 2.5 convert_element_type.32
  436.1 10.2 %shard_map.233 = f32[2048,2048]{1,0:T(8,128)} custom-call(bf16[2048,1024]{1,0:T(8,128)(2,1)} %get-tuple-element.138.near, bf16[2048,1024]{1,0:T(8,128)(2,1)} %get-tuple-element.139.far), custom_call_target="tpu_custom_call" | custom-call | bytes 25165824 | tf_op jit(solution)/shard_map/pallas_call | solution.py:1777
  446.3 1.2 fusion.9
  447.5 0.5 copy-done.2
  448.0 0.3 copy-done.7
  448.4 1.2 fusion.6
  449.5 2.2 collective-permute-done.4.refs_1_
  451.7 0.1 collective-permute-done.5.refs_3_
  451.8 0.0 collective-permute-start.8
  451.8 1.7 collective-permute-start.6
  453.4 0.2 collective-permute-start.9
  453.7 0.3 collective-permute-start.10
  454.0 0.2 collective-permute-start.11
  454.2 0.3 collective-permute-done.8.refs_4_
  454.4 1.0 copy-done.6
  455.4 1.6 collective-permute-start.7
  457.0 0.6 pad_add_fusion.starts
  457.6 0.0 collective-permute-done.9.refs_5_
  457.6 0.4 collective-permute-done.10.refs_6_
  457.9 1.5 collective-permute-done.11.refs_7_
  459.4 12.0 %shard_map.234 = f32[2048,2048]{1,0:T(8,128)} custom-call(s32[4]{0:T(128)} %pad_add_fusion.starts, bf16[512,1024]{1,0:T(8,128)(2,1)} %get-tuple-element.157.refs_0_, bf16[512,1024]{1,0:T(8,128)(2,1)} %collective-permute-done.4.refs_1_, bf16[512,1024]{1,0:T(8,128)(2,1)} %get-tuple-element.159.refs_2_, bf16[512,1024]{1,0:T(8,128)(2,1)} %collective-permute-done.5.refs_3_, ...), custom_call_target="tpu_custom_call" | custom-call | bytes 25165824 | tf_op jit(solution)/shard_map/pallas_call | solution.py:1802
  471.5 6.2 %collective-permute-done.6.refs_1_ = bf16[512,1024]{1,0:T(8,128)(2,1)} collective-permute-done((bf16[512,1024]{1,0:T(8,128)(2,1)}, bf16[512,1024]{1,0:T(8,128)(2,1)}, u32[]{:S(2)}, u32[]{:S(2)}) %collective-permute-start.6) | collective-permute-done | bytes 1048608 | tf_op jit(solution)/shard_map/ppermute | solution.py:1993
  477.7 3.3 collective-permute-done.7.refs_3_
  480.9 0.0 collective-permute-start.12
  480.9 0.5 collective-permute-start.13
  481.4 0.0 collective-permute-start.14
  481.4 0.5 collective-permute-start.15
  481.9 2.1 fusion.8
  484.1 1.3 slice_bitcast_fusion
  485.4 1.5 fusion.10
  486.9 1.3 copy.29
  488.2 1.3 copy.30
  489.5 0.6 pad_add_fusion.1.starts
  490.2 0.0 collective-permute-done.12.refs_4_
  490.2 0.0 collective-permute-done.14.refs_6_
  490.2 0.0 collective-permute-done.15.refs_7_
  490.2 12.0 %shard_map.235 = f32[2048,2048]{1,0:T(8,128)} custom-call(s32[4]{0:T(128)} %pad_add_fusion.1.starts, bf16[512,1024]{1,0:T(8,128)(2,1)} %get-tuple-element.166.refs_0_, bf16[512,1024]{1,0:T(8,128)(2,1)} %collective-permute-done.6.refs_1_, bf16[512,1024]{1,0:T(8,128)(2,1)} %get-tuple-element.168.refs_2_, bf16[512,1024]{1,0:T(8,128)(2,1)} %collective-permute-done.7.refs_3_, ...), custom_call_target="tpu_custom_call" | custom-call | bytes 25165824 | tf_op jit(solution)/shard_map/pallas_call | solution.py:1802
  (22 shorter events, 0.1 us)
Async XLA Ops:
  278.4 34.2 %collective-permute-start = (bf16[512,1024]{1,0:T(8,128)(2,1)}, bf16[512,1024]{1,0:T(8,128)(2,1)}, u32[]{:S(2)}, u32[]{:S(2)}) collective-permute-start(bf16[512,1024]{1,0:T(8,128)(2,1)} %get-tuple-element.123.rest_0_), channel_id=1, source_target_pairs={{0,16},{4,20},{8,24},{12,28},{16,0},{20,4},{24,8},{28,12},{1,17},{... | collective-permute-start | bytes 3145736 | tf_op jit(solution)/shard_map/ppermute | solution.py:1993
  279.5 33.1 %collective-permute-start.1 = (bf16[512,1024]{1,0:T(8,128)(2,1)}, bf16[512,1024]{1,0:T(8,128)(2,1)}, u32[]{:S(2)}, u32[]{:S(2)}) collective-permute-start(bf16[512,1024]{1,0:T(8,128)(2,1)} %get-tuple-element.124.rest_1_), channel_id=1, source_target_pairs={{0,8},{4,12},{8,0},{12,4},{16,24},{20,28},{24,16},{28,20},{1,9},{5... | collective-permute-start | bytes 3145736 | tf_op jit(solution)/shard_map/ppermute | solution.py:1993
  280.5 45.2 %collective-permute-start.2 = (bf16[512,1024]{1,0:T(8,128)(2,1)}, bf16[512,1024]{1,0:T(8,128)(2,1)}, u32[]{:S(2)}, u32[]{:S(2)}) collective-permute-start(bf16[512,1024]{1,0:T(8,128)(2,1)} %get-tuple-element.125.rest_2_), channel_id=1, source_target_pairs={{0,16},{4,20},{8,24},{12,28},{16,0},{20,4},{24,8},{28,12},{1,17},{... | collective-permute-start | bytes 3145736 | tf_op jit(solution)/shard_map/ppermute | solution.py:1993
  281.5 45.7 %collective-permute-start.3 = (bf16[512,1024]{1,0:T(8,128)(2,1)}, bf16[512,1024]{1,0:T(8,128)(2,1)}, u32[]{:S(2)}, u32[]{:S(2)}) collective-permute-start(bf16[512,1024]{1,0:T(8,128)(2,1)} %get-tuple-element.126.rest_3_), channel_id=1, source_target_pairs={{0,8},{4,12},{8,0},{12,4},{16,24},{20,28},{24,16},{28,20},{1,9},{5... | collective-permute-start | bytes 3145736 | tf_op jit(solution)/shard_map/ppermute | solution.py:1993
  282.6 29.4 %copy-start.9 = (f32[1,2048]{1,0:T(1,128)S(1)}, f32[1,2048]{1,0:T(1,128)}, u32[]{:S(2)}) copy-start(f32[1,2048]{1,0:T(1,128)} %get-tuple-element.121) | copy-start | bytes 24580
  327.2 96.9 %copy-start.8 = (f32[2048]{0:T(1024)S(1)}, f32[2048]{0:T(1024)}, u32[]{:S(2)}) copy-start(f32[2048]{0:T(1024)} %param.15) | copy-start | bytes 24580
  425.7 25.9 %collective-permute-start.4 = (bf16[512,1024]{1,0:T(8,128)(2,1)}, bf16[512,1024]{1,0:T(8,128)(2,1)}, u32[]{:S(2)}, u32[]{:S(2)}) collective-permute-start(bf16[512,1024]{1,0:T(8,128)(2,1)} %get-tuple-element.157.refs_0_), channel_id=1, source_target_pairs={{0,8},{4,12},{8,0},{12,4},{16,24},{20,28},{24,16},{28,20},{1,9},{5... | collective-permute-start | bytes 3145736 | tf_op jit(solution)/shard_map/ppermute | solution.py:1993
  425.8 25.9 %collective-permute-start.5 = (bf16[512,1024]{1,0:T(8,128)(2,1)}, bf16[512,1024]{1,0:T(8,128)(2,1)}, u32[]{:S(2)}, u32[]{:S(2)}) collective-permute-start(bf16[512,1024]{1,0:T(8,128)(2,1)} %get-tuple-element.159.refs_2_), channel_id=1, source_target_pairs={{0,16},{4,20},{8,24},{12,28},{16,0},{20,4},{24,8},{28,12},{1,17},{... | collective-permute-start | bytes 3145736 | tf_op jit(solution)/shard_map/ppermute | solution.py:1993
  429.2 4.3 copy-start.4
  446.3 1.3 copy-start
  446.3 1.8 copy-start.2
  446.3 2.1 copy-start.7
  446.3 5.5 %copy-start.5 = (bf16[512,1024]{1,0:T(8,128)(2,1)S(1)}, bf16[512,1024]{1,0:T(8,128)(2,1)}, u32[]{:S(2)}) copy-start(bf16[512,1024]{1,0:T(8,128)(2,1)} %get-tuple-element.157.refs_0_) | copy-start | bytes 3145732
  451.8 2.7 collective-permute-start.8
  451.8 25.9 %collective-permute-start.6 = (bf16[512,1024]{1,0:T(8,128)(2,1)}, bf16[512,1024]{1,0:T(8,128)(2,1)}, u32[]{:S(2)}, u32[]{:S(2)}) collective-permute-start(bf16[512,1024]{1,0:T(8,128)(2,1)} %get-tuple-element.166.refs_0_), channel_id=1, source_target_pairs={{0,8},{4,12},{8,0},{12,4},{16,24},{20,28},{24,16},{28,20},{1,9},{5... | collective-permute-start | bytes 3145736 | tf_op jit(solution)/shard_map/ppermute | solution.py:1993
  453.4 4.1 collective-permute-start.9
  453.7 4.3 collective-permute-start.10
  454.0 5.5 %collective-permute-start.11 = (bf16[512,1024]{1,0:T(8,128)(2,1)}, bf16[512,1024]{1,0:T(8,128)(2,1)}, u32[]{:S(2)}, u32[]{:S(2)}) collective-permute-start(bf16[512,1024]{1,0:T(8,128)(2,1)} %collective-permute-done.5.refs_3_), channel_id=1, source_target_pairs={{0,4},{4,0},{8,12},{12,8},{16,20},{20,16},{24,28},{28,24},{1,5},{5... | collective-permute-start | bytes 3145736 | tf_op jit(solution)/shard_map/ppermute | solution.py:1993
  454.4 1.0 copy-start.6
  455.4 25.5 %collective-permute-start.7 = (bf16[512,1024]{1,0:T(8,128)(2,1)}, bf16[512,1024]{1,0:T(8,128)(2,1)}, u32[]{:S(2)}, u32[]{:S(2)}) collective-permute-start(bf16[512,1024]{1,0:T(8,128)(2,1)} %get-tuple-element.168.refs_2_), channel_id=1, source_target_pairs={{0,16},{4,20},{8,24},{12,28},{16,0},{20,4},{24,8},{28,12},{1,17},{... | collective-permute-start | bytes 3145736 | tf_op jit(solution)/shard_map/ppermute | solution.py:1993
  457.6 24.4 %copy-start.1 = (f32[128,2048]{1,0:T(8,128)S(1)}, f32[128,2048]{1,0:T(8,128)}, u32[]{:S(2)}) copy-start(f32[128,2048]{1,0:T(8,128)} %get-tuple-element.92.middle) | copy-start | bytes 3145732
  457.6 29.4 %copy-start.3 = (f32[8,512,1,64]{1,3,2,0:T(8,128)S(1)}, f32[8,512,1,64]{1,3,2,0:T(8,128)}, u32[]{:S(2)}) copy-start(f32[8,512,1,64]{1,3,2,0:T(8,128)} %get-tuple-element.187) | copy-start | bytes 3145732
  480.9 9.2 %collective-permute-start.12 = (bf16[512,1024]{1,0:T(8,128)(2,1)}, bf16[512,1024]{1,0:T(8,128)(2,1)}, u32[]{:S(2)}, u32[]{:S(2)}) collective-permute-start(bf16[512,1024]{1,0:T(8,128)(2,1)} %get-tuple-element.166.refs_0_), channel_id=1, source_target_pairs={{0,4},{4,0},{8,12},{12,8},{16,20},{20,16},{24,28},{28,24},{1,5},{5... | collective-permute-start | bytes 3145736 | tf_op jit(solution)/shard_map/ppermute | solution.py:1993
  480.9 9.2 %collective-permute-start.13 = (bf16[512,1024]{1,0:T(8,128)(2,1)}, bf16[512,1024]{1,0:T(8,128)(2,1)}, u32[]{:S(2)}, u32[]{:S(2)}) collective-permute-start(bf16[512,1024]{1,0:T(8,128)(2,1)} %collective-permute-done.6.refs_1_), channel_id=1, source_target_pairs={{0,4},{4,0},{8,12},{12,8},{16,20},{20,16},{24,28},{28,24},{1,5},{5... | collective-permute-start | bytes 3145736 | tf_op jit(solution)/shard_map/ppermute | solution.py:1993
  481.4 8.7 %collective-permute-start.14 = (bf16[512,1024]{1,0:T(8,128)(2,1)}, bf16[512,1024]{1,0:T(8,128)(2,1)}, u32[]{:S(2)}, u32[]{:S(2)}) collective-permute-start(bf16[512,1024]{1,0:T(8,128)(2,1)} %get-tuple-element.168.refs_2_), channel_id=1, source_target_pairs={{0,4},{4,0},{8,12},{12,8},{16,20},{20,16},{24,28},{28,24},{1,5},{5... | collective-permute-start | bytes 3145736 | tf_op jit(solution)/shard_map/ppermute | solution.py:1993
  481.4 8.7 %collective-permute-start.15 = (bf16[512,1024]{1,0:T(8,128)(2,1)}, bf16[512,1024]{1,0:T(8,128)(2,1)}, u32[]{:S(2)}, u32[]{:S(2)}) collective-permute-start(bf16[512,1024]{1,0:T(8,128)(2,1)} %collective-permute-done.7.refs_3_), channel_id=1, source_target_pairs={{0,4},{4,0},{8,12},{12,8},{16,20},{20,16},{24,28},{28,24},{1,5},{5... | collective-permute-start | bytes 3145736 | tf_op jit(solution)/shard_map/ppermute | solution.py:1993

commit v8 on v7

--- a/solution.py
+++ b/solution.py
@@ -589,29 +589,36 @@
 
     def stage(self, position):
         here = self.here
-        self.moved = {}
-        for color, bits in enumerate(here.colors()):
-            bit = bits[position]
-            done = sum(bits[:position])
-            for mask in range(here.parts // 2):
-                if mask * 2 & bit and not mask * 2 & done:
+        self.moved = getattr(self, "moved", {})
+        for onward in (True, False):
+            for color, bits in enumerate(here.colors()):
+                bit = bits[position]
+                done = sum(bits[:position])
+                for mask in range(here.parts // 2):
                     low = mask ^ (bit // 2)
-                    self.moved[(color, low)] = self.wire.send(
+                    if not mask * 2 & bit or mask * 2 & done:
+                        continue
+                    if self._onward(position, color, low) != onward:
+                        continue
+                    self.moved[(position, color, low)] = self.wire.send(
                         self.current.at[color, mask],
                         self.landing.at[position, color, low],
                         {"seq": here.at(bit)},
                     )
 
-    def settle(self, position, out):
+    def _onward(self, position, color, low):
+        bits = self.here.colors()[color]
+        return position + 1 < len(bits) and bool(low * 2 & bits[position + 1])
+
+    def settle(self, position, out, onward):
         half = self.model // 2
         last = position == len(self.here.chip_bits) - 1
-        for (color, low), copy in self.moved.items():
+        for (stage, color, low), copy in self.moved.items():
+            if stage != position or self._onward(position, color, low) != onward:
+                continue
             copy.wait_recv()
             mine = self.current.at[color, low]
-            if last:
-                target = out.at[:, pl.ds(color * half, half)]
-            else:
-                target = mine
+            target = out.at[:, pl.ds(color * half, half)] if last else mine
             add_rows(target, mine, self.landing.at[position, color, low])
 
 
@@ -645,9 +652,10 @@
     column = lax.broadcasted_iota(jnp.int32, (block, block), 1)
     allowed = row >= column
     contract = (((1,), (1,)), ((), ()))
-    totals = []
-    for number in range(heads // 2):
-        at = pl.ds(number * columns, columns)
+    lane = lax.broadcasted_iota(jnp.int32, (block, 128), 1)
+
+    def two_heads(number, table):
+        at = pl.ds(pl.multiple_of(number * columns, columns), columns)
         both = queries[rows, at]
         both = (both.astype(jnp.float32) * width**-0.5).astype(both.dtype)
         zero = jnp.zeros_like(both)
@@ -673,14 +681,13 @@
                     values[0:before, :],
                     preferred_element_type=jnp.float32,
                 )
-            totals.append(total)
+            table = jnp.where(lane == 2 * number + side, total, table)
             part = summed / total
             result = part if result is None else result + part
         out_rows[rows, at] = result.astype(out_rows.dtype)
-    lane = lax.broadcasted_iota(jnp.int32, (block, 128), 1)
-    table = jnp.ones((block, 128), jnp.float32)
-    for number, total in enumerate(totals):
-        table = jnp.where(lane == number, total, table)
+        return table
+
+    table = lax.fori_loop(0, heads // 2, two_heads, jnp.ones((block, 128), jnp.float32))
     logs[rows, :] = jnp.log(table)
 
 
@@ -693,47 +700,46 @@
     row = lax.broadcasted_iota(jnp.int32, (block, block), 0)
     column = lax.broadcasted_iota(jnp.int32, (block, block), 1)
     allowed = row >= column
+    lane = lax.broadcasted_iota(jnp.int32, (block, 2 * width), 1)
     across = (((1,), (1,)), ((), ()))
     down = (((0,), (0,)), ((), ()))
     f32 = jnp.float32
     spans = [(rows, True)] + ([(slice(0, before), False)] if before else [])
-    for number in range(heads // 2):
-        at = pl.ds(number * 2 * width, 2 * width)
-        both, both_grad = queries[rows, at], grads[rows, at]
-        product = both_grad.astype(f32) * outs[rows, at].astype(f32)
-        zero = jnp.zeros_like(both)
-        total = None
-        for side in (0, 1):
-            pick = (
-                (lambda value, nothing: pick_lanes(value, nothing, width))
-                if side == 0
-                else (lambda value, nothing: pick_lanes(nothing, value, width))
-            )
-            query, grad = pick(both, zero), pick(both_grad, zero)
-            scaled = (query.astype(f32) * scale).astype(query.dtype)
-            shift = jnp.sum(pick(product, jnp.zeros_like(product)), axis=1, keepdims=True)
-            head = 2 * number + side
-            log = logs[rows, head : head + 1]
-            for span, masked in spans:
-                scores = lax.dot_general(
-                    scaled, keys[0][span, :], across, preferred_element_type=f32
-                )
-                weights = jnp.exp(scores - log)
-                if masked:
-                    weights = jnp.where(allowed, weights, 0.0)
-                prob_grad = lax.dot_general(
-                    grad, values[0][span, :], across, preferred_element_type=f32
-                )
-                score_grad = (weights * (prob_grad - shift) * scale).astype(query.dtype)
-                part = jnp.dot(score_grad, keys[1 + side][span, :], preferred_element_type=f32)
-                total = part if total is None else total + part
-                key_back[span, :] += lax.dot_general(
-                    score_grad, query, down, preferred_element_type=f32
-                )
-                value_back[span, :] += lax.dot_general(
-                    weights.astype(query.dtype), grad, down, preferred_element_type=f32
-                )
+
+    def one_head(head, carry):
+        number, side = head // 2, head % 2
+        at = pl.ds(pl.multiple_of(number * 2 * width, 2 * width), 2 * width)
+        mine = lane // width == side
+        query = jnp.where(mine, queries[rows, at], 0)
+        grad = jnp.where(mine, grads[rows, at], 0)
+        scaled = (query.astype(f32) * scale).astype(query.dtype)
+        shift = jnp.sum(grad.astype(f32) * outs[rows, at].astype(f32), axis=1, keepdims=True)
+        log = jnp.sum(jnp.where(lane == head, logs[rows, :], 0.0), axis=1, keepdims=True)
+        total = query_back[rows, at]
+        for span, masked in spans:
+            scores = lax.dot_general(
+                scaled, keys[0, span, :], across, preferred_element_type=f32
+            )
+            weights = jnp.exp(scores - log)
+            if masked:
+                weights = jnp.where(allowed, weights, 0.0)
+            prob_grad = lax.dot_general(
+                grad, values[span, :], across, preferred_element_type=f32
+            )
+            score_grad = (weights * (prob_grad - shift) * scale).astype(query.dtype)
+            total = total + jnp.dot(
+                score_grad, keys[1 + side, span, :], preferred_element_type=f32
+            )
+            key_back[span, :] += lax.dot_general(
+                score_grad, query, down, preferred_element_type=f32
+            )
+            value_back[span, :] += lax.dot_general(
+                weights.astype(query.dtype), grad, down, preferred_element_type=f32
+            )
         query_back[rows, at] = total
+        return carry
+
+    lax.fori_loop(0, heads, one_head, 0)
 
 
 def back_kernel(
@@ -758,15 +764,16 @@
     query_back,
     key_back,
     value_back,
-    *twins,
+    keys,
+    values,
 ):
     length = normed.shape[0]
     block = min(256, length)
     blocks = length // block
     query_cols = queries.shape[1]
     heads = query_cols // width
-    keys, values = twins[:3], twins[3:]
     f32 = jnp.float32
+    query_back[...] = jnp.zeros_like(query_back)
     key_back[...] = jnp.zeros_like(key_back)
     value_back[...] = jnp.zeros_like(value_back)
 
@@ -778,13 +785,10 @@
         both = pair[at, :].astype(f32)
         swapped = pltpu.roll(both, width, 1)
         zero = jnp.zeros_like(both)
-        for refs, low, high in (
-            (keys, both, swapped),
-            (values, swapped, both),
-        ):
-            refs[0][at, :] = pick_lanes(low, high, width).astype(refs[0].dtype)
-            refs[1][at, :] = pick_lanes(low, zero, width).astype(refs[0].dtype)
-            refs[2][at, :] = pick_lanes(zero, high, width).astype(refs[0].dtype)
+        keys[0, at, :] = pick_lanes(both, swapped, width).astype(keys.dtype)
+        keys[1, at, :] = pick_lanes(both, zero, width).astype(keys.dtype)
+        keys[2, at, :] = pick_lanes(zero, swapped, width).astype(keys.dtype)
+        values[at, :] = pick_lanes(swapped, both, width).astype(values.dtype)
         return carry
 
     lax.fori_loop(0, blocks, ready, 0)
@@ -869,6 +873,20 @@
     mid_gain,
     gain,
     rates,
+    x_store,
+    w_store,
+    o_store,
+    proj_store,
+    query_store,
+    pair_store,
+    out_store,
+    log_store,
+    cosine_store,
+    sine_store,
+    group_store,
+    middle,
+    mid,
+    c_store,
     x_all,
     w_all,
     o_slice,
@@ -880,8 +898,6 @@
     cosine,
     sine,
     group,
-    middle,
-    mid,
     c_all,
     o_all,
     twin,
@@ -976,7 +992,7 @@
         0.0,
     ).astype(group.dtype)
     length = x_all.shape[0]
-    row_blocks(length // 2, 32, table_rows)
+    row_blocks(length, 32, table_rows)
     weights.members[0].arrive(1)
     if planes > 2:
         weights.members[0].start(2)
@@ -985,9 +1001,6 @@
     if planes > 2:
         weights.members[1].start(2)
     outer.start(1)
-    row_blocks(
-        length // 2, 32, lambda at: table_rows(pl.ds(at.start + length // 2, at.size))
-    )
     plane_rows.hops(2)
     spot = o_slice.at[pl.ds(pl.multiple_of(here.chip * rows, rows), rows)]
     deals = []
@@ -1008,6 +1021,13 @@
     for step in range(2, planes):
         weights.pass_on(step)
     plane_rows.finish()
+    stores = [
+        wire.local(x_all, x_store),
+        wire.local(w_all, w_store),
+        wire.local(cosine, cosine_store),
+        wire.local(sine, sine_store),
+        wire.local(group, group_store),
+    ]
     block = min(256, length)
     blocks = length // block
     heads = query_cols // width
@@ -1064,17 +1084,26 @@
             jnp.concatenate(chosen, axis=0), o_slice[:, at], preferred_element_type=f32
         )
 
+    stores += [
+        wire.local(o_slice, o_store),
+        wire.local(proj, proj_store),
+        wire.local(queries, query_store),
+        wire.local(pair, pair_store),
+        wire.local(out_rows, out_store),
+        wire.local(logs, log_store),
+    ]
     sums = PlaneScatter(wire, here, product, give, take, current, landing, model)
     sums.start()
     sums.join()
     sums.stage(0)
     stages = len(here.chip_bits)
     for stage in range(stages):
+        sums.settle(stage, middle, True)
+        if stage + 1 < stages:
+            sums.stage(stage + 1)
         if cot_waits:
             cots.pass_on(cot_waits.pop(0))
-        sums.settle(stage, middle)
-        if stage + 1 < stages:
-            sums.stage(stage + 1)
+        sums.settle(stage, middle, False)
 
     def mid_rows(at):
         value = x[at, :].astype(f32) + middle[at, :]
@@ -1082,15 +1111,18 @@
         factor = lax.rsqrt(jnp.mean(value * value, axis=-1, keepdims=True) + EPS)
         mid[at, :] = (value * factor * mid_gain[...]).astype(mid.dtype)
 
-    row_blocks(tokens, 32, mid_rows)
     for step in cot_waits:
         cots.pass_on(step)
+    cots.close()
     c_own.wait()
     across.wait_recv()
+    stores.append(wire.local(c_all, c_store))
+    row_blocks(tokens, 32, mid_rows)
+    for copy in stores:
+        copy.wait()
     wire.close()
     weights.close()
     outer.close()
-    cots.close()
 
 
 def feed_kernel(
@@ -1104,10 +1136,8 @@
     up_weight,
     down_weight,
     s_down,
-    s_gate_a,
-    s_gate_b,
-    s_up_a,
-    s_up_b,
+    s_first,
+    s_second,
     mid,
     mid_half,
     mid_slope,
@@ -1118,8 +1148,7 @@
     down_half,
     mids,
     hidden,
-    gate_grads,
-    lifted_grads,
+    unit_grads,
     away,
     *rest,
 ):
@@ -1162,8 +1191,8 @@
             sigma = 1.0 / (1.0 + jnp.exp(-gate))
             active = gate * sigma
             hidden[rows, at] = (active * lifted).astype(hidden.dtype)
-            lifted_grads[rows, at] = (hidden_grad * active).astype(hidden.dtype)
-            gate_grads[rows, at] = (
+            unit_grads[1, rows, at] = (hidden_grad * active).astype(hidden.dtype)
+            unit_grads[0, rows, at] = (
                 hidden_grad * lifted * sigma * (1.0 + gate * (1.0 - sigma))
             ).astype(hidden.dtype)
             return carry
@@ -1196,41 +1225,43 @@
         lax.fori_loop(0, ups + downs, arrived, 0)
 
     flat_mids = mids.reshape(2 * planes * tokens, model)
-    pairs = ((cots, hidden), (flat_mids, gate_grads), (flat_mids, lifted_grads))
     quarter = model // 4
     moved = {}
 
-    def gradient(target, pair, start):
-        left, right = pair
+    def gradients(left, right, target, start, count):
+        parts_of = quarter // 256
 
         def part(number, carry):
-            at = pl.ds(pl.multiple_of(start + number * 256, 256), 256)
-            target[pl.ds(pl.multiple_of(number * 256, 256), 256), :] = lax.dot_general(
+            k, inside = number // parts_of, number % parts_of * 256
+            at = pl.ds(pl.multiple_of(start(k) + inside, 256), 256)
+            target(k)[pl.ds(pl.multiple_of(inside, 256), 256), :] = lax.dot_general(
                 left[:, at],
-                right[...],
+                right(k)[...],
                 (((0,), (0,)), ((), ())),
                 preferred_element_type=jnp.float32,
-            ).astype(target.dtype)
+            ).astype(away.dtype)
             return carry
 
-        lax.fori_loop(0, quarter // 256, part, 0)
+        lax.fori_loop(0, count * parts_of, part, 0)
 
     def first_half(color, mine):
-        bit = here.colors()[color][0]
-        side = here.side(bit) if mine else 1 - here.side(bit)
+        sides = [here.side(bits[0]) if mine else 1 - here.side(bits[0]) for bits in here.colors()]
+        if isinstance(color, int):
+            side = sides[color]
+        else:
+            side = sides[0] * (1 - color) + sides[1] * color
         return pl.multiple_of(color * (model // 2) + side * quarter, quarter)
 
     def send_away(number):
         for color, bits in enumerate(here.colors()):
-            gradient(away.at[number, color], pairs[number], first_half(color, False))
             moved[(number, color)] = wire.send(
                 away.at[number, color], landings[0].at[number, color], {"seq": here.at(bits[0])}
             )
 
     def mid_term(target, core):
         rows = [pl.ds(pl.multiple_of((2 * p + core) * tokens, tokens), tokens) for p in range(planes)]
-        gates = jnp.concatenate([gate_grads[at, :] for at in rows], axis=0)
-        lifts = jnp.concatenate([lifted_grads[at, :] for at in rows], axis=0)
+        gates = jnp.concatenate([unit_grads[0, at, :] for at in rows], axis=0)
+        lifts = jnp.concatenate([unit_grads[1, at, :] for at in rows], axis=0)
 
         def part(number, carry):
             at = pl.ds(pl.multiple_of(number * 256, 256), 256)
@@ -1258,14 +1289,28 @@
 
         lax.fori_loop(0, model // 256, part, 0)
 
+    gradients(
+        cots,
+        lambda k: hidden,
+        lambda k: away.at[0, k],
+        lambda k: first_half(k, False),
+        2,
+    )
     send_away(0)
     swaps = TokenSum(wire, here, current, take, line_landing)
     mid_term(give, 1 - here.core)
     swaps.start(give)
-    send_away(1)
     mid_term(current, here.core)
     swaps.join()
     swaps.step(1)
+    gradients(
+        flat_mids,
+        lambda k: unit_grads.at[k // 2],
+        lambda k: away.at[1 + k // 2, k % 2],
+        lambda k: first_half(k % 2, False),
+        4,
+    )
+    send_away(1)
     send_away(2)
     for step in range(2, planes):
         swaps.step(step)
@@ -1273,7 +1318,7 @@
     def final(number, color):
         if number == 0:
             return s_down.at[color]
-        return ((s_gate_a, s_gate_b), (s_up_a, s_up_b))[number - 1][color]
+        return (s_first, s_second)[color].at[number - 1]
 
     wire.sent(swaps.across)
     down_term(give, 1 - here.core)
@@ -1281,12 +1326,27 @@
     handed = [wire.local(give, down_give), wire.local(take, down_keep)]
     rows = quarter
     keeps = {}
+    if stages > 1:
+        for copy in moved.values():
+            wire.sent(copy)
+    gradients(
+        cots,
+        lambda k: hidden,
+        lambda k: s_down.at[k] if stages == 1 else away.at[0, k],
+        lambda k: first_half(k, True),
+        2,
+    )
+    for color in (0, 1):
+        gradients(
+            flat_mids,
+            lambda k: unit_grads.at[k],
+            lambda k: (s_first, s_second)[color].at[k] if stages == 1 else away.at[1 + k, color],
+            lambda k: first_half(color, True),
+            2,
+        )
     for number in range(3):
         for color in (0, 1):
             keep = final(number, color) if stages == 1 else away.at[number, color]
-            if stages > 1:
-                wire.sent(moved[(number, color)])
-            gradient(keep, pairs[number], first_half(color, True))
             keeps[(number, color)] = (keep, 0)
     swaps.finish(mid)
     f32 = jnp.float32
@@ -1386,7 +1446,7 @@
 
 
 def spread_kernel(
-    parts, planes, h, s, give, keep, h_all, t, block, current, take, line_landing, *sems
+    parts, planes, h, s, give, keep, h_store, t, block, h_all, current, take, line_landing, *sems
 ):
     here = Place(parts, planes)
     wire = Wire(*sems)
@@ -1419,11 +1479,13 @@
     if planes <= 3:
         rows.hops(2)
     rows.finish()
+    own.wait()
+    store = wire.local(h_all, h_store)
     for color in (0, 1):
         moved[color].wait_recv()
         add_rows(t.at[color], t.at[color], s.at[color])
-    own.wait()
     swaps.finish(block)
+    store.wait()
     wire.close()
     swaps.close()
 
@@ -1440,8 +1502,7 @@
     slope,
     *rest,
 ):
-    sent, rest = rest[:4], rest[4:]
-    came, rest = rest[:4], rest[4:]
+    sent, came, rest = rest[:2], rest[2:4], rest[4:]
     out, near, far, query_all, pair_all, outer_all, slope_out, *rest = rest
     joined, rest = rest[:4], rest[4:]
     (
@@ -1513,8 +1574,8 @@
     for number in range(4):
         loads.append(
             (
-                wire.local(sent[number], left.at[number]),
-                wire.local(came[number], right.at[number]),
+                wire.local(sent[number % 2].at[number // 2], left.at[number]),
+                wire.local(came[number % 2].at[number // 2], right.at[number]),
             )
         )
     heads.step(2)
@@ -1538,15 +1599,14 @@
     stages = len(here.chip_bits)
     for step in range(3, planes):
         heads.step(step)
-    rows.settle(0, out)
     for stage in range(1, stages):
+        rows.settle(stage - 1, out, True)
         rows.stage(stage)
+        rows.settle(stage - 1, out, False)
         if stage + 1 < planes:
             outer.step(stage + 1)
         if stage == 1:
             heads.finish(head_sum)
-        if stage + 1 < stages:
-            rows.settle(stage, out)
     half, half_out = shard // 2, rows_out // 2
 
     def seat_columns(seat):
@@ -1595,7 +1655,7 @@
 
     weights[1].start()
     weights[1].own()
-    rows.settle(stages - 1, out)
+    rows.settle(stages - 1, out, False)
     slope_sums[0] = slope[...]
     value = source[...].astype(jnp.float32)
     factor = lax.rsqrt(jnp.mean(value * value, axis=-1, keepdims=True) + EPS)
@@ -1733,7 +1793,7 @@
 
 
 def widen_pieces_kernel(count, steps, starts, *refs):
-    nears, fars, out = refs[:count], refs[count : 2 * count], refs[2 * count]
+    nears, fars, out = refs[:count], refs[count : 2 * count], refs[-1]
     core = lax.axis_index("seq") % 2
     units = nears[0].shape[1]
     index = pl.program_id(0)
@@ -1745,6 +1805,30 @@
             other = pl.ds(pl.multiple_of((1 - core) * units, units), units)
             out[:, own] = near[...].astype(out.dtype)
             out[:, other] = far[...].astype(out.dtype)
+
+
+def results_kernel(
+    copies, width, query, pair, outer, slope, grad_query, grad_key, grad_value, grad_output, *gains
+):
+    f32 = jnp.float32
+    grad_query[...] = query[...].astype(f32)
+    grad_output[...] = outer[...].astype(f32)
+    columns = 2 * width
+    for number in range(pair.shape[0] // (2 * copies)):
+        low, high = (
+            sum(
+                pair[(2 * number + side) * copies + copy].astype(f32) for copy in range(copies)
+            )
+            for side in (0, 1)
+        )
+        at = pl.ds(number * columns, columns)
+        grad_key[:, at] = pick_lanes(low, pltpu.roll(high, width, 1), width)
+        grad_value[:, at] = pick_lanes(pltpu.roll(low, width, 1), high, width)
+    in_slope, mid_slope, query_slope, key_slope = gains
+    in_slope[...] = slope[0:1, :]
+    mid_slope[...] = slope[1:2, :]
+    query_slope[...] = slope[2:3, 0:width]
+    key_slope[...] = slope[3:4, 0:width]
 
 
 SENDS, LOCALS = 192, 32
@@ -1786,12 +1870,12 @@
     )(near, far)
 
 
-def widen_pieces(pieces, fars):
+def widen_pieces(pieces, fars, whole=None, into=None):
     rows, units = fars[0].shape
     count = len(fars)
     step = min(256, rows)
     steps = rows // step
-    starts = jnp.stack([jnp.asarray(start, jnp.int32) // step for start, _ in pieces])
+    starts = jnp.stack([jnp.asarray(start, jnp.int32) >> (step.bit_length() - 1) for start, _ in pieces])
 
     def block(number):
         return pl.BlockSpec(
@@ -1799,21 +1883,60 @@
             lambda index, starts: (jnp.clip(index - number * steps, 0, steps - 1), 0),
         )
 
+    more = () if into is None else (into,)
     return pl.pallas_call(
         functools.partial(widen_pieces_kernel, count, steps),
-        out_shape=jax.ShapeDtypeStruct((count * rows, 2 * units), jnp.float32),
+        out_shape=jax.ShapeDtypeStruct((whole or count * rows, 2 * units), jnp.float32),
         grid_spec=pltpu.PrefetchScalarGridSpec(
             num_scalar_prefetch=1,
             grid=(count * steps,),
-            in_specs=[block(number) for number in range(count)] * 2,
+            in_specs=[block(number) for number in range(count)] * 2
+            + [pl.BlockSpec(memory_space=pl.ANY) for _ in more],
             out_specs=pl.BlockSpec(
                 (step, 2 * units), lambda index, starts: (starts[index // steps] + index % steps, 0)
             ),
         ),
+        input_output_aliases={2 * count + 1: 0} if more else {},
         cost_estimate=pl.CostEstimate(
             flops=0, transcendentals=0, bytes_accessed=12 * count * rows * units
         ),
-    )(starts, *[value for _, value in pieces], *fars)
+    )(starts, *[value for _, value in pieces], *fars, *more)
+
+
+def results(copies, width, query, pair, outer, slope):
+    shard, model = query.shape
+    seats = pair.shape[0]
+    step = min(128, shard)
+    f32 = jnp.float32
+    pair_cols = seats // copies * width
+    row = pl.BlockSpec((step, model), lambda index: (index, 0))
+    row_pair = pl.BlockSpec((step, pair_cols), lambda index: (index, 0))
+    fixed = lambda *shape: pl.BlockSpec(shape, lambda index: (0, 0))
+    return pl.pallas_call(
+        functools.partial(results_kernel, copies, width),
+        grid=(shard // step,),
+        out_shape=[
+            jax.ShapeDtypeStruct((shard, model), f32),
+            jax.ShapeDtypeStruct((shard, pair_cols), f32),
+            jax.ShapeDtypeStruct((shard, pair_cols), f32),
+            jax.ShapeDtypeStruct((shard, model), f32),
+            jax.ShapeDtypeStruct((1, model), f32),
+            jax.ShapeDtypeStruct((1, model), f32),
+            jax.ShapeDtypeStruct((1, width), f32),
+            jax.ShapeDtypeStruct((1, width), f32),
+        ],
+        in_specs=[
+            row,
+            pl.BlockSpec((seats, step, 2 * width), lambda index: (0, index, 0)),
+            row,
+            fixed(8, model),
+        ],
+        out_specs=[row, row_pair, row_pair, row]
+        + [fixed(1, model), fixed(1, model), fixed(1, width), fixed(1, width)],
+        cost_estimate=pl.CostEstimate(
+            flops=0, transcendentals=0, bytes_accessed=16 * shard * model
+        ),
+    )(query, pair, outer, slope)
 
 
 VMEM_BYTES = 67_000_000
@@ -1871,6 +1994,20 @@
         ((halvings + 1, 2, chips, tokens, half), bf16),
     ]
     mid_gain = feedforward_gain[None, :]
+    kept = [
+        ((length, model), bf16),
+        ((model, head_cols), bf16),
+        ((query_cols, model), bf16),
+        ((length, head_cols), f32),
+        ((length, query_cols), bf16),
+        ((length, 2 * width), bf16),
+        ((length, query_cols), bf16),
+        ((length, 128), f32),
+        ((length, 2 * width), f32),
+        ((length, 2 * width), f32),
+        ((head_cols, head_cols), bf16),
+        ((planes, 2, tokens, model), bf16),
+    ]
     (
         normed_all,
         head_full,
@@ -1903,26 +2040,13 @@
             rates,
         ),
         (True, True, False, False, False, False, True, True, True, True),
-        [
-            ((length, model), bf16),
-            ((model, head_cols), bf16),
-            ((query_cols, model), bf16),
-            ((length, head_cols), f32),
-            ((length, query_cols), bf16),
-            ((length, 2 * width), bf16),
-            ((length, query_cols), bf16),
-            ((length, 128), f32),
-            ((length, 2 * width), f32),
-            ((length, 2 * width), f32),
-            ((head_cols, head_cols), bf16),
-            ((tokens, model), f32),
-            ((tokens, model), bf16),
-            ((planes, 2, tokens, model), bf16),
-        ],
-        [((planes, piece_rows, model), bf16)]
+        kept[:11] + [((tokens, model), f32), ((tokens, model), bf16)] + kept[11:],
+        kept
+        + [((planes, piece_rows, model), bf16)]
         + [((length, 2 * width), bf16)] * 3
         + [((shard, 2 * width), bf16)] * 2
         + scatter_scratch,
+        [False] * 11 + [True] * 2 + [False],
     )
     tables = (gain_row, cosine, sine, group)
 
@@ -1936,10 +2060,8 @@
     acts = (2 * planes * tokens, units)
     (
         s_down,
-        s_gate_a,
-        s_gate_b,
-        s_up_a,
-        s_up_b,
+        s_first,
+        s_second,
         middle_grad,
         middle_half,
         mid_slope,
@@ -1959,8 +2081,7 @@
             down_weight,
         ),
         (True, True, True, True, False, False, False),
-        [((2, last_rows, units), bf16)]
-        + [((last_rows, units), bf16)] * 4
+        [((2, last_rows, units), bf16)] * 3
         + [
             ((tokens, model), f32),
             ((tokens, model), bf16),
@@ -1970,12 +2091,12 @@
         ],
         [((model, units), bf16)] * 3
         + [((planes, 2, tokens, model), bf16)]
-        + [(acts, bf16)] * 3
+        + [(acts, bf16), ((2,) + acts, bf16)]
         + [((3, 2, quarter, units), bf16)]
         + [((3, 2, quarter >> stage, units), bf16) for stage in range(halvings)]
         + [(rows_shape, bf16)]
         + line_scratch,
-        [True] * 8 + [False] * 2,
+        [True] * 6 + [False] * 2,
     )
 
     middle_all, t_down, down_sum = call(
@@ -1985,16 +2106,16 @@
         (middle_half, s_down, down_give, down_keep),
         (True, True, False, False),
         [((length, model), bf16), ((2, last_rows, units), bf16), ((tokens, model), f32)],
-        line_scratch,
-    )
-    block_rows = middle + down_sum
+        [((length, model), bf16)] + line_scratch,
+        [False, True, True],
+    )
 
     def swap(value, bit):
         return lax.ppermute(value, "seq", [(i, i ^ bit) for i in range(parts)])
 
-    *sent, middle_all = lax.optimization_barrier((s_gate_a, s_gate_b, s_up_a, s_up_b, middle_all))
+    *sent, middle_all = lax.optimization_barrier((s_first, s_second, middle_all))
     bit_orders = ([2 << i for i in range(halvings + 1)], [chips >> i for i in range(halvings + 1)])
-    came = [swap(piece, bit_orders[number % 2][-1]) for number, piece in enumerate(sent)]
+    came = [swap(value, order[-1]) for value, order in zip(sent, bit_orders)]
 
     vmem = pl.BlockSpec(memory_space=pltpu.VMEM)
     halves, head_part, out_part, head_slopes = pl.pallas_call(
@@ -2013,7 +2134,7 @@
             pltpu.VMEM((length, 2 * width), f32),
             pltpu.VMEM((length, 2 * width), f32),
         ]
-        + [pltpu.VMEM((length, 2 * width), bf16)] * 6,
+        + [pltpu.VMEM((3, length, 2 * width), bf16), pltpu.VMEM((length, 2 * width), bf16)],
         compiler_params=pltpu.CompilerParams(vmem_limit_bytes=VMEM_BYTES),
         cost_estimate=pl.CostEstimate(
             flops=10 * length * model * head_cols,
@@ -2032,13 +2153,12 @@
         *tables,
     )
     head_part = head_part.reshape(planes, shard, head_cols)
-    query_slope = head_slopes[0, :query_cols].reshape(local_groups, width).sum(axis=0)
+    query_slope = head_slopes[:1, :query_cols].reshape(local_groups, width).sum(axis=0)
     key_slope = head_slopes[0, query_cols : query_cols + width]
-
-    gains = jnp.concatenate([query_slope, key_slope])
-    gains = jnp.pad(gains, (0, model - gains.shape[0]))
-    slopes = jnp.concatenate([jnp.zeros_like(mid_slope), mid_slope, gains[None, :]], axis=0)
-    slopes = jnp.pad(slopes, ((0, 5), (0, 0)))
+    gains = jnp.pad(jnp.stack([query_slope, key_slope]), ((0, 0), (0, model - width)))
+    slopes = jnp.concatenate(
+        [jnp.zeros_like(mid_slope), mid_slope, gains, jnp.zeros((4, model), f32)], axis=0
+    )
     rounds = (parts * planes).bit_length() - 1
     side = ((model, units), bf16)
     piece = ((last_rows, units), bf16)
@@ -2047,7 +2167,7 @@
         sizes,
         5,
         (halves, head_full, head_part, out_part, t_down, rows_in, slopes, *sent, *came),
-        (True, True, False, False, True, True, True) + (False,) * 8,
+        (True, True, False, False, True, True, True) + (False,) * 4,
         [
             ((tokens, model), f32),
             side,
@@ -2100,22 +2220,30 @@
 
     gate_pieces = plane_pieces(pieces[:2])
     grad_down = widen(near_down, far_down)
-    grad_query = query_all.astype(f32)
-    grad_pair = pair_all.astype(f32)
-    grad_pair = grad_pair.reshape(parts // copies, copies, shard, 2, width).sum(axis=1)
-    grad_key = grad_pair[:, :, 0].transpose(1, 0, 2).reshape(shard, -1)
-    grad_value = grad_pair[:, :, 1].transpose(1, 0, 2).reshape(shard, -1)
-    grad_output = outer_all.astype(f32)
-    written = (grad_down, grad_query, grad_key, grad_value, grad_output, input_rows)
-    pieces[2:], gate_pieces, written = lax.optimization_barrier((pieces[2:], gate_pieces, written))
-    grad_down, grad_query, grad_key, grad_value, grad_output, input_rows = written
+    (
+        grad_query,
+        grad_key,
+        grad_value,
+        grad_output,
+        attention_slope,
+        feedforward_slope,
+        query_slope,
+        key_slope,
+    ) = results(copies, width, query_all, pair_all, outer_all, slopes)
+    block_out = (middle + down_sum).astype(bf16).reshape(1, tokens, model)
+    pieces[2:], grad_down = lax.optimization_barrier((pieces[2:], grad_down))
     up_pieces = plane_pieces(pieces[2:])
+    written = (grad_down, grad_query, grad_key, grad_value, grad_output, input_rows, block_out)
+    gate_pieces, written = lax.optimization_barrier((gate_pieces, written))
+    grad_down, grad_query, grad_key, grad_value, grad_output, input_rows, block_out = written
     grad_gate = widen_pieces(gate_pieces, [swap(value, 1) for _, value in gate_pieces])
-    up_pieces, grad_gate = lax.optimization_barrier((up_pieces, grad_gate))
-    grad_up = widen_pieces(up_pieces, [swap(value, 1) for _, value in up_pieces])
-    attention_slope, feedforward_slope = slopes[0], slopes[1]
-    query_slope, key_slope = slopes[2, :width], slopes[2, width : 2 * width]
-    block_out = block_rows.astype(bf16).reshape(1, tokens, model)
+    own = [up_pieces[0], up_pieces[len(up_pieces) // 2]]
+    others = [piece for piece in up_pieces if all(piece is not mine for mine in own)]
+    grad_up = widen_pieces(own, [swap(value, 1) for _, value in own], model)
+    others, grad_gate, grad_up = lax.optimization_barrier((others, grad_gate, grad_up))
+    grad_up = widen_pieces(others, [swap(value, 1) for _, value in others], model, grad_up)
+    attention_slope, feedforward_slope = attention_slope[0], feedforward_slope[0]
+    query_slope, key_slope = query_slope[0], key_slope[0]
     input_grad = input_rows.reshape(1, tokens, model)
     return (
         block_out,

time: 512 us -> 493 us (0.963)
  local copies, waits for them, and re-layouts: 13.6 us -> 4 us
  other arithmetic: 13.8 us -> 8.45 us
    pallas_call x0 -> x1, Pallas kernels: none -> 7.04 us  [results(): pl.pallas_call(functools.partial(results_kernel, copies, width), grid=(sh...]
    pallas_call x4, Pallas kernels: 373 us -> 366 us  [call(): pl.pallas_call(functools.partial(kernel, *mesh_sizes), out_shape=[jax.Sha...]
    convert_element_type x2 -> x0, other arithmetic: 6.82 us -> none  [the longest x1 4.28 us: per_device(): grad_query = query_all.astype(f32)]
    ppermute x16 -> x14, waiting for transfers between devices: 28.4 us -> 24.2 us  [swap(): return lax.ppermute(value, 'seq', [(i, i ^ bit) for i in range(parts)])]
    ppermute x16 -> x14, starting transfers between devices: 11.1 us -> 7.09 us  [swap(): return lax.ppermute(value, 'seq', [(i, i ^ bit) for i in range(parts)])]
    pallas_call x2 -> x3, Pallas kernels: 24.1 us -> 26 us  [widen_pieces(): pl.pallas_call(functools.partial(widen_pieces_kernel, count, steps), out_...]
  transfers between devices with their start and end apart: 16 -> 14, of which waited for: 9 -> 9; matrix products, arithmetic and copies ran while one was open for 4% -> 2% of each run, Pallas kernels for 10% -> 14%
where the time goes in v8:
time: 493 us; the launch traced here: 484 us
  Pallas kernels  439 us (89%)
  waiting for transfers between devices  24.2 us (5%)
  other arithmetic  8.45 us (2%)
  starting transfers between devices  7.09 us (1%)
    pallas_call x4, Pallas kernels, call(): pl.pallas_call(functools.partial(kernel, *mesh_sizes), out_shape=[jax.Sha...  366 us
    pallas_call x1, Pallas kernels, per_device(): pl.pallas_call(functools.partial(back_kernel, width), out_shape=[jax.Shap...  30 us
    pallas_call x3, Pallas kernels, widen_pieces(): pl.pallas_call(functools.partial(widen_pieces_kernel, count, steps), out_...  26 us
    ppermute x14, waiting for transfers between devices, swap(): return lax.ppermute(value, 'seq', [(i, i ^ bit) for i in range(parts)])  24.2 us
    pallas_call x1, Pallas kernels, widen(): pl.pallas_call(widen_kernel, grid=(rows // step,), out_shape=jax.ShapeDty...  10.3 us
  transfers between devices with their start and end apart: 14, of which 9 were waited for; matrix products, arithmetic and copies ran while one was open for 2% of the time, Pallas kernels for 14%

profile of v8, /device:TPU:0, one launch (start us, length us, event | category | flops | bytes accessed | tf_op | source)
XLA Modules:
  0.0 483.9 jit_solution(9091622588779837310)
XLA Ops:
  0.7 0.6 maximum_bitcast_fusion.rates
  1.2 0.9 concatenate.9
  2.1 0.6 broadcast_in_dim.23.gain
  2.7 91.2 %shard_map.228 = (bf16[1024,2048]{1,0:T(8,128)(2,1)}, bf16[2048,384]{1,0:T(8,128)(2,1)}, bf16[256,2048]{1,0:T(8,128)(2,1)}, f32[1024,384]{1,0:T(8,128)}, bf16[10...) custom-call(bf16[128,2048]{1,0:T(8,128)(2,1)} %bitcast.28, ...), custom_call_target="tpu_custom_call" | custom-call | tf_op jit(solution)/shard_map/pallas_call | solution.py:1846
  93.9 127.0 %shard_map.229 = (bf16[2,512,1024]{2,1,0:T(8,128)(2,1)}, bf16[2,512,1024]{2,1,0:T(8,128)(2,1)}, bf16[2,512,1024]{2,1,0:T(8,128)(2,1)}, f32[128,2048]{1,0:T(8,128...) custom-call(bf16[128,2048]{1,0:T(8,128)(2,1)} %get-tuple-element.96., ...), custom_call_target="tpu_custom_call" | custom-call | tf_op jit(solution)/shard_map/pallas_call | solution.py:1846
  221.0 51.1 %shard_map.230 = (bf16[1024,2048]{1,0:T(8,128)(2,1)}, bf16[2,512,1024]{2,1,0:T(8,128)(2,1)}, f32[128,2048]{1,0:T(8,128)}) custom-call(bf16[128,2048]{1,0:T(8,128)(2,1)} %get-tuple-element.101.h, bf16[2,512,1024]{2,1,0:T(8,128)(2,1)} %get-tuple-element.102.s, bf16[4,128,2048]{2,1,0:T(8,128)(2,1)} %get-tuple-element.103.give, ...), custom_call_target="tpu_custom_call" | custom-call | tf_op jit(solution)/shard_map/pallas_call | solution.py:1846
  272.1 1.7 collective-permute-start
  273.8 0.4 collective-permute-start.1
  274.2 0.1 pad.16.clone
  274.3 0.0 copy-start.9
  274.3 30.0 %shard_map.231 = (bf16[1024,384]{1,0:T(8,128)(2,1)}, bf16[2048,384]{1,0:T(8,128)(2,1)}, bf16[256,2048]{1,0:T(8,128)(2,1)}, f32[8,384]{1,0:T(8,128)}) custom-call(bf16[1024,2048]{1,0:T(8,128)(2,1)} %get-tuple-element.95.normed, bf16[1024,2048]{1,0:T(8,128)(2,1)} %get-tuple-element.106.middle, bf16[256,2048]{1,0:T(8,128)(2,1)} %get-tuple-element.107.out_slice, ...), custom_call_target="tpu_custom_call" | custom-call | flops 8053063680 | bytes 33554432 | tf_op jit(solution)/shard_map/pallas_call | solution.py:2121
  304.3 0.7 slice.7
  305.0 0.7 slice_reduce_fusion
  305.7 0.1 reshape.64
  305.8 0.0 copy-done.9
  305.8 0.7 maximum_maximum_fusion.slope
  306.5 12.5 %collective-permute-done.rest_2_ = bf16[2,512,1024]{2,1,0:T(8,128)(2,1)} collective-permute-done((bf16[2,512,1024]{2,1,0:T(8,128)(2,1)}, bf16[2,512,1024]{2,1,0:T(8,128)(2,1)}, u32[]{:S(2)}, u32[]{:S(2)}) %collective-permute-start) | collective-permute-done | bytes 2097184 | tf_op jit(solution)/shard_map/ppermute | solution.py:2114
  319.0 0.9 collective-permute-done.1.rest_3_
  319.9 96.2 %shard_map.232 = (f32[128,2048]{1,0:T(8,128)}, bf16[2048,1024]{1,0:T(8,128)(2,1)}, bf16[2048,1024]{1,0:T(8,128)(2,1)}, bf16[512,2048]{1,0:T(8,128)(2,1)}, bf16[8...) custom-call(bf16[1024,384]{1,0:T(8,128)(2,1)} %get-tuple-element.116, ...), custom_call_target="tpu_custom_call" | custom-call | tf_op jit(solution)/shard_map/pallas_call | solution.py:1846
  416.2 1.6 collective-permute-start.2
  417.8 0.4 collective-permute-start.3
  418.2 2.5 fusion.8
  420.7 10.3 %shard_map.233 = f32[2048,2048]{1,0:T(8,128)} custom-call(bf16[2048,1024]{1,0:T(8,128)(2,1)} %get-tuple-element.136.near, bf16[2048,1024]{1,0:T(8,128)(2,1)} %get-tuple-element.137.far), custom_call_target="tpu_custom_call" | custom-call | bytes 25165824 | tf_op jit(solution)/shard_map/pallas_call | solution.py:1861
  431.0 0.0 collective-permute-start.10
  431.0 0.0 copy-done.2
  431.0 0.5 collective-permute-start.11
  431.5 7.0 %shard_map.234 = (f32[512,2048]{1,0:T(8,128)}, f32[512,512]{1,0:T(8,128)}, f32[512,512]{1,0:T(8,128)}, f32[512,2048]{1,0:T(8,128)}, f32[1,2048]{1,0:T(1,128)}, /...) custom-call(bf16[512,2048]{1,0:T(8,128)(2,1)} %get-tuple-element.139.query, ...), custom_call_target="tpu_custom_call" | custom-call | bytes 16777216 | tf_op jit(solution)/shard_map/pallas_call | solution.py:1915
  438.5 0.0 copy-done
  438.5 0.0 copy-done.1
  438.5 0.0 copy-done.8
  438.5 0.0 copy-start.3
  438.6 0.3 fusion
  438.9 2.4 fusion.6
  441.2 0.9 collective-permute-done.2.refs_1_
  442.1 1.3 collective-permute-done.3.refs_3_
  443.4 0.0 copy-done.3
  443.4 0.0 collective-permute-start.6
  443.4 0.5 collective-permute-start.7
  443.9 0.0 collective-permute-start.8
  443.9 0.0 collective-permute-done.10.refs_2_
  443.9 0.5 collective-permute-start.9
  444.4 0.0 collective-permute-done.11.refs_3_
  444.4 0.5 collective-permute-start.4
  444.9 1.2 collective-permute-done.6.refs_4_
  446.0 1.0 copy-done.6
  447.0 0.4 collective-permute-start.5
  447.4 0.7 pad_add_fusion.1.starts
  448.1 7.0 %shard_map.236.refs_4_ = f32[2048,2048]{1,0:T(8,128)} custom-call(s32[2]{0:T(128)} %pad_add_fusion.1.starts, bf16[512,1024]{1,0:T(8,128)(2,1)} %get-tuple-element.160.refs_0_, bf16[512,1024]{1,0:T(8,128)(2,1)} %get-tuple-element.161.refs_1_, bf16[512,1024]{1,0:T(8,128)(2,1)} %collective-permute-done.10.refs_2_, bf16[512,1024]{1,0:T(8,128)(2,1)} %collective-permute-done.11.refs_3_), custom_call_target="tpu_custom_call" | custom-call | bytes 12582912 | tf_op jit(solution)/shard_map/pallas_call | solution.py:1887
  455.1 0.7 pad_add_fusion.starts
  455.8 0.0 collective-permute-done.7.refs_5_
  455.8 0.0 collective-permute-done.8.refs_6_
  455.8 0.0 collective-permute-done.9.refs_7_
  455.8 12.0 %shard_map.235 = f32[2048,2048]{1,0:T(8,128)} custom-call(s32[4]{0:T(128)} %pad_add_fusion.starts, bf16[512,1024]{1,0:T(8,128)(2,1)} %get-tuple-element.166.refs_0_, bf16[512,1024]{1,0:T(8,128)(2,1)} %collective-permute-done.2.refs_1_, bf16[512,1024]{1,0:T(8,128)(2,1)} %get-tuple-element.168.refs_2_, bf16[512,1024]{1,0:T(8,128)(2,1)} %collective-permute-done.3.refs_3_, ...), custom_call_target="tpu_custom_call" | custom-call | bytes 25165824 | tf_op jit(solution)/shard_map/pallas_call | solution.py:1887
  467.8 1.9 collective-permute-done.4.refs_0_
  469.8 2.4 collective-permute-done.5.refs_1_
  472.2 0.0 collective-permute-start.12
  472.2 0.5 collective-permute-start.13
  472.7 0.7 pad_add_fusion.2.starts
  473.4 1.5 collective-permute-done.12.refs_2_
  474.9 1.6 collective-permute-done.13.refs_3_
  476.5 0.0 copy-done.4
  476.5 0.0 copy-done.5
  476.5 0.0 copy-done.7
  476.5 7.0 %shard_map.237 = f32[2048,2048]{1,0:T(8,128)} custom-call(s32[2]{0:T(128)} %pad_add_fusion.2.starts, bf16[512,1024]{1,0:T(8,128)(2,1)} %copy-done.4, bf16[512,1024]{1,0:T(8,128)(2,1)} %copy-done.5, bf16[512,1024]{1,0:T(8,128)(2,1)} %copy-done.7, bf16[512,1024]{1,0:T(8,128)(2,1)} %collective-permute-done.13.refs_3_, ...), custom_call_target="tpu_custom_call", output_to_operand_aliasing={{}: (5, {})} | custom-call | bytes 12582912 | tf_op jit(solution)/shard_map/pallas_call | solution.py:1887
  (14 shorter events, 0.1 us)
Async XLA Ops:
  272.1 47.0 %collective-permute-start = (bf16[2,512,1024]{2,1,0:T(8,128)(2,1)}, bf16[2,512,1024]{2,1,0:T(8,128)(2,1)}, u32[]{:S(2)}, u32[]{:S(2)}) collective-permute-start(bf16[2,512,1024]{2,1,0:T(8,128)(2,1)} %get-tuple-element.123.rest_0_), channel_id=1, source_target_pairs={{0,16},{4,20},{8,24},{12,28},{16,0},{20,4},{24,8},{28,12},{1,17},{... | collective-permute-start | bytes 6291464 | tf_op jit(solution)/shard_map/ppermute | solution.py:2114
  273.8 46.1 %collective-permute-start.1 = (bf16[2,512,1024]{2,1,0:T(8,128)(2,1)}, bf16[2,512,1024]{2,1,0:T(8,128)(2,1)}, u32[]{:S(2)}, u32[]{:S(2)}) collective-permute-start(bf16[2,512,1024]{2,1,0:T(8,128)(2,1)} %get-tuple-element.124.rest_1_), channel_id=1, source_target_pairs={{0,8},{4,12},{8,0},{12,4},{16,24},{20,28},{24,16},{28,20},{1,9},{5... | collective-permute-start | bytes 6291464 | tf_op jit(solution)/shard_map/ppermute | solution.py:2114
  274.3 31.6 %copy-start.9 = (f32[1,2048]{1,0:T(1,128)S(1)}, f32[1,2048]{1,0:T(1,128)}, u32[]{:S(2)}) copy-start(f32[1,2048]{1,0:T(1,128)} %get-tuple-element.121) | copy-start | bytes 24580
  416.2 25.9 %collective-permute-start.2 = (bf16[512,1024]{1,0:T(8,128)(2,1)}, bf16[512,1024]{1,0:T(8,128)(2,1)}, u32[]{:S(2)}, u32[]{:S(2)}) collective-permute-start(bf16[512,1024]{1,0:T(8,128)(2,1)} %get-tuple-element.166.refs_0_), channel_id=1, source_target_pairs={{0,8},{4,12},{8,0},{12,4},{16,24},{20,28},{24,16},{28,20},{1,9},{5... | collective-permute-start | bytes 3145736 | tf_op jit(solution)/shard_map/ppermute | solution.py:2114
  417.8 25.6 %collective-permute-start.3 = (bf16[512,1024]{1,0:T(8,128)(2,1)}, bf16[512,1024]{1,0:T(8,128)(2,1)}, u32[]{:S(2)}, u32[]{:S(2)}) collective-permute-start(bf16[512,1024]{1,0:T(8,128)(2,1)} %get-tuple-element.168.refs_2_), channel_id=1, source_target_pairs={{0,16},{4,20},{8,24},{12,28},{16,0},{20,4},{24,8},{28,12},{1,17},{... | collective-permute-start | bytes 3145736 | tf_op jit(solution)/shard_map/ppermute | solution.py:2114
  420.7 10.3 %copy-start.2 = (bf16[512,1024]{1,0:T(8,128)(2,1)S(1)}, bf16[512,1024]{1,0:T(8,128)(2,1)}, u32[]{:S(2)}) copy-start(bf16[512,1024]{1,0:T(8,128)(2,1)} %get-tuple-element.161.refs_1_) | copy-start | bytes 3145732
  431.0 12.9 %collective-permute-start.10 = (bf16[512,1024]{1,0:T(8,128)(2,1)}, bf16[512,1024]{1,0:T(8,128)(2,1)}, u32[]{:S(2)}, u32[]{:S(2)}) collective-permute-start(bf16[512,1024]{1,0:T(8,128)(2,1)} %get-tuple-element.160.refs_0_), channel_id=1, source_target_pairs={{0,4},{4,0},{8,12},{12,8},{16,20},{20,16},{24,28},{28,24},{1,5},{5... | collective-permute-start | bytes 3145736 | tf_op jit(solution)/shard_map/ppermute | solution.py:2114
  431.0 13.4 %collective-permute-start.11 = (bf16[512,1024]{1,0:T(8,128)(2,1)S(1)}, bf16[512,1024]{1,0:T(8,128)(2,1)}, u32[]{:S(2)}, u32[]{:S(2)}) collective-permute-start(bf16[512,1024]{1,0:T(8,128)(2,1)S(1)} %copy-done.2), channel_id=1, source_target_pairs={{0,4},{4,0},{8,12},{12,8},{16,20},{20,16},{24,28},{28,24},{1,5},{5... | collective-permute-start | bytes 3145736 | tf_op jit(solution)/shard_map/ppermute | solution.py:2114
  431.5 7.1 %copy-start = (bf16[1,128,2048]{2,1,0:T(8,128)(2,1)S(1)}, bf16[1,128,2048]{2,1,0:T(8,128)(2,1)}, u32[]{:S(2)}) copy-start(bf16[1,128,2048]{2,1,0:T(8,128)(2,1)} %param.13) | copy-start | bytes 1572868
  431.5 7.1 %copy-start.1 = (f32[128,2048]{1,0:T(8,128)S(1)}, f32[128,2048]{1,0:T(8,128)}, u32[]{:S(2)}) copy-start(f32[128,2048]{1,0:T(8,128)} %get-tuple-element.148) | copy-start | bytes 3145732
  431.5 7.1 %copy-start.8 = (f32[2048]{0:T(1024)S(1)}, f32[2048]{0:T(1024)}, u32[]{:S(2)}) copy-start(f32[2048]{0:T(1024)} %param.15) | copy-start | bytes 24580
  438.5 4.8 copy-start.3
  443.4 2.7 collective-permute-start.6
  443.4 12.4 %collective-permute-start.7 = (bf16[512,1024]{1,0:T(8,128)(2,1)}, bf16[512,1024]{1,0:T(8,128)(2,1)}, u32[]{:S(2)}, u32[]{:S(2)}) collective-permute-start(bf16[512,1024]{1,0:T(8,128)(2,1)} %collective-permute-done.2.refs_1_), channel_id=1, source_target_pairs={{0,4},{4,0},{8,12},{12,8},{16,20},{20,16},{24,28},{28,24},{1,5},{5... | collective-permute-start | bytes 3145736 | tf_op jit(solution)/shard_map/ppermute | solution.py:2114
  443.9 11.9 %collective-permute-start.8 = (bf16[512,1024]{1,0:T(8,128)(2,1)}, bf16[512,1024]{1,0:T(8,128)(2,1)}, u32[]{:S(2)}, u32[]{:S(2)}) collective-permute-start(bf16[512,1024]{1,0:T(8,128)(2,1)} %get-tuple-element.168.refs_2_), channel_id=1, source_target_pairs={{0,4},{4,0},{8,12},{12,8},{16,20},{20,16},{24,28},{28,24},{1,5},{5... | collective-permute-start | bytes 3145736 | tf_op jit(solution)/shard_map/ppermute | solution.py:2114
  443.9 11.9 %collective-permute-start.9 = (bf16[512,1024]{1,0:T(8,128)(2,1)}, bf16[512,1024]{1,0:T(8,128)(2,1)}, u32[]{:S(2)}, u32[]{:S(2)}) collective-permute-start(bf16[512,1024]{1,0:T(8,128)(2,1)} %collective-permute-done.3.refs_3_), channel_id=1, source_target_pairs={{0,4},{4,0},{8,12},{12,8},{16,20},{20,16},{24,28},{28,24},{1,5},{5... | collective-permute-start | bytes 3145736 | tf_op jit(solution)/shard_map/ppermute | solution.py:2114
  444.4 25.3 %collective-permute-start.4 = (bf16[512,1024]{1,0:T(8,128)(2,1)}, bf16[512,1024]{1,0:T(8,128)(2,1)S(1)}, u32[]{:S(2)}, u32[]{:S(2)}) collective-permute-start(bf16[512,1024]{1,0:T(8,128)(2,1)} %get-tuple-element.160.refs_0_), channel_id=1, source_target_pairs={{0,8},{4,12},{8,0},{12,4},{16,24},{20,28},{24,16},{28,20},{1,9},{5... | collective-permute-start | bytes 3145736 | tf_op jit(solution)/shard_map/ppermute | solution.py:2114
  446.0 1.0 copy-start.6
  447.0 25.2 %collective-permute-start.5 = (bf16[512,1024]{1,0:T(8,128)(2,1)S(1)}, bf16[512,1024]{1,0:T(8,128)(2,1)S(1)}, u32[]{:S(2)}, u32[]{:S(2)}) collective-permute-start(bf16[512,1024]{1,0:T(8,128)(2,1)S(1)} %copy-done.2), channel_id=1, source_target_pairs={{0,16},{4,20},{8,24},{12,28},{16,0},{20,4},{24,8},{28,12},{1,17},{... | collective-permute-start | bytes 3145736 | tf_op jit(solution)/shard_map/ppermute | solution.py:2114
  469.7 6.7 %copy-start.4 = (bf16[512,1024]{1,0:T(8,128)(2,1)}, bf16[512,1024]{1,0:T(8,128)(2,1)S(1)}, u32[]{:S(2)}) copy-start(bf16[512,1024]{1,0:T(8,128)(2,1)S(1)} %collective-permute-done.4.refs_0_) | copy-start | bytes 3145732
  472.2 4.3 copy-start.5
  472.2 2.7 collective-permute-start.12
  472.2 4.3 collective-permute-start.13
  474.9 1.6 copy-start.7

commit v9 on v8

--- a/solution.py
+++ b/solution.py
@@ -1018,9 +1018,12 @@
 
     o_own.wait()
     deal(0)
+    plane_rows.finish()
+    block = min(256, length)
+    blocks = length // block
+
     for step in range(2, planes):
         weights.pass_on(step)
-    plane_rows.finish()
     stores = [
         wire.local(x_all, x_store),
         wire.local(w_all, w_store),
@@ -1028,8 +1031,6 @@
         wire.local(sine, sine_store),
         wire.local(group, group_store),
     ]
-    block = min(256, length)
-    blocks = length // block
     heads = query_cols // width
 
     def project(index, carry):
@@ -1062,9 +1063,8 @@
             step = waits.pop(0)
             outer.pass_on(step)
             deal(step)
-            if not waits or (step == 2 and planes > 3):
-                if len(waits) == planes - 3 or planes <= 3:
-                    cots.start(1)
+            if step == min(2, planes - 1):
+                cots.start(1)
         attend_block(
             index, block, width, heads, queries, pair, twin, left, right, out_rows, logs
         )
@@ -1129,27 +1129,33 @@
     parts,
     planes,
     m,
-    cots,
-    middle,
     mid_gain,
+    cots_whole,
+    middle_whole,
     gate_weight,
     up_weight,
     down_weight,
-    s_down,
-    s_first,
-    s_second,
-    mid,
     mid_half,
     mid_slope,
+    mid_store,
+    s_down,
+    s_early_a,
+    s_early_b,
+    s_late_a,
+    s_late_b,
     down_give,
     down_keep,
     gate_half,
     up_half,
     down_half,
+    cots,
+    middle,
+    mid,
     mids,
     hidden,
     unit_grads,
     away,
+    sums,
     *rest,
 ):
     here = Place(parts, planes)
@@ -1160,6 +1166,15 @@
     tokens, model = m.shape
     units = gate_half.shape[1]
     own_units = pl.ds(pl.multiple_of(here.core * units, units), units)
+    here.enter(here.seat_bits, line=True)
+
+    def spot(index):
+        return mids.at[index, here.core]
+
+    lines = gather_lines(wire, here, m, spot, spot)
+    lines.start(1)
+    across = wire.send(m, spot(here.plane), {"seq": here.at(1)})
+    own = wire.local(m, spot(here.plane))
     loads = [
         wire.local(whole.at[:, own_units], part)
         for whole, part in (
@@ -1168,15 +1183,7 @@
             (down_weight, down_half),
         )
     ]
-    here.enter(here.seat_bits, line=True)
-
-    def spot(index):
-        return mids.at[index, here.core]
-
-    lines = gather_lines(wire, here, m, spot, spot)
-    lines.start(1)
-    across = wire.send(m, spot(here.plane), {"seq": here.at(1)})
-    own = wire.local(m, spot(here.plane))
+    loads += [wire.local(cots_whole, cots), wire.local(middle_whole, middle)]
 
     def block(index):
         rows = pl.ds(pl.multiple_of(index * 2 * tokens, 2 * tokens), 2 * tokens)
@@ -1204,25 +1211,35 @@
     own.wait()
     across.wait_recv()
     plane = here.plane
-    block(plane)
-    for step in range(1, planes):
-        lines.pass_on(step)
-        ups = jnp.where(plane >= step, 1, 0)
-        downs = jnp.where(plane + step <= planes - 1, 1, 0)
-
-        def arrived(number, carry, step=step, ups=ups):
+
+    def arrivals(step, carry):
+        for number in range(1, planes):
+
+            @pl.when(step == number)
+            def _(number=number):
+                lines.pass_on(number)
+
+        own_turn = step == 0
+        ups = jnp.where(own_turn | (plane >= step), 1, 0)
+        downs = jnp.where(jnp.logical_not(own_turn) & (plane + step <= planes - 1), 1, 0)
+
+        def arrived(number, carry):
             from_up = (number == 0) & (ups == 1)
-            for way, chosen in ((0, from_up), (1, jnp.logical_not(from_up))):
-
-                @pl.when(chosen)
-                def _(way=way):
-                    for line in lines.members:
-                        line.shared[(step, way)].wait_recv()
+            for stage in range(1, planes):
+                for way, chosen in ((0, from_up), (1, jnp.logical_not(from_up))):
+
+                    @pl.when((step == stage) & chosen)
+                    def _(stage=stage, way=way):
+                        for line in lines.members:
+                            line.shared[(stage, way)].wait_recv()
 
             block(jnp.where(from_up, plane + planes - step, plane + step) % planes)
             return carry
 
         lax.fori_loop(0, ups + downs, arrived, 0)
+        return carry
+
+    lax.fori_loop(0, planes, arrivals, 0)
 
     flat_mids = mids.reshape(2 * planes * tokens, model)
     quarter = model // 4
@@ -1315,10 +1332,20 @@
     for step in range(2, planes):
         swaps.step(step)
 
-    def final(number, color):
+    early = s_early_a.shape[0]
+
+    def store(number, color):
+        done = sums.at[number, color]
         if number == 0:
-            return s_down.at[color]
-        return (s_first, s_second)[color].at[number - 1]
+            return [wire.local(done, s_down.at[color])]
+        late = (s_late_a, s_late_b)[color]
+        size = done.shape[0]
+        if number == 1:
+            return [
+                wire.local(done.at[pl.ds(0, early)], (s_early_a, s_early_b)[color]),
+                wire.local(done.at[pl.ds(early, size - early)], late.at[pl.ds(0, size - early)]),
+            ]
+        return [wire.local(done, late.at[pl.ds(size - early, size)])]
 
     wire.sent(swaps.across)
     down_term(give, 1 - here.core)
@@ -1329,25 +1356,24 @@
     if stages > 1:
         for copy in moved.values():
             wire.sent(copy)
+    keep_in = sums if stages == 1 else away
     gradients(
         cots,
         lambda k: hidden,
-        lambda k: s_down.at[k] if stages == 1 else away.at[0, k],
+        lambda k: keep_in.at[0, k],
         lambda k: first_half(k, True),
         2,
     )
-    for color in (0, 1):
-        gradients(
-            flat_mids,
-            lambda k: unit_grads.at[k],
-            lambda k: (s_first, s_second)[color].at[k] if stages == 1 else away.at[1 + k, color],
-            lambda k: first_half(color, True),
-            2,
-        )
+    gradients(
+        flat_mids,
+        lambda k: unit_grads.at[k // 2],
+        lambda k: keep_in.at[1 + k // 2, k % 2],
+        lambda k: first_half(k % 2, True),
+        4,
+    )
     for number in range(3):
         for color in (0, 1):
-            keep = final(number, color) if stages == 1 else away.at[number, color]
-            keeps[(number, color)] = (keep, 0)
+            keeps[(number, color)] = (keep_in.at[number, color], 0)
     swaps.finish(mid)
     f32 = jnp.float32
 
@@ -1369,6 +1395,7 @@
     mid_slope[...] = lax.fori_loop(
         0, tokens // 32, norm_back_rows, jnp.zeros((1, model), f32)
     )
+    handed.append(wire.local(mid, mid_store))
     for stage in range(stages):
         last = stage == stages - 1
         for number in range(3):
@@ -1377,7 +1404,10 @@
                 moved[(number, color)].wait_recv()
                 mine = keep.at[pl.ds(begin, rows)]
                 if last:
-                    add_rows(final(number, color), mine, landings[stage].at[number, color])
+                    add_rows(
+                        sums.at[number, color], mine, landings[stage].at[number, color]
+                    )
+                    handed.extend(store(number, color))
                 else:
                     add_rows(mine, mine, landings[stage].at[number, color])
                     bit = bits[stage + 1]
@@ -1446,7 +1476,24 @@
 
 
 def spread_kernel(
-    parts, planes, h, s, give, keep, h_store, t, block, h_all, current, take, line_landing, *sems
+    parts,
+    planes,
+    h,
+    s,
+    early_a,
+    early_b,
+    give,
+    keep,
+    h_store,
+    t,
+    came_a,
+    came_b,
+    block,
+    h_all,
+    current,
+    take,
+    line_landing,
+    *sems,
 ):
     here = Place(parts, planes)
     wire = Wire(*sems)
@@ -1471,6 +1518,10 @@
     moved = [
         wire.send(s.at[color], t.at[color], {"seq": here.at(bits[-1])})
         for color, bits in enumerate(here.colors())
+    ]
+    moved += [
+        wire.send(source, target, {"seq": here.at(bits[-1])})
+        for source, target, bits in zip((early_a, early_b), (came_a, came_b), here.colors())
     ]
     for step in range(2, planes):
         if step == 3:
@@ -1485,6 +1536,8 @@
         moved[color].wait_recv()
         add_rows(t.at[color], t.at[color], s.at[color])
     swaps.finish(block)
+    for copy in moved[2:]:
+        copy.wait_recv()
     store.wait()
     wire.close()
     swaps.close()
@@ -1502,7 +1555,7 @@
     slope,
     *rest,
 ):
-    sent, came, rest = rest[:2], rest[2:4], rest[4:]
+    sent, came, rest = rest[:4], rest[4:8], rest[8:]
     out, near, far, query_all, pair_all, outer_all, slope_out, *rest = rest
     joined, rest = rest[:4], rest[4:]
     (
@@ -1571,13 +1624,23 @@
     rows = PlaneScatter(wire, here, product, give, take, current, landing, model)
     rows.start()
     loads = []
+    size, early = left.shape[1], sent[0].shape[0]
     for number in range(4):
-        loads.append(
-            (
-                wire.local(sent[number % 2].at[number // 2], left.at[number]),
-                wire.local(came[number % 2].at[number // 2], right.at[number]),
-            )
-        )
+        color = number % 2
+        copies = []
+        for pieces, working in ((sent, left), (came, right)):
+            first, late = pieces[color], pieces[2 + color]
+            if number < 2:
+                copies.append(wire.local(first, working.at[number, pl.ds(0, early)]))
+                copies.append(
+                    wire.local(
+                        late.at[pl.ds(0, size - early)],
+                        working.at[number, pl.ds(early, size - early)],
+                    )
+                )
+            else:
+                copies.append(wire.local(late.at[pl.ds(size - early, size)], working.at[number]))
+        loads.append(copies)
     heads.step(2)
     rows.join()
     rows.stage(0)
@@ -1697,9 +1760,12 @@
             slope_send(number + 1)
         if number < 3:
             join(number + 1)
-    gathers[2].hop(1)
-    for gather in gathers:
-        gather.hops(2)
+        if number == 2:
+            gathers[0].hops(2)
+            gathers[1].hops(2)
+        if number == 3:
+            gathers[2].hop(1)
+    gathers[2].hops(2)
     weights[1].forward()
     for gather in gathers:
         gather.finish()
@@ -1831,7 +1897,7 @@
     key_slope[...] = slope[3:4, 0:width]
 
 
-SENDS, LOCALS = 192, 32
+SENDS, LOCALS = 192, 48
 
 
 def call(kernel, mesh_sizes, number, inputs, in_vmem, outputs, scratch, out_vmem=None):
@@ -2058,13 +2124,17 @@
         ((2, planes - 1, tokens, model), bf16),
     ]
     acts = (2 * planes * tokens, units)
+    early = last_rows // 2
+    early_piece, late_piece = ((early, units), bf16), ((2 * last_rows - early, units), bf16)
     (
-        s_down,
-        s_first,
-        s_second,
-        middle_grad,
         middle_half,
         mid_slope,
+        middle_grad,
+        s_down,
+        early_a,
+        early_b,
+        late_a,
+        late_b,
         down_give,
         down_keep,
     ) = call(
@@ -2073,49 +2143,67 @@
         2,
         (
             normed_mid,
+            mid_gain,
             cot_all.reshape(-1, model),
             middle,
-            mid_gain,
             gate_weight,
             up_weight,
             down_weight,
         ),
-        (True, True, True, True, False, False, False),
-        [((2, last_rows, units), bf16)] * 3
-        + [
-            ((tokens, model), f32),
+        (True, True, False, False, False, False, False),
+        [
             ((tokens, model), bf16),
             ((1, model), f32),
+            ((tokens, model), f32),
+            ((2, last_rows, units), bf16),
+            early_piece,
+            early_piece,
+            late_piece,
+            late_piece,
             (rows_shape, bf16),
             (rows_shape, bf16),
         ],
         [((model, units), bf16)] * 3
-        + [((planes, 2, tokens, model), bf16)]
-        + [(acts, bf16), ((2,) + acts, bf16)]
-        + [((3, 2, quarter, units), bf16)]
+        + [
+            ((2 * planes * tokens, model), bf16),
+            ((tokens, model), f32),
+            ((tokens, model), f32),
+            ((planes, 2, tokens, model), bf16),
+            (acts, bf16),
+            ((2,) + acts, bf16),
+            ((3, 2, quarter, units), bf16),
+            ((3, 2, last_rows, units), bf16),
+        ]
         + [((3, 2, quarter >> stage, units), bf16) for stage in range(halvings)]
         + [(rows_shape, bf16)]
         + line_scratch,
-        [True] * 6 + [False] * 2,
-    )
-
-    middle_all, t_down, down_sum = call(
+        [True] * 2 + [False] * 8,
+    )
+
+    middle_all, t_down, came_a, came_b, down_sum = call(
         spread_kernel,
         sizes,
         4,
-        (middle_half, s_down, down_give, down_keep),
-        (True, True, False, False),
-        [((length, model), bf16), ((2, last_rows, units), bf16), ((tokens, model), f32)],
+        (middle_half, s_down, early_a, early_b, down_give, down_keep),
+        (True, True, False, False, False, False),
+        [
+            ((length, model), bf16),
+            ((2, last_rows, units), bf16),
+            early_piece,
+            early_piece,
+            ((tokens, model), f32),
+        ],
         [((length, model), bf16)] + line_scratch,
-        [False, True, True],
+        [False, True, False, False, True],
     )
 
     def swap(value, bit):
         return lax.ppermute(value, "seq", [(i, i ^ bit) for i in range(parts)])
 
-    *sent, middle_all = lax.optimization_barrier((s_first, s_second, middle_all))
+    late_a, late_b, middle_all = lax.optimization_barrier((late_a, late_b, middle_all))
     bit_orders = ([2 << i for i in range(halvings + 1)], [chips >> i for i in range(halvings + 1)])
-    came = [swap(value, order[-1]) for value, order in zip(sent, bit_orders)]
+    sent = [early_a, early_b, late_a, late_b]
+    came = [came_a, came_b, swap(late_a, bit_orders[0][-1]), swap(late_b, bit_orders[1][-1])]
 
     vmem = pl.BlockSpec(memory_space=pltpu.VMEM)
     halves, head_part, out_part, head_slopes = pl.pallas_call(
@@ -2167,7 +2255,7 @@
         sizes,
         5,
         (halves, head_full, head_part, out_part, t_down, rows_in, slopes, *sent, *came),
-        (True, True, False, False, True, True, True) + (False,) * 4,
+        (True, True, False, False, True, True, True) + (False,) * 8,
         [
             ((tokens, model), f32),
             side,

time: 493 us -> 476 us (0.966); the launches traced: 484 us -> 475 us
  waiting for transfers between devices: 24.2 us -> 10.4 us
    ppermute x14, waiting for transfers between devices: 24.2 us -> 10.4 us  [swap(): return lax.ppermute(value, 'seq', [(i, i ^ bit) for i in range(parts)])]
where the time goes in v9:
time: 476 us; the launch traced here: 475 us
  Pallas kernels  443 us (93%)
  waiting for transfers between devices  10.4 us (2%)
  other arithmetic  8.3 us (2%)
  starting transfers between devices  8.14 us (2%)
    pallas_call x4, Pallas kernels, call(): pl.pallas_call(functools.partial(kernel, *mesh_sizes), out_shape=[jax.Sha...  370 us
    pallas_call x1, Pallas kernels, per_device(): pl.pallas_call(functools.partial(back_kernel, width), out_shape=[jax.Shap...  30 us
    pallas_call x3, Pallas kernels, widen_pieces(): pl.pallas_call(functools.partial(widen_pieces_kernel, count, steps), out_...  26 us
    ppermute x14, waiting for transfers between devices, swap(): return lax.ppermute(value, 'seq', [(i, i ^ bit) for i in range(parts)])  10.4 us
    pallas_call x1, Pallas kernels, widen(): pl.pallas_call(widen_kernel, grid=(rows // step,), out_shape=jax.ShapeDty...  10.3 us
  transfers between devices with their start and end apart: 14, of which 9 were waited for; matrix products, arithmetic and copies ran while one was open for 2% of the time, Pallas kernels for 14%

profile of v9, /device:TPU:0, one launch (start us, length us, event | category | flops | bytes accessed | tf_op | source)
XLA Modules:
  0.0 475.1 jit_solution(5672616099525452855)
XLA Ops:
  0.7 0.6 maximum_bitcast_fusion.rates
  1.2 0.9 concatenate.9
  2.1 0.6 broadcast_in_dim.23.gain
  2.7 91.4 %shard_map.228 = (bf16[1024,2048]{1,0:T(8,128)(2,1)}, bf16[2048,384]{1,0:T(8,128)(2,1)}, bf16[256,2048]{1,0:T(8,128)(2,1)}, f32[1024,384]{1,0:T(8,128)}, bf16[10...) custom-call(bf16[128,2048]{1,0:T(8,128)(2,1)} %bitcast.28, ...), custom_call_target="tpu_custom_call" | custom-call | tf_op jit(solution)/shard_map/pallas_call | solution.py:1912
  94.1 123.8 %shard_map.229 = (bf16[128,2048]{1,0:T(8,128)(2,1)}, f32[1,2048]{1,0:T(1,128)}, f32[128,2048]{1,0:T(8,128)}, bf16[2,512,1024]{2,1,0:T(8,128)(2,1)}, bf16[256,102...) custom-call(bf16[128,2048]{1,0:T(8,128)(2,1)} %get-tuple-element.100, ...), custom_call_target="tpu_custom_call" | custom-call | tf_op jit(solution)/shard_map/pallas_call | solution.py:1912
  217.8 61.2 %shard_map.230 = (bf16[1024,2048]{1,0:T(8,128)(2,1)}, bf16[2,512,1024]{2,1,0:T(8,128)(2,1)}, bf16[256,1024]{1,0:T(8,128)(2,1)}, bf16[256,1024]{1,0:T(8,128)(2,1)}, f32[128,2048]{1,0:T(8,128)}) custom-call(bf16[128,2048]{1,0:T(8,128)(2,1)} %get-tuple-element.105.h, bf16[2,512,1024]{2,1,0:T(8,128)(2,1)} %get-tuple-element.106.s, ...), custom_call_target="tpu_custom_call" | custom-call | tf_op jit(solution)/shard_map/pallas_call | solution.py:1912
  279.1 1.1 collective-permute-start
  280.2 1.0 collective-permute-start.1
  281.2 0.1 pad.16.clone
  281.3 0.0 copy-start.9
  281.3 30.0 %shard_map.231 = (bf16[1024,384]{1,0:T(8,128)(2,1)}, bf16[2048,384]{1,0:T(8,128)(2,1)}, bf16[256,2048]{1,0:T(8,128)(2,1)}, f32[8,384]{1,0:T(8,128)}) custom-call(bf16[1024,2048]{1,0:T(8,128)(2,1)} %get-tuple-element.99.normed, bf16[1024,2048]{1,0:T(8,128)(2,1)} %get-tuple-element.112.middle, bf16[256,2048]{1,0:T(8,128)(2,1)} %get-tuple-element.113.out_slice, ...), custom_call_target="tpu_custom_call" | custom-call | flops 8053063680 | bytes 33554432 | tf_op jit(solution)/shard_map/pallas_call | solution.py:2209
  311.3 0.7 slice.7
  312.0 0.7 slice_reduce_fusion
  312.7 0.1 reshape.64
  312.8 0.0 copy-done.9
  312.8 0.7 maximum_maximum_fusion.slope
  313.5 0.4 collective-permute-done.rest_6_
  313.9 0.7 collective-permute-done.1.rest_7_
  314.6 93.7 %shard_map.232 = (f32[128,2048]{1,0:T(8,128)}, bf16[2048,1024]{1,0:T(8,128)(2,1)}, bf16[2048,1024]{1,0:T(8,128)(2,1)}, bf16[512,2048]{1,0:T(8,128)(2,1)}, bf16[8...) custom-call(bf16[1024,384]{1,0:T(8,128)(2,1)} %get-tuple-element.122, ...), custom_call_target="tpu_custom_call" | custom-call | tf_op jit(solution)/shard_map/pallas_call | solution.py:1912
  408.3 1.1 collective-permute-start.2
  409.4 1.0 collective-permute-start.3
  410.3 2.5 fusion.8
  412.8 10.3 %shard_map.233 = f32[2048,2048]{1,0:T(8,128)} custom-call(bf16[2048,1024]{1,0:T(8,128)(2,1)} %get-tuple-element.144.near, bf16[2048,1024]{1,0:T(8,128)(2,1)} %get-tuple-element.145.far), custom_call_target="tpu_custom_call" | custom-call | bytes 25165824 | tf_op jit(solution)/shard_map/pallas_call | solution.py:1927
  423.1 0.0 collective-permute-start.10
  423.1 0.0 copy-done.2
  423.1 0.5 collective-permute-start.11
  423.6 7.0 %shard_map.234 = (f32[512,2048]{1,0:T(8,128)}, f32[512,512]{1,0:T(8,128)}, f32[512,512]{1,0:T(8,128)}, f32[512,2048]{1,0:T(8,128)}, f32[1,2048]{1,0:T(1,128)}, /...) custom-call(bf16[512,2048]{1,0:T(8,128)(2,1)} %get-tuple-element.147.query, ...), custom_call_target="tpu_custom_call" | custom-call | bytes 16777216 | tf_op jit(solution)/shard_map/pallas_call | solution.py:1981
  430.6 0.0 copy-done
  430.6 0.0 copy-done.1
  430.6 0.0 copy-done.8
  430.7 0.0 copy-start.3
  430.7 0.3 fusion
  431.0 2.4 fusion.6
  433.3 0.9 collective-permute-done.2.refs_1_
  434.2 0.7 collective-permute-done.3.refs_3_
  435.0 0.0 copy-done.3
  435.0 0.0 collective-permute-start.6
  435.0 0.5 collective-permute-start.7
  435.5 0.0 collective-permute-start.8
  435.5 0.0 collective-permute-done.10.refs_2_
  435.5 0.5 collective-permute-start.9
  436.0 0.0 collective-permute-done.11.refs_3_
  436.0 1.0 collective-permute-start.4
  437.0 0.6 collective-permute-done.6.refs_4_
  437.6 1.0 copy-done.6
  438.6 1.0 collective-permute-start.5
  439.6 0.6 pad_add_fusion.1.starts
  440.2 7.0 %shard_map.236.refs_4_ = f32[2048,2048]{1,0:T(8,128)} custom-call(s32[2]{0:T(128)} %pad_add_fusion.1.starts, bf16[512,1024]{1,0:T(8,128)(2,1)} %get-tuple-element.168.refs_0_, bf16[512,1024]{1,0:T(8,128)(2,1)} %get-tuple-element.169.refs_1_, bf16[512,1024]{1,0:T(8,128)(2,1)} %collective-permute-done.10.refs_2_, bf16[512,1024]{1,0:T(8,128)(2,1)} %collective-permute-done.11.refs_3_), custom_call_target="tpu_custom_call" | custom-call | bytes 12582912 | tf_op jit(solution)/shard_map/pallas_call | solution.py:1953
  447.2 0.6 pad_add_fusion.starts
  447.7 0.0 collective-permute-done.7.refs_5_
  447.7 0.0 collective-permute-done.8.refs_6_
  447.7 0.0 collective-permute-done.9.refs_7_
  447.8 12.0 %shard_map.235 = f32[2048,2048]{1,0:T(8,128)} custom-call(s32[4]{0:T(128)} %pad_add_fusion.starts, bf16[512,1024]{1,0:T(8,128)(2,1)} %get-tuple-element.174.refs_0_, bf16[512,1024]{1,0:T(8,128)(2,1)} %collective-permute-done.2.refs_1_, bf16[512,1024]{1,0:T(8,128)(2,1)} %get-tuple-element.176.refs_2_, bf16[512,1024]{1,0:T(8,128)(2,1)} %collective-permute-done.3.refs_3_, ...), custom_call_target="tpu_custom_call" | custom-call | bytes 25165824 | tf_op jit(solution)/shard_map/pallas_call | solution.py:1953
  459.8 1.6 collective-permute-done.4.refs_0_
  461.3 2.5 collective-permute-done.5.refs_1_
  463.8 0.0 collective-permute-start.12
  463.8 0.5 collective-permute-start.13
  464.3 0.7 pad_add_fusion.2.starts
  465.0 1.5 collective-permute-done.12.refs_2_
  466.5 1.6 collective-permute-done.13.refs_3_
  468.1 0.0 copy-done.4
  468.1 0.0 copy-done.5
  468.1 0.0 copy-done.7
  468.1 7.0 %shard_map.237 = f32[2048,2048]{1,0:T(8,128)} custom-call(s32[2]{0:T(128)} %pad_add_fusion.2.starts, bf16[512,1024]{1,0:T(8,128)(2,1)} %copy-done.4, bf16[512,1024]{1,0:T(8,128)(2,1)} %copy-done.5, bf16[512,1024]{1,0:T(8,128)(2,1)} %copy-done.7, bf16[512,1024]{1,0:T(8,128)(2,1)} %collective-permute-done.13.refs_3_, ...), custom_call_target="tpu_custom_call", output_to_operand_aliasing={{}: (5, {})} | custom-call | bytes 12582912 | tf_op jit(solution)/shard_map/pallas_call | solution.py:1953
  (14 shorter events, 0.1 us)
Async XLA Ops:
  279.1 34.8 %collective-permute-start = (bf16[768,1024]{1,0:T(8,128)(2,1)}, bf16[768,1024]{1,0:T(8,128)(2,1)}, u32[]{:S(2)}, u32[]{:S(2)}) collective-permute-start(bf16[768,1024]{1,0:T(8,128)(2,1)} %get-tuple-element.129.rest_2_), channel_id=1, source_target_pairs={{0,16},{4,20},{8,24},{12,28},{16,0},{20,4},{24,8},{28,12},{1,17},{... | collective-permute-start | bytes 4718600 | tf_op jit(solution)/shard_map/ppermute | solution.py:2201
  280.2 34.4 %collective-permute-start.1 = (bf16[768,1024]{1,0:T(8,128)(2,1)}, bf16[768,1024]{1,0:T(8,128)(2,1)}, u32[]{:S(2)}, u32[]{:S(2)}) collective-permute-start(bf16[768,1024]{1,0:T(8,128)(2,1)} %get-tuple-element.130.rest_3_), channel_id=1, source_target_pairs={{0,8},{4,12},{8,0},{12,4},{16,24},{20,28},{24,16},{28,20},{1,9},{5... | collective-permute-start | bytes 4718600 | tf_op jit(solution)/shard_map/ppermute | solution.py:2201
  281.3 31.6 %copy-start.9 = (f32[1,2048]{1,0:T(1,128)S(1)}, f32[1,2048]{1,0:T(1,128)}, u32[]{:S(2)}) copy-start(f32[1,2048]{1,0:T(1,128)} %get-tuple-element.127) | copy-start | bytes 24580
  408.3 25.9 %collective-permute-start.2 = (bf16[512,1024]{1,0:T(8,128)(2,1)}, bf16[512,1024]{1,0:T(8,128)(2,1)}, u32[]{:S(2)}, u32[]{:S(2)}) collective-permute-start(bf16[512,1024]{1,0:T(8,128)(2,1)} %get-tuple-element.174.refs_0_), channel_id=1, source_target_pairs={{0,8},{4,12},{8,0},{12,4},{16,24},{20,28},{24,16},{28,20},{1,9},{5... | collective-permute-start | bytes 3145736 | tf_op jit(solution)/shard_map/ppermute | solution.py:2201
  409.4 25.6 %collective-permute-start.3 = (bf16[512,1024]{1,0:T(8,128)(2,1)}, bf16[512,1024]{1,0:T(8,128)(2,1)}, u32[]{:S(2)}, u32[]{:S(2)}) collective-permute-start(bf16[512,1024]{1,0:T(8,128)(2,1)} %get-tuple-element.176.refs_2_), channel_id=1, source_target_pairs={{0,16},{4,20},{8,24},{12,28},{16,0},{20,4},{24,8},{28,12},{1,17},{... | collective-permute-start | bytes 3145736 | tf_op jit(solution)/shard_map/ppermute | solution.py:2201
  412.8 10.3 %copy-start.2 = (bf16[512,1024]{1,0:T(8,128)(2,1)S(1)}, bf16[512,1024]{1,0:T(8,128)(2,1)}, u32[]{:S(2)}) copy-start(bf16[512,1024]{1,0:T(8,128)(2,1)} %get-tuple-element.169.refs_1_) | copy-start | bytes 3145732
  423.1 12.4 %collective-permute-start.10 = (bf16[512,1024]{1,0:T(8,128)(2,1)}, bf16[512,1024]{1,0:T(8,128)(2,1)}, u32[]{:S(2)}, u32[]{:S(2)}) collective-permute-start(bf16[512,1024]{1,0:T(8,128)(2,1)} %get-tuple-element.168.refs_0_), channel_id=1, source_target_pairs={{0,4},{4,0},{8,12},{12,8},{16,20},{20,16},{24,28},{28,24},{1,5},{5... | collective-permute-start | bytes 3145736 | tf_op jit(solution)/shard_map/ppermute | solution.py:2201
  423.1 12.9 %collective-permute-start.11 = (bf16[512,1024]{1,0:T(8,128)(2,1)S(1)}, bf16[512,1024]{1,0:T(8,128)(2,1)}, u32[]{:S(2)}, u32[]{:S(2)}) collective-permute-start(bf16[512,1024]{1,0:T(8,128)(2,1)S(1)} %copy-done.2), channel_id=1, source_target_pairs={{0,4},{4,0},{8,12},{12,8},{16,20},{20,16},{24,28},{28,24},{1,5},{5... | collective-permute-start | bytes 3145736 | tf_op jit(solution)/shard_map/ppermute | solution.py:2201
  423.6 7.1 %copy-start = (bf16[1,128,2048]{2,1,0:T(8,128)(2,1)S(1)}, bf16[1,128,2048]{2,1,0:T(8,128)(2,1)}, u32[]{:S(2)}) copy-start(bf16[1,128,2048]{2,1,0:T(8,128)(2,1)} %param.13) | copy-start | bytes 1572868
  423.6 7.1 %copy-start.1 = (f32[128,2048]{1,0:T(8,128)S(1)}, f32[128,2048]{1,0:T(8,128)}, u32[]{:S(2)}) copy-start(f32[128,2048]{1,0:T(8,128)} %get-tuple-element.156) | copy-start | bytes 3145732
  423.6 7.1 %copy-start.8 = (f32[2048]{0:T(1024)S(1)}, f32[2048]{0:T(1024)}, u32[]{:S(2)}) copy-start(f32[2048]{0:T(1024)} %param.15) | copy-start | bytes 24580
  430.7 4.3 copy-start.3
  435.0 2.7 collective-permute-start.6
  435.0 12.8 %collective-permute-start.7 = (bf16[512,1024]{1,0:T(8,128)(2,1)}, bf16[512,1024]{1,0:T(8,128)(2,1)}, u32[]{:S(2)}, u32[]{:S(2)}) collective-permute-start(bf16[512,1024]{1,0:T(8,128)(2,1)} %collective-permute-done.2.refs_1_), channel_id=1, source_target_pairs={{0,4},{4,0},{8,12},{12,8},{16,20},{20,16},{24,28},{28,24},{1,5},{5... | collective-permute-start | bytes 3145736 | tf_op jit(solution)/shard_map/ppermute | solution.py:2201
  435.5 12.3 %collective-permute-start.8 = (bf16[512,1024]{1,0:T(8,128)(2,1)}, bf16[512,1024]{1,0:T(8,128)(2,1)}, u32[]{:S(2)}, u32[]{:S(2)}) collective-permute-start(bf16[512,1024]{1,0:T(8,128)(2,1)} %get-tuple-element.176.refs_2_), channel_id=1, source_target_pairs={{0,4},{4,0},{8,12},{12,8},{16,20},{20,16},{24,28},{28,24},{1,5},{5... | collective-permute-start | bytes 3145736 | tf_op jit(solution)/shard_map/ppermute | solution.py:2201
  435.5 12.3 %collective-permute-start.9 = (bf16[512,1024]{1,0:T(8,128)(2,1)}, bf16[512,1024]{1,0:T(8,128)(2,1)}, u32[]{:S(2)}, u32[]{:S(2)}) collective-permute-start(bf16[512,1024]{1,0:T(8,128)(2,1)} %collective-permute-done.3.refs_3_), channel_id=1, source_target_pairs={{0,4},{4,0},{8,12},{12,8},{16,20},{20,16},{24,28},{28,24},{1,5},{5... | collective-permute-start | bytes 3145736 | tf_op jit(solution)/shard_map/ppermute | solution.py:2201
  436.0 25.3 %collective-permute-start.4 = (bf16[512,1024]{1,0:T(8,128)(2,1)}, bf16[512,1024]{1,0:T(8,128)(2,1)S(1)}, u32[]{:S(2)}, u32[]{:S(2)}) collective-permute-start(bf16[512,1024]{1,0:T(8,128)(2,1)} %get-tuple-element.168.refs_0_), channel_id=1, source_target_pairs={{0,8},{4,12},{8,0},{12,4},{16,24},{20,28},{24,16},{28,20},{1,9},{5... | collective-permute-start | bytes 3145736 | tf_op jit(solution)/shard_map/ppermute | solution.py:2201
  437.6 1.0 copy-start.6
  438.6 25.2 %collective-permute-start.5 = (bf16[512,1024]{1,0:T(8,128)(2,1)S(1)}, bf16[512,1024]{1,0:T(8,128)(2,1)S(1)}, u32[]{:S(2)}, u32[]{:S(2)}) collective-permute-start(bf16[512,1024]{1,0:T(8,128)(2,1)S(1)} %copy-done.2), channel_id=1, source_target_pairs={{0,16},{4,20},{8,24},{12,28},{16,0},{20,4},{24,8},{28,12},{1,17},{... | collective-permute-start | bytes 3145736 | tf_op jit(solution)/shard_map/ppermute | solution.py:2201
  461.3 6.8 %copy-start.4 = (bf16[512,1024]{1,0:T(8,128)(2,1)}, bf16[512,1024]{1,0:T(8,128)(2,1)S(1)}, u32[]{:S(2)}) copy-start(bf16[512,1024]{1,0:T(8,128)(2,1)S(1)} %collective-permute-done.4.refs_0_) | copy-start | bytes 3145732
  463.8 4.3 copy-start.5
  463.8 2.7 collective-permute-start.12
  463.8 4.3 collective-permute-start.13
  466.5 1.6 copy-start.7
